TPU v7x, 16 devices: a whole 2x2x2 slice. The times are simulated.
16 devices in a mesh: pp: 4 (over z, y), ep: 4 (over x, core).
Axes of the slice: x: 2, y: 2, z: 2, core: 2. Of those that a mesh axis runs over, the one named last changes fastest.
Arguments:
- x_fwd: bfloat16 [4, 16384, 256], P('pp', 'ep')
- ids_fwd: int32 [4, 16384, 4], P('pp', 'ep')
- slots_fwd: int32 [4, 16384, 4], P('pp', 'ep')
- gates_fwd: bfloat16 [4, 16384, 4], P('pp', 'ep')
- x_saved: bfloat16 [4, 16384, 256], P('pp', 'ep')
- grad_in: bfloat16 [4, 16384, 256], P('pp', 'ep')
- ids_bwd: int32 [4, 16384, 4], P('pp', 'ep')
- slots_bwd: int32 [4, 16384, 4], P('pp', 'ep')
- gates_bwd: bfloat16 [4, 16384, 4], P('pp', 'ep')
- w_one: bfloat16 [4, 256, 256], P('pp')
- w_two: bfloat16 [4, 256, 256], P('pp')
- w_gate: bfloat16 [4, 32, 256, 256], P('pp', 'ep')
- w_up: bfloat16 [4, 32, 256, 256], P('pp', 'ep')
- w_down: bfloat16 [4, 32, 256, 256], P('pp', 'ep')
Outputs:
- output 1: bfloat16 [4, 16384, 256], P('pp', 'ep')
- output 2: bfloat16 [4, 16384, 256], P('pp', 'ep')
- output 3: float32 [4, 32, 256, 256], P('pp', 'ep')
- output 4: float32 [4, 32, 256, 256], P('pp', 'ep')
- output 5: float32 [4, 32, 256, 256], P('pp', 'ep')
All inputs are finite; a program needn't handle non-finite values.
Results may differ from a plain program's by a relative error of at most 0.0104285.
Values are sent between devices in bfloat16 or wider.
A program may use at most 1 GiB of HBM per device.

v0:
```python
import jax
import jax.numpy as jnp
from jax import lax
from jax.sharding import PartitionSpec as P

NORM_EPS = 1e-6


def rms_norm(values):
    return values * lax.rsqrt(jnp.mean(values * values, axis=-1, keepdims=True) + NORM_EPS)


def silu_grad(values):
    sigmoid_vals = jax.nn.sigmoid(values)
    return sigmoid_vals * (1.0 + values * (1.0 - sigmoid_vals))


def capacity(tok_rows, top_k, n_experts):
    return 8 * ((2 * tok_rows * top_k + 8 * n_experts - 1) // (8 * n_experts))


def dense_forward(x_rows, w_one, w_two):
    normed = rms_norm(x_rows.astype(jnp.float32)).astype(jnp.bfloat16)
    hidden_pre = jnp.dot(normed, w_one, preferred_element_type=jnp.float32)
    dense_act = jax.nn.silu(hidden_pre).astype(jnp.bfloat16)
    dense_out = jnp.dot(dense_act, w_two, preferred_element_type=jnp.float32)
    return (x_rows.astype(jnp.float32) + dense_out).astype(jnp.bfloat16), hidden_pre


def dense_backward(x_rows, hidden_pre, w_one, w_two, grad_h):
    _, norm_vjp = jax.vjp(rms_norm, x_rows.astype(jnp.float32))
    grad_act = jnp.einsum("th,fh->tf", grad_h.astype(jnp.bfloat16), w_two, preferred_element_type=jnp.float32)
    grad_pre = (grad_act * silu_grad(hidden_pre)).astype(jnp.bfloat16)
    grad_norm = jnp.einsum("tf,hf->th", grad_pre, w_one, preferred_element_type=jnp.float32)
    return grad_h + norm_vjp(grad_norm)[0]


def expert_forward(buf_rows, w_gate, w_up, w_down):
    pre_gate = jnp.einsum("ech,ehf->ecf", buf_rows, w_gate, preferred_element_type=jnp.float32)
    pre_up = jnp.einsum("ech,ehf->ecf", buf_rows, w_up, preferred_element_type=jnp.float32)
    expert_act = (jax.nn.silu(pre_gate) * pre_up).astype(jnp.bfloat16)
    return jnp.einsum("ecf,efh->ech", expert_act, w_down, preferred_element_type=jnp.float32).astype(jnp.bfloat16)


def expert_backward(buf_rows, grad_out, w_gate, w_up, w_down):
    pre_gate = jnp.einsum("ech,ehf->ecf", buf_rows, w_gate, preferred_element_type=jnp.float32)
    pre_up = jnp.einsum("ech,ehf->ecf", buf_rows, w_up, preferred_element_type=jnp.float32)
    silu_gate = jax.nn.silu(pre_gate)
    expert_act = (silu_gate * pre_up).astype(jnp.bfloat16)
    dw_down = jnp.einsum("ecf,ech->efh", expert_act, grad_out, preferred_element_type=jnp.float32)
    grad_act = jnp.einsum("ech,efh->ecf", grad_out, w_down, preferred_element_type=jnp.float32).astype(jnp.bfloat16).astype(jnp.float32)
    grad_gate = (grad_act * pre_up * silu_grad(pre_gate)).astype(jnp.bfloat16)
    grad_up = (grad_act * silu_gate).astype(jnp.bfloat16)
    dw_gate = jnp.einsum("ech,ecf->ehf", buf_rows, grad_gate, preferred_element_type=jnp.float32)
    dw_up = jnp.einsum("ech,ecf->ehf", buf_rows, grad_up, preferred_element_type=jnp.float32)
    grad_rows = jnp.einsum("ecf,ehf->ech", grad_gate, w_gate, preferred_element_type=jnp.float32) + jnp.einsum("ecf,ehf->ech", grad_up, w_up, preferred_element_type=jnp.float32)
    return grad_rows.astype(jnp.bfloat16), dw_gate, dw_up, dw_down


def route_maps(expert_ids, slot_ids, n_experts, cap_rows):
    tok_rows = expert_ids.shape[0]
    row_index = jnp.where(slot_ids >= 0, expert_ids * cap_rows + slot_ids, n_experts * cap_rows)
    token_ids = jnp.broadcast_to(jnp.arange(tok_rows, dtype=jnp.int32)[:, None], expert_ids.shape)
    token_of_row = jnp.full((n_experts * cap_rows,), tok_rows, jnp.int32).at[row_index.reshape(-1)].set(token_ids.reshape(-1), mode="drop")
    return row_index, token_of_row


def solution(mesh):
    stages = mesh.shape["pp"]
    ep_size = mesh.shape["ep"]
    next_perm = [(stage_idx, (stage_idx + 1) % stages) for stage_idx in range(stages)]
    prev_perm = [(stage_idx, (stage_idx - 1) % stages) for stage_idx in range(stages)]
    tok_spec = P("pp", "ep", None)
    dense_spec = P("pp", None, None)
    expert_spec = P("pp", "ep", None, None)

    def device_step(x_fwd, ids_fwd, slots_fwd, gates_fwd, x_saved, grad_in, ids_bwd, slots_bwd, gates_bwd, w_one, w_two, w_gate, w_up, w_down):
        x_fwd, ids_fwd, slots_fwd, gates_fwd = x_fwd[0], ids_fwd[0], slots_fwd[0], gates_fwd[0]
        x_saved, grad_in, ids_bwd, slots_bwd, gates_bwd = x_saved[0], grad_in[0], ids_bwd[0], slots_bwd[0], gates_bwd[0]
        w_one, w_two, w_gate, w_up, w_down = w_one[0], w_two[0], w_gate[0], w_up[0], w_down[0]
        tok_rows, top_k = ids_fwd.shape
        hidden = x_fwd.shape[1]
        n_experts = w_gate.shape[0] * ep_size
        cap_rows = capacity(tok_rows, top_k, n_experts)
        n_rows = n_experts * cap_rows

        h_fwd, _ = dense_forward(x_fwd, w_one, w_two)
        xn_fwd = rms_norm(h_fwd.astype(jnp.float32)).astype(jnp.bfloat16)
        row_fwd, tok_fwd = route_maps(ids_fwd, slots_fwd, n_experts, cap_rows)
        send_fwd = jnp.take(xn_fwd, tok_fwd, axis=0, mode="fill", fill_value=0).reshape(n_experts, cap_rows, hidden)
        recv_fwd = lax.all_to_all(send_fwd, "ep", 0, 1, tiled=True)
        out_fwd = expert_forward(recv_fwd, w_gate, w_up, w_down)
        back_fwd = lax.all_to_all(out_fwd, "ep", 1, 0, tiled=True).reshape(n_rows, hidden)
        routed = jnp.take(back_fwd, row_fwd, axis=0, mode="fill", fill_value=0)
        mix_sum = jnp.einsum("tr,trh->th", gates_fwd, routed, preferred_element_type=jnp.float32)
        y_out = (h_fwd.astype(jnp.float32) + mix_sum).astype(jnp.bfloat16)

        h_bwd, hidden_pre = dense_forward(x_saved, w_one, w_two)
        xn_bwd = rms_norm(h_bwd.astype(jnp.float32)).astype(jnp.bfloat16)
        row_bwd, tok_bwd = route_maps(ids_bwd, slots_bwd, n_experts, cap_rows)
        gate_of_row = jnp.zeros((n_rows,), jnp.bfloat16).at[row_bwd.reshape(-1)].set(gates_bwd.reshape(-1), mode="drop")
        send_rows = jnp.take(xn_bwd, tok_bwd, axis=0, mode="fill", fill_value=0).reshape(n_experts, cap_rows, hidden)
        send_grad = (jnp.take(grad_in, tok_bwd, axis=0, mode="fill", fill_value=0) * gate_of_row[:, None]).reshape(n_experts, cap_rows, hidden)
        recv_rows = lax.all_to_all(send_rows, "ep", 0, 1, tiled=True)
        recv_grad = lax.all_to_all(send_grad, "ep", 0, 1, tiled=True)
        grad_rows, dw_gate, dw_up, dw_down = expert_backward(recv_rows, recv_grad, w_gate, w_up, w_down)
        back_grad = lax.all_to_all(grad_rows, "ep", 1, 0, tiled=True).reshape(n_rows, hidden)
        grad_xn = jnp.sum(jnp.take(back_grad, row_bwd, axis=0, mode="fill", fill_value=0), axis=1, dtype=jnp.float32)
        _, rms_vjp = jax.vjp(rms_norm, h_bwd.astype(jnp.float32))
        grad_h = grad_in.astype(jnp.float32) + rms_vjp(grad_xn)[0]
        grad_x = dense_backward(x_saved, hidden_pre, w_one, w_two, grad_h).astype(jnp.bfloat16)

        y_next = lax.ppermute(y_out, "pp", next_perm)
        dx_prev = lax.ppermute(grad_x, "pp", prev_perm)
        return y_next[None], dx_prev[None], dw_gate[None], dw_up[None], dw_down[None]

    in_specs = (tok_spec,) * 9 + (dense_spec, dense_spec, expert_spec, expert_spec, expert_spec)
    out_specs = (tok_spec, tok_spec, expert_spec, expert_spec, expert_spec)
    return jax.shard_map(device_step, mesh=mesh, in_specs=in_specs, out_specs=out_specs, check_vma=False)
```

profile of v0, /device:TPU:0, one launch (start us, length us, event | category | flops | bytes accessed | tf_op | source)
XLA Modules:
  0.0 1665.5 jit_solution(4516351147353102489)
XLA Ops:
  7.2 61.0 %scatter_custom_fusion.1 = s32[32768]{0:T(1024)S(1)} fusion(s32[16384]{0:T(1024)} %bitcast.173, s32[16384]{0:T(1024)S(1)} %reshape.289, s32[]{:T(128)} %constant.30.clone.1), kind=kCustom, calls=%fused_computation.111 | custom fusion | bytes 131584 | tf_op jit(solution)/shard_map/scatter | solution.py:64
  80.3 123.5 %gather_fusion.3 = bf16[32768,256]{1,0:T(8,128)(2,1)} fusion(bf16[4096,256]{1,0:T(8,128)(2,1)} %copy.72, s32[32768]{0:T(1024)S(1)} %fusion.75), kind=kCustom, calls=%fused_computation.3.clone | custom fusion | bytes 33685504 | tf_op jit(solution)/shard_map/jit(_take)/gather | solution.py:102
  203.8 129.4 %gather_fusion.2 = bf16[32768,256]{1,0:T(8,128)(2,1)} fusion(bf16[4096,256]{1,0:T(8,128)(2,1)S(1)} %bitcast.158, s32[32768]{0:T(1024)S(1)} %fusion.75), kind=kCustom, calls=%fused_computation.2.clone | custom fusion | bytes 33685504 | tf_op jit(solution)/shard_map/jit(_take)/gather | solution.py:103
  335.6 112.8 %scatter_custom_fusion.2 = bf16[32768]{0:T(1024)(128)(2,1)S(1)} fusion(s32[16384]{0:T(1024)} %bitcast.174, bf16[16384]{0:T(1024)(128)(2,1)S(1)} %reshape.297, bf16[]{:T(256)} %constant.34.clone.1), kind=kCustom, calls=%fused_computation.120 | custom fusion | bytes 66048 | tf_op jit(solution)/shard_map/scatter | solution.py:101
  448.5 27.5 %select_multiply_fusion = (bf16[32768,256]{1,0:T(8,128)(2,1)}, bf16[32768,256]{1,0:T(8,128)(2,1)}) fusion(bf16[32768,256]{1,0:T(8,128)(2,1)} %gather_fusion.2, pred[32768]{0:T(1024)(128)(4,1)S(1)} %compare_and_fusion, bf16[32768]{0:T(1024)(128)(2,1)S(1)} %scatter_custom_fusion.2, bf16[32768,256]{1,0:T(8,128)(2,1)} %gather_fusion.3), kind=kLoop, calls=%fused_computation.20 | loop fusion | flops 25165824 | bytes 67207168 | tf_op jit(solution)/shard_map/mul | solution.py:103
  503.3 163.3 %all-to-all-done.3 = bf16[32,1024,256]{2,1,0:T(8,128)(2,1)} async-done(((bf16[32,1024,256]{2,1,0:T(8,128)(2,1)}), bf16[32,1024,256]{2,1,0:T(8,128)(2,1)}, u32[]{:S(2)}, u32[]{:S(2)}) %all-to-all-start.3) | async-done | bytes 16777248 | tf_op jit(solution)/shard_map/all_to_all | solution.py:104
  673.8 60.4 %scatter_custom_fusion = s32[32768]{0:T(1024)S(1)} fusion(s32[16384]{0:T(1024)S(1)} %bitcast.175, s32[16384]{0:T(1024)S(1)} %reshape.289, s32[]{:T(128)} %constant.30.clone.1), kind=kCustom, calls=%fused_computation.113 | custom fusion | bytes 131076 | tf_op jit(solution)/shard_map/scatter | solution.py:64
  734.2 129.4 %gather_fusion = bf16[32768,256]{1,0:T(8,128)(2,1)} fusion(bf16[4096,256]{1,0:T(8,128)(2,1)S(1)} %copy.60, s32[32768]{0:T(1024)S(1)} %fusion.74), kind=kCustom, calls=%fused_computation.clone | custom fusion | bytes 33685504 | tf_op jit(solution)/shard_map/jit(_take)/gather | solution.py:90
  863.7 19.0 %broadcast_select_fusion.1 = bf16[32768,256]{1,0:T(8,128)(2,1)} fusion(bf16[32768,256]{1,0:T(8,128)(2,1)} %gather_fusion, pred[32768]{0:T(1024)(128)(4,1)S(1)} %compare_and_fusion.1), kind=kLoop, calls=%fused_computation.23 | loop fusion | flops 8388608 | bytes 33587200 | tf_op jit(solution)/shard_map/jit(_take)/select_n | solution.py:90
  934.1 16.6 fusion.60
  950.6 40.8 %fusion.2 = (bf16[8,4096,256]{2,1,0:T(8,128)(2,1)}, bf16[8,4096,256]{2,1,0:T(8,128)(2,1)}) fusion(f32[8,4096,256]{2,1,0:T(8,128)} %fusion.60, f32[8,4096,256]{2,1,0:T(8,128)} %fusion.54, bf16[8,4096,256]{2,1,0:T(8,128)(2,1)} %bitcast.170, bf16[1,8,256,256]{3,2,1,0:T(8,128)(2,1)S(1)} %copy-done.32), kind=kOutput, calls=%fused_computation.12 | convolution fusion | flops 4420796416 | bytes 118489088 | tf_op jit(solution)/shard_map/ech,efh->ecf/dot_general | solution.py:51
  991.5 16.6 fusion.58
  1008.1 23.8 %add_convert_fusion = bf16[8,4096,256]{2,1,0:T(8,128)(2,1)} fusion(f32[8,4096,256]{2,1,0:T(8,128)} %fusion.58, bf16[8,4096,256]{2,1,0:T(8,128)(2,1)} %get-tuple-element.26, bf16[1,8,256,256]{3,2,1,0:T(8,128)(2,1)S(1)} %copy-done.10), kind=kOutput, calls=%fused_computation.14 | convolution fusion | flops 4311744512 | bytes 68157440 | tf_op jit(solution)/shard_map/ecf,ehf->ech/dot_general | solution.py:56
  1031.9 17.9 %copy.74 = bf16[8,4096,256]{2,0,1:T(8,128)(2,1)} copy(bf16[8,4096,256]{2,1,0:T(8,128)(2,1)} %add_convert_fusion) | data formatting | bytes 33554432 | tf_op jit(solution)/shard_map/convert_element_type | solution.py:57
  1049.8 36.7 %all-to-all-done = bf16[32,1024,256]{2,1,0:T(8,128)(2,1)} async-done(((bf16[32,1024,256]{2,1,0:T(8,128)(2,1)}), bf16[32,1024,256]{2,1,0:T(8,128)(2,1)}, u32[]{:S(2)}, u32[]{:S(2)}) %all-to-all-start) | async-done | bytes 16777248 | tf_op jit(solution)/shard_map/all_to_all | solution.py:91
  1107.3 16.5 fusion.62
  1123.9 24.6 %fusion.6 = bf16[8,4096,256]{2,1,0:T(8,128)(2,1)} fusion(f32[8,4096,256]{2,1,0:T(8,128)} %fusion.62, bf16[8,4096,256]{2,1,0:T(8,128)(2,1)} %bitcast.166, bf16[1,8,256,256]{3,2,1,0:T(8,128)(2,1)S(1)} %copy-done.32, bf16[1,8,256,256]{3,2,1,0:T(8,128)(2,1)S(1)} %copy-done.10), kind=kOutput, calls=%fused_computation.26 | convolution fusion | flops 8648654848 | bytes 69206016 | tf_op jit(solution)/shard_map/ecf,efh->ech/dot_general | solution.py:42
  1148.5 17.9 %copy.62 = bf16[8,4096,256]{2,0,1:T(8,128)(2,1)} copy(bf16[8,4096,256]{2,1,0:T(8,128)(2,1)} %fusion.6) | data formatting | bytes 33554432 | tf_op jit(solution)/shard_map/convert_element_type | solution.py:42
  1166.3 109.9 %all-to-all-done.4 = bf16[8,4096,256]{2,0,1:T(8,128)(2,1)} async-done(((bf16[8,4096,256]{2,0,1:T(8,128)(2,1)}), bf16[8,4096,256]{2,0,1:T(8,128)(2,1)}, u32[]{:S(2)}, u32[]{:S(2)}) %all-to-all-start.4) | async-done | bytes 16777248 | tf_op jit(solution)/shard_map/all_to_all | solution.py:107
  1295.5 29.4 %fusion.50 = f32[1,8,256,256]{3,2,1,0:T(8,128)} fusion(bf16[8,4096,256]{2,1,0:T(8,128)(2,1)} %bitcast.171, f32[8,4096,256]{2,1,0:T(8,128)} %fusion.54, f32[8,4096,256]{2,1,0:T(8,128)} %fusion.60), kind=kOutput, calls=%fused_computation.78 | convolution fusion | flops 4345298944 | bytes 85983232 | tf_op jit(solution)/shard_map/ecf,ech->efh/dot_general | solution.py:50
  1340.8 69.1 %gather_fusion.4 = bf16[16384,256]{1,0:T(8,128)(2,1)} fusion(bf16[32768,256]{1,0:T(8,128)(2,1)} %bitcast.159, s32[16384]{0:T(1024)S(1)} %broadcast_clamp_fusion), kind=kCustom, calls=%fused_computation.4.clone | custom fusion | bytes 16842752 | tf_op jit(solution)/shard_map/jit(_take)/gather | solution.py:108
  1422.3 26.5 %convert_reduce_fusion = f32[4096,256]{1,0:T(8,128)} fusion(bf16[4096,4,256]{2,1,0:T(4,128)(2,1)} %reshape.321, pred[4096,4]{1,0:T(8,128)(4,1)S(1)} %copy.66), kind=kLoop, calls=%fused_computation.21 | loop fusion | flops 11534336 | bytes 12599296 | tf_op jit(solution)/shard_map/reduce_sum | solution.py:108
  1495.1 69.1 %gather_fusion.1 = bf16[16384,256]{1,0:T(8,128)(2,1)} fusion(bf16[32768,256]{1,0:T(8,128)(2,1)} %bitcast.160, s32[16384]{0:T(1024)S(1)} %broadcast_clamp_fusion.1), kind=kCustom, calls=%fused_computation.1.clone | custom fusion | bytes 16842752 | tf_op jit(solution)/shard_map/jit(_take)/gather | solution.py:94
  1577.0 26.9 %multiply_reduce_fusion = f32[4096,256]{1,0:T(8,128)} fusion(f32[4096,4]{1,0:T(8,128)S(1)} %copy-done.9, bf16[4096,4,256]{2,1,0:T(4,128)(2,1)} %reshape.313, pred[4096,4]{1,0:T(8,128)(4,1)S(1)} %copy-done.11), kind=kLoop, calls=%fused_computation.19 | loop fusion | flops 15728640 | bytes 12664832
  (145 shorter events, 295.3 us)
Async XLA Ops:
  0.6 933.4 %copy-start = (bf16[1,8,256,256]{3,2,1,0:T(8,128)(2,1)S(1)}, bf16[1,8,256,256]{3,2,1,0:T(8,128)(2,1)}, u32[]{:S(2)}) copy-start(bf16[1,8,256,256]{3,2,1,0:T(8,128)(2,1)} %param.29) | copy-start | bytes 3145732
  5.5 67.6 %copy-start.22 = (bf16[1,256,256]{2,1,0:T(8,128)(2,1)S(1)}, bf16[1,256,256]{2,1,0:T(8,128)(2,1)}, u32[]{:S(2)}) copy-start(bf16[1,256,256]{2,1,0:T(8,128)(2,1)} %param.27) | copy-start | bytes 393220
  80.3 123.5 %copy-start.2 = (bf16[1,4096,256]{2,1,0:T(8,128)(2,1)S(1)}, bf16[1,4096,256]{2,1,0:T(8,128)(2,1)}, u32[]{:S(2)}) copy-start(bf16[1,4096,256]{2,1,0:T(8,128)(2,1)} %param.23) | copy-start | bytes 6291460
  203.8 129.4 %copy-start.30 = (bf16[1,4096,4]{1,2,0:T(4,128)(2,1)S(1)}, bf16[1,4096,4]{1,2,0:T(4,128)(2,1)}, u32[]{:S(2)}) copy-start(bf16[1,4096,4]{1,2,0:T(4,128)(2,1)} %param.26) | copy-start | bytes 98308
  475.9 190.6 %all-to-all-start.3 = ((bf16[32,1024,256]{2,1,0:T(8,128)(2,1)}), bf16[32,1024,256]{2,1,0:T(8,128)(2,1)}, u32[]{:S(2)}, u32[]{:S(2)}) async-start(bf16[32,1024,256]{2,1,0:T(8,128)(2,1)} %bitcast.168), calls=%async_computation.3 | async-start | bytes 33554432 | tf_op jit(solution)/shard_map/all_to_all | solution.py:104
  490.6 6.7 copy-start.26
  490.6 6.7 copy-start.27
  498.0 168.5 %copy-start.14 = (s32[1,4096,4]{1,2,0:T(4,128)}, s32[1,4096,4]{1,2,0:T(4,128)S(1)}, u32[]{:S(2)}) copy-start(s32[1,4096,4]{1,2,0:T(4,128)S(1)} %get-tuple-element.25) | copy-start | bytes 196612
  666.6 229.8 %all-to-all-start.2 = ((bf16[32,1024,256]{2,1,0:T(8,128)(2,1)}), bf16[32,1024,256]{2,1,0:T(8,128)(2,1)}, u32[]{:S(2)}, u32[]{:S(2)}) async-start(bf16[32,1024,256]{2,1,0:T(8,128)(2,1)} %bitcast.167), calls=%async_computation.2 | async-start | bytes 33554432 | tf_op jit(solution)/shard_map/all_to_all | solution.py:105
  896.4 190.0 %all-to-all-start = ((bf16[32,1024,256]{2,1,0:T(8,128)(2,1)}), bf16[32,1024,256]{2,1,0:T(8,128)(2,1)}, u32[]{:S(2)}, u32[]{:S(2)}) async-start(bf16[32,1024,256]{2,1,0:T(8,128)(2,1)} %bitcast.169), calls=%async_computation | async-start | bytes 33554432 | tf_op jit(solution)/shard_map/all_to_all | solution.py:91
  903.7 13.9 copy-start.10
  934.1 16.6 copy-start.32
  1086.4 189.8 %all-to-all-start.4 = ((bf16[8,4096,256]{2,0,1:T(8,128)(2,1)}), bf16[8,4096,256]{2,0,1:T(8,128)(2,1)}, u32[]{:S(2)}, u32[]{:S(2)}) async-start(bf16[8,4096,256]{2,0,1:T(8,128)(2,1)} %copy.74), calls=%async_computation.4 | async-start | bytes 33554432 | tf_op jit(solution)/shard_map/all_to_all | solution.py:107
  1166.3 117.1 %copy-start.13 = (s32[1,4096,4]{1,2,0:T(4,128)S(1)}, s32[1,4096,4]{1,2,0:T(4,128)}, u32[]{:S(2)}) copy-start(s32[1,4096,4]{1,2,0:T(4,128)} %copy-done.12) | copy-start | bytes 196612
  1166.3 117.2 %copy-start.3 = (bf16[1,4096,256]{2,1,0:T(8,128)(2,1)S(1)}, bf16[1,4096,256]{2,1,0:T(8,128)(2,1)}, u32[]{:S(2)}) copy-start(bf16[1,4096,256]{2,1,0:T(8,128)(2,1)} %param.23) | copy-start | bytes 6291460
  1276.3 202.9 %all-to-all-start.1 = ((bf16[8,4096,256]{2,0,1:T(8,128)(2,1)}), bf16[8,4096,256]{2,0,1:T(8,128)(2,1)}, u32[]{:S(2)}, u32[]{:S(2)}) async-start(bf16[8,4096,256]{2,0,1:T(8,128)(2,1)} %copy.62), calls=%async_computation.1 | async-start | bytes 33554432 | tf_op jit(solution)/shard_map/all_to_all | solution.py:93
  1287.2 6.3 copy-start.31
  1458.2 9.7 copy-start.19
  1458.2 9.8 copy-start.17
  1475.8 168.5 %collective-permute-start.1 = (bf16[4096,256]{0,1:T(8,128)(2,1)}, bf16[4096,256]{0,1:T(8,128)(2,1)}, u32[]{:S(2)}, u32[]{:S(2)}) collective-permute-start(bf16[4096,256]{0,1:T(8,128)(2,1)} %fusion.27), channel_id=1, source_target_pairs={{0,12},{4,0},{8,4},{12,8},{1,13},{5,1},{9,5},{13,9},{2,14},{6,2},{... | collective-permute-start | bytes 6291464 | tf_op jit(solution)/shard_map/ppermute | solution.py:114
  1564.3 12.7 copy-start.9
  1564.3 12.7 copy-start.11
  1613.8 48.8 %collective-permute-start = (bf16[4096,256]{0,1:T(8,128)(2,1)}, bf16[4096,256]{0,1:T(8,128)(2,1)S(1)}, u32[]{:S(2)}, u32[]{:S(2)}) collective-permute-start(bf16[4096,256]{0,1:T(8,128)(2,1)} %fusion.24), channel_id=1, source_target_pairs={{0,4},{4,8},{8,12},{12,0},{1,5},{5,9},{9,13},{13,1},{2,6},{6,10},{... | collective-permute-start | bytes 6291464 | tf_op jit(solution)/shard_map/ppermute | solution.py:113
  1644.3 20.7 %copy-start.1 = (bf16[1,8,256,256]{3,2,1,0:T(8,128)(2,1)S(1)}, bf16[1,8,256,256]{3,2,1,0:T(8,128)(2,1)}, u32[]{:S(2)}) copy-start(bf16[1,8,256,256]{3,2,1,0:T(8,128)(2,1)} %param.29) | copy-start | bytes 3145732
  (18 other events, 55.6 us)
where the time goes:
time: 1670 us
  local copies, waits for them, and re-layouts  945 us (57%)
  waiting for transfers between devices  324 us (19%)
  matrix products  232 us (14%)
  other arithmetic  123 us (7%)
  starting transfers between devices  39.1 us (2%)
    all_to_all x1, waiting for transfers between devices, device_step(): recv_rows = lax.all_to_all(send_rows, 'ep', 0, 1, tiled=True)  163 us
    gather x1, local copies, waits for them, and re-layouts, device_step(): jnp.take(xn_fwd, tok_fwd, axis=0, mode='fill', fill_value=0)  129 us
    gather x1, local copies, waits for them, and re-layouts, device_step(): jnp.take(grad_in, tok_bwd, axis=0, mode='fill', fill_value=0)  129 us
    gather x1, local copies, waits for them, and re-layouts, device_step(): jnp.take(xn_bwd, tok_bwd, axis=0, mode='fill', fill_value=0)  123 us
    scatter x2, local copies, waits for them, and re-layouts, route_maps(): jnp.full((n_experts * cap_rows,), tok_rows, jnp.int32)  121 us
    scatter x1, local copies, waits for them, and re-layouts, device_step(): jnp.zeros((n_rows,), jnp.bfloat16).at[row_bwd.reshape(-1)]  113 us
    all_to_all x1, waiting for transfers between devices, device_step(): lax.all_to_all(grad_rows, 'ep', 1, 0, tiled=True).reshape(n_rows, hidden)  110 us
    gather x2, local copies, waits for them, and re-layouts, device_step(): routed = jnp.take(back_fwd, row_fwd, axis=0, mode='fill', fill_value=0)  81.8 us
  transfers between devices with their start and end apart: 7, of which 4 were waited for; matrix products, arithmetic and copies ran while one was open for 49% of the time, Pallas kernels for 0%

commit v1 on v0

v1 whole, which is shorter than its diff:
```python
import functools

import jax
import jax.numpy as jnp
from jax import lax
from jax.experimental import pallas as pl
from jax.experimental.pallas import tpu as pltpu
from jax.sharding import PartitionSpec as P

NORM_EPS = 1e-6
TM = 256
BT = 512
F32 = jnp.float32
BF16 = jnp.bfloat16
VMEM_LIMIT = 60 * 1024 * 1024


def dot(a, b):
    return jnp.dot(a, b, preferred_element_type=F32)


def dot_nt(a, b):
    return lax.dot_general(a, b, (((1,), (1,)), ((), ())), preferred_element_type=F32)


def dot_tn(a, b):
    return lax.dot_general(a, b, (((0,), (0,)), ((), ())), preferred_element_type=F32)


def rms_scale(v):
    return lax.rsqrt(jnp.mean(v * v, axis=-1, keepdims=True) + NORM_EPS)


def rms_back(v, dy):
    r = rms_scale(v)
    return r * dy - v * (r * r * r * jnp.mean(dy * v, axis=-1, keepdims=True))


def dense_forward(xf, w1, w2):
    u = dot((xf * rms_scale(xf)).astype(BF16), w1)
    act = (u * jax.nn.sigmoid(u)).astype(BF16)
    return (xf + dot(act, w2)).astype(BF16)


def rank_kernel(n_exp, dump, ids_ref, slots_ref, pos_ref, tab_ref):
    ids = jnp.where(slots_ref[...] >= 0, ids_ref[...], -1)
    n = ids.shape[1]
    row = lax.broadcasted_iota(jnp.int32, (n, n), 0)
    col = lax.broadcasted_iota(jnp.int32, (n, n), 1)
    ones = jnp.ones((n, n), BF16)
    right = jnp.concatenate([jnp.where(row < col, 1.0, 0.0).astype(BF16), ones], axis=1)
    left = jnp.concatenate([jnp.where(col < row, 1.0, 0.0).astype(BF16), ones], axis=0)
    start = jnp.zeros((8, n), F32)
    pos = jnp.full((n, n), float(dump), F32)
    tab_ref[...] = jnp.zeros_like(tab_ref)
    for e in range(n_exp):
        mask = ids == e
        both = dot(jnp.where(mask, 1.0, 0.0).astype(BF16), right)
        pre = dot(left, both[:, n:].astype(BF16))
        pos = jnp.where(mask, both[:, :n] + pre[:n] + start[0:1], pos)
        tab_ref[e : e + 1, :] = (start[0:1] * (1.0 / TM)).astype(jnp.int32)
        count = pre[n : n + 8]
        start = start + TM * jnp.maximum(jnp.floor((count + (TM - 1.0)) * (1.0 / TM)), 1.0)
    tab_ref[n_exp : n_exp + 1, :] = (start[0:1] * (1.0 / TM)).astype(jnp.int32)
    pos_ref[...] = (pos * 2.0).astype(jnp.int32)


def route_ranks(ids, slots, n_exp, rows):
    n_routes = ids.size
    lanes = 128
    flat = lambda a: a.T.reshape(n_routes // lanes, lanes)
    pos, tab = pl.pallas_call(
        functools.partial(rank_kernel, n_exp, rows),
        out_shape=(
            jax.ShapeDtypeStruct((n_routes // lanes, lanes), jnp.int32),
            jax.ShapeDtypeStruct((n_exp + 8, lanes), jnp.int32),
        ),
        name="rank",
    )(flat(ids), flat(slots))
    return pos.reshape(-1), tab[:, 0]


def put_pairs(ref, rows, vals):
    n = vals.shape[0]
    half = vals.shape[1] // 2
    ref[pl.ds(rows, n, stride=2), :] = vals[:, :half]
    ref[pl.ds(rows + 1, n, stride=2), :] = vals[:, half:]


def get_pairs(ref, rows, n):
    return jnp.concatenate([ref[pl.ds(rows, n, stride=2), :], ref[pl.ds(rows + 1, n, stride=2), :]], axis=1)


def pair(p):
    return pl.ds(pl.multiple_of(p, 2), 2)


def zero_rows(ref):
    step = 512
    n = ref.shape[0]
    whole = n // step

    def body(i, c):
        ref[pl.ds(pl.multiple_of(i * step, step), step), :] = jnp.zeros((step, ref.shape[1]), F32)
        return c

    lax.fori_loop(0, whole, body, 0)
    if n % step:
        ref[whole * step :, :] = jnp.zeros((n % step, ref.shape[1]), F32)


def pre_bwd_kernel(pos_ref, gate_ref, tab_ref, x_ref, g_ref, w1_ref, w2_ref, h_ref, xs_hbm, qs_hbm, xbuf, qbuf, nsc, gsc, xst, qst, sems, *, n_blocks, top_k, n_exp):
    step = pl.program_id(0)
    n_tok = n_blocks * BT

    @pl.when(step == 0)
    def _():
        zero_rows(xbuf)
        zero_rows(qbuf)

    h = dense_forward(x_ref[...].astype(F32), w1_ref[...], w2_ref[...])
    h_ref[...] = h
    hf = h.astype(F32)
    put_pairs(nsc, 0, (hf * rms_scale(hf)).astype(BF16).astype(F32))
    put_pairs(gsc, 0, g_ref[...].astype(F32))
    base = step * BT
    unroll = 8

    def scatter(j, c):
        for k in range(unroll):
            t = j * unroll + k
            nv = nsc[pair(2 * t), :]
            gv = gsc[pair(2 * t), :]
            for r in range(top_k):
                p = pos_ref[r * n_tok + base + t]
                xbuf[pair(p), :] = nv
                qbuf[pair(p), :] = gv * gate_ref[r * n_tok + base + t]
        return c

    lax.fori_loop(0, BT // unroll, scatter, 0)

    @pl.when(step == n_blocks - 1)
    def _():
        n_tiles = tab_ref[n_exp]

        def copies(t, slot):
            rows = pl.ds(pl.multiple_of(t * TM, TM), TM)
            return (
                pltpu.make_async_copy(xst.at[slot], xs_hbm.at[rows], sems.at[0, slot]),
                pltpu.make_async_copy(qst.at[slot], qs_hbm.at[rows], sems.at[1, slot]),
            )

        def convert(t, c):
            slot = lax.rem(t, 2)

            @pl.when(t >= 2)
            def _():
                for cp in copies(t - 2, slot):
                    cp.wait()

            rows = pl.multiple_of(t * (2 * TM), 2 * TM)
            xst[slot] = get_pairs(xbuf, rows, TM).astype(BF16)
            qst[slot] = get_pairs(qbuf, rows, TM).astype(BF16)
            for cp in copies(t, slot):
                cp.start()
            return c

        lax.fori_loop(0, n_tiles, convert, 0)
        for back in (2, 1):
            for cp in copies(n_tiles - back, lax.rem(n_tiles - back, 2)):
                cp.wait()


def pre_bwd(pos, gates, tab, x, g, w1, w2, rows, n_exp, top_k):
    n_tok, hid = x.shape
    n_blocks = n_tok // BT
    smem = pl.BlockSpec(memory_space=pltpu.SMEM)
    blk = pl.BlockSpec((BT, hid), lambda i: (i, 0))
    whole = pl.BlockSpec((hid, hid), lambda i: (0, 0))
    return pl.pallas_call(
        functools.partial(pre_bwd_kernel, n_blocks=n_blocks, top_k=top_k, n_exp=n_exp),
        grid=(n_blocks,),
        in_specs=[smem, smem, smem, blk, blk, whole, whole],
        out_specs=[blk, pl.BlockSpec(memory_space=pl.ANY), pl.BlockSpec(memory_space=pl.ANY)],
        out_shape=(
            jax.ShapeDtypeStruct((n_tok, hid), BF16),
            jax.ShapeDtypeStruct((rows, hid), BF16),
            jax.ShapeDtypeStruct((rows, hid), BF16),
        ),
        scratch_shapes=[
            pltpu.VMEM((2 * rows + 8, hid // 2), F32),
            pltpu.VMEM((2 * rows + 8, hid // 2), F32),
            pltpu.VMEM((2 * BT, hid // 2), F32),
            pltpu.VMEM((2 * BT, hid // 2), F32),
            pltpu.VMEM((2, TM, hid), BF16),
            pltpu.VMEM((2, TM, hid), BF16),
            pltpu.SemaphoreType.DMA((2, 2)),
        ],
        compiler_params=pltpu.CompilerParams(vmem_limit_bytes=VMEM_LIMIT),
        cost_estimate=pl.CostEstimate(flops=30_000_000_000, bytes_accessed=30_000_000, transcendentals=0),
        name="pre_bwd",
    )(pos, gates, tab, x, g, w1, w2)


def exp_bwd_kernel(first_ref, tab_ref, wg_ref, wu_ref, wd_ref, xs_hbm, qs_hbm, rs_hbm, dwg_ref, dwu_ref, dwd_ref, xb, qb, rb, sems, *, n_loc):
    first = first_ref[0]
    begin = tab_ref[first]
    end = tab_ref[first + n_loc]

    def rows_of(t):
        return pl.ds(pl.multiple_of(t * TM, TM), TM)

    def loads(t, slot):
        return (
            pltpu.make_async_copy(xs_hbm.at[rows_of(t)], xb.at[slot], sems.at[0, slot]),
            pltpu.make_async_copy(qs_hbm.at[rows_of(t)], qb.at[slot], sems.at[1, slot]),
        )

    def save(t, slot):
        return pltpu.make_async_copy(rb.at[slot], rs_hbm.at[rows_of(t)], sems.at[2, slot])

    for cp in loads(begin, lax.rem(begin, 2)):
        cp.start()
    dwg_ref[...] = jnp.zeros_like(dwg_ref)
    dwu_ref[...] = jnp.zeros_like(dwu_ref)
    dwd_ref[...] = jnp.zeros_like(dwd_ref)

    def body(t, e):
        slot = lax.rem(t, 2)
        e = jnp.where(t >= tab_ref[first + e + 1], e + 1, e)

        @pl.when(t + 1 < end)
        def _():
            for cp in loads(t + 1, 1 - slot):
                cp.start()

        for cp in loads(t, slot):
            cp.wait()

        @pl.when(t >= begin + 2)
        def _():
            save(t - 2, slot).wait()

        x = xb[slot]
        q = qb[slot]
        wg, wu, wd = wg_ref[e], wu_ref[e], wd_ref[e]
        pre = dot(x, wg)
        up = dot(x, wu)
        sig = jax.nn.sigmoid(pre)
        sil = pre * sig
        act = (sil * up).astype(BF16)
        dwd_ref[e] += dot_tn(act, q)
        da = dot_nt(q, wd).astype(BF16).astype(F32)
        dpre = (da * up * (sig * (1.0 + pre * (1.0 - sig)))).astype(BF16)
        dup = (da * sil).astype(BF16)
        dwg_ref[e] += dot_tn(x, dpre)
        dwu_ref[e] += dot_tn(x, dup)
        rb[slot] = (dot_nt(dpre, wg) + dot_nt(dup, wu)).astype(BF16)
        save(t, slot).start()
        return e

    lax.fori_loop(begin, end, body, 0)
    for back in (2, 1):
        save(end - back, lax.rem(end - back, 2)).wait()


def exp_bwd(first, tab, wg, wu, wd, xs, qs):
    n_loc, hid, ff = wg.shape
    smem = pl.BlockSpec(memory_space=pltpu.SMEM)
    vmem = pl.BlockSpec(memory_space=pltpu.VMEM)
    hbm = pl.BlockSpec(memory_space=pl.ANY)
    dw = jax.ShapeDtypeStruct((n_loc, hid, ff), F32)
    return pl.pallas_call(
        functools.partial(exp_bwd_kernel, n_loc=n_loc),
        in_specs=[smem, smem, vmem, vmem, vmem, hbm, hbm],
        out_specs=[hbm, vmem, vmem, vmem],
        out_shape=(jax.ShapeDtypeStruct(xs.shape, BF16), dw, dw, dw),
        input_output_aliases={5: 0},
        scratch_shapes=[
            pltpu.VMEM((2, TM, hid), BF16),
            pltpu.VMEM((2, TM, hid), BF16),
            pltpu.VMEM((2, TM, hid), BF16),
            pltpu.SemaphoreType.DMA((3, 2)),
        ],
        compiler_params=pltpu.CompilerParams(vmem_limit_bytes=VMEM_LIMIT),
        cost_estimate=pl.CostEstimate(flops=8_000_000_000, bytes_accessed=20_000_000, transcendentals=0),
        name="exp_bwd",
    )(first, tab, wg, wu, wd, xs, qs)


def post_bwd_kernel(pos_ref, tab_ref, x_ref, g_ref, h_ref, w1_ref, w2_ref, rs_hbm, dx_ref, rbuf, acc, st, sems, *, n_blocks, top_k, n_exp, rows):
    step = pl.program_id(0)
    n_tok = n_blocks * BT

    @pl.when(step == 0)
    def _():
        n_tiles = tab_ref[n_exp]

        def load(t, slot):
            return pltpu.make_async_copy(rs_hbm.at[pl.ds(pl.multiple_of(t * TM, TM), TM)], st.at[slot], sems.at[slot])

        load(0, 0).start()
        rbuf[2 * rows : 2 * rows + 8, :] = jnp.zeros((8, rbuf.shape[1]), F32)

        def expand(t, c):
            slot = lax.rem(t, 2)

            @pl.when(t + 1 < n_tiles)
            def _():
                load(t + 1, 1 - slot).start()

            load(t, slot).wait()
            put_pairs(rbuf, pl.multiple_of(t * (2 * TM), 2 * TM), st[slot].astype(F32))
            return c

        lax.fori_loop(0, n_tiles, expand, 0)

    base = step * BT
    unroll = 8

    def gather(j, c):
        for k in range(unroll):
            t = j * unroll + k
            total = rbuf[pair(pos_ref[base + t]), :]
            for r in range(1, top_k):
                total = total + rbuf[pair(pos_ref[r * n_tok + base + t]), :]
            acc[pair(2 * t), :] = total
        return c

    lax.fori_loop(0, BT // unroll, gather, 0)
    dn = get_pairs(acc, 0, BT)
    xf = x_ref[...].astype(F32)
    u = dot((xf * rms_scale(xf)).astype(BF16), w1_ref[...])
    dh = g_ref[...].astype(F32) + rms_back(h_ref[...].astype(F32), dn)
    sig = jax.nn.sigmoid(u)
    du = (dot_nt(dh.astype(BF16), w2_ref[...]) * (sig * (1.0 + u * (1.0 - sig)))).astype(BF16)
    dx_ref[...] = (dh + rms_back(xf, dot_nt(du, w1_ref[...]))).astype(BF16)


def post_bwd(pos, tab, x, g, h, w1, w2, rs, n_exp, top_k):
    n_tok, hid = x.shape
    rows = rs.shape[0]
    n_blocks = n_tok // BT
    smem = pl.BlockSpec(memory_space=pltpu.SMEM)
    blk = pl.BlockSpec((BT, hid), lambda i: (i, 0))
    whole = pl.BlockSpec((hid, hid), lambda i: (0, 0))
    return pl.pallas_call(
        functools.partial(post_bwd_kernel, n_blocks=n_blocks, top_k=top_k, n_exp=n_exp, rows=rows),
        grid=(n_blocks,),
        in_specs=[smem, smem, blk, blk, blk, whole, whole, pl.BlockSpec(memory_space=pl.ANY)],
        out_specs=blk,
        out_shape=jax.ShapeDtypeStruct((n_tok, hid), BF16),
        scratch_shapes=[
            pltpu.VMEM((2 * rows + 8, hid // 2), F32),
            pltpu.VMEM((2 * BT, hid // 2), F32),
            pltpu.VMEM((2, TM, hid), BF16),
            pltpu.SemaphoreType.DMA((2,)),
        ],
        compiler_params=pltpu.CompilerParams(vmem_limit_bytes=VMEM_LIMIT),
        cost_estimate=pl.CostEstimate(flops=30_000_000_000, bytes_accessed=30_000_000, transcendentals=0),
        name="post_bwd",
    )(pos, tab, x, g, h, w1, w2, rs)


def fwd_kernel(firsts_ref, pos_ref, gate_ref, tab_ref, x_ref, w1_ref, w2_ref, *rest, n_blocks, top_k, n_exp, n_groups, rows):
    w_hbm = rest[: 3 * n_groups]
    y_ref, buf, nsc, hsc, wsc, sems = rest[3 * n_groups :]
    step = pl.program_id(0)
    n_tok = n_blocks * BT
    n_loc = n_exp // n_groups
    unroll = 8

    def w_copy(i):
        return pltpu.make_async_copy(w_hbm[i], wsc.at[i], sems.at[i])

    @pl.when(step == 0)
    def _():
        for i in range(3 * n_groups):
            w_copy(i).start()
        zero_rows(buf)

    @pl.when(step < n_blocks)
    def _():
        h = dense_forward(x_ref[...].astype(F32), w1_ref[...], w2_ref[...])
        base = step * BT
        hsc[pl.ds(pl.multiple_of(base, BT), BT), :] = h
        hf = h.astype(F32)
        put_pairs(nsc, 0, (hf * rms_scale(hf)).astype(BF16).astype(F32))

        def scatter(j, c):
            for k in range(unroll):
                t = j * unroll + k
                nv = nsc[pair(2 * t), :]
                for r in range(top_k):
                    buf[pair(pos_ref[r * n_tok + base + t]), :] = nv
            return c

        lax.fori_loop(0, BT // unroll, scatter, 0)

    @pl.when(step == n_blocks)
    def _():
        buf[2 * rows : 2 * rows + 8, :] = jnp.zeros((8, buf.shape[1]), F32)
        for g in range(n_groups):
            for i in range(3):
                w_copy(3 * g + i).wait()
            first = firsts_ref[g]

            def body(t, e):
                e = jnp.where(t >= tab_ref[first + e + 1], e + 1, e)
                at = pl.multiple_of(t * (2 * TM), 2 * TM)
                x = get_pairs(buf, at, TM).astype(BF16)
                pre = dot(x, wsc[3 * g, e])
                up = dot(x, wsc[3 * g + 1, e])
                act = (pre * jax.nn.sigmoid(pre) * up).astype(BF16)
                put_pairs(buf, at, dot(act, wsc[3 * g + 2, e]).astype(BF16).astype(F32))
                return e

            lax.fori_loop(tab_ref[first], tab_ref[first + n_loc], body, 0)

    @pl.when(step > n_blocks)
    def _():
        base = (step - n_blocks - 1) * BT

        def gather(j, c):
            for k in range(unroll):
                t = j * unroll + k
                total = None
                for r in range(top_k):
                    at = r * n_tok + base + t
                    term = buf[pair(pos_ref[at]), :] * gate_ref[at]
                    total = term if total is None else total + term
                nsc[pair(2 * t), :] = total
            return c

        lax.fori_loop(0, BT // unroll, gather, 0)
        h = hsc[pl.ds(pl.multiple_of(base, BT), BT), :]
        y_ref[...] = (h.astype(F32) + get_pairs(nsc, 0, BT)).astype(BF16)


def fwd(firsts, pos, gates, tab, x, w1, w2, weights, rows, n_exp, top_k):
    n_tok, hid = x.shape
    n_blocks = n_tok // BT
    n_groups = len(weights)
    n_loc = n_exp // n_groups
    smem = pl.BlockSpec(memory_space=pltpu.SMEM)
    whole = pl.BlockSpec((hid, hid), lambda i: (0, 0))
    flat = [w for group in weights for w in group]
    return pl.pallas_call(
        functools.partial(fwd_kernel, n_blocks=n_blocks, top_k=top_k, n_exp=n_exp, n_groups=n_groups, rows=rows),
        grid=(2 * n_blocks + 1,),
        in_specs=[smem, smem, smem, smem, pl.BlockSpec((BT, hid), lambda i: (jnp.minimum(i, n_blocks - 1), 0)), whole, whole]
        + [pl.BlockSpec(memory_space=pl.ANY)] * len(flat),
        out_specs=pl.BlockSpec((BT, hid), lambda i: (jnp.maximum(i - n_blocks - 1, 0), 0)),
        out_shape=jax.ShapeDtypeStruct((n_tok, hid), BF16),
        scratch_shapes=[
            pltpu.VMEM((2 * rows + 8, hid // 2), F32),
            pltpu.VMEM((2 * BT, hid // 2), F32),
            pltpu.VMEM((n_tok, hid), BF16),
            pltpu.VMEM((len(flat), n_loc, hid, hid), BF16),
            pltpu.SemaphoreType.DMA((len(flat),)),
        ],
        compiler_params=pltpu.CompilerParams(vmem_limit_bytes=VMEM_LIMIT),
        cost_estimate=pl.CostEstimate(flops=80_000_000_000, bytes_accessed=30_000_000, transcendentals=0),
        name="fwd",
    )(firsts, pos, gates, tab, x, w1, w2, *flat)


def solution(mesh):
    stages = mesh.shape["pp"]
    ep_size = mesh.shape["ep"]
    next_perm = [(i, (i + 1) % stages) for i in range(stages)]
    prev_perm = [(i, (i - 1) % stages) for i in range(stages)]
    mate_perm = [(i, i ^ 1) for i in range(ep_size)]
    chip_perm = [(i, i ^ 2) for i in range(ep_size)]
    tok_spec = P("pp", "ep", None)
    dense_spec = P("pp", None, None)
    expert_spec = P("pp", "ep", None, None)

    def mate(a):
        return lax.ppermute(a, "ep", mate_perm)

    def chip(a):
        return lax.ppermute(a, "ep", chip_perm)

    def device_step(x_fwd, ids_fwd, slots_fwd, gates_fwd, x_saved, grad_in, ids_bwd, slots_bwd, gates_bwd, w_one, w_two, w_gate, w_up, w_down):
        x_fwd, ids_fwd, slots_fwd, gates_fwd = x_fwd[0], ids_fwd[0], slots_fwd[0], gates_fwd[0]
        x_saved, grad_in, ids_bwd, slots_bwd, gates_bwd = x_saved[0], grad_in[0], ids_bwd[0], slots_bwd[0], gates_bwd[0]
        w1, w2, w_gate, w_up, w_down = w_one[0], w_two[0], w_gate[0], w_up[0], w_down[0]
        top_k = ids_fwd.shape[1]
        n_loc = w_gate.shape[0]
        n_exp = n_loc * ep_size
        rows = TM * (ids_fwd.size // TM + n_exp)
        me = lax.axis_index("ep")

        own = (w_gate, w_up, w_down)
        far = tuple(chip(w) for w in own)
        near = tuple(mate(w) for w in own)
        far_near = tuple(mate(w) for w in far)
        weights = (own, near, far, far_near)
        firsts = [(me ^ g) * n_loc for g in range(ep_size)]

        pos_b, tab_b = route_ranks(ids_bwd, slots_bwd, n_exp, rows)
        pos_f, tab_f = route_ranks(ids_fwd, slots_fwd, n_exp, rows)
        gates_b = gates_bwd.T.reshape(-1).astype(F32)
        gates_f = gates_fwd.T.reshape(-1).astype(F32)

        h_bwd, xs, qs = pre_bwd(pos_b, gates_b, tab_b, x_saved, grad_in, w1, w2, rows, n_exp, top_k)
        parts = []
        for g in range(ep_size):
            xs, *dw = exp_bwd(firsts[g].reshape(1), tab_b, *weights[g], xs, qs)
            parts.append(dw)
        grad_x = post_bwd(pos_b, tab_b, x_saved, grad_in, h_bwd, w1, w2, xs, n_exp, top_k)
        dx_prev = lax.ppermute(grad_x, "pp", prev_perm)

        dws = []
        for i in range(3):
            there = chip(parts[2][i] + mate(parts[3][i]))
            dws.append(parts[0][i] + mate(parts[1][i]) + there)

        y_out = fwd(jnp.stack(firsts), pos_f, gates_f, tab_f, x_fwd, w1, w2, weights, rows, n_exp, top_k)
        y_next = lax.ppermute(y_out, "pp", next_perm)
        return y_next[None], dx_prev[None], dws[0][None], dws[1][None], dws[2][None]

    in_specs = (tok_spec,) * 9 + (dense_spec, dense_spec, expert_spec, expert_spec, expert_spec)
    out_specs = (tok_spec, tok_spec, expert_spec, expert_spec, expert_spec)
    return jax.shard_map(device_step, mesh=mesh, in_specs=in_specs, out_specs=out_specs, check_vma=False)
```

time: 1670 us -> 498 us (0.30)
  local copies, waits for them, and re-layouts: 945 us -> 13.7 us
  Pallas kernels: 0 us -> 316 us
  matrix products: 232 us -> 0 us
  waiting for transfers between devices: 324 us -> 120 us
  other arithmetic: 123 us -> 14.6 us
    gather x7 -> x0, local copies, waits for them, and re-layouts: 546 us -> none  [the longest x1 129 us: device_step(): jnp.take(xn_fwd, tok_fwd, axis=0, mode='fill', fill_value=0)]
    pallas_call x0 -> x9, Pallas kernels: none -> 316 us  [the longest x4 90.6 us: exp_bwd(): pl.pallas_call(functools.partial(exp_bwd_kernel, n_loc=n_loc), in_specs=[...]
    all_to_all x5 -> x0, waiting for transfers between devices: 310 us -> none  [the longest x1 163 us: device_step(): recv_rows = lax.all_to_all(send_rows, 'ep', 0, 1, tiled=True)]
    scatter x3 -> x0, local copies, waits for them, and re-layouts: 234 us -> none  [the longest x2 121 us: route_maps(): jnp.full((n_experts * cap_rows,), tok_rows, jnp.int32)]
    dot_general x14 -> x0, matrix products: 232 us -> none  [the longest x1 40.8 us: expert_backward(): jnp.einsum('ech,efh->ecf', grad_out, w_down, preferred_element_type=jnp.f...]
    ppermute x0 -> x18, waiting for transfers between devices: none -> 82.4 us  [the longest x6 82.3 us: chip(): return lax.ppermute(a, 'ep', chip_perm)]
    all_to_all x5 -> x0, local copies, waits for them, and re-layouts: 73.1 us -> none  [the longest x1 15.9 us: device_step(): lax.all_to_all(out_fwd, 'ep', 1, 0, tiled=True).reshape(n_rows, hidden)]
    convert_element_type x4 -> x0, local copies, waits for them, and re-layouts: 41.5 us -> none  [the longest x1 17.9 us: expert_backward(): return (grad_rows.astype(jnp.bfloat16), dw_gate, dw_up, dw_down)]
  transfers between devices with their start and end apart: 7 -> 20, of which waited for: 4 -> 3; matrix products, arithmetic and copies ran while one was open for 49% -> 4% of each run, Pallas kernels for 0% -> 64%
where the time goes in v1:
time: 498 us; the launch traced here: 490 us
  Pallas kernels  316 us (63%)
  waiting for transfers between devices  120 us (24%)
  starting transfers between devices  24.9 us (5%)
  other arithmetic  14.6 us (3%)
  local copies, waits for them, and re-layouts  13.7 us (3%)
    pallas_call x4, Pallas kernels, exp_bwd(): pl.pallas_call(functools.partial(exp_bwd_kernel, n_loc=n_loc), in_specs=[...  90.6 us
    pallas_call x1, Pallas kernels, fwd(): pl.pallas_call(functools.partial(fwd_kernel, n_blocks=n_blocks, top_k=top...  83.5 us
    ppermute x6, waiting for transfers between devices, chip(): return lax.ppermute(a, 'ep', chip_perm)  82.3 us
    pallas_call x1, Pallas kernels, pre_bwd(): pl.pallas_call(functools.partial(pre_bwd_kernel, n_blocks=n_blocks, top_k...  73.4 us
    pallas_call x1, Pallas kernels, post_bwd(): pl.pallas_call(functools.partial(post_bwd_kernel, n_blocks=n_blocks, top_...  62.3 us
    ppermute x1, waiting for transfers between devices, device_step(): dx_prev = lax.ppermute(grad_x, 'pp', prev_perm)  38.1 us
    ppermute x6, starting transfers between devices, chip(): return lax.ppermute(a, 'ep', chip_perm)  15.3 us
  transfers between devices with their start and end apart: 20, of which 3 were waited for; matrix products, arithmetic and copies ran while one was open for 4% of the time, Pallas kernels for 64%

profile of v1, /device:TPU:0, one launch (start us, length us, event | category | flops | bytes accessed | tf_op | source)
XLA Modules:
  0.0 490.1 jit_solution(5529192258254887212)
XLA Ops:
  0.6 3.3 collective-permute-start.3
  9.2 2.9 rank.3
  14.9 73.4 %pre_bwd.1 = (bf16[4096,256]{1,0:T(8,128)(2,1)}, bf16[24576,256]{1,0:T(8,128)(2,1)}, bf16[24576,256]{1,0:T(8,128)(2,1)}) custom-call(s32[16384]{0:T(1024)} %bitcast.78, f32[16384]{0:T(1024)} %bitcast.54, s32[40]{0:T(128)} %slice_reduce_fusion.tab_ref, bf16[4096,256]{1,0:T(8,128)(2,1)} %bitcast.56, bf16[4096,256]{1,0:T(8,128)(2,1)} %bitcast.58, ...), custom_call_target="tpu_custom_call" | custom-call | flops 30000001024 | bytes 30000000 | tf_op jit(solution)/shard_map/pre_bwd/pallas_call | solution.py:180
  90.9 2.9 rank.2
  95.8 16.5 %exp_bwd.4 = (bf16[24576,256]{1,0:T(8,128)(2,1)}, f32[8,256,256]{2,1,0:T(8,128)}, f32[8,256,256]{2,1,0:T(8,128)}, f32[8,256,256]{2,1,0:T(8,128)}) custom-call(s32[1]{0:T(128)} %bitcast.first_ref, s32[40]{0:T(128)} %slice_reduce_fusion.tab_ref, bf16[8,256,256]{2,1,0:T(8,128)(2,1)} %bitcast.62, ...), custom_call_target="tpu_custom_call", output_to_operand_aliasing={{0}: (5, {})} | custom-call | flops 8000000000 | bytes 20000000 | tf_op jit(solution)/shard_map/exp_bwd/pallas_call | solution.py:273
  112.3 3.7 collective-permute-start.6
  116.6 26.2 %exp_bwd.5 = (bf16[24576,256]{1,0:T(8,128)(2,1)}, f32[8,256,256]{2,1,0:T(8,128)}, f32[8,256,256]{2,1,0:T(8,128)}, f32[8,256,256]{2,1,0:T(8,128)}) custom-call(s32[1]{0:T(128)} %bitcast.1.first_ref, s32[40]{0:T(128)} %slice_reduce_fusion.tab_ref, bf16[8,256,256]{2,1,0:T(8,128)(2,1)} %copy-done.13, ...), custom_call_target="tpu_custom_call", output_to_operand_aliasing={{0}: (5, {})} | custom-call | flops 8000000000 | bytes 20000000 | tf_op jit(solution)/shard_map/exp_bwd/pallas_call | solution.py:273
  144.1 29.7 %exp_bwd.6 = (bf16[24576,256]{1,0:T(8,128)(2,1)}, f32[8,256,256]{2,1,0:T(8,128)}, f32[8,256,256]{2,1,0:T(8,128)}, f32[8,256,256]{2,1,0:T(8,128)}) custom-call(s32[1]{0:T(128)} %bitcast.2.first_ref, s32[40]{0:T(128)} %slice_reduce_fusion.tab_ref, bf16[8,256,256]{2,1,0:T(8,128)(2,1)} %copy-done.12, ...), custom_call_target="tpu_custom_call", output_to_operand_aliasing={{0}: (5, {})} | custom-call | flops 8000000000 | bytes 20000000 | tf_op jit(solution)/shard_map/exp_bwd/pallas_call | solution.py:273
  173.8 83.5 %fwd.1 = bf16[4096,256]{1,0:T(8,128)(2,1)} custom-call(s32[4]{0:T(128)} %pad_add_fusion.firsts_ref, s32[16384]{0:T(1024)} %bitcast.80, f32[16384]{0:T(1024)} %bitcast.53, s32[40]{0:T(128)} %slice_reduce_fusion.1.tab_ref, bf16[4096,256]{1,0:T(8,128)(2,1)} %bitcast.55, bf16[256,256]{1,0:T(8,128)(2,1)} %bitcast.73, bf16[256,256]{1,0:T(8,128)(2,1)} %bitcast.76, ...), custom_call_target="tpu_custom_call" | custom-call | flops 80000000000 | bytes 30000000 | tf_op jit(solution)/shard_map/fwd/pallas_call | solution.py:448
  257.3 2.5 collective-permute-start.9
  259.8 18.2 %exp_bwd.7 = (bf16[24576,256]{1,0:T(8,128)(2,1)}, f32[8,256,256]{2,1,0:T(8,128)}, f32[8,256,256]{2,1,0:T(8,128)}, f32[8,256,256]{2,1,0:T(8,128)}) custom-call(s32[1]{0:T(128)} %bitcast.3.first_ref, s32[40]{0:T(128)} %slice_reduce_fusion.tab_ref, bf16[8,256,256]{2,1,0:T(8,128)(2,1)} %collective-permute-done.6.rest_9_.wg_ref, ...), custom_call_target="tpu_custom_call", output_to_operand_aliasing={{0}: (5, {})} | custom-call | flops 8000000000 | bytes 20000000 | tf_op jit(solution)/shard_map/exp_bwd/pallas_call | solution.py:273
  278.6 62.3 %post_bwd.1 = bf16[4096,256]{1,0:T(8,128)(2,1)} custom-call(s32[16384]{0:T(1024)} %bitcast.79, s32[40]{0:T(128)} %slice_reduce_fusion.tab_ref, bf16[4096,256]{1,0:T(8,128)(2,1)} %bitcast.57, bf16[4096,256]{1,0:T(8,128)(2,1)} %bitcast.59, bf16[4096,256]{1,0:T(8,128)(2,1)} %get-tuple-element.32.h_ref, bf16[256,256]{1,0:T(8,128)(2,1)} %bitcast.74, ...), custom_call_target="tpu_custom_call" | custom-call | flops 30000001024 | bytes 30000000 | tf_op jit(solution)/shard_map/post_bwd/pallas_call | solution.py:347
  341.0 2.1 add.28
  343.1 6.3 %collective-permute-start.13 = (f32[8,256,256]{2,1,0:T(8,128)S(1)}, f32[8,256,256]{2,1,0:T(8,128)S(1)}, u32[]{:S(2)}, u32[]{:S(2)}) collective-permute-start(f32[8,256,256]{2,1,0:T(8,128)S(1)} %add.28), channel_id=1, source_target_pairs={{0,2},{1,3},{2,0},{3,1},{4,6},{5,7},{6,4},{7,5},{8,10},{9,11},{10,... | collective-permute-start | bytes 6291464 | tf_op jit(solution)/shard_map/ppermute | solution.py:483
  349.4 2.0 add.31
  352.3 2.0 add.34
  354.5 38.1 %collective-permute-done.10 = bf16[4096,256]{1,0:T(8,128)(2,1)S(1)} collective-permute-done((bf16[4096,256]{1,0:T(8,128)(2,1)}, bf16[4096,256]{1,0:T(8,128)(2,1)S(1)}, u32[]{:S(2)}, u32[]{:S(2)}) %collective-permute-start.10) | collective-permute-done | bytes 2097184 | tf_op jit(solution)/shard_map/ppermute | solution.py:513
  392.6 3.7 collective-permute-start.19
  396.3 3.5 add_bitcast_fusion.2
  399.8 41.1 %collective-permute-done.16 = f32[8,256,256]{2,1,0:T(8,128)S(1)} collective-permute-done((f32[8,256,256]{2,1,0:T(8,128)S(1)}, f32[8,256,256]{2,1,0:T(8,128)S(1)}, u32[]{:S(2)}, u32[]{:S(2)}) %collective-permute-start.16) | collective-permute-done | bytes 2097184 | tf_op jit(solution)/shard_map/ppermute | solution.py:483
  440.9 1.8 add_bitcast_fusion.1
  442.7 41.3 %collective-permute-done.19 = f32[8,256,256]{2,1,0:T(8,128)S(1)} collective-permute-done((f32[8,256,256]{2,1,0:T(8,128)S(1)}, f32[8,256,256]{2,1,0:T(8,128)S(1)}, u32[]{:S(2)}, u32[]{:S(2)}) %collective-permute-start.19) | collective-permute-done | bytes 2097184 | tf_op jit(solution)/shard_map/ppermute | solution.py:483
  483.9 1.8 add_bitcast_fusion
  485.8 3.0 copy.31
  (72 shorter events, 17.5 us)
Async XLA Ops:
  0.6 87.6 %collective-permute-start.3 = (bf16[8,256,256]{2,1,0:T(8,128)(2,1)}, bf16[8,256,256]{2,1,0:T(8,128)(2,1)S(1)}, u32[]{:S(2)}, u32[]{:S(2)}) collective-permute-start(bf16[8,256,256]{2,1,0:T(8,128)(2,1)} %bitcast.60), channel_id=1, source_target_pairs={{0,2},{1,3},{2,0},{3,1},{4,6},{5,7},{6,4},{7,5},{8,10},{9,11},{10,... | collective-permute-start | bytes 3145736 | tf_op jit(solution)/shard_map/ppermute | solution.py:483
  3.9 108.4 %collective-permute-start = (bf16[8,256,256]{2,1,0:T(8,128)(2,1)}, bf16[8,256,256]{2,1,0:T(8,128)(2,1)S(1)}, u32[]{:S(2)}, u32[]{:S(2)}) collective-permute-start(bf16[8,256,256]{2,1,0:T(8,128)(2,1)} %bitcast.61), channel_id=1, source_target_pairs={{0,1},{1,0},{2,3},{3,2},{4,5},{5,4},{6,7},{7,6},{8,9},{9,8},{10,11... | collective-permute-start | bytes 3145736 | tf_op jit(solution)/shard_map/ppermute | solution.py:480
  3.9 112.2 %collective-permute-start.4 = (bf16[8,256,256]{2,1,0:T(8,128)(2,1)}, bf16[8,256,256]{2,1,0:T(8,128)(2,1)}, u32[]{:S(2)}, u32[]{:S(2)}) collective-permute-start(bf16[8,256,256]{2,1,0:T(8,128)(2,1)} %bitcast.64), channel_id=1, source_target_pairs={{0,2},{1,3},{2,0},{3,1},{4,6},{5,7},{6,4},{7,5},{8,10},{9,11},{10,... | collective-permute-start | bytes 3145736 | tf_op jit(solution)/shard_map/ppermute | solution.py:483
  4.0 112.6 %collective-permute-start.1 = (bf16[8,256,256]{2,1,0:T(8,128)(2,1)}, bf16[8,256,256]{2,1,0:T(8,128)(2,1)}, u32[]{:S(2)}, u32[]{:S(2)}) collective-permute-start(bf16[8,256,256]{2,1,0:T(8,128)(2,1)} %bitcast.65), channel_id=1, source_target_pairs={{0,1},{1,0},{2,3},{3,2},{4,5},{5,4},{6,7},{7,6},{8,9},{9,8},{10,11... | collective-permute-start | bytes 3145736 | tf_op jit(solution)/shard_map/ppermute | solution.py:480
  4.4 111.7 %collective-permute-start.5 = (bf16[8,256,256]{2,1,0:T(8,128)(2,1)}, bf16[8,256,256]{2,1,0:T(8,128)(2,1)}, u32[]{:S(2)}, u32[]{:S(2)}) collective-permute-start(bf16[8,256,256]{2,1,0:T(8,128)(2,1)} %bitcast.68), channel_id=1, source_target_pairs={{0,2},{1,3},{2,0},{3,1},{4,6},{5,7},{6,4},{7,5},{8,10},{9,11},{10,... | collective-permute-start | bytes 3145736 | tf_op jit(solution)/shard_map/ppermute | solution.py:483
  14.9 73.4 %copy-start.11 = (bf16[1,8,256,256]{3,2,1,0:T(8,128)(2,1)S(1)}, bf16[1,8,256,256]{3,2,1,0:T(8,128)(2,1)}, u32[]{:S(2)}) copy-start(bf16[1,8,256,256]{3,2,1,0:T(8,128)(2,1)} %param.27) | copy-start | bytes 3145732
  14.9 74.0 %copy-start.8 = (bf16[1,4096,4]{1,2,0:T(4,128)(2,1)S(1)}, bf16[1,4096,4]{1,2,0:T(4,128)(2,1)}, u32[]{:S(2)}) copy-start(bf16[1,4096,4]{1,2,0:T(4,128)(2,1)} %param.17) | copy-start | bytes 98308
  14.9 74.1 %copy-start.6 = (s32[1,4096,4]{1,2,0:T(4,128)S(1)}, s32[1,4096,4]{1,2,0:T(4,128)}, u32[]{:S(2)}) copy-start(s32[1,4096,4]{1,2,0:T(4,128)} %param.15) | copy-start | bytes 196612
  14.9 74.8 %copy-start.7 = (s32[1,4096,4]{1,2,0:T(4,128)S(1)}, s32[1,4096,4]{1,2,0:T(4,128)}, u32[]{:S(2)}) copy-start(s32[1,4096,4]{1,2,0:T(4,128)} %param.16) | copy-start | bytes 196612
  88.3 28.3 %collective-permute-start.2 = (bf16[8,256,256]{2,1,0:T(8,128)(2,1)S(1)}, bf16[8,256,256]{2,1,0:T(8,128)(2,1)}, u32[]{:S(2)}, u32[]{:S(2)}) collective-permute-start(bf16[8,256,256]{2,1,0:T(8,128)(2,1)S(1)} %bitcast.71), channel_id=1, source_target_pairs={{0,1},{1,0},{2,3},{3,2},{4,5},{5,4},{6,7},{7,6},{8,9},{9,8},{10,11... | collective-permute-start | bytes 3145736 | tf_op jit(solution)/shard_map/ppermute | solution.py:480
  112.3 61.5 %collective-permute-start.6 = (bf16[8,256,256]{2,1,0:T(8,128)(2,1)S(1)}, bf16[8,256,256]{2,1,0:T(8,128)(2,1)}, u32[]{:S(2)}, u32[]{:S(2)}) collective-permute-start(bf16[8,256,256]{2,1,0:T(8,128)(2,1)S(1)} %collective-permute-done.3.rest_6_.wg_ref), channel_id=1, source_target_pairs={{0,1},{1,0},{2,3},{3,2},{4,5},{5,4},{6,7},{7,6},{8,9},{9,8},{10,11... | collective-permute-start | bytes 3145736 | tf_op jit(solution)/shard_map/ppermute | solution.py:480
  116.1 57.7 %collective-permute-start.7 = (bf16[8,256,256]{2,1,0:T(8,128)(2,1)}, bf16[8,256,256]{2,1,0:T(8,128)(2,1)}, u32[]{:S(2)}, u32[]{:S(2)}) collective-permute-start(bf16[8,256,256]{2,1,0:T(8,128)(2,1)} %collective-permute-done.4.rest_7_.wu_ref), channel_id=1, source_target_pairs={{0,1},{1,0},{2,3},{3,2},{4,5},{5,4},{6,7},{7,6},{8,9},{9,8},{10,11... | collective-permute-start | bytes 3145736 | tf_op jit(solution)/shard_map/ppermute | solution.py:480
  116.1 57.7 %collective-permute-start.8 = (bf16[8,256,256]{2,1,0:T(8,128)(2,1)}, bf16[8,256,256]{2,1,0:T(8,128)(2,1)}, u32[]{:S(2)}, u32[]{:S(2)}) collective-permute-start(bf16[8,256,256]{2,1,0:T(8,128)(2,1)} %collective-permute-done.5.rest_8_.wd_ref), channel_id=1, source_target_pairs={{0,1},{1,0},{2,3},{3,2},{4,5},{5,4},{6,7},{7,6},{8,9},{9,8},{10,11... | collective-permute-start | bytes 3145736 | tf_op jit(solution)/shard_map/ppermute | solution.py:480
  142.8 208.7 %collective-permute-start.11 = (f32[8,256,256]{2,1,0:T(8,128)}, f32[8,256,256]{2,1,0:T(8,128)}, u32[]{:S(2)}, u32[]{:S(2)}) collective-permute-start(f32[8,256,256]{2,1,0:T(8,128)} %get-tuple-element.40), channel_id=1, source_target_pairs={{0,1},{1,0},{2,3},{3,2},{4,5},{5,4},{6,7},{7,6},{8,9},{9,8},{10,11... | collective-permute-start | bytes 6291464 | tf_op jit(solution)/shard_map/ppermute | solution.py:480
  257.3 97.0 %collective-permute-start.9 = (bf16[4096,256]{1,0:T(8,128)(2,1)}, bf16[4096,256]{1,0:T(8,128)(2,1)}, u32[]{:S(2)}, u32[]{:S(2)}) collective-permute-start(bf16[4096,256]{1,0:T(8,128)(2,1)} %fwd.1), channel_id=1, source_target_pairs={{0,4},{4,8},{8,12},{12,0},{1,5},{5,9},{9,13},{13,1},{2,6},{6,10},{... | collective-permute-start | bytes 6291464 | tf_op jit(solution)/shard_map/ppermute | solution.py:521
  278.0 62.9 %collective-permute-start.12 = (f32[8,256,256]{2,1,0:T(8,128)}, f32[8,256,256]{2,1,0:T(8,128)}, u32[]{:S(2)}, u32[]{:S(2)}) collective-permute-start(f32[8,256,256]{2,1,0:T(8,128)} %get-tuple-element.42), channel_id=1, source_target_pairs={{0,1},{1,0},{2,3},{3,2},{4,5},{5,4},{6,7},{7,6},{8,9},{9,8},{10,11... | collective-permute-start | bytes 6291464 | tf_op jit(solution)/shard_map/ppermute | solution.py:480
  278.0 65.1 %collective-permute-start.15 = (f32[8,256,256]{2,1,0:T(8,128)}, f32[8,256,256]{2,1,0:T(8,128)}, u32[]{:S(2)}, u32[]{:S(2)}) collective-permute-start(f32[8,256,256]{2,1,0:T(8,128)} %get-tuple-element.46), channel_id=1, source_target_pairs={{0,1},{1,0},{2,3},{3,2},{4,5},{5,4},{6,7},{7,6},{8,9},{9,8},{10,11... | collective-permute-start | bytes 6291464 | tf_op jit(solution)/shard_map/ppermute | solution.py:480
  278.5 73.1 %collective-permute-start.18 = (f32[8,256,256]{2,1,0:T(8,128)}, f32[8,256,256]{2,1,0:T(8,128)}, u32[]{:S(2)}, u32[]{:S(2)}) collective-permute-start(f32[8,256,256]{2,1,0:T(8,128)} %get-tuple-element.50), channel_id=1, source_target_pairs={{0,1},{1,0},{2,3},{3,2},{4,5},{5,4},{6,7},{7,6},{8,9},{9,8},{10,11... | collective-permute-start | bytes 6291464 | tf_op jit(solution)/shard_map/ppermute | solution.py:480
  340.9 51.6 %collective-permute-start.10 = (bf16[4096,256]{1,0:T(8,128)(2,1)}, bf16[4096,256]{1,0:T(8,128)(2,1)S(1)}, u32[]{:S(2)}, u32[]{:S(2)}) collective-permute-start(bf16[4096,256]{1,0:T(8,128)(2,1)} %post_bwd.1), channel_id=1, source_target_pairs={{0,12},{4,0},{8,4},{12,8},{1,13},{5,1},{9,5},{13,9},{2,14},{6,2},{... | collective-permute-start | bytes 6291464 | tf_op jit(solution)/shard_map/ppermute | solution.py:513
  343.1 53.2 %collective-permute-start.13 = (f32[8,256,256]{2,1,0:T(8,128)S(1)}, f32[8,256,256]{2,1,0:T(8,128)S(1)}, u32[]{:S(2)}, u32[]{:S(2)}) collective-permute-start(f32[8,256,256]{2,1,0:T(8,128)S(1)} %add.28), channel_id=1, source_target_pairs={{0,2},{1,3},{2,0},{3,1},{4,6},{5,7},{6,4},{7,5},{8,10},{9,11},{10,... | collective-permute-start | bytes 6291464 | tf_op jit(solution)/shard_map/ppermute | solution.py:483
  351.7 48.1 %collective-permute-start.14 = (f32[8,256,256]{2,1,0:T(8,128)S(1)}, f32[8,256,256]{2,1,0:T(8,128)S(1)}, u32[]{:S(2)}, u32[]{:S(2)}) collective-permute-start(f32[8,256,256]{2,1,0:T(8,128)S(1)} %copy-done.10), channel_id=1, source_target_pairs={{0,1},{1,0},{2,3},{3,2},{4,5},{5,4},{6,7},{7,6},{8,9},{9,8},{10,11... | collective-permute-start | bytes 6291464 | tf_op jit(solution)/shard_map/ppermute | solution.py:480
  351.7 89.2 %collective-permute-start.16 = (f32[8,256,256]{2,1,0:T(8,128)S(1)}, f32[8,256,256]{2,1,0:T(8,128)S(1)}, u32[]{:S(2)}, u32[]{:S(2)}) collective-permute-start(f32[8,256,256]{2,1,0:T(8,128)S(1)} %add.31), channel_id=1, source_target_pairs={{0,2},{1,3},{2,0},{3,1},{4,6},{5,7},{6,4},{7,5},{8,10},{9,11},{10,... | collective-permute-start | bytes 6291464 | tf_op jit(solution)/shard_map/ppermute | solution.py:483
  354.5 88.2 %collective-permute-start.17 = (f32[8,256,256]{2,1,0:T(8,128)S(1)}, f32[8,256,256]{2,1,0:T(8,128)S(1)}, u32[]{:S(2)}, u32[]{:S(2)}) collective-permute-start(f32[8,256,256]{2,1,0:T(8,128)S(1)} %copy-done.9), channel_id=1, source_target_pairs={{0,1},{1,0},{2,3},{3,2},{4,5},{5,4},{6,7},{7,6},{8,9},{9,8},{10,11... | collective-permute-start | bytes 6291464 | tf_op jit(solution)/shard_map/ppermute | solution.py:480
  392.6 91.4 %collective-permute-start.19 = (f32[8,256,256]{2,1,0:T(8,128)S(1)}, f32[8,256,256]{2,1,0:T(8,128)S(1)}, u32[]{:S(2)}, u32[]{:S(2)}) collective-permute-start(f32[8,256,256]{2,1,0:T(8,128)S(1)} %add.34), channel_id=1, source_target_pairs={{0,2},{1,3},{2,0},{3,1},{4,6},{5,7},{6,4},{7,5},{8,10},{9,11},{10,... | collective-permute-start | bytes 6291464 | tf_op jit(solution)/shard_map/ppermute | solution.py:483
  (10 other events, 238.1 us)

commit v2 on v1

--- a/solution.py
+++ b/solution.py
@@ -10,6 +10,7 @@
 NORM_EPS = 1e-6
 TM = 256
 BT = 512
+DEPTH = 4
 F32 = jnp.float32
 BF16 = jnp.bfloat16
 VMEM_LIMIT = 60 * 1024 * 1024
@@ -62,7 +63,7 @@
         count = pre[n : n + 8]
         start = start + TM * jnp.maximum(jnp.floor((count + (TM - 1.0)) * (1.0 / TM)), 1.0)
     tab_ref[n_exp : n_exp + 1, :] = (start[0:1] * (1.0 / TM)).astype(jnp.int32)
-    pos_ref[...] = (pos * 2.0).astype(jnp.int32)
+    pos_ref[...] = pos.astype(jnp.int32)
 
 
 def route_ranks(ids, slots, n_exp, rows):
@@ -80,19 +81,39 @@
     return pos.reshape(-1), tab[:, 0]
 
 
-def put_pairs(ref, rows, vals):
+def put_rows(ref, at, vals, pitch=2, off=0):
     n = vals.shape[0]
     half = vals.shape[1] // 2
-    ref[pl.ds(rows, n, stride=2), :] = vals[:, :half]
-    ref[pl.ds(rows + 1, n, stride=2), :] = vals[:, half:]
-
-
-def get_pairs(ref, rows, n):
-    return jnp.concatenate([ref[pl.ds(rows, n, stride=2), :], ref[pl.ds(rows + 1, n, stride=2), :]], axis=1)
+    ref[pl.ds(at + off, n, stride=pitch), :] = vals[:, :half]
+    ref[pl.ds(at + off + 1, n, stride=pitch), :] = vals[:, half:]
+
+
+def get_rows(ref, at, n, pitch=2, off=0):
+    return jnp.concatenate([ref[pl.ds(at + off + i, n, stride=pitch), :] for i in range(2)], axis=1)
 
 
 def pair(p):
-    return pl.ds(pl.multiple_of(p, 2), 2)
+    return pl.ds(pl.multiple_of(p * 2, 2), 2)
+
+
+def gather_sum(buf, acc, pos_ref, gate_ref, first, n_tok, top_k):
+    unroll = 8
+
+    def body(j, c):
+        base = first + j * unroll
+        at = pl.multiple_of(j * (2 * unroll), 2 * unroll)
+        for k in range(unroll):
+            total = None
+            for r in range(top_k):
+                i = base + (r * n_tok + k)
+                term = buf[pair(pos_ref[i]), :]
+                if gate_ref is not None:
+                    term = term * gate_ref[i]
+                total = term if total is None else total + term
+            acc[pl.ds(at + 2 * k, 2), :] = total
+        return c
+
+    lax.fori_loop(0, BT // unroll, body, 0)
 
 
 def zero_rows(ref):
@@ -109,32 +130,30 @@
         ref[whole * step :, :] = jnp.zeros((n % step, ref.shape[1]), F32)
 
 
-def pre_bwd_kernel(pos_ref, gate_ref, tab_ref, x_ref, g_ref, w1_ref, w2_ref, h_ref, xs_hbm, qs_hbm, xbuf, qbuf, nsc, gsc, xst, qst, sems, *, n_blocks, top_k, n_exp):
+def pre_bwd_kernel(pos_ref, gate_ref, tab_ref, x_ref, g_ref, w1_ref, w2_ref, h_ref, xs_hbm, qs_hbm, buf, src, xst, qst, sems, *, n_blocks, top_k, n_exp):
     step = pl.program_id(0)
     n_tok = n_blocks * BT
 
     @pl.when(step == 0)
     def _():
-        zero_rows(xbuf)
-        zero_rows(qbuf)
+        zero_rows(buf)
 
     h = dense_forward(x_ref[...].astype(F32), w1_ref[...], w2_ref[...])
     h_ref[...] = h
     hf = h.astype(F32)
-    put_pairs(nsc, 0, (hf * rms_scale(hf)).astype(BF16).astype(F32))
-    put_pairs(gsc, 0, g_ref[...].astype(F32))
-    base = step * BT
+    put_rows(src, 0, (hf * rms_scale(hf)).astype(BF16).astype(F32), 4, 0)
+    put_rows(src, 0, g_ref[...].astype(F32), 4, 2)
     unroll = 8
+    is_row = lax.broadcasted_iota(jnp.int32, (4, buf.shape[1]), 0) < 2
 
     def scatter(j, c):
+        base = step * BT + j * unroll
+        at = pl.multiple_of(j * (4 * unroll), 4 * unroll)
         for k in range(unroll):
-            t = j * unroll + k
-            nv = nsc[pair(2 * t), :]
-            gv = gsc[pair(2 * t), :]
+            v = src[pl.ds(at + 4 * k, 4), :]
             for r in range(top_k):
-                p = pos_ref[r * n_tok + base + t]
-                xbuf[pair(p), :] = nv
-                qbuf[pair(p), :] = gv * gate_ref[r * n_tok + base + t]
+                p = pl.multiple_of(pos_ref[base + (r * n_tok + k)] * 4, 4)
+                buf[pl.ds(p, 4), :] = v * jnp.where(is_row, 1.0, gate_ref[base + (r * n_tok + k)])
         return c
 
     lax.fori_loop(0, BT // unroll, scatter, 0)
@@ -151,23 +170,23 @@
             )
 
         def convert(t, c):
-            slot = lax.rem(t, 2)
-
-            @pl.when(t >= 2)
+            slot = lax.rem(t, DEPTH)
+
+            @pl.when(t >= DEPTH)
             def _():
-                for cp in copies(t - 2, slot):
+                for cp in copies(t - DEPTH, slot):
                     cp.wait()
 
-            rows = pl.multiple_of(t * (2 * TM), 2 * TM)
-            xst[slot] = get_pairs(xbuf, rows, TM).astype(BF16)
-            qst[slot] = get_pairs(qbuf, rows, TM).astype(BF16)
+            rows = pl.multiple_of(t * (4 * TM), 4 * TM)
+            xst[slot] = get_rows(buf, rows, TM, 4, 0).astype(BF16)
+            qst[slot] = get_rows(buf, rows, TM, 4, 2).astype(BF16)
             for cp in copies(t, slot):
                 cp.start()
             return c
 
         lax.fori_loop(0, n_tiles, convert, 0)
-        for back in (2, 1):
-            for cp in copies(n_tiles - back, lax.rem(n_tiles - back, 2)):
+        for back in range(DEPTH, 0, -1):
+            for cp in copies(n_tiles - back, lax.rem(n_tiles - back, DEPTH)):
                 cp.wait()
 
 
@@ -188,13 +207,11 @@
             jax.ShapeDtypeStruct((rows, hid), BF16),
         ),
         scratch_shapes=[
-            pltpu.VMEM((2 * rows + 8, hid // 2), F32),
-            pltpu.VMEM((2 * rows + 8, hid // 2), F32),
-            pltpu.VMEM((2 * BT, hid // 2), F32),
-            pltpu.VMEM((2 * BT, hid // 2), F32),
-            pltpu.VMEM((2, TM, hid), BF16),
-            pltpu.VMEM((2, TM, hid), BF16),
-            pltpu.SemaphoreType.DMA((2, 2)),
+            pltpu.VMEM((4 * rows + 8, hid // 2), F32),
+            pltpu.VMEM((4 * BT, hid // 2), F32),
+            pltpu.VMEM((DEPTH, TM, hid), BF16),
+            pltpu.VMEM((DEPTH, TM, hid), BF16),
+            pltpu.SemaphoreType.DMA((2, DEPTH)),
         ],
         compiler_params=pltpu.CompilerParams(vmem_limit_bytes=VMEM_LIMIT),
         cost_estimate=pl.CostEstimate(flops=30_000_000_000, bytes_accessed=30_000_000, transcendentals=0),
@@ -202,84 +219,123 @@
     )(pos, gates, tab, x, g, w1, w2)
 
 
-def exp_bwd_kernel(first_ref, tab_ref, wg_ref, wu_ref, wd_ref, xs_hbm, qs_hbm, rs_hbm, dwg_ref, dwu_ref, dwd_ref, xb, qb, rb, sems, *, n_loc):
+def exp_bwd_kernel(first_ref, tab_ref, wg_hbm, wu_hbm, wd_hbm, xs_hbm, qs_hbm, rs_hbm, dwg_hbm, dwu_hbm, dwd_hbm, wb, dwb, xb, qb, rb, sems, wsems, dsems, *, n_loc):
     first = first_ref[0]
     begin = tab_ref[first]
     end = tab_ref[first + n_loc]
+    w_hbm = (wg_hbm, wu_hbm, wd_hbm)
+    dw_hbm = (dwg_hbm, dwu_hbm, dwd_hbm)
 
     def rows_of(t):
         return pl.ds(pl.multiple_of(t * TM, TM), TM)
 
-    def loads(t, slot):
+    def loads(t):
+        slot = lax.rem(t, DEPTH)
         return (
             pltpu.make_async_copy(xs_hbm.at[rows_of(t)], xb.at[slot], sems.at[0, slot]),
             pltpu.make_async_copy(qs_hbm.at[rows_of(t)], qb.at[slot], sems.at[1, slot]),
         )
 
-    def save(t, slot):
+    def save(t):
+        slot = lax.rem(t, DEPTH)
         return pltpu.make_async_copy(rb.at[slot], rs_hbm.at[rows_of(t)], sems.at[2, slot])
 
-    for cp in loads(begin, lax.rem(begin, 2)):
+    def w_loads(e):
+        slot = lax.rem(e, 2)
+        return [pltpu.make_async_copy(w_hbm[i].at[e], wb.at[slot, i], wsems.at[i, slot]) for i in range(3)]
+
+    def dw_saves(e):
+        slot = lax.rem(e, 2)
+        return [pltpu.make_async_copy(dwb.at[slot, i], dw_hbm[i].at[e], dsems.at[i, slot]) for i in range(3)]
+
+    for cp in w_loads(0):
         cp.start()
-    dwg_ref[...] = jnp.zeros_like(dwg_ref)
-    dwu_ref[...] = jnp.zeros_like(dwu_ref)
-    dwd_ref[...] = jnp.zeros_like(dwd_ref)
-
-    def body(t, e):
-        slot = lax.rem(t, 2)
-        e = jnp.where(t >= tab_ref[first + e + 1], e + 1, e)
-
-        @pl.when(t + 1 < end)
+    for ahead in range(DEPTH - 1):
+        for cp in loads(begin + ahead):
+            cp.start()
+
+    def expert(e, c):
+        wslot = lax.rem(e, 2)
+        for cp in w_loads(e):
+            cp.wait()
+
+        @pl.when(e + 1 < n_loc)
         def _():
-            for cp in loads(t + 1, 1 - slot):
+            for cp in w_loads(e + 1):
                 cp.start()
 
-        for cp in loads(t, slot):
+        @pl.when(e >= 2)
+        def _():
+            for cp in dw_saves(e - 2):
+                cp.wait()
+
+        dwb[wslot] = jnp.zeros(dwb.shape[1:], F32)
+
+        def body(t, c):
+            slot = lax.rem(t, DEPTH)
+
+            @pl.when(t + (DEPTH - 1) < end)
+            def _():
+                for cp in loads(t + (DEPTH - 1)):
+                    cp.start()
+
+            for cp in loads(t):
+                cp.wait()
+
+            @pl.when(t >= begin + DEPTH)
+            def _():
+                save(t - DEPTH).wait()
+
+            x = xb[slot]
+            q = qb[slot]
+            wg, wu, wd = wb[wslot, 0], wb[wslot, 1], wb[wslot, 2]
+            pre = dot(x, wg)
+            up = dot(x, wu)
+            sig = jax.nn.sigmoid(pre)
+            sil = pre * sig
+            act = (sil * up).astype(BF16)
+            dwb[wslot, 2] += dot_tn(act, q)
+            da = dot_nt(q, wd).astype(BF16).astype(F32)
+            dpre = (da * up * (sig * (1.0 + pre * (1.0 - sig)))).astype(BF16)
+            dup = (da * sil).astype(BF16)
+            dwb[wslot, 0] += dot_tn(x, dpre)
+            dwb[wslot, 1] += dot_tn(x, dup)
+            rb[slot] = (dot_nt(dpre, wg) + dot_nt(dup, wu)).astype(BF16)
+            save(t).start()
+            return c
+
+        lax.fori_loop(tab_ref[first + e], tab_ref[first + e + 1], body, 0)
+        for cp in dw_saves(e):
+            cp.start()
+        return c
+
+    lax.fori_loop(0, n_loc, expert, 0)
+    for back in range(DEPTH, 0, -1):
+        save(end - back).wait()
+    for e in (n_loc - 2, n_loc - 1):
+        for cp in dw_saves(e):
             cp.wait()
-
-        @pl.when(t >= begin + 2)
-        def _():
-            save(t - 2, slot).wait()
-
-        x = xb[slot]
-        q = qb[slot]
-        wg, wu, wd = wg_ref[e], wu_ref[e], wd_ref[e]
-        pre = dot(x, wg)
-        up = dot(x, wu)
-        sig = jax.nn.sigmoid(pre)
-        sil = pre * sig
-        act = (sil * up).astype(BF16)
-        dwd_ref[e] += dot_tn(act, q)
-        da = dot_nt(q, wd).astype(BF16).astype(F32)
-        dpre = (da * up * (sig * (1.0 + pre * (1.0 - sig)))).astype(BF16)
-        dup = (da * sil).astype(BF16)
-        dwg_ref[e] += dot_tn(x, dpre)
-        dwu_ref[e] += dot_tn(x, dup)
-        rb[slot] = (dot_nt(dpre, wg) + dot_nt(dup, wu)).astype(BF16)
-        save(t, slot).start()
-        return e
-
-    lax.fori_loop(begin, end, body, 0)
-    for back in (2, 1):
-        save(end - back, lax.rem(end - back, 2)).wait()
 
 
 def exp_bwd(first, tab, wg, wu, wd, xs, qs):
     n_loc, hid, ff = wg.shape
     smem = pl.BlockSpec(memory_space=pltpu.SMEM)
-    vmem = pl.BlockSpec(memory_space=pltpu.VMEM)
     hbm = pl.BlockSpec(memory_space=pl.ANY)
     dw = jax.ShapeDtypeStruct((n_loc, hid, ff), F32)
     return pl.pallas_call(
         functools.partial(exp_bwd_kernel, n_loc=n_loc),
-        in_specs=[smem, smem, vmem, vmem, vmem, hbm, hbm],
-        out_specs=[hbm, vmem, vmem, vmem],
+        in_specs=[smem, smem, hbm, hbm, hbm, hbm, hbm],
+        out_specs=[hbm, hbm, hbm, hbm],
         out_shape=(jax.ShapeDtypeStruct(xs.shape, BF16), dw, dw, dw),
         input_output_aliases={5: 0},
         scratch_shapes=[
-            pltpu.VMEM((2, TM, hid), BF16),
-            pltpu.VMEM((2, TM, hid), BF16),
-            pltpu.VMEM((2, TM, hid), BF16),
+            pltpu.VMEM((2, 3, hid, ff), BF16),
+            pltpu.VMEM((2, 3, hid, ff), F32),
+            pltpu.VMEM((DEPTH, TM, hid), BF16),
+            pltpu.VMEM((DEPTH, TM, hid), BF16),
+            pltpu.VMEM((DEPTH, TM, hid), BF16),
+            pltpu.SemaphoreType.DMA((3, DEPTH)),
+            pltpu.SemaphoreType.DMA((3, 2)),
             pltpu.SemaphoreType.DMA((3, 2)),
         ],
         compiler_params=pltpu.CompilerParams(vmem_limit_bytes=VMEM_LIMIT),
@@ -296,39 +352,27 @@
     def _():
         n_tiles = tab_ref[n_exp]
 
-        def load(t, slot):
+        def load(t):
+            slot = lax.rem(t, DEPTH)
             return pltpu.make_async_copy(rs_hbm.at[pl.ds(pl.multiple_of(t * TM, TM), TM)], st.at[slot], sems.at[slot])
 
-        load(0, 0).start()
+        for ahead in range(DEPTH - 1):
+            load(ahead).start()
         rbuf[2 * rows : 2 * rows + 8, :] = jnp.zeros((8, rbuf.shape[1]), F32)
 
         def expand(t, c):
-            slot = lax.rem(t, 2)
-
-            @pl.when(t + 1 < n_tiles)
+            @pl.when(t + (DEPTH - 1) < n_tiles)
             def _():
-                load(t + 1, 1 - slot).start()
-
-            load(t, slot).wait()
-            put_pairs(rbuf, pl.multiple_of(t * (2 * TM), 2 * TM), st[slot].astype(F32))
+                load(t + (DEPTH - 1)).start()
+
+            load(t).wait()
+            put_rows(rbuf, pl.multiple_of(t * (2 * TM), 2 * TM), st[lax.rem(t, DEPTH)].astype(F32))
             return c
 
         lax.fori_loop(0, n_tiles, expand, 0)
 
-    base = step * BT
-    unroll = 8
-
-    def gather(j, c):
-        for k in range(unroll):
-            t = j * unroll + k
-            total = rbuf[pair(pos_ref[base + t]), :]
-            for r in range(1, top_k):
-                total = total + rbuf[pair(pos_ref[r * n_tok + base + t]), :]
-            acc[pair(2 * t), :] = total
-        return c
-
-    lax.fori_loop(0, BT // unroll, gather, 0)
-    dn = get_pairs(acc, 0, BT)
+    gather_sum(rbuf, acc, pos_ref, None, step * BT, n_tok, top_k)
+    dn = get_rows(acc, 0, BT)
     xf = x_ref[...].astype(F32)
     u = dot((xf * rms_scale(xf)).astype(BF16), w1_ref[...])
     dh = g_ref[...].astype(F32) + rms_back(h_ref[...].astype(F32), dn)
@@ -353,8 +397,8 @@
         scratch_shapes=[
             pltpu.VMEM((2 * rows + 8, hid // 2), F32),
             pltpu.VMEM((2 * BT, hid // 2), F32),
-            pltpu.VMEM((2, TM, hid), BF16),
-            pltpu.SemaphoreType.DMA((2,)),
+            pltpu.VMEM((DEPTH, TM, hid), BF16),
+            pltpu.SemaphoreType.DMA((DEPTH,)),
         ],
         compiler_params=pltpu.CompilerParams(vmem_limit_bytes=VMEM_LIMIT),
         cost_estimate=pl.CostEstimate(flops=30_000_000_000, bytes_accessed=30_000_000, transcendentals=0),
@@ -385,14 +429,15 @@
         base = step * BT
         hsc[pl.ds(pl.multiple_of(base, BT), BT), :] = h
         hf = h.astype(F32)
-        put_pairs(nsc, 0, (hf * rms_scale(hf)).astype(BF16).astype(F32))
+        put_rows(nsc, 0, (hf * rms_scale(hf)).astype(BF16).astype(F32))
 
         def scatter(j, c):
+            first = base + j * unroll
+            at = pl.multiple_of(j * (2 * unroll), 2 * unroll)
             for k in range(unroll):
-                t = j * unroll + k
-                nv = nsc[pair(2 * t), :]
+                nv = nsc[pl.ds(at + 2 * k, 2), :]
                 for r in range(top_k):
-                    buf[pair(pos_ref[r * n_tok + base + t]), :] = nv
+                    buf[pair(pos_ref[first + (r * n_tok + k)]), :] = nv
             return c
 
         lax.fori_loop(0, BT // unroll, scatter, 0)
@@ -408,11 +453,11 @@
             def body(t, e):
                 e = jnp.where(t >= tab_ref[first + e + 1], e + 1, e)
                 at = pl.multiple_of(t * (2 * TM), 2 * TM)
-                x = get_pairs(buf, at, TM).astype(BF16)
+                x = get_rows(buf, at, TM).astype(BF16)
                 pre = dot(x, wsc[3 * g, e])
                 up = dot(x, wsc[3 * g + 1, e])
                 act = (pre * jax.nn.sigmoid(pre) * up).astype(BF16)
-                put_pairs(buf, at, dot(act, wsc[3 * g + 2, e]).astype(BF16).astype(F32))
+                put_rows(buf, at, dot(act, wsc[3 * g + 2, e]).astype(BF16).astype(F32))
                 return e
 
             lax.fori_loop(tab_ref[first], tab_ref[first + n_loc], body, 0)
@@ -421,20 +466,9 @@
     def _():
         base = (step - n_blocks - 1) * BT
 
-        def gather(j, c):
-            for k in range(unroll):
-                t = j * unroll + k
-                total = None
-                for r in range(top_k):
-                    at = r * n_tok + base + t
-                    term = buf[pair(pos_ref[at]), :] * gate_ref[at]
-                    total = term if total is None else total + term
-                nsc[pair(2 * t), :] = total
-            return c
-
-        lax.fori_loop(0, BT // unroll, gather, 0)
+        gather_sum(buf, nsc, pos_ref, gate_ref, base, n_tok, top_k)
         h = hsc[pl.ds(pl.multiple_of(base, BT), BT), :]
-        y_ref[...] = (h.astype(F32) + get_pairs(nsc, 0, BT)).astype(BF16)
+        y_ref[...] = (h.astype(F32) + get_rows(nsc, 0, BT)).astype(BF16)
 
 
 def fwd(firsts, pos, gates, tab, x, w1, w2, weights, rows, n_exp, top_k):
@@ -505,21 +539,20 @@
         gates_f = gates_fwd.T.reshape(-1).astype(F32)
 
         h_bwd, xs, qs = pre_bwd(pos_b, gates_b, tab_b, x_saved, grad_in, w1, w2, rows, n_exp, top_k)
-        parts = []
-        for g in range(ep_size):
-            xs, *dw = exp_bwd(firsts[g].reshape(1), tab_b, *weights[g], xs, qs)
-            parts.append(dw)
+        parts = [None] * ep_size
+        for g in (0, 3, 2):
+            xs, *parts[g] = exp_bwd(firsts[g].reshape(1), tab_b, *weights[g], xs, qs)
+        sums = [parts[2][i] + mate(parts[3][i]) for i in range(3)]
+        xs, *sums = lax.optimization_barrier((xs, *sums))
+        there = [chip(v) for v in sums]
+        xs, *parts[1] = exp_bwd(firsts[1].reshape(1), tab_b, *weights[1], xs, qs)
         grad_x = post_bwd(pos_b, tab_b, x_saved, grad_in, h_bwd, w1, w2, xs, n_exp, top_k)
-        dx_prev = lax.ppermute(grad_x, "pp", prev_perm)
-
-        dws = []
-        for i in range(3):
-            there = chip(parts[2][i] + mate(parts[3][i]))
-            dws.append(parts[0][i] + mate(parts[1][i]) + there)
-
+        x_fwd, grad_x = lax.optimization_barrier((x_fwd, grad_x))
+        dx_prev = lax.ppermute(grad_x[None], "pp", prev_perm)
+        dws = [parts[0][i] + mate(parts[1][i]) + there[i] for i in range(3)]
         y_out = fwd(jnp.stack(firsts), pos_f, gates_f, tab_f, x_fwd, w1, w2, weights, rows, n_exp, top_k)
-        y_next = lax.ppermute(y_out, "pp", next_perm)
-        return y_next[None], dx_prev[None], dws[0][None], dws[1][None], dws[2][None]
+        y_next = lax.ppermute(y_out[None], "pp", next_perm)
+        return y_next, dx_prev, dws[0][None], dws[1][None], dws[2][None]
 
     in_specs = (tok_spec,) * 9 + (dense_spec, dense_spec, expert_spec, expert_spec, expert_spec)
     out_specs = (tok_spec, tok_spec, expert_spec, expert_spec, expert_spec)

time: 498 us -> 518 us (1.040); the launches traced: 490 us -> 517 us
  waiting for transfers between devices: 120 us -> 181 us
  Pallas kernels: 316 us -> 270 us
  starting transfers between devices: 24.9 us -> 34.5 us
    ppermute x2, waiting for transfers between devices: 38.1 us -> 79.1 us  [the longest x1 44.7 us: device_step(): dx_prev = lax.ppermute(grad_x[None], 'pp', prev_perm)]
    pallas_call x4, Pallas kernels: 90.6 us -> 69.7 us  [exp_bwd(): pl.pallas_call(functools.partial(exp_bwd_kernel, n_loc=n_loc), in_specs=[...]
    ppermute x6, waiting for transfers between devices: 82.3 us -> 99.2 us  [chip(): return lax.ppermute(a, 'ep', chip_perm)]
    pallas_call x1, Pallas kernels: 62.3 us -> 47.9 us  [post_bwd(): pl.pallas_call(functools.partial(post_bwd_kernel, n_blocks=n_blocks, top_...]
    pallas_call x1, Pallas kernels: 73.4 us -> 59.6 us  [pre_bwd(): pl.pallas_call(functools.partial(pre_bwd_kernel, n_blocks=n_blocks, top_k...]
    ppermute x6, starting transfers between devices: 15.3 us -> 23 us  [chip(): return lax.ppermute(a, 'ep', chip_perm)]
  transfers between devices with their start and end apart: 20 -> 20, of which waited for: 3 -> 7; matrix products, arithmetic and copies ran while one was open for 4% -> 5% of each run, Pallas kernels for 64% -> 45%
where the time goes in v2:
time: 518 us; the launch traced here: 517 us
  Pallas kernels  270 us (52%)
  waiting for transfers between devices  181 us (35%)
  starting transfers between devices  34.5 us (7%)
  other arithmetic  18.6 us (4%)
  local copies, waits for them, and re-layouts  12.4 us (2%)
    ppermute x6, waiting for transfers between devices, chip(): return lax.ppermute(a, 'ep', chip_perm)  99.2 us
    pallas_call x1, Pallas kernels, fwd(): pl.pallas_call(functools.partial(fwd_kernel, n_blocks=n_blocks, top_k=top...  86.8 us
    pallas_call x4, Pallas kernels, exp_bwd(): pl.pallas_call(functools.partial(exp_bwd_kernel, n_loc=n_loc), in_specs=[...  69.7 us
    pallas_call x1, Pallas kernels, pre_bwd(): pl.pallas_call(functools.partial(pre_bwd_kernel, n_blocks=n_blocks, top_k...  59.6 us
    pallas_call x1, Pallas kernels, post_bwd(): pl.pallas_call(functools.partial(post_bwd_kernel, n_blocks=n_blocks, top_...  47.9 us
    ppermute x1, waiting for transfers between devices, device_step(): dx_prev = lax.ppermute(grad_x[None], 'pp', prev_perm)  44.7 us
    ppermute x1, waiting for transfers between devices, device_step(): y_next = lax.ppermute(y_out[None], 'pp', next_perm)  34.4 us
    ppermute x6, starting transfers between devices, chip(): return lax.ppermute(a, 'ep', chip_perm)  23 us
  transfers between devices with their start and end apart: 20, of which 7 were waited for; matrix products, arithmetic and copies ran while one was open for 5% of the time, Pallas kernels for 45%

profile of v2, /device:TPU:0, one launch (start us, length us, event | category | flops | bytes accessed | tf_op | source)
XLA Modules:
  0.0 517.4 jit_solution(13096840128277613307)
XLA Ops:
  0.6 3.3 collective-permute-start.3
  10.4 2.9 rank.3
  14.7 13.3 %collective-permute-done.3.wg_hbm.rest_6_ = bf16[8,256,256]{2,1,0:T(8,128)(2,1)S(1)} collective-permute-done((bf16[8,256,256]{2,1,0:T(8,128)(2,1)}, bf16[8,256,256]{2,1,0:T(8,128)(2,1)S(1)}, u32[]{:S(2)}, u32[]{:S(2)}) %collective-permute-start.3) | collective-permute-done | bytes 1048608 | tf_op jit(solution)/shard_map/ppermute | solution.py:517
  27.9 22.5 %collective-permute-done.4.wu_hbm.rest_7_ = bf16[8,256,256]{2,1,0:T(8,128)(2,1)S(1)} collective-permute-done((bf16[8,256,256]{2,1,0:T(8,128)(2,1)}, bf16[8,256,256]{2,1,0:T(8,128)(2,1)S(1)}, u32[]{:S(2)}, u32[]{:S(2)}) %collective-permute-start.4) | collective-permute-done | bytes 1048608 | tf_op jit(solution)/shard_map/ppermute | solution.py:517
  50.4 21.6 %collective-permute-done.5.wd_hbm.rest_8_ = bf16[8,256,256]{2,1,0:T(8,128)(2,1)S(1)} collective-permute-done((bf16[8,256,256]{2,1,0:T(8,128)(2,1)}, bf16[8,256,256]{2,1,0:T(8,128)(2,1)S(1)}, u32[]{:S(2)}, u32[]{:S(2)}) %collective-permute-start.5) | collective-permute-done | bytes 1048608 | tf_op jit(solution)/shard_map/ppermute | solution.py:517
  72.0 59.6 %pre_bwd.1 = (bf16[4096,256]{1,0:T(8,128)(2,1)}, bf16[24576,256]{1,0:T(8,128)(2,1)}, bf16[24576,256]{1,0:T(8,128)(2,1)}) custom-call(s32[16384]{0:T(1024)} %bitcast.79, f32[16384]{0:T(1024)} %bitcast.53, s32[40]{0:T(128)} %slice_reduce_fusion.tab_ref, bf16[4096,256]{1,0:T(8,128)(2,1)} %bitcast.54, bf16[4096,256]{1,0:T(8,128)(2,1)} %bitcast.56, ...), custom_call_target="tpu_custom_call" | custom-call | flops 30000001024 | bytes 30000000 | tf_op jit(solution)/shard_map/pre_bwd/pallas_call | solution.py:199
  131.6 18.3 %exp_bwd.4 = (bf16[24576,256]{1,0:T(8,128)(2,1)}, f32[8,256,256]{2,1,0:T(8,128)}, f32[8,256,256]{2,1,0:T(8,128)}, f32[8,256,256]{2,1,0:T(8,128)}) custom-call(s32[1]{0:T(128)} %bitcast.first_ref, s32[40]{0:T(128)} %slice_reduce_fusion.tab_ref, bf16[8,256,256]{2,1,0:T(8,128)(2,1)} %bitcast.62, ...), custom_call_target="tpu_custom_call", output_to_operand_aliasing={{0}: (5, {})} | custom-call | flops 8000000000 | bytes 20000000 | tf_op jit(solution)/shard_map/exp_bwd/pallas_call | solution.py:325
  150.0 19.2 %exp_bwd.5 = (bf16[24576,256]{1,0:T(8,128)(2,1)}, f32[8,256,256]{2,1,0:T(8,128)}, f32[8,256,256]{2,1,0:T(8,128)}, f32[8,256,256]{2,1,0:T(8,128)}) custom-call(s32[1]{0:T(128)} %bitcast.3.first_ref, s32[40]{0:T(128)} %slice_reduce_fusion.tab_ref, bf16[8,256,256]{2,1,0:T(8,128)(2,1)} %collective-permute-done.6.wg_hbm.rest_9_, ...), custom_call_target="tpu_custom_call", output_to_operand_aliasing={{0}: (5, {})} | custom-call | flops 8000000000 | bytes 20000000 | tf_op jit(solution)/shard_map/exp_bwd/pallas_call | solution.py:325
  170.3 3.0 collective-permute-done.11
  175.5 2.9 rank.2
  180.3 16.9 %exp_bwd.6 = (bf16[24576,256]{1,0:T(8,128)(2,1)}, f32[8,256,256]{2,1,0:T(8,128)}, f32[8,256,256]{2,1,0:T(8,128)}, f32[8,256,256]{2,1,0:T(8,128)}) custom-call(s32[1]{0:T(128)} %bitcast.2.first_ref, s32[40]{0:T(128)} %slice_reduce_fusion.tab_ref, bf16[8,256,256]{2,1,0:T(8,128)(2,1)} %copy-done.9, ...), custom_call_target="tpu_custom_call", output_to_operand_aliasing={{0}: (5, {})} | custom-call | flops 8000000000 | bytes 20000000 | tf_op jit(solution)/shard_map/exp_bwd/pallas_call | solution.py:325
  197.2 4.0 add.29
  201.2 3.5 add.28
  208.1 15.4 %exp_bwd.7 = (bf16[24576,256]{1,0:T(8,128)(2,1)}, f32[8,256,256]{2,1,0:T(8,128)}, f32[8,256,256]{2,1,0:T(8,128)}, f32[8,256,256]{2,1,0:T(8,128)}) custom-call(s32[1]{0:T(128)} %bitcast.1.first_ref, s32[40]{0:T(128)} %slice_reduce_fusion.tab_ref, bf16[8,256,256]{2,1,0:T(8,128)(2,1)} %collective-permute-done.wg_hbm.rest_3_, ...), custom_call_target="tpu_custom_call", output_to_operand_aliasing={{0}: (5, {})} | custom-call | flops 8000000000 | bytes 20000000 | tf_op jit(solution)/shard_map/exp_bwd/pallas_call | solution.py:325
  223.5 5.1 collective-permute-start.18
  228.6 47.9 %post_bwd.1 = bf16[4096,256]{1,0:T(8,128)(2,1)} custom-call(s32[16384]{0:T(1024)} %bitcast.80, s32[40]{0:T(128)} %slice_reduce_fusion.tab_ref, bf16[4096,256]{1,0:T(8,128)(2,1)} %bitcast.55, bf16[4096,256]{1,0:T(8,128)(2,1)} %bitcast.57, bf16[4096,256]{1,0:T(8,128)(2,1)} %get-tuple-element.38.h_ref, bf16[256,256]{1,0:T(8,128)(2,1)} %bitcast.74, ...), custom_call_target="tpu_custom_call" | custom-call | flops 30000001024 | bytes 30000000 | tf_op jit(solution)/shard_map/post_bwd/pallas_call | solution.py:391
  276.5 86.8 %fwd.1 = bf16[4096,256]{1,0:T(8,128)(2,1)} custom-call(s32[4]{0:T(128)} %pad_add_fusion.firsts_ref, s32[16384]{0:T(1024)} %bitcast.81, f32[16384]{0:T(1024)} %bitcast.52, s32[40]{0:T(128)} %slice_reduce_fusion.1.tab_ref, bf16[4096,256]{1,0:T(8,128)(2,1)} %bitcast.58, bf16[256,256]{1,0:T(8,128)(2,1)} %bitcast.75, bf16[256,256]{1,0:T(8,128)(2,1)} %bitcast.78, ...), custom_call_target="tpu_custom_call" | custom-call | flops 80000000000 | bytes 30000000 | tf_op jit(solution)/shard_map/fwd/pallas_call | solution.py:482
  364.4 2.0 collective-permute-start.13
  366.4 10.8 %collective-permute-start.19 = (f32[8,256,256]{2,1,0:T(8,128)}, f32[8,256,256]{2,1,0:T(8,128)S(1)}, u32[]{:S(2)}, u32[]{:S(2)}) collective-permute-start(f32[8,256,256]{2,1,0:T(8,128)} %add.29), channel_id=1, source_target_pairs={{0,2},{1,3},{2,0},{3,1},{4,6},{5,7},{6,4},{7,5},{8,10},{9,11},{10,... | collective-permute-start | bytes 6291464 | tf_op jit(solution)/shard_map/ppermute | solution.py:517
  377.3 34.4 %collective-permute-done.12 = bf16[1,4096,256]{2,1,0:T(8,128)(2,1)S(1)} collective-permute-done((bf16[1,4096,256]{2,1,0:T(8,128)(2,1)}, bf16[1,4096,256]{2,1,0:T(8,128)(2,1)S(1)}, u32[]{:S(2)}, u32[]{:S(2)}) %collective-permute-start.12) | collective-permute-done | bytes 2097184 | tf_op jit(solution)/shard_map/ppermute | solution.py:554
  413.7 44.7 %collective-permute-done.13 = bf16[1,4096,256]{2,1,0:T(8,128)(2,1)S(1)} collective-permute-done((bf16[1,4096,256]{2,1,0:T(8,128)(2,1)}, bf16[1,4096,256]{2,1,0:T(8,128)(2,1)S(1)}, u32[]{:S(2)}, u32[]{:S(2)}) %collective-permute-start.13) | collective-permute-done | bytes 2097184 | tf_op jit(solution)/shard_map/ppermute | solution.py:551
  458.4 6.8 %collective-permute-start.15 = (f32[8,256,256]{2,1,0:T(8,128)S(1)}, f32[8,256,256]{2,1,0:T(8,128)S(1)}, u32[]{:S(2)}, u32[]{:S(2)}) collective-permute-start(f32[8,256,256]{2,1,0:T(8,128)S(1)} %add.27), channel_id=1, source_target_pairs={{0,2},{1,3},{2,0},{3,1},{4,6},{5,7},{6,4},{7,5},{8,10},{9,11},{10,... | collective-permute-start | bytes 6291464 | tf_op jit(solution)/shard_map/ppermute | solution.py:517
  465.2 4.1 add_bitcast_fusion
  471.2 41.8 %collective-permute-done.15 = f32[8,256,256]{2,1,0:T(8,128)S(1)} collective-permute-done((f32[8,256,256]{2,1,0:T(8,128)S(1)}, f32[8,256,256]{2,1,0:T(8,128)S(1)}, u32[]{:S(2)}, u32[]{:S(2)}) %collective-permute-start.15) | collective-permute-done | bytes 2097184 | tf_op jit(solution)/shard_map/ppermute | solution.py:517
  (68 shorter events, 25.9 us)
Async XLA Ops:
  0.6 27.3 %collective-permute-start.3 = (bf16[8,256,256]{2,1,0:T(8,128)(2,1)}, bf16[8,256,256]{2,1,0:T(8,128)(2,1)S(1)}, u32[]{:S(2)}, u32[]{:S(2)}) collective-permute-start(bf16[8,256,256]{2,1,0:T(8,128)(2,1)} %bitcast.61), channel_id=1, source_target_pairs={{0,2},{1,3},{2,0},{3,1},{4,6},{5,7},{6,4},{7,5},{8,10},{9,11},{10,... | collective-permute-start | bytes 3145736 | tf_op jit(solution)/shard_map/ppermute | solution.py:517
  3.9 46.5 %collective-permute-start.4 = (bf16[8,256,256]{2,1,0:T(8,128)(2,1)}, bf16[8,256,256]{2,1,0:T(8,128)(2,1)S(1)}, u32[]{:S(2)}, u32[]{:S(2)}) collective-permute-start(bf16[8,256,256]{2,1,0:T(8,128)(2,1)} %bitcast.65), channel_id=1, source_target_pairs={{0,2},{1,3},{2,0},{3,1},{4,6},{5,7},{6,4},{7,5},{8,10},{9,11},{10,... | collective-permute-start | bytes 3145736 | tf_op jit(solution)/shard_map/ppermute | solution.py:517
  3.9 68.1 %collective-permute-start.5 = (bf16[8,256,256]{2,1,0:T(8,128)(2,1)}, bf16[8,256,256]{2,1,0:T(8,128)(2,1)S(1)}, u32[]{:S(2)}, u32[]{:S(2)}) collective-permute-start(bf16[8,256,256]{2,1,0:T(8,128)(2,1)} %bitcast.69), channel_id=1, source_target_pairs={{0,2},{1,3},{2,0},{3,1},{4,6},{5,7},{6,4},{7,5},{8,10},{9,11},{10,... | collective-permute-start | bytes 3145736 | tf_op jit(solution)/shard_map/ppermute | solution.py:517
  27.9 103.7 %copy-start.9 = (bf16[8,256,256]{2,1,0:T(8,128)(2,1)}, bf16[8,256,256]{2,1,0:T(8,128)(2,1)S(1)}, u32[]{:S(2)}) copy-start(bf16[8,256,256]{2,1,0:T(8,128)(2,1)S(1)} %collective-permute-done.3.wg_hbm.rest_6_) | copy-start | bytes 3145732
  27.9 122.0 %collective-permute-start.6 = (bf16[8,256,256]{2,1,0:T(8,128)(2,1)S(1)}, bf16[8,256,256]{2,1,0:T(8,128)(2,1)}, u32[]{:S(2)}, u32[]{:S(2)}) collective-permute-start(bf16[8,256,256]{2,1,0:T(8,128)(2,1)S(1)} %collective-permute-done.3.wg_hbm.rest_6_), channel_id=1, source_target_pairs={{0,1},{1,0},{2,3},{3,2},{4,5},{5,4},{6,7},{7,6},{8,9},{9,8},{10,11... | collective-permute-start | bytes 3145736 | tf_op jit(solution)/shard_map/ppermute | solution.py:514
  50.4 81.2 %copy-start.10 = (bf16[8,256,256]{2,1,0:T(8,128)(2,1)}, bf16[8,256,256]{2,1,0:T(8,128)(2,1)S(1)}, u32[]{:S(2)}) copy-start(bf16[8,256,256]{2,1,0:T(8,128)(2,1)S(1)} %collective-permute-done.4.wu_hbm.rest_7_) | copy-start | bytes 3145732
  50.4 99.6 %collective-permute-start.7 = (bf16[8,256,256]{2,1,0:T(8,128)(2,1)S(1)}, bf16[8,256,256]{2,1,0:T(8,128)(2,1)}, u32[]{:S(2)}, u32[]{:S(2)}) collective-permute-start(bf16[8,256,256]{2,1,0:T(8,128)(2,1)S(1)} %collective-permute-done.4.wu_hbm.rest_7_), channel_id=1, source_target_pairs={{0,1},{1,0},{2,3},{3,2},{4,5},{5,4},{6,7},{7,6},{8,9},{9,8},{10,11... | collective-permute-start | bytes 3145736 | tf_op jit(solution)/shard_map/ppermute | solution.py:514
  72.0 59.6 %copy-start.11 = (bf16[8,256,256]{2,1,0:T(8,128)(2,1)}, bf16[8,256,256]{2,1,0:T(8,128)(2,1)S(1)}, u32[]{:S(2)}) copy-start(bf16[8,256,256]{2,1,0:T(8,128)(2,1)S(1)} %collective-permute-done.5.wd_hbm.rest_8_) | copy-start | bytes 3145732
  72.0 78.0 %collective-permute-start.8 = (bf16[8,256,256]{2,1,0:T(8,128)(2,1)S(1)}, bf16[8,256,256]{2,1,0:T(8,128)(2,1)}, u32[]{:S(2)}, u32[]{:S(2)}) collective-permute-start(bf16[8,256,256]{2,1,0:T(8,128)(2,1)S(1)} %collective-permute-done.5.wd_hbm.rest_8_), channel_id=1, source_target_pairs={{0,1},{1,0},{2,3},{3,2},{4,5},{5,4},{6,7},{7,6},{8,9},{9,8},{10,11... | collective-permute-start | bytes 3145736 | tf_op jit(solution)/shard_map/ppermute | solution.py:514
  169.2 4.1 collective-permute-start.11
  169.3 32.0 %collective-permute-start.10 = (f32[8,256,256]{2,1,0:T(8,128)}, f32[8,256,256]{2,1,0:T(8,128)}, u32[]{:S(2)}, u32[]{:S(2)}) collective-permute-start(f32[8,256,256]{2,1,0:T(8,128)} %get-tuple-element.47), channel_id=1, source_target_pairs={{0,1},{1,0},{2,3},{3,2},{4,5},{5,4},{6,7},{7,6},{8,9},{9,8},{10,11... | collective-permute-start | bytes 6291464 | tf_op jit(solution)/shard_map/ppermute | solution.py:514
  169.8 35.0 %collective-permute-start.9 = (f32[8,256,256]{2,1,0:T(8,128)}, f32[8,256,256]{2,1,0:T(8,128)S(1)}, u32[]{:S(2)}, u32[]{:S(2)}) collective-permute-start(f32[8,256,256]{2,1,0:T(8,128)} %get-tuple-element.45), channel_id=1, source_target_pairs={{0,1},{1,0},{2,3},{3,2},{4,5},{5,4},{6,7},{7,6},{8,9},{9,8},{10,11... | collective-permute-start | bytes 6291464 | tf_op jit(solution)/shard_map/ppermute | solution.py:514
  169.8 38.3 %collective-permute-start = (bf16[8,256,256]{2,1,0:T(8,128)(2,1)S(1)}, bf16[8,256,256]{2,1,0:T(8,128)(2,1)}, u32[]{:S(2)}, u32[]{:S(2)}) collective-permute-start(bf16[8,256,256]{2,1,0:T(8,128)(2,1)S(1)} %bitcast.64), channel_id=1, source_target_pairs={{0,1},{1,0},{2,3},{3,2},{4,5},{5,4},{6,7},{7,6},{8,9},{9,8},{10,11... | collective-permute-start | bytes 3145736 | tf_op jit(solution)/shard_map/ppermute | solution.py:514
  170.3 37.8 %collective-permute-start.1 = (bf16[8,256,256]{2,1,0:T(8,128)(2,1)}, bf16[8,256,256]{2,1,0:T(8,128)(2,1)}, u32[]{:S(2)}, u32[]{:S(2)}) collective-permute-start(bf16[8,256,256]{2,1,0:T(8,128)(2,1)} %bitcast.67), channel_id=1, source_target_pairs={{0,1},{1,0},{2,3},{3,2},{4,5},{5,4},{6,7},{7,6},{8,9},{9,8},{10,11... | collective-permute-start | bytes 3145736 | tf_op jit(solution)/shard_map/ppermute | solution.py:514
  173.4 34.7 %collective-permute-start.2 = (bf16[8,256,256]{2,1,0:T(8,128)(2,1)}, bf16[8,256,256]{2,1,0:T(8,128)(2,1)}, u32[]{:S(2)}, u32[]{:S(2)}) collective-permute-start(bf16[8,256,256]{2,1,0:T(8,128)(2,1)} %bitcast.71), channel_id=1, source_target_pairs={{0,1},{1,0},{2,3},{3,2},{4,5},{5,4},{6,7},{7,6},{8,9},{9,8},{10,11... | collective-permute-start | bytes 3145736 | tf_op jit(solution)/shard_map/ppermute | solution.py:514
  223.5 153.7 %collective-permute-start.18 = (f32[8,256,256]{2,1,0:T(8,128)}, f32[8,256,256]{2,1,0:T(8,128)}, u32[]{:S(2)}, u32[]{:S(2)}) collective-permute-start(f32[8,256,256]{2,1,0:T(8,128)} %get-tuple-element.61), channel_id=1, source_target_pairs={{0,1},{1,0},{2,3},{3,2},{4,5},{5,4},{6,7},{7,6},{8,9},{9,8},{10,11... | collective-permute-start | bytes 6291464 | tf_op jit(solution)/shard_map/ppermute | solution.py:514
  363.3 48.4 %collective-permute-start.12 = (bf16[1,4096,256]{2,1,0:T(8,128)(2,1)}, bf16[1,4096,256]{2,1,0:T(8,128)(2,1)S(1)}, u32[]{:S(2)}, u32[]{:S(2)}) collective-permute-start(bf16[1,4096,256]{2,1,0:T(8,128)(2,1)} %bitcast.60), channel_id=1, source_target_pairs={{0,4},{4,8},{8,12},{12,0},{1,5},{5,9},{9,13},{13,1},{2,6},{6,10},{... | collective-permute-start | bytes 6291464 | tf_op jit(solution)/shard_map/ppermute | solution.py:554
  364.4 94.1 %collective-permute-start.13 = (bf16[1,4096,256]{2,1,0:T(8,128)(2,1)}, bf16[1,4096,256]{2,1,0:T(8,128)(2,1)S(1)}, u32[]{:S(2)}, u32[]{:S(2)}) collective-permute-start(bf16[1,4096,256]{2,1,0:T(8,128)(2,1)} %bitcast.59), channel_id=1, source_target_pairs={{0,12},{4,0},{8,4},{12,8},{1,13},{5,1},{9,5},{13,9},{2,14},{6,2},{... | collective-permute-start | bytes 6291464 | tf_op jit(solution)/shard_map/ppermute | solution.py:551
  366.4 98.8 %collective-permute-start.19 = (f32[8,256,256]{2,1,0:T(8,128)}, f32[8,256,256]{2,1,0:T(8,128)S(1)}, u32[]{:S(2)}, u32[]{:S(2)}) collective-permute-start(f32[8,256,256]{2,1,0:T(8,128)} %add.29), channel_id=1, source_target_pairs={{0,2},{1,3},{2,0},{3,1},{4,6},{5,7},{6,4},{7,5},{8,10},{9,11},{10,... | collective-permute-start | bytes 6291464 | tf_op jit(solution)/shard_map/ppermute | solution.py:517
  377.2 92.1 %collective-permute-start.16 = (f32[8,256,256]{2,1,0:T(8,128)}, f32[8,256,256]{2,1,0:T(8,128)S(1)}, u32[]{:S(2)}, u32[]{:S(2)}) collective-permute-start(f32[8,256,256]{2,1,0:T(8,128)} %get-tuple-element.58), channel_id=1, source_target_pairs={{0,1},{1,0},{2,3},{3,2},{4,5},{5,4},{6,7},{7,6},{8,9},{9,8},{10,11... | collective-permute-start | bytes 6291464 | tf_op jit(solution)/shard_map/ppermute | solution.py:514
  377.2 92.1 %collective-permute-start.17 = (f32[8,256,256]{2,1,0:T(8,128)}, f32[8,256,256]{2,1,0:T(8,128)S(1)}, u32[]{:S(2)}, u32[]{:S(2)}) collective-permute-start(f32[8,256,256]{2,1,0:T(8,128)} %add.28), channel_id=1, source_target_pairs={{0,2},{1,3},{2,0},{3,1},{4,6},{5,7},{6,4},{7,5},{8,10},{9,11},{10,... | collective-permute-start | bytes 6291464 | tf_op jit(solution)/shard_map/ppermute | solution.py:517
  411.7 59.4 %collective-permute-start.14 = (f32[8,256,256]{2,1,0:T(8,128)}, f32[8,256,256]{2,1,0:T(8,128)S(1)}, u32[]{:S(2)}, u32[]{:S(2)}) collective-permute-start(f32[8,256,256]{2,1,0:T(8,128)} %get-tuple-element.55), channel_id=1, source_target_pairs={{0,1},{1,0},{2,3},{3,2},{4,5},{5,4},{6,7},{7,6},{8,9},{9,8},{10,11... | collective-permute-start | bytes 6291464 | tf_op jit(solution)/shard_map/ppermute | solution.py:514
  458.4 54.6 %collective-permute-start.15 = (f32[8,256,256]{2,1,0:T(8,128)S(1)}, f32[8,256,256]{2,1,0:T(8,128)S(1)}, u32[]{:S(2)}, u32[]{:S(2)}) collective-permute-start(f32[8,256,256]{2,1,0:T(8,128)S(1)} %add.27), channel_id=1, source_target_pairs={{0,2},{1,3},{2,0},{3,1},{4,6},{5,7},{6,4},{7,5},{8,10},{9,11},{10,... | collective-permute-start | bytes 6291464 | tf_op jit(solution)/shard_map/ppermute | solution.py:517
  469.3 43.7 %copy-start.3 = (f32[8,256,256]{2,1,0:T(8,128)S(1)}, f32[8,256,256]{2,1,0:T(8,128)}, u32[]{:S(2)}) copy-start(f32[8,256,256]{2,1,0:T(8,128)} %get-tuple-element.54) | copy-start | bytes 6291460
  (8 other events, 105.5 us)

commit v3 on v2

--- a/solution.py
+++ b/solution.py
@@ -6,6 +6,7 @@
 from jax.experimental import pallas as pl
 from jax.experimental.pallas import tpu as pltpu
 from jax.sharding import PartitionSpec as P
+
 
 NORM_EPS = 1e-6
 TM = 256
@@ -43,7 +44,7 @@
     return (xf + dot(act, w2)).astype(BF16)
 
 
-def rank_kernel(n_exp, dump, ids_ref, slots_ref, pos_ref, tab_ref):
+def rank_kernel(n_exp, dump, scales, ids_ref, slots_ref, tab_ref, *pos_refs):
     ids = jnp.where(slots_ref[...] >= 0, ids_ref[...], -1)
     n = ids.shape[1]
     row = lax.broadcasted_iota(jnp.int32, (n, n), 0)
@@ -63,22 +64,24 @@
         count = pre[n : n + 8]
         start = start + TM * jnp.maximum(jnp.floor((count + (TM - 1.0)) * (1.0 / TM)), 1.0)
     tab_ref[n_exp : n_exp + 1, :] = (start[0:1] * (1.0 / TM)).astype(jnp.int32)
-    pos_ref[...] = pos.astype(jnp.int32)
-
-
-def route_ranks(ids, slots, n_exp, rows):
-    n_routes = ids.size
+    for pos_ref, scale in zip(pos_refs, scales):
+        pos_ref[...] = (pos * float(scale)).astype(jnp.int32)
+
+
+def by_block(a):
+    n_tok, top_k = a.shape
+    return a.T.reshape(top_k, n_tok // BT, BT).swapaxes(0, 1)
+
+
+def route_ranks(ids, slots, n_exp, rows, scales):
     lanes = 128
-    flat = lambda a: a.T.reshape(n_routes // lanes, lanes)
-    pos, tab = pl.pallas_call(
-        functools.partial(rank_kernel, n_exp, rows),
-        out_shape=(
-            jax.ShapeDtypeStruct((n_routes // lanes, lanes), jnp.int32),
-            jax.ShapeDtypeStruct((n_exp + 8, lanes), jnp.int32),
-        ),
+    flat = (ids.size // lanes, lanes)
+    tab, *pos = pl.pallas_call(
+        functools.partial(rank_kernel, n_exp, rows, scales),
+        out_shape=(jax.ShapeDtypeStruct((n_exp + 8, lanes), jnp.int32),) + (jax.ShapeDtypeStruct(flat, jnp.int32),) * len(scales),
         name="rank",
-    )(flat(ids), flat(slots))
-    return pos.reshape(-1), tab[:, 0]
+    )(by_block(ids).reshape(flat), by_block(slots).reshape(flat))
+    return (tab[:, 0], *[p.reshape(-1) for p in pos])
 
 
 def put_rows(ref, at, vals, pitch=2, off=0):
@@ -92,71 +95,66 @@
     return jnp.concatenate([ref[pl.ds(at + off + i, n, stride=pitch), :] for i in range(2)], axis=1)
 
 
-def pair(p):
-    return pl.ds(pl.multiple_of(p * 2, 2), 2)
-
-
-def gather_sum(buf, acc, pos_ref, gate_ref, first, n_tok, top_k):
+def rows_at(p, n):
+    return pl.ds(pl.multiple_of(p, n), n)
+
+
+def gather_rows(buf, acc, pos_ref, top_k):
     unroll = 8
 
     def body(j, c):
-        base = first + j * unroll
+        base = j * unroll
         at = pl.multiple_of(j * (2 * unroll), 2 * unroll)
         for k in range(unroll):
-            total = None
             for r in range(top_k):
-                i = base + (r * n_tok + k)
-                term = buf[pair(pos_ref[i]), :]
-                if gate_ref is not None:
-                    term = term * gate_ref[i]
-                total = term if total is None else total + term
-            acc[pl.ds(at + 2 * k, 2), :] = total
+                acc[r, pl.ds(at + 2 * k, 2), :] = buf[rows_at(pos_ref[base + (r * BT + k)], 2), :]
         return c
 
     lax.fori_loop(0, BT // unroll, body, 0)
 
 
-def zero_rows(ref):
-    step = 512
-    n = ref.shape[0]
-    whole = n // step
-
-    def body(i, c):
-        ref[pl.ds(pl.multiple_of(i * step, step), step), :] = jnp.zeros((step, ref.shape[1]), F32)
+def scatter_rows(src, buf, pos_ref, top_k, n, shared):
+    unroll = 8
+
+    def body(j, c):
+        base = j * unroll
+        at = pl.multiple_of(j * (n * unroll), n * unroll)
+        for k in range(unroll):
+            v = src[pl.ds(at + n * k, n), :] if shared else None
+            for r in range(top_k):
+                row = v if shared else src[r, pl.ds(at + n * k, n), :]
+                buf[rows_at(pos_ref[base + (r * BT + k)], n), :] = row
         return c
 
-    lax.fori_loop(0, whole, body, 0)
-    if n % step:
-        ref[whole * step :, :] = jnp.zeros((n % step, ref.shape[1]), F32)
-
-
-def pre_bwd_kernel(pos_ref, gate_ref, tab_ref, x_ref, g_ref, w1_ref, w2_ref, h_ref, xs_hbm, qs_hbm, buf, src, xst, qst, sems, *, n_blocks, top_k, n_exp):
+    lax.fori_loop(0, BT // unroll, body, 0)
+
+
+def zero_tails(buf, tab_ref, n_exp, pitch):
+    def body(e, c):
+        at = pl.multiple_of((tab_ref[e + 1] - 1) * (pitch * TM), pitch * TM)
+        buf[pl.ds(at, pitch * TM), :] = jnp.zeros((pitch * TM, buf.shape[1]), F32)
+        return c
+
+    lax.fori_loop(0, n_exp, body, 0)
+
+
+def pre_bwd_kernel(pos_ref, tab_ref, gate_ref, x_ref, g_ref, w1_ref, w2_ref, h_ref, xs_hbm, qs_hbm, buf, src, xst, qst, sems, *, n_blocks, top_k, n_exp):
     step = pl.program_id(0)
-    n_tok = n_blocks * BT
 
     @pl.when(step == 0)
     def _():
-        zero_rows(buf)
+        zero_tails(buf, tab_ref, n_exp, 4)
 
     h = dense_forward(x_ref[...].astype(F32), w1_ref[...], w2_ref[...])
     h_ref[...] = h
     hf = h.astype(F32)
-    put_rows(src, 0, (hf * rms_scale(hf)).astype(BF16).astype(F32), 4, 0)
-    put_rows(src, 0, g_ref[...].astype(F32), 4, 2)
-    unroll = 8
-    is_row = lax.broadcasted_iota(jnp.int32, (4, buf.shape[1]), 0) < 2
-
-    def scatter(j, c):
-        base = step * BT + j * unroll
-        at = pl.multiple_of(j * (4 * unroll), 4 * unroll)
-        for k in range(unroll):
-            v = src[pl.ds(at + 4 * k, 4), :]
-            for r in range(top_k):
-                p = pl.multiple_of(pos_ref[base + (r * n_tok + k)] * 4, 4)
-                buf[pl.ds(p, 4), :] = v * jnp.where(is_row, 1.0, gate_ref[base + (r * n_tok + k)])
-        return c
-
-    lax.fori_loop(0, BT // unroll, scatter, 0)
+    n = (hf * rms_scale(hf)).astype(BF16).astype(F32)
+    g = g_ref[...].astype(F32)
+    gates = gate_ref[...].T
+    for r in range(top_k):
+        put_rows(src.at[r], 0, n, 4, 0)
+        put_rows(src.at[r], 0, g * gates[:, r : r + 1], 4, 2)
+    scatter_rows(src, buf, pos_ref, top_k, 4, False)
 
     @pl.when(step == n_blocks - 1)
     def _():
@@ -190,7 +188,15 @@
                 cp.wait()
 
 
-def pre_bwd(pos, gates, tab, x, g, w1, w2, rows, n_exp, top_k):
+def route_spec(top_k, n_blocks, first=0):
+    return pl.BlockSpec((top_k * BT,), lambda i: (jnp.clip(i - first, 0, n_blocks - 1),), memory_space=pltpu.SMEM)
+
+
+def gate_spec(top_k, n_blocks, first=0):
+    return pl.BlockSpec((top_k, BT), lambda i: (0, jnp.clip(i - first, 0, n_blocks - 1)))
+
+
+def pre_bwd(pos, tab, gates, x, g, w1, w2, rows, n_exp, top_k):
     n_tok, hid = x.shape
     n_blocks = n_tok // BT
     smem = pl.BlockSpec(memory_space=pltpu.SMEM)
@@ -199,7 +205,7 @@
     return pl.pallas_call(
         functools.partial(pre_bwd_kernel, n_blocks=n_blocks, top_k=top_k, n_exp=n_exp),
         grid=(n_blocks,),
-        in_specs=[smem, smem, smem, blk, blk, whole, whole],
+        in_specs=[route_spec(top_k, n_blocks), smem, gate_spec(top_k, n_blocks), blk, blk, whole, whole],
         out_specs=[blk, pl.BlockSpec(memory_space=pl.ANY), pl.BlockSpec(memory_space=pl.ANY)],
         out_shape=(
             jax.ShapeDtypeStruct((n_tok, hid), BF16),
@@ -208,7 +214,7 @@
         ),
         scratch_shapes=[
             pltpu.VMEM((4 * rows + 8, hid // 2), F32),
-            pltpu.VMEM((4 * BT, hid // 2), F32),
+            pltpu.VMEM((top_k, 4 * BT, hid // 2), F32),
             pltpu.VMEM((DEPTH, TM, hid), BF16),
             pltpu.VMEM((DEPTH, TM, hid), BF16),
             pltpu.SemaphoreType.DMA((2, DEPTH)),
@@ -216,7 +222,7 @@
         compiler_params=pltpu.CompilerParams(vmem_limit_bytes=VMEM_LIMIT),
         cost_estimate=pl.CostEstimate(flops=30_000_000_000, bytes_accessed=30_000_000, transcendentals=0),
         name="pre_bwd",
-    )(pos, gates, tab, x, g, w1, w2)
+    )(pos, tab, gates, x, g, w1, w2)
 
 
 def exp_bwd_kernel(first_ref, tab_ref, wg_hbm, wu_hbm, wd_hbm, xs_hbm, qs_hbm, rs_hbm, dwg_hbm, dwu_hbm, dwd_hbm, wb, dwb, xb, qb, rb, sems, wsems, dsems, *, n_loc):
@@ -345,10 +351,7 @@
 
 
 def post_bwd_kernel(pos_ref, tab_ref, x_ref, g_ref, h_ref, w1_ref, w2_ref, rs_hbm, dx_ref, rbuf, acc, st, sems, *, n_blocks, top_k, n_exp, rows):
-    step = pl.program_id(0)
-    n_tok = n_blocks * BT
-
-    @pl.when(step == 0)
+    @pl.when(pl.program_id(0) == 0)
     def _():
         n_tiles = tab_ref[n_exp]
 
@@ -371,8 +374,10 @@
 
         lax.fori_loop(0, n_tiles, expand, 0)
 
-    gather_sum(rbuf, acc, pos_ref, None, step * BT, n_tok, top_k)
-    dn = get_rows(acc, 0, BT)
+    gather_rows(rbuf, acc, pos_ref, top_k)
+    dn = get_rows(acc.at[0], 0, BT)
+    for r in range(1, top_k):
+        dn = dn + get_rows(acc.at[r], 0, BT)
     xf = x_ref[...].astype(F32)
     u = dot((xf * rms_scale(xf)).astype(BF16), w1_ref[...])
     dh = g_ref[...].astype(F32) + rms_back(h_ref[...].astype(F32), dn)
@@ -391,12 +396,12 @@
     return pl.pallas_call(
         functools.partial(post_bwd_kernel, n_blocks=n_blocks, top_k=top_k, n_exp=n_exp, rows=rows),
         grid=(n_blocks,),
-        in_specs=[smem, smem, blk, blk, blk, whole, whole, pl.BlockSpec(memory_space=pl.ANY)],
+        in_specs=[route_spec(top_k, n_blocks), smem, blk, blk, blk, whole, whole, pl.BlockSpec(memory_space=pl.ANY)],
         out_specs=blk,
         out_shape=jax.ShapeDtypeStruct((n_tok, hid), BF16),
         scratch_shapes=[
             pltpu.VMEM((2 * rows + 8, hid // 2), F32),
-            pltpu.VMEM((2 * BT, hid // 2), F32),
+            pltpu.VMEM((top_k, 2 * BT, hid // 2), F32),
             pltpu.VMEM((DEPTH, TM, hid), BF16),
             pltpu.SemaphoreType.DMA((DEPTH,)),
         ],
@@ -406,13 +411,12 @@
     )(pos, tab, x, g, h, w1, w2, rs)
 
 
-def fwd_kernel(firsts_ref, pos_ref, gate_ref, tab_ref, x_ref, w1_ref, w2_ref, *rest, n_blocks, top_k, n_exp, n_groups, rows):
+def fwd_kernel(firsts_ref, tab_ref, pos_ref, pos_out_ref, gate_ref, x_ref, w1_ref, w2_ref, *rest, n_blocks, top_k, n_exp, n_groups, rows):
     w_hbm = rest[: 3 * n_groups]
-    y_ref, buf, nsc, hsc, wsc, sems = rest[3 * n_groups :]
+    y_ref, buf, acc, hsc, wsc, sems = rest[3 * n_groups :]
+    nsc = acc.at[0]
     step = pl.program_id(0)
-    n_tok = n_blocks * BT
     n_loc = n_exp // n_groups
-    unroll = 8
 
     def w_copy(i):
         return pltpu.make_async_copy(w_hbm[i], wsc.at[i], sems.at[i])
@@ -421,7 +425,7 @@
     def _():
         for i in range(3 * n_groups):
             w_copy(i).start()
-        zero_rows(buf)
+        zero_tails(buf, tab_ref, n_exp, 2)
 
     @pl.when(step < n_blocks)
     def _():
@@ -431,16 +435,7 @@
         hf = h.astype(F32)
         put_rows(nsc, 0, (hf * rms_scale(hf)).astype(BF16).astype(F32))
 
-        def scatter(j, c):
-            first = base + j * unroll
-            at = pl.multiple_of(j * (2 * unroll), 2 * unroll)
-            for k in range(unroll):
-                nv = nsc[pl.ds(at + 2 * k, 2), :]
-                for r in range(top_k):
-                    buf[pair(pos_ref[first + (r * n_tok + k)]), :] = nv
-            return c
-
-        lax.fori_loop(0, BT // unroll, scatter, 0)
+        scatter_rows(nsc, buf, pos_ref, top_k, 2, True)
 
     @pl.when(step == n_blocks)
     def _():
@@ -466,12 +461,16 @@
     def _():
         base = (step - n_blocks - 1) * BT
 
-        gather_sum(buf, nsc, pos_ref, gate_ref, base, n_tok, top_k)
+        gather_rows(buf, acc, pos_out_ref, top_k)
+        gates = gate_ref[...].T
         h = hsc[pl.ds(pl.multiple_of(base, BT), BT), :]
-        y_ref[...] = (h.astype(F32) + get_rows(nsc, 0, BT)).astype(BF16)
-
-
-def fwd(firsts, pos, gates, tab, x, w1, w2, weights, rows, n_exp, top_k):
+        mix = get_rows(acc.at[0], 0, BT) * gates[:, 0:1]
+        for r in range(1, top_k):
+            mix = mix + get_rows(acc.at[r], 0, BT) * gates[:, r : r + 1]
+        y_ref[...] = (h.astype(F32) + mix).astype(BF16)
+
+
+def fwd(firsts, tab, pos, gates, x, w1, w2, weights, rows, n_exp, top_k):
     n_tok, hid = x.shape
     n_blocks = n_tok // BT
     n_groups = len(weights)
@@ -482,13 +481,14 @@
     return pl.pallas_call(
         functools.partial(fwd_kernel, n_blocks=n_blocks, top_k=top_k, n_exp=n_exp, n_groups=n_groups, rows=rows),
         grid=(2 * n_blocks + 1,),
-        in_specs=[smem, smem, smem, smem, pl.BlockSpec((BT, hid), lambda i: (jnp.minimum(i, n_blocks - 1), 0)), whole, whole]
+        in_specs=[smem, smem, route_spec(top_k, n_blocks), route_spec(top_k, n_blocks, n_blocks + 1), gate_spec(top_k, n_blocks, n_blocks + 1)]
+        + [pl.BlockSpec((BT, hid), lambda i: (jnp.minimum(i, n_blocks - 1), 0)), whole, whole]
         + [pl.BlockSpec(memory_space=pl.ANY)] * len(flat),
         out_specs=pl.BlockSpec((BT, hid), lambda i: (jnp.maximum(i - n_blocks - 1, 0), 0)),
         out_shape=jax.ShapeDtypeStruct((n_tok, hid), BF16),
         scratch_shapes=[
             pltpu.VMEM((2 * rows + 8, hid // 2), F32),
-            pltpu.VMEM((2 * BT, hid // 2), F32),
+            pltpu.VMEM((top_k, 2 * BT, hid // 2), F32),
             pltpu.VMEM((n_tok, hid), BF16),
             pltpu.VMEM((len(flat), n_loc, hid, hid), BF16),
             pltpu.SemaphoreType.DMA((len(flat),)),
@@ -496,7 +496,7 @@
         compiler_params=pltpu.CompilerParams(vmem_limit_bytes=VMEM_LIMIT),
         cost_estimate=pl.CostEstimate(flops=80_000_000_000, bytes_accessed=30_000_000, transcendentals=0),
         name="fwd",
-    )(firsts, pos, gates, tab, x, w1, w2, *flat)
+    )(firsts, tab, pos, pos, gates, x, w1, w2, *flat)
 
 
 def solution(mesh):
@@ -516,7 +516,7 @@
     def chip(a):
         return lax.ppermute(a, "ep", chip_perm)
 
-    def device_step(x_fwd, ids_fwd, slots_fwd, gates_fwd, x_saved, grad_in, ids_bwd, slots_bwd, gates_bwd, w_one, w_two, w_gate, w_up, w_down):
+    def slot(x_fwd, ids_fwd, slots_fwd, gates_fwd, x_saved, grad_in, ids_bwd, slots_bwd, gates_bwd, w_one, w_two, w_gate, w_up, w_down):
         x_fwd, ids_fwd, slots_fwd, gates_fwd = x_fwd[0], ids_fwd[0], slots_fwd[0], gates_fwd[0]
         x_saved, grad_in, ids_bwd, slots_bwd, gates_bwd = x_saved[0], grad_in[0], ids_bwd[0], slots_bwd[0], gates_bwd[0]
         w1, w2, w_gate, w_up, w_down = w_one[0], w_two[0], w_gate[0], w_up[0], w_down[0]
@@ -533,27 +533,26 @@
         weights = (own, near, far, far_near)
         firsts = [(me ^ g) * n_loc for g in range(ep_size)]
 
-        pos_b, tab_b = route_ranks(ids_bwd, slots_bwd, n_exp, rows)
-        pos_f, tab_f = route_ranks(ids_fwd, slots_fwd, n_exp, rows)
-        gates_b = gates_bwd.T.reshape(-1).astype(F32)
-        gates_f = gates_fwd.T.reshape(-1).astype(F32)
-
-        h_bwd, xs, qs = pre_bwd(pos_b, gates_b, tab_b, x_saved, grad_in, w1, w2, rows, n_exp, top_k)
+        tab_b, pos4_b, pos2_b = route_ranks(ids_bwd, slots_bwd, n_exp, rows, (4, 2))
+        tab_f, pos2_f = route_ranks(ids_fwd, slots_fwd, n_exp, rows, (2,))
+        gates_b = gates_bwd.T.astype(F32)
+        gates_f = gates_fwd.T.astype(F32)
+
+        h_bwd, xs, qs = pre_bwd(pos4_b, tab_b, gates_b, x_saved, grad_in, w1, w2, rows, n_exp, top_k)
         parts = [None] * ep_size
-        for g in (0, 3, 2):
+        for g in (0, 3, 2, 1):
             xs, *parts[g] = exp_bwd(firsts[g].reshape(1), tab_b, *weights[g], xs, qs)
         sums = [parts[2][i] + mate(parts[3][i]) for i in range(3)]
-        xs, *sums = lax.optimization_barrier((xs, *sums))
         there = [chip(v) for v in sums]
-        xs, *parts[1] = exp_bwd(firsts[1].reshape(1), tab_b, *weights[1], xs, qs)
-        grad_x = post_bwd(pos_b, tab_b, x_saved, grad_in, h_bwd, w1, w2, xs, n_exp, top_k)
+        grad_x = post_bwd(pos2_b, tab_b, x_saved, grad_in, h_bwd, w1, w2, xs, n_exp, top_k)
         x_fwd, grad_x = lax.optimization_barrier((x_fwd, grad_x))
         dx_prev = lax.ppermute(grad_x[None], "pp", prev_perm)
         dws = [parts[0][i] + mate(parts[1][i]) + there[i] for i in range(3)]
-        y_out = fwd(jnp.stack(firsts), pos_f, gates_f, tab_f, x_fwd, w1, w2, weights, rows, n_exp, top_k)
+
+        y_out = fwd(jnp.stack(firsts), tab_f, pos2_f, gates_f, x_fwd, w1, w2, weights, rows, n_exp, top_k)
         y_next = lax.ppermute(y_out[None], "pp", next_perm)
         return y_next, dx_prev, dws[0][None], dws[1][None], dws[2][None]
 
     in_specs = (tok_spec,) * 9 + (dense_spec, dense_spec, expert_spec, expert_spec, expert_spec)
     out_specs = (tok_spec, tok_spec, expert_spec, expert_spec, expert_spec)
-    return jax.shard_map(device_step, mesh=mesh, in_specs=in_specs, out_specs=out_specs, check_vma=False)
+    return jax.shard_map(slot, mesh=mesh, in_specs=in_specs, out_specs=out_specs, check_vma=False)

time: 518 us -> 416 us (0.80)
  waiting for transfers between devices: 181 us -> 127 us
  Pallas kernels: 270 us -> 236 us
  starting transfers between devices: 34.5 us -> 24.9 us
  other arithmetic: 18.6 us -> 13.1 us
    ppermute x2, waiting for transfers between devices: 79.1 us -> 35.3 us  [the longest x1 35.3 us: slot(): y_next = lax.ppermute(y_out[None], 'pp', next_perm)]
    pallas_call x1, Pallas kernels: 59.6 us -> 44.6 us  [pre_bwd(): pl.pallas_call(functools.partial(pre_bwd_kernel, n_blocks=n_blocks, top_k...]
    pallas_call x1, Pallas kernels: 86.8 us -> 72 us  [fwd(): pl.pallas_call(functools.partial(fwd_kernel, n_blocks=n_blocks, top_k=top...]
    ppermute x6, starting transfers between devices: 23 us -> 9.43 us  [chip(): return lax.ppermute(a, 'ep', chip_perm)]
    ppermute x6, waiting for transfers between devices: 99.2 us -> 92 us  [chip(): return lax.ppermute(a, 'ep', chip_perm)]
    ppermute x2, starting transfers between devices: 3.07 us -> 8.52 us  [the longest x1 8.47 us: slot(): dx_prev = lax.ppermute(grad_x[None], 'pp', prev_perm)]
    pallas_call x1, Pallas kernels: 47.9 us -> 42.6 us  [post_bwd(): pl.pallas_call(functools.partial(post_bwd_kernel, n_blocks=n_blocks, top_...]
  transfers between devices with their start and end apart: 20 -> 20, of which waited for: 7 -> 4; matrix products, arithmetic and copies ran while one was open for 5% -> 4% of each run, Pallas kernels for 45% -> 57%
where the time goes in v3:
time: 416 us; the launch traced here: 414 us
  Pallas kernels  236 us (57%)
  waiting for transfers between devices  127 us (31%)
  starting transfers between devices  24.9 us (6%)
  other arithmetic  13.1 us (3%)
  local copies, waits for them, and re-layouts  12.2 us (3%)
    ppermute x6, waiting for transfers between devices, chip(): return lax.ppermute(a, 'ep', chip_perm)  92 us
    pallas_call x1, Pallas kernels, fwd(): pl.pallas_call(functools.partial(fwd_kernel, n_blocks=n_blocks, top_k=top...  72 us
    pallas_call x4, Pallas kernels, exp_bwd(): pl.pallas_call(functools.partial(exp_bwd_kernel, n_loc=n_loc), in_specs=[...  71 us
    pallas_call x1, Pallas kernels, pre_bwd(): pl.pallas_call(functools.partial(pre_bwd_kernel, n_blocks=n_blocks, top_k...  44.6 us
    pallas_call x1, Pallas kernels, post_bwd(): pl.pallas_call(functools.partial(post_bwd_kernel, n_blocks=n_blocks, top_...  42.6 us
    ppermute x1, waiting for transfers between devices, slot(): y_next = lax.ppermute(y_out[None], 'pp', next_perm)  35.3 us
    ppermute x6, starting transfers between devices, chip(): return lax.ppermute(a, 'ep', chip_perm)  9.43 us
    ppermute x1, starting transfers between devices, slot(): dx_prev = lax.ppermute(grad_x[None], 'pp', prev_perm)  8.47 us
  transfers between devices with their start and end apart: 20, of which 4 were waited for; matrix products, arithmetic and copies ran while one was open for 4% of the time, Pallas kernels for 57%

profile of v3, /device:TPU:0, one launch (start us, length us, event | category | flops | bytes accessed | tf_op | source)
XLA Modules:
  0.0 414.4 jit_solution(1949517989809770238)
XLA Ops:
  0.6 3.2 collective-permute-start.3
  4.4 1.7 collective-permute-start.5
  9.1 2.9 rank.3
  14.8 44.6 %pre_bwd.1 = (bf16[4096,256]{1,0:T(8,128)(2,1)}, bf16[24576,256]{1,0:T(8,128)(2,1)}, bf16[24576,256]{1,0:T(8,128)(2,1)}) custom-call(s32[16384]{0:T(1024)} %bitcast.93, s32[40]{0:T(128)} %slice_reduce_fusion.tab_ref, f32[4,4096]{1,0:T(4,128)} %convert_bitcast_fusion.gate_ref, bf16[4096,256]{1,0:T(8,128)(2,1)} %bitcast.65, bf16[4096,256]{1,0:T(8,128)(2,1)} %bitcast.67, ...), custom_call_target="tpu_custom_call" | custom-call | flops 30000001024 | bytes 30000000 | tf_op jit(solution)/shard_map/pre_bwd/pallas_call | solution.py:205
  59.5 16.6 %exp_bwd.4 = (bf16[24576,256]{1,0:T(8,128)(2,1)}, f32[8,256,256]{2,1,0:T(8,128)}, f32[8,256,256]{2,1,0:T(8,128)}, f32[8,256,256]{2,1,0:T(8,128)}) custom-call(s32[1]{0:T(128)} %bitcast.first_ref, s32[40]{0:T(128)} %slice_reduce_fusion.tab_ref, bf16[8,256,256]{2,1,0:T(8,128)(2,1)} %bitcast.74, ...), custom_call_target="tpu_custom_call", output_to_operand_aliasing={{0}: (5, {})} | custom-call | flops 8000000000 | bytes 20000000 | tf_op jit(solution)/shard_map/exp_bwd/pallas_call | solution.py:331
  78.7 2.9 rank.2
  84.1 12.6 %exp_bwd.5 = (bf16[24576,256]{1,0:T(8,128)(2,1)}, f32[8,256,256]{2,1,0:T(8,128)}, f32[8,256,256]{2,1,0:T(8,128)}, f32[8,256,256]{2,1,0:T(8,128)}) custom-call(s32[1]{0:T(128)} %bitcast.3.first_ref, s32[40]{0:T(128)} %slice_reduce_fusion.tab_ref, bf16[8,256,256]{2,1,0:T(8,128)(2,1)} %collective-permute-done.6.wg_hbm.rest_9_, ...), custom_call_target="tpu_custom_call", output_to_operand_aliasing={{0}: (5, {})} | custom-call | flops 8000000000 | bytes 20000000 | tf_op jit(solution)/shard_map/exp_bwd/pallas_call | solution.py:331
  96.7 4.1 collective-permute-start.12
  100.9 19.0 %exp_bwd.6 = (bf16[24576,256]{1,0:T(8,128)(2,1)}, f32[8,256,256]{2,1,0:T(8,128)}, f32[8,256,256]{2,1,0:T(8,128)}, f32[8,256,256]{2,1,0:T(8,128)}) custom-call(s32[1]{0:T(128)} %bitcast.2.first_ref, s32[40]{0:T(128)} %slice_reduce_fusion.tab_ref, bf16[8,256,256]{2,1,0:T(8,128)(2,1)} %copy-done.11, ...), custom_call_target="tpu_custom_call", output_to_operand_aliasing={{0}: (5, {})} | custom-call | flops 8000000000 | bytes 20000000 | tf_op jit(solution)/shard_map/exp_bwd/pallas_call | solution.py:331
  121.2 22.7 %exp_bwd.7 = (bf16[24576,256]{1,0:T(8,128)(2,1)}, f32[8,256,256]{2,1,0:T(8,128)}, f32[8,256,256]{2,1,0:T(8,128)}, f32[8,256,256]{2,1,0:T(8,128)}) custom-call(s32[1]{0:T(128)} %bitcast.1.first_ref, s32[40]{0:T(128)} %slice_reduce_fusion.tab_ref, bf16[8,256,256]{2,1,0:T(8,128)(2,1)} %collective-permute-done.wg_hbm.rest_3_, ...), custom_call_target="tpu_custom_call", output_to_operand_aliasing={{0}: (5, {})} | custom-call | flops 8000000000 | bytes 20000000 | tf_op jit(solution)/shard_map/exp_bwd/pallas_call | solution.py:331
  143.9 42.6 %post_bwd.1 = bf16[4096,256]{1,0:T(8,128)(2,1)} custom-call(s32[16384]{0:T(1024)} %bitcast.90, s32[40]{0:T(128)} %slice_reduce_fusion.tab_ref, bf16[4096,256]{1,0:T(8,128)(2,1)} %bitcast.66, bf16[4096,256]{1,0:T(8,128)(2,1)} %bitcast.68, bf16[4096,256]{1,0:T(8,128)(2,1)} %get-tuple-element.36.h_ref, bf16[256,256]{1,0:T(8,128)(2,1)} %bitcast.85, ...), custom_call_target="tpu_custom_call" | custom-call | flops 30000001024 | bytes 30000000 | tf_op jit(solution)/shard_map/post_bwd/pallas_call | solution.py:396
  186.5 8.5 %collective-permute-start.10 = (bf16[1,4096,256]{2,1,0:T(8,128)(2,1)}, bf16[1,4096,256]{2,1,0:T(8,128)(2,1)}, u32[]{:S(2)}, u32[]{:S(2)}) collective-permute-start(bf16[1,4096,256]{2,1,0:T(8,128)(2,1)} %bitcast.71), channel_id=1, source_target_pairs={{0,12},{4,0},{8,4},{12,8},{1,13},{5,1},{9,5},{13,9},{2,14},{6,2},{... | collective-permute-start | bytes 6291464 | tf_op jit(solution)/shard_map/ppermute | solution.py:549
  195.0 72.0 %fwd.1 = bf16[4096,256]{1,0:T(8,128)(2,1)} custom-call(s32[4]{0:T(128)} %pad_add_fusion.firsts_ref, s32[40]{0:T(128)} %slice_reduce_fusion.1.tab_ref, s32[16384]{0:T(1024)} %bitcast.91, s32[16384]{0:T(1024)} %bitcast.92, f32[4,4096]{1,0:T(4,128)} %convert_bitcast_fusion.1.gate_ref, bf16[4096,256]{1,0:T(8,128)(2,1)} %bitcast.69, bf16[256,256]{1,0:T(8,128)(2,1)} %bitcast.86, ...), custom_call_target="tpu_custom_call" | custom-call | flops 80000000000 | bytes 30000000 | tf_op jit(solution)/shard_map/fwd/pallas_call | solution.py:481
  267.1 2.7 add.28
  269.9 2.6 collective-permute-start.13
  272.5 2.0 add.31
  275.6 35.3 %collective-permute-done.9 = bf16[1,4096,256]{2,1,0:T(8,128)(2,1)S(1)} collective-permute-done((bf16[1,4096,256]{2,1,0:T(8,128)(2,1)}, bf16[1,4096,256]{2,1,0:T(8,128)(2,1)S(1)}, u32[]{:S(2)}, u32[]{:S(2)}) %collective-permute-start.9) | collective-permute-done | bytes 2097184 | tf_op jit(solution)/shard_map/ppermute | solution.py:553
  312.5 6.4 %collective-permute-done.13 = f32[8,256,256]{2,1,0:T(8,128)S(1)} collective-permute-done((f32[8,256,256]{2,1,0:T(8,128)S(1)}, f32[8,256,256]{2,1,0:T(8,128)S(1)}, u32[]{:S(2)}, u32[]{:S(2)}) %collective-permute-start.13) | collective-permute-done | bytes 2097184 | tf_op jit(solution)/shard_map/ppermute | solution.py:517
  319.0 1.8 add_bitcast_fusion.2
  320.8 43.1 %collective-permute-done.16 = f32[8,256,256]{2,1,0:T(8,128)S(1)} collective-permute-done((f32[8,256,256]{2,1,0:T(8,128)S(1)}, f32[8,256,256]{2,1,0:T(8,128)S(1)}, u32[]{:S(2)}, u32[]{:S(2)}) %collective-permute-start.16) | collective-permute-done | bytes 2097184 | tf_op jit(solution)/shard_map/ppermute | solution.py:517
  363.9 1.8 add_bitcast_fusion.1
  365.7 42.5 %collective-permute-done.19 = f32[8,256,256]{2,1,0:T(8,128)S(1)} collective-permute-done((f32[8,256,256]{2,1,0:T(8,128)S(1)}, f32[8,256,256]{2,1,0:T(8,128)S(1)}, u32[]{:S(2)}, u32[]{:S(2)}) %collective-permute-start.19) | collective-permute-done | bytes 2097184 | tf_op jit(solution)/shard_map/ppermute | solution.py:517
  408.2 1.8 add_bitcast_fusion
  411.3 3.0 copy.38
  (66 shorter events, 16.8 us)
Async XLA Ops:
  0.6 75.5 %collective-permute-start.3 = (bf16[8,256,256]{2,1,0:T(8,128)(2,1)}, bf16[8,256,256]{2,1,0:T(8,128)(2,1)S(1)}, u32[]{:S(2)}, u32[]{:S(2)}) collective-permute-start(bf16[8,256,256]{2,1,0:T(8,128)(2,1)} %bitcast.72), channel_id=1, source_target_pairs={{0,2},{1,3},{2,0},{3,1},{4,6},{5,7},{6,4},{7,5},{8,10},{9,11},{10,... | collective-permute-start | bytes 3145736 | tf_op jit(solution)/shard_map/ppermute | solution.py:517
  3.9 116.1 %collective-permute-start = (bf16[8,256,256]{2,1,0:T(8,128)(2,1)}, bf16[8,256,256]{2,1,0:T(8,128)(2,1)}, u32[]{:S(2)}, u32[]{:S(2)}) collective-permute-start(bf16[8,256,256]{2,1,0:T(8,128)(2,1)} %bitcast.73), channel_id=1, source_target_pairs={{0,1},{1,0},{2,3},{3,2},{4,5},{5,4},{6,7},{7,6},{8,9},{9,8},{10,11... | collective-permute-start | bytes 3145736 | tf_op jit(solution)/shard_map/ppermute | solution.py:514
  3.9 72.3 %collective-permute-start.4 = (bf16[8,256,256]{2,1,0:T(8,128)(2,1)}, bf16[8,256,256]{2,1,0:T(8,128)(2,1)}, u32[]{:S(2)}, u32[]{:S(2)}) collective-permute-start(bf16[8,256,256]{2,1,0:T(8,128)(2,1)} %bitcast.76), channel_id=1, source_target_pairs={{0,2},{1,3},{2,0},{3,1},{4,6},{5,7},{6,4},{7,5},{8,10},{9,11},{10,... | collective-permute-start | bytes 3145736 | tf_op jit(solution)/shard_map/ppermute | solution.py:517
  4.0 117.2 %collective-permute-start.1 = (bf16[8,256,256]{2,1,0:T(8,128)(2,1)}, bf16[8,256,256]{2,1,0:T(8,128)(2,1)}, u32[]{:S(2)}, u32[]{:S(2)}) collective-permute-start(bf16[8,256,256]{2,1,0:T(8,128)(2,1)} %bitcast.77), channel_id=1, source_target_pairs={{0,1},{1,0},{2,3},{3,2},{4,5},{5,4},{6,7},{7,6},{8,9},{9,8},{10,11... | collective-permute-start | bytes 3145736 | tf_op jit(solution)/shard_map/ppermute | solution.py:514
  4.4 72.3 %collective-permute-start.5 = (bf16[8,256,256]{2,1,0:T(8,128)(2,1)}, bf16[8,256,256]{2,1,0:T(8,128)(2,1)}, u32[]{:S(2)}, u32[]{:S(2)}) collective-permute-start(bf16[8,256,256]{2,1,0:T(8,128)(2,1)} %bitcast.80), channel_id=1, source_target_pairs={{0,2},{1,3},{2,0},{3,1},{4,6},{5,7},{6,4},{7,5},{8,10},{9,11},{10,... | collective-permute-start | bytes 3145736 | tf_op jit(solution)/shard_map/ppermute | solution.py:517
  76.1 7.5 %collective-permute-start.6 = (bf16[8,256,256]{2,1,0:T(8,128)(2,1)S(1)}, bf16[8,256,256]{2,1,0:T(8,128)(2,1)}, u32[]{:S(2)}, u32[]{:S(2)}) collective-permute-start(bf16[8,256,256]{2,1,0:T(8,128)(2,1)S(1)} %collective-permute-done.3.wg_hbm.rest_6_), channel_id=1, source_target_pairs={{0,1},{1,0},{2,3},{3,2},{4,5},{5,4},{6,7},{7,6},{8,9},{9,8},{10,11... | collective-permute-start | bytes 3145736 | tf_op jit(solution)/shard_map/ppermute | solution.py:514
  76.2 7.9 %collective-permute-start.7 = (bf16[8,256,256]{2,1,0:T(8,128)(2,1)}, bf16[8,256,256]{2,1,0:T(8,128)(2,1)}, u32[]{:S(2)}, u32[]{:S(2)}) collective-permute-start(bf16[8,256,256]{2,1,0:T(8,128)(2,1)} %collective-permute-done.4.wu_hbm.rest_7_), channel_id=1, source_target_pairs={{0,1},{1,0},{2,3},{3,2},{4,5},{5,4},{6,7},{7,6},{8,9},{9,8},{10,11... | collective-permute-start | bytes 3145736 | tf_op jit(solution)/shard_map/ppermute | solution.py:514
  76.7 7.4 %collective-permute-start.8 = (bf16[8,256,256]{2,1,0:T(8,128)(2,1)}, bf16[8,256,256]{2,1,0:T(8,128)(2,1)}, u32[]{:S(2)}, u32[]{:S(2)}) collective-permute-start(bf16[8,256,256]{2,1,0:T(8,128)(2,1)} %collective-permute-done.5.wd_hbm.rest_8_), channel_id=1, source_target_pairs={{0,1},{1,0},{2,3},{3,2},{4,5},{5,4},{6,7},{7,6},{8,9},{9,8},{10,11... | collective-permute-start | bytes 3145736 | tf_op jit(solution)/shard_map/ppermute | solution.py:514
  83.6 37.6 %collective-permute-start.2 = (bf16[8,256,256]{2,1,0:T(8,128)(2,1)S(1)}, bf16[8,256,256]{2,1,0:T(8,128)(2,1)}, u32[]{:S(2)}, u32[]{:S(2)}) collective-permute-start(bf16[8,256,256]{2,1,0:T(8,128)(2,1)S(1)} %bitcast.83), channel_id=1, source_target_pairs={{0,1},{1,0},{2,3},{3,2},{4,5},{5,4},{6,7},{7,6},{8,9},{9,8},{10,11... | collective-permute-start | bytes 3145736 | tf_op jit(solution)/shard_map/ppermute | solution.py:514
  96.7 170.4 %collective-permute-start.12 = (f32[8,256,256]{2,1,0:T(8,128)}, f32[8,256,256]{2,1,0:T(8,128)}, u32[]{:S(2)}, u32[]{:S(2)}) collective-permute-start(f32[8,256,256]{2,1,0:T(8,128)} %get-tuple-element.48), channel_id=1, source_target_pairs={{0,1},{1,0},{2,3},{3,2},{4,5},{5,4},{6,7},{7,6},{8,9},{9,8},{10,11... | collective-permute-start | bytes 6291464 | tf_op jit(solution)/shard_map/ppermute | solution.py:514
  100.8 169.0 %collective-permute-start.15 = (f32[8,256,256]{2,1,0:T(8,128)}, f32[8,256,256]{2,1,0:T(8,128)}, u32[]{:S(2)}, u32[]{:S(2)}) collective-permute-start(f32[8,256,256]{2,1,0:T(8,128)} %get-tuple-element.52), channel_id=1, source_target_pairs={{0,1},{1,0},{2,3},{3,2},{4,5},{5,4},{6,7},{7,6},{8,9},{9,8},{10,11... | collective-permute-start | bytes 6291464 | tf_op jit(solution)/shard_map/ppermute | solution.py:514
  120.0 154.6 %collective-permute-start.18 = (f32[8,256,256]{2,1,0:T(8,128)}, f32[8,256,256]{2,1,0:T(8,128)S(1)}, u32[]{:S(2)}, u32[]{:S(2)}) collective-permute-start(f32[8,256,256]{2,1,0:T(8,128)} %get-tuple-element.56), channel_id=1, source_target_pairs={{0,1},{1,0},{2,3},{3,2},{4,5},{5,4},{6,7},{7,6},{8,9},{9,8},{10,11... | collective-permute-start | bytes 6291464 | tf_op jit(solution)/shard_map/ppermute | solution.py:514
  186.5 88.2 %collective-permute-start.10 = (bf16[1,4096,256]{2,1,0:T(8,128)(2,1)}, bf16[1,4096,256]{2,1,0:T(8,128)(2,1)}, u32[]{:S(2)}, u32[]{:S(2)}) collective-permute-start(bf16[1,4096,256]{2,1,0:T(8,128)(2,1)} %bitcast.71), channel_id=1, source_target_pairs={{0,12},{4,0},{8,4},{12,8},{1,13},{5,1},{9,5},{13,9},{2,14},{6,2},{... | collective-permute-start | bytes 6291464 | tf_op jit(solution)/shard_map/ppermute | solution.py:549
  267.0 43.9 %collective-permute-start.9 = (bf16[1,4096,256]{2,1,0:T(8,128)(2,1)}, bf16[1,4096,256]{2,1,0:T(8,128)(2,1)S(1)}, u32[]{:S(2)}, u32[]{:S(2)}) collective-permute-start(bf16[1,4096,256]{2,1,0:T(8,128)(2,1)} %bitcast.70), channel_id=1, source_target_pairs={{0,4},{4,8},{8,12},{12,0},{1,5},{5,9},{9,13},{13,1},{2,6},{6,10},{... | collective-permute-start | bytes 6291464 | tf_op jit(solution)/shard_map/ppermute | solution.py:553
  267.1 43.8 %collective-permute-start.11 = (f32[8,256,256]{2,1,0:T(8,128)}, f32[8,256,256]{2,1,0:T(8,128)S(1)}, u32[]{:S(2)}, u32[]{:S(2)}) collective-permute-start(f32[8,256,256]{2,1,0:T(8,128)} %get-tuple-element.46), channel_id=1, source_target_pairs={{0,1},{1,0},{2,3},{3,2},{4,5},{5,4},{6,7},{7,6},{8,9},{9,8},{10,11... | collective-permute-start | bytes 6291464 | tf_op jit(solution)/shard_map/ppermute | solution.py:514
  269.9 49.1 %collective-permute-start.13 = (f32[8,256,256]{2,1,0:T(8,128)S(1)}, f32[8,256,256]{2,1,0:T(8,128)S(1)}, u32[]{:S(2)}, u32[]{:S(2)}) collective-permute-start(f32[8,256,256]{2,1,0:T(8,128)S(1)} %add.28), channel_id=1, source_target_pairs={{0,2},{1,3},{2,0},{3,1},{4,6},{5,7},{6,4},{7,5},{8,10},{9,11},{10,... | collective-permute-start | bytes 6291464 | tf_op jit(solution)/shard_map/ppermute | solution.py:517
  274.7 46.1 %collective-permute-start.14 = (f32[8,256,256]{2,1,0:T(8,128)S(1)}, f32[8,256,256]{2,1,0:T(8,128)S(1)}, u32[]{:S(2)}, u32[]{:S(2)}) collective-permute-start(f32[8,256,256]{2,1,0:T(8,128)S(1)} %copy-done.9), channel_id=1, source_target_pairs={{0,1},{1,0},{2,3},{3,2},{4,5},{5,4},{6,7},{7,6},{8,9},{9,8},{10,11... | collective-permute-start | bytes 6291464 | tf_op jit(solution)/shard_map/ppermute | solution.py:514
  274.7 89.2 %collective-permute-start.16 = (f32[8,256,256]{2,1,0:T(8,128)S(1)}, f32[8,256,256]{2,1,0:T(8,128)S(1)}, u32[]{:S(2)}, u32[]{:S(2)}) collective-permute-start(f32[8,256,256]{2,1,0:T(8,128)S(1)} %add.31), channel_id=1, source_target_pairs={{0,2},{1,3},{2,0},{3,1},{4,6},{5,7},{6,4},{7,5},{8,10},{9,11},{10,... | collective-permute-start | bytes 6291464 | tf_op jit(solution)/shard_map/ppermute | solution.py:517
  275.4 35.5 %copy-start.8 = (f32[8,256,256]{2,1,0:T(8,128)S(1)}, f32[8,256,256]{2,1,0:T(8,128)}, u32[]{:S(2)}) copy-start(f32[8,256,256]{2,1,0:T(8,128)} %get-tuple-element.54) | copy-start | bytes 6291460
  275.4 43.6 %copy-start.4 = (f32[8,256,256]{2,1,0:T(8,128)S(1)}, f32[8,256,256]{2,1,0:T(8,128)}, u32[]{:S(2)}) copy-start(f32[8,256,256]{2,1,0:T(8,128)} %get-tuple-element.45) | copy-start | bytes 6291460
  310.9 54.8 %collective-permute-start.17 = (f32[8,256,256]{2,1,0:T(8,128)S(1)}, f32[8,256,256]{2,1,0:T(8,128)S(1)}, u32[]{:S(2)}, u32[]{:S(2)}) collective-permute-start(f32[8,256,256]{2,1,0:T(8,128)S(1)} %copy-done.8), channel_id=1, source_target_pairs={{0,1},{1,0},{2,3},{3,2},{4,5},{5,4},{6,7},{7,6},{8,9},{9,8},{10,11... | collective-permute-start | bytes 6291464 | tf_op jit(solution)/shard_map/ppermute | solution.py:514
  310.9 97.3 %collective-permute-start.19 = (f32[8,256,256]{2,1,0:T(8,128)S(1)}, f32[8,256,256]{2,1,0:T(8,128)S(1)}, u32[]{:S(2)}, u32[]{:S(2)}) collective-permute-start(f32[8,256,256]{2,1,0:T(8,128)S(1)} %add.34), channel_id=1, source_target_pairs={{0,2},{1,3},{2,0},{3,1},{4,6},{5,7},{6,4},{7,5},{8,10},{9,11},{10,... | collective-permute-start | bytes 6291464 | tf_op jit(solution)/shard_map/ppermute | solution.py:517
  319.0 44.9 %copy-start.3 = (f32[8,256,256]{2,1,0:T(8,128)S(1)}, f32[8,256,256]{2,1,0:T(8,128)}, u32[]{:S(2)}) copy-start(f32[8,256,256]{2,1,0:T(8,128)} %get-tuple-element.49) | copy-start | bytes 6291460
  363.9 44.3 %copy-start.2 = (f32[8,256,256]{2,1,0:T(8,128)S(1)}, f32[8,256,256]{2,1,0:T(8,128)}, u32[]{:S(2)}) copy-start(f32[8,256,256]{2,1,0:T(8,128)} %get-tuple-element.53) | copy-start | bytes 6291460
  (8 other events, 115.3 us)

commit v4 on v3

--- a/solution.py
+++ b/solution.py
@@ -12,6 +12,7 @@
 TM = 256
 BT = 512
 DEPTH = 4
+HALVES = 2
 F32 = jnp.float32
 BF16 = jnp.bfloat16
 VMEM_LIMIT = 60 * 1024 * 1024
@@ -44,44 +45,62 @@
     return (xf + dot(act, w2)).astype(BF16)
 
 
-def rank_kernel(n_exp, dump, scales, ids_ref, slots_ref, tab_ref, *pos_refs):
-    ids = jnp.where(slots_ref[...] >= 0, ids_ref[...], -1)
-    n = ids.shape[1]
-    row = lax.broadcasted_iota(jnp.int32, (n, n), 0)
-    col = lax.broadcasted_iota(jnp.int32, (n, n), 1)
-    ones = jnp.ones((n, n), BF16)
-    right = jnp.concatenate([jnp.where(row < col, 1.0, 0.0).astype(BF16), ones], axis=1)
-    left = jnp.concatenate([jnp.where(col < row, 1.0, 0.0).astype(BF16), ones], axis=0)
-    start = jnp.zeros((8, n), F32)
-    pos = jnp.full((n, n), float(dump), F32)
-    tab_ref[...] = jnp.zeros_like(tab_ref)
+def rank_routes(ids, slots, n_exp, dump):
+    ids = jnp.where(slots >= 0, ids, -1)
+    n, lanes = ids.shape
+    row = lax.broadcasted_iota(jnp.int32, (lanes, lanes), 0)
+    col = lax.broadcasted_iota(jnp.int32, (lanes, lanes), 1)
+    right = jnp.concatenate([jnp.where(row < col, 1.0, 0.0).astype(BF16), jnp.ones((lanes, lanes), BF16)], axis=1)
+    row = lax.broadcasted_iota(jnp.int32, (n + 8, n), 0)
+    col = lax.broadcasted_iota(jnp.int32, (n + 8, n), 1)
+    left = jnp.where((col < row) | (row >= n), 1.0, 0.0).astype(BF16)
+    lane = lax.broadcasted_iota(jnp.int32, (8, lanes), 1)
+    start = jnp.zeros((8, lanes), F32)
+    tab = jnp.zeros((8, lanes), F32)
+    pos = jnp.full((n, lanes), float(dump), F32)
     for e in range(n_exp):
         mask = ids == e
         both = dot(jnp.where(mask, 1.0, 0.0).astype(BF16), right)
-        pre = dot(left, both[:, n:].astype(BF16))
-        pos = jnp.where(mask, both[:, :n] + pre[:n] + start[0:1], pos)
-        tab_ref[e : e + 1, :] = (start[0:1] * (1.0 / TM)).astype(jnp.int32)
-        count = pre[n : n + 8]
-        start = start + TM * jnp.maximum(jnp.floor((count + (TM - 1.0)) * (1.0 / TM)), 1.0)
-    tab_ref[n_exp : n_exp + 1, :] = (start[0:1] * (1.0 / TM)).astype(jnp.int32)
-    for pos_ref, scale in zip(pos_refs, scales):
-        pos_ref[...] = (pos * float(scale)).astype(jnp.int32)
-
-
-def by_block(a):
-    n_tok, top_k = a.shape
-    return a.T.reshape(top_k, n_tok // BT, BT).swapaxes(0, 1)
-
-
-def route_ranks(ids, slots, n_exp, rows, scales):
-    lanes = 128
-    flat = (ids.size // lanes, lanes)
-    tab, *pos = pl.pallas_call(
-        functools.partial(rank_kernel, n_exp, rows, scales),
-        out_shape=(jax.ShapeDtypeStruct((n_exp + 8, lanes), jnp.int32),) + (jax.ShapeDtypeStruct(flat, jnp.int32),) * len(scales),
+        pre = dot(left, both[:, lanes:].astype(BF16))
+        pos = jnp.where(mask, both[:, :lanes] + pre[:n] + start[0:1], pos)
+        tab = jnp.where(lane == e, start, tab)
+        start = start + TM * jnp.maximum(jnp.floor((pre[n:] + (TM - 1.0)) * (1.0 / TM)), 1.0)
+    tab = jnp.where(lane == n_exp, start, tab) * (1.0 / TM)
+    return pos, tab.astype(jnp.int32)
+
+
+def chunks(ref, first, last):
+    return jnp.concatenate([ref[:, c * 128 : (c + 1) * 128] for c in range(first, last)], axis=0)
+
+
+def rank_kernel(n_exp, rows_b, rows_f, ids_b, slots_b, ids_f, slots_f, tab_b, pos4_b, pos2_b, tab_f, pos2_f):
+    n = ids_b.shape[1] // 128
+    pos, tab_b[...] = rank_routes(chunks(ids_b, 0, n), chunks(slots_b, 0, n), n_exp, rows_b)
+    pos4_b[...] = (pos * 4.0).astype(jnp.int32)
+    pos2_b[...] = (pos * 2.0).astype(jnp.int32)
+    step = n // HALVES
+    for h in range(HALVES):
+        at = (h * step, (h + 1) * step)
+        pos, tab_f[h] = rank_routes(chunks(ids_f, *at), chunks(slots_f, *at), n_exp, rows_f)
+        k = pos.shape[0]
+        pos2_f[h * k : (h + 1) * k, :] = (pos * 2.0).astype(jnp.int32)
+
+
+def route_ranks(ids_b, slots_b, ids_f, slots_f, n_exp, rows_b, rows_f):
+    pos = jax.ShapeDtypeStruct((ids_b.size // 128, 128), jnp.int32)
+    tab = (8, 128)
+    tab_b, pos4_b, pos2_b, tab_f, pos2_f = pl.pallas_call(
+        functools.partial(rank_kernel, n_exp, rows_b, rows_f),
+        out_shape=(
+            jax.ShapeDtypeStruct(tab, jnp.int32),
+            pos,
+            pos,
+            jax.ShapeDtypeStruct((HALVES, *tab), jnp.int32),
+            pos,
+        ),
         name="rank",
-    )(by_block(ids).reshape(flat), by_block(slots).reshape(flat))
-    return (tab[:, 0], *[p.reshape(-1) for p in pos])
+    )(ids_b.T, slots_b.T, ids_f.T, slots_f.T)
+    return tab_b, pos4_b.reshape(-1), pos2_b.reshape(-1), tab_f, pos2_f.reshape(-1)
 
 
 def put_rows(ref, at, vals, pitch=2, off=0):
@@ -99,31 +118,36 @@
     return pl.ds(pl.multiple_of(p, n), n)
 
 
+def table_at(j, unroll, top_k):
+    per = 128 // unroll
+    return lax.div(j, per) * (128 * top_k) + lax.rem(j, per) * unroll
+
+
 def gather_rows(buf, acc, pos_ref, top_k):
-    unroll = 8
+    unroll = 16
 
     def body(j, c):
-        base = j * unroll
+        base = table_at(j, unroll, top_k)
         at = pl.multiple_of(j * (2 * unroll), 2 * unroll)
         for k in range(unroll):
             for r in range(top_k):
-                acc[r, pl.ds(at + 2 * k, 2), :] = buf[rows_at(pos_ref[base + (r * BT + k)], 2), :]
+                acc[r, pl.ds(at + 2 * k, 2), :] = buf[rows_at(pos_ref[base + (r * 128 + k)], 2), :]
         return c
 
     lax.fori_loop(0, BT // unroll, body, 0)
 
 
 def scatter_rows(src, buf, pos_ref, top_k, n, shared):
-    unroll = 8
+    unroll = 16
 
     def body(j, c):
-        base = j * unroll
+        base = table_at(j, unroll, top_k)
         at = pl.multiple_of(j * (n * unroll), n * unroll)
         for k in range(unroll):
             v = src[pl.ds(at + n * k, n), :] if shared else None
             for r in range(top_k):
                 row = v if shared else src[r, pl.ds(at + n * k, n), :]
-                buf[rows_at(pos_ref[base + (r * BT + k)], n), :] = row
+                buf[rows_at(pos_ref[base + (r * 128 + k)], n), :] = row
         return c
 
     lax.fori_loop(0, BT // unroll, body, 0)
@@ -131,7 +155,7 @@
 
 def zero_tails(buf, tab_ref, n_exp, pitch):
     def body(e, c):
-        at = pl.multiple_of((tab_ref[e + 1] - 1) * (pitch * TM), pitch * TM)
+        at = pl.multiple_of((tab_ref[0, e + 1] - 1) * (pitch * TM), pitch * TM)
         buf[pl.ds(at, pitch * TM), :] = jnp.zeros((pitch * TM, buf.shape[1]), F32)
         return c
 
@@ -150,7 +174,7 @@
     hf = h.astype(F32)
     n = (hf * rms_scale(hf)).astype(BF16).astype(F32)
     g = g_ref[...].astype(F32)
-    gates = gate_ref[...].T
+    gates = gate_ref[...].astype(F32).T
     for r in range(top_k):
         put_rows(src.at[r], 0, n, 4, 0)
         put_rows(src.at[r], 0, g * gates[:, r : r + 1], 4, 2)
@@ -158,7 +182,7 @@
 
     @pl.when(step == n_blocks - 1)
     def _():
-        n_tiles = tab_ref[n_exp]
+        n_tiles = tab_ref[0, n_exp]
 
         def copies(t, slot):
             rows = pl.ds(pl.multiple_of(t * TM, TM), TM)
@@ -188,12 +212,12 @@
                 cp.wait()
 
 
-def route_spec(top_k, n_blocks, first=0):
-    return pl.BlockSpec((top_k * BT,), lambda i: (jnp.clip(i - first, 0, n_blocks - 1),), memory_space=pltpu.SMEM)
-
-
-def gate_spec(top_k, n_blocks, first=0):
-    return pl.BlockSpec((top_k, BT), lambda i: (0, jnp.clip(i - first, 0, n_blocks - 1)))
+def route_spec(top_k, n_blocks, first=0, skip=0):
+    return pl.BlockSpec((top_k * BT,), lambda i: (skip + jnp.clip(i - first, 0, n_blocks - 1),), memory_space=pltpu.SMEM)
+
+
+def gate_spec(top_k, n_blocks, first=0, skip=0):
+    return pl.BlockSpec((top_k, BT), lambda i: (0, skip + jnp.clip(i - first, 0, n_blocks - 1)))
 
 
 def pre_bwd(pos, tab, gates, x, g, w1, w2, rows, n_exp, top_k):
@@ -225,12 +249,13 @@
     )(pos, tab, gates, x, g, w1, w2)
 
 
-def exp_bwd_kernel(first_ref, tab_ref, wg_hbm, wu_hbm, wd_hbm, xs_hbm, qs_hbm, rs_hbm, dwg_hbm, dwu_hbm, dwd_hbm, wb, dwb, xb, qb, rb, sems, wsems, dsems, *, n_loc):
+def exp_bwd_kernel(first_ref, tab_ref, *refs, n_loc, has_init):
+    w_hbm, (xs_hbm, qs_hbm), refs = refs[:3], refs[3:5], refs[5:]
+    init_hbm, refs = (refs[:3], refs[3:]) if has_init else ((), refs)
+    rs_hbm, *dw_hbm, wb, dwb, xb, qb, rb, sems, wsems, dsems, isems = refs
     first = first_ref[0]
-    begin = tab_ref[first]
-    end = tab_ref[first + n_loc]
-    w_hbm = (wg_hbm, wu_hbm, wd_hbm)
-    dw_hbm = (dwg_hbm, dwu_hbm, dwd_hbm)
+    begin = tab_ref[0, first]
+    end = tab_ref[0, first + n_loc]
 
     def rows_of(t):
         return pl.ds(pl.multiple_of(t * TM, TM), TM)
@@ -250,11 +275,15 @@
         slot = lax.rem(e, 2)
         return [pltpu.make_async_copy(w_hbm[i].at[e], wb.at[slot, i], wsems.at[i, slot]) for i in range(3)]
 
+    def init_loads(e):
+        slot = lax.rem(e, 3)
+        return [pltpu.make_async_copy(ref.at[e], dwb.at[slot, i], isems.at[i, slot]) for i, ref in enumerate(init_hbm)]
+
     def dw_saves(e):
-        slot = lax.rem(e, 2)
+        slot = lax.rem(e, 3)
         return [pltpu.make_async_copy(dwb.at[slot, i], dw_hbm[i].at[e], dsems.at[i, slot]) for i in range(3)]
 
-    for cp in w_loads(0):
+    for cp in w_loads(0) + init_loads(0):
         cp.start()
     for ahead in range(DEPTH - 1):
         for cp in loads(begin + ahead):
@@ -262,20 +291,22 @@
 
     def expert(e, c):
         wslot = lax.rem(e, 2)
-        for cp in w_loads(e):
+        dslot = lax.rem(e, 3)
+        for cp in w_loads(e) + init_loads(e):
             cp.wait()
-
-        @pl.when(e + 1 < n_loc)
-        def _():
-            for cp in w_loads(e + 1):
-                cp.start()
 
         @pl.when(e >= 2)
         def _():
             for cp in dw_saves(e - 2):
                 cp.wait()
 
-        dwb[wslot] = jnp.zeros(dwb.shape[1:], F32)
+        @pl.when(e + 1 < n_loc)
+        def _():
+            for cp in w_loads(e + 1) + init_loads(e + 1):
+                cp.start()
+
+        if not has_init:
+            dwb[dslot] = jnp.zeros(dwb.shape[1:], F32)
 
         def body(t, c):
             slot = lax.rem(t, DEPTH)
@@ -300,17 +331,17 @@
             sig = jax.nn.sigmoid(pre)
             sil = pre * sig
             act = (sil * up).astype(BF16)
-            dwb[wslot, 2] += dot_tn(act, q)
+            dwb[dslot, 2] += dot_tn(act, q)
             da = dot_nt(q, wd).astype(BF16).astype(F32)
             dpre = (da * up * (sig * (1.0 + pre * (1.0 - sig)))).astype(BF16)
             dup = (da * sil).astype(BF16)
-            dwb[wslot, 0] += dot_tn(x, dpre)
-            dwb[wslot, 1] += dot_tn(x, dup)
+            dwb[dslot, 0] += dot_tn(x, dpre)
+            dwb[dslot, 1] += dot_tn(x, dup)
             rb[slot] = (dot_nt(dpre, wg) + dot_nt(dup, wu)).astype(BF16)
             save(t).start()
             return c
 
-        lax.fori_loop(tab_ref[first + e], tab_ref[first + e + 1], body, 0)
+        lax.fori_loop(tab_ref[0, first + e], tab_ref[0, first + e + 1], body, 0)
         for cp in dw_saves(e):
             cp.start()
         return c
@@ -323,37 +354,38 @@
             cp.wait()
 
 
-def exp_bwd(first, tab, wg, wu, wd, xs, qs):
+def exp_bwd(first, tab, wg, wu, wd, xs, qs, init=()):
     n_loc, hid, ff = wg.shape
     smem = pl.BlockSpec(memory_space=pltpu.SMEM)
     hbm = pl.BlockSpec(memory_space=pl.ANY)
     dw = jax.ShapeDtypeStruct((n_loc, hid, ff), F32)
     return pl.pallas_call(
-        functools.partial(exp_bwd_kernel, n_loc=n_loc),
-        in_specs=[smem, smem, hbm, hbm, hbm, hbm, hbm],
+        functools.partial(exp_bwd_kernel, n_loc=n_loc, has_init=bool(init)),
+        in_specs=[smem, smem] + [hbm] * (5 + len(init)),
         out_specs=[hbm, hbm, hbm, hbm],
         out_shape=(jax.ShapeDtypeStruct(xs.shape, BF16), dw, dw, dw),
         input_output_aliases={5: 0},
         scratch_shapes=[
             pltpu.VMEM((2, 3, hid, ff), BF16),
-            pltpu.VMEM((2, 3, hid, ff), F32),
+            pltpu.VMEM((3, 3, hid, ff), F32),
             pltpu.VMEM((DEPTH, TM, hid), BF16),
             pltpu.VMEM((DEPTH, TM, hid), BF16),
             pltpu.VMEM((DEPTH, TM, hid), BF16),
             pltpu.SemaphoreType.DMA((3, DEPTH)),
             pltpu.SemaphoreType.DMA((3, 2)),
-            pltpu.SemaphoreType.DMA((3, 2)),
+            pltpu.SemaphoreType.DMA((3, 3)),
+            pltpu.SemaphoreType.DMA((3, 3)),
         ],
         compiler_params=pltpu.CompilerParams(vmem_limit_bytes=VMEM_LIMIT),
         cost_estimate=pl.CostEstimate(flops=8_000_000_000, bytes_accessed=20_000_000, transcendentals=0),
         name="exp_bwd",
-    )(first, tab, wg, wu, wd, xs, qs)
+    )(first, tab, wg, wu, wd, xs, qs, *init)
 
 
 def post_bwd_kernel(pos_ref, tab_ref, x_ref, g_ref, h_ref, w1_ref, w2_ref, rs_hbm, dx_ref, rbuf, acc, st, sems, *, n_blocks, top_k, n_exp, rows):
     @pl.when(pl.program_id(0) == 0)
     def _():
-        n_tiles = tab_ref[n_exp]
+        n_tiles = tab_ref[0, n_exp]
 
         def load(t):
             slot = lax.rem(t, DEPTH)
@@ -446,7 +478,7 @@
             first = firsts_ref[g]
 
             def body(t, e):
-                e = jnp.where(t >= tab_ref[first + e + 1], e + 1, e)
+                e = jnp.where(t >= tab_ref[0, first + e + 1], e + 1, e)
                 at = pl.multiple_of(t * (2 * TM), 2 * TM)
                 x = get_rows(buf, at, TM).astype(BF16)
                 pre = dot(x, wsc[3 * g, e])
@@ -455,14 +487,14 @@
                 put_rows(buf, at, dot(act, wsc[3 * g + 2, e]).astype(BF16).astype(F32))
                 return e
 
-            lax.fori_loop(tab_ref[first], tab_ref[first + n_loc], body, 0)
+            lax.fori_loop(tab_ref[0, first], tab_ref[0, first + n_loc], body, 0)
 
     @pl.when(step > n_blocks)
     def _():
         base = (step - n_blocks - 1) * BT
 
         gather_rows(buf, acc, pos_out_ref, top_k)
-        gates = gate_ref[...].T
+        gates = gate_ref[...].astype(F32).T
         h = hsc[pl.ds(pl.multiple_of(base, BT), BT), :]
         mix = get_rows(acc.at[0], 0, BT) * gates[:, 0:1]
         for r in range(1, top_k):
@@ -470,9 +502,10 @@
         y_ref[...] = (h.astype(F32) + mix).astype(BF16)
 
 
-def fwd(firsts, tab, pos, gates, x, w1, w2, weights, rows, n_exp, top_k):
-    n_tok, hid = x.shape
+def fwd(half, firsts, tab, pos, gates, x, w1, w2, weights, rows, n_exp, top_k):
+    n_tok, hid = x.shape[0] // HALVES, x.shape[1]
     n_blocks = n_tok // BT
+    skip = half * n_blocks
     n_groups = len(weights)
     n_loc = n_exp // n_groups
     smem = pl.BlockSpec(memory_space=pltpu.SMEM)
@@ -481,8 +514,8 @@
     return pl.pallas_call(
         functools.partial(fwd_kernel, n_blocks=n_blocks, top_k=top_k, n_exp=n_exp, n_groups=n_groups, rows=rows),
         grid=(2 * n_blocks + 1,),
-        in_specs=[smem, smem, route_spec(top_k, n_blocks), route_spec(top_k, n_blocks, n_blocks + 1), gate_spec(top_k, n_blocks, n_blocks + 1)]
-        + [pl.BlockSpec((BT, hid), lambda i: (jnp.minimum(i, n_blocks - 1), 0)), whole, whole]
+        in_specs=[smem, smem, route_spec(top_k, n_blocks, 0, skip), route_spec(top_k, n_blocks, n_blocks + 1, skip), gate_spec(top_k, n_blocks, n_blocks + 1, skip)]
+        + [pl.BlockSpec((BT, hid), lambda i: (skip + jnp.minimum(i, n_blocks - 1), 0)), whole, whole]
         + [pl.BlockSpec(memory_space=pl.ANY)] * len(flat),
         out_specs=pl.BlockSpec((BT, hid), lambda i: (jnp.maximum(i - n_blocks - 1, 0), 0)),
         out_shape=jax.ShapeDtypeStruct((n_tok, hid), BF16),
@@ -524,6 +557,7 @@
         n_loc = w_gate.shape[0]
         n_exp = n_loc * ep_size
         rows = TM * (ids_fwd.size // TM + n_exp)
+        rows_f = TM * (ids_fwd.size // HALVES // TM + n_exp)
         me = lax.axis_index("ep")
 
         own = (w_gate, w_up, w_down)
@@ -533,25 +567,36 @@
         weights = (own, near, far, far_near)
         firsts = [(me ^ g) * n_loc for g in range(ep_size)]
 
-        tab_b, pos4_b, pos2_b = route_ranks(ids_bwd, slots_bwd, n_exp, rows, (4, 2))
-        tab_f, pos2_f = route_ranks(ids_fwd, slots_fwd, n_exp, rows, (2,))
-        gates_b = gates_bwd.T.astype(F32)
-        gates_f = gates_fwd.T.astype(F32)
+        tab_b, pos4_b, pos2_b, tab_f, pos2_f = route_ranks(ids_bwd, slots_bwd, ids_fwd, slots_fwd, n_exp, rows, rows_f)
+        gates_b = gates_bwd.T
+        gates_f = gates_fwd.T
 
         h_bwd, xs, qs = pre_bwd(pos4_b, tab_b, gates_b, x_saved, grad_in, w1, w2, rows, n_exp, top_k)
-        parts = [None] * ep_size
-        for g in (0, 3, 2, 1):
-            xs, *parts[g] = exp_bwd(firsts[g].reshape(1), tab_b, *weights[g], xs, qs)
-        sums = [parts[2][i] + mate(parts[3][i]) for i in range(3)]
-        there = [chip(v) for v in sums]
+
+        def experts(g, xs, init=()):
+            return exp_bwd(firsts[g].reshape(1), tab_b, *weights[g], xs, qs, init)
+
+        xs, *part = experts(1, xs)
+        near_sum = [mate(v) for v in part]
+        xs, *part = experts(3, xs)
+        far_sum = [mate(v) for v in part]
+        xs, *dw_own = experts(0, xs, near_sum)
+        xs, *part = experts(2, xs, far_sum)
+        there = [chip(v) for v in part]
         grad_x = post_bwd(pos2_b, tab_b, x_saved, grad_in, h_bwd, w1, w2, xs, n_exp, top_k)
         x_fwd, grad_x = lax.optimization_barrier((x_fwd, grad_x))
         dx_prev = lax.ppermute(grad_x[None], "pp", prev_perm)
-        dws = [parts[0][i] + mate(parts[1][i]) + there[i] for i in range(3)]
-
-        y_out = fwd(jnp.stack(firsts), tab_f, pos2_f, gates_f, x_fwd, w1, w2, weights, rows, n_exp, top_k)
-        y_next = lax.ppermute(y_out[None], "pp", next_perm)
-        return y_next, dx_prev, dws[0][None], dws[1][None], dws[2][None]
+
+        halves = []
+        first_stack = jnp.stack(firsts)
+        for h in range(HALVES):
+            y_half = fwd(h, first_stack, tab_f[h], pos2_f, gates_f, x_fwd, w1, w2, weights, rows_f, n_exp, top_k)
+            if h + 1 < HALVES:
+                x_fwd, y_half = lax.optimization_barrier((x_fwd, y_half))
+            halves.append(lax.ppermute(y_half, "pp", next_perm))
+        y_next = jnp.concatenate(halves, axis=0)[None]
+        dws = [(a + b)[None] for a, b in zip(dw_own, there)]
+        return y_next, dx_prev, *dws
 
     in_specs = (tok_spec,) * 9 + (dense_spec, dense_spec, expert_spec, expert_spec, expert_spec)
     out_specs = (tok_spec, tok_spec, expert_spec, expert_spec, expert_spec)

time: 416 us -> 379 us (0.911)
  waiting for transfers between devices: 127 us -> 94 us
  Pallas kernels: 236 us -> 244 us
  local copies, waits for them, and re-layouts: 12.2 us -> 5.61 us
  other arithmetic: 13.1 us -> 8.74 us
    ppermute x6, waiting for transfers between devices: 92 us -> 40.1 us  [chip(): return lax.ppermute(a, 'ep', chip_perm)]
    ppermute x1 -> x2, waiting for transfers between devices: 35.3 us -> 46.3 us  [slot(): halves.append(lax.ppermute(y_half, 'pp', next_perm))]
    pallas_call x1 -> x2, Pallas kernels: 72 us -> 82 us  [fwd(): pl.pallas_call(functools.partial(fwd_kernel, n_blocks=n_blocks, top_k=top...]
    ppermute x12, waiting for transfers between devices: 0.03 us -> 7.67 us  [mate(): return lax.ppermute(a, 'ep', mate_perm)]
    pallas_call x1, Pallas kernels: 44.6 us -> 38.1 us  [pre_bwd(): pl.pallas_call(functools.partial(pre_bwd_kernel, n_blocks=n_blocks, top_k...]
    pallas_call x6 -> x5, Pallas kernels: 76.7 us -> 82.5 us  [the longest x4 72.7 us: exp_bwd(): pl.pallas_call(functools.partial(exp_bwd_kernel, n_loc=n_loc, has_init=bo...]
    add x3 -> x0, other arithmetic: 5 us -> none  [slot(): sums = [parts[2][i] + mate(parts[3][i]) for i in range(3)]]
    reshape x4 -> x0, local copies, waits for them, and re-layouts: 4.3 us -> none  [the longest x2 2.15 us: route_ranks(): by_block(ids).reshape(flat)]
  transfers between devices with their start and end apart: 20 -> 21, of which waited for: 4 -> 5; matrix products, arithmetic and copies ran while one was open for 4% -> 2% of each run, Pallas kernels for 57% -> 37%
where the time goes in v4:
time: 379 us; the launch traced here: 378 us
  Pallas kernels  244 us (64%)
  waiting for transfers between devices  94 us (25%)
  starting transfers between devices  24 us (6%)
  other arithmetic  8.74 us (2%)
  local copies, waits for them, and re-layouts  5.61 us (1%)
    pallas_call x2, Pallas kernels, fwd(): pl.pallas_call(functools.partial(fwd_kernel, n_blocks=n_blocks, top_k=top...  82 us
    pallas_call x4, Pallas kernels, exp_bwd(): pl.pallas_call(functools.partial(exp_bwd_kernel, n_loc=n_loc, has_init=bo...  72.7 us
    ppermute x2, waiting for transfers between devices, slot(): halves.append(lax.ppermute(y_half, 'pp', next_perm))  46.3 us
    pallas_call x1, Pallas kernels, post_bwd(): pl.pallas_call(functools.partial(post_bwd_kernel, n_blocks=n_blocks, top_...  41.8 us
    ppermute x6, waiting for transfers between devices, chip(): return lax.ppermute(a, 'ep', chip_perm)  40.1 us
    pallas_call x1, Pallas kernels, pre_bwd(): pl.pallas_call(functools.partial(pre_bwd_kernel, n_blocks=n_blocks, top_k...  38.1 us
    pallas_call x1, Pallas kernels, route_ranks(): pl.pallas_call(functools.partial(rank_kernel, n_exp, rows_b, rows_f), out...  9.83 us
    ppermute x6, starting transfers between devices, chip(): return lax.ppermute(a, 'ep', chip_perm)  9.49 us
  transfers between devices with their start and end apart: 21, of which 5 were waited for; matrix products, arithmetic and copies ran while one was open for 2% of the time, Pallas kernels for 37%

profile of v4, /device:TPU:0, one launch (start us, length us, event | category | flops | bytes accessed | tf_op | source)
XLA Modules:
  0.0 377.7 jit_solution(12774736209458751848)
XLA Ops:
  1.4 2.5 collective-permute-start
  4.4 9.8 %rank.1 = (s32[8,128]{1,0:T(8,128)}, s32[128,128]{1,0:T(8,128)}, s32[128,128]{1,0:T(8,128)}, s32[2,8,128]{2,1,0:T(8,128)}, s32[128,128]{1,0:T(8,128)}) custom-call(s32[4,4096]{1,0:T(4,128)} %bitcast.61, s32[4,4096]{1,0:T(4,128)} %bitcast.62, s32[4,4096]{1,0:T(4,128)} %bitcast.63, s32[4,4096]{1,0:T(4,128)} %bitcast.64), custom_call_target="tpu_custom_call" | custom-call | tf_op jit(solution)/shard_map/rank/pallas_call | solution.py:92
  14.3 38.1 %pre_bwd.1 = (bf16[4096,256]{1,0:T(8,128)(2,1)}, bf16[24576,256]{1,0:T(8,128)(2,1)}, bf16[24576,256]{1,0:T(8,128)(2,1)}) custom-call(s32[16384]{0:T(1024)} %bitcast.84, s32[8,128]{1,0:T(8,128)} %get-tuple-element.34.tab_ref, bf16[4,4096]{1,0:T(4,128)(2,1)} %bitcast.85, bf16[4096,256]{1,0:T(8,128)(2,1)} %bitcast.65, bf16[4096,256]{1,0:T(8,128)(2,1)} %bitcast.67, ...), custom_call_target="tpu_custom_call" | custom-call | flops 30000001024 | bytes 30000000 | tf_op jit(solution)/shard_map/pre_bwd/pallas_call | solution.py:229
  52.4 1.8 collective-permute-start.2
  55.2 22.9 %exp_bwd.4 = (bf16[24576,256]{1,0:T(8,128)(2,1)}, f32[8,256,256]{2,1,0:T(8,128)}, f32[8,256,256]{2,1,0:T(8,128)}, f32[8,256,256]{2,1,0:T(8,128)}) custom-call(s32[1]{0:T(128)} %bitcast.23.first_ref, s32[8,128]{1,0:T(8,128)} %get-tuple-element.34.tab_ref, bf16[8,256,256]{2,1,0:T(8,128)(2,1)} %copy-done.6, ...), custom_call_target="tpu_custom_call", output_to_operand_aliasing={{0}: (5, {})} | custom-call | flops 8000000000 | bytes 20000000 | tf_op jit(solution)/shard_map/exp_bwd/pallas_call | solution.py:362
  79.2 4.9 %collective-permute-done.3.refs_0_.rest_9_ = bf16[8,256,256]{2,1,0:T(8,128)(2,1)} collective-permute-done((bf16[8,256,256]{2,1,0:T(8,128)(2,1)}, bf16[8,256,256]{2,1,0:T(8,128)(2,1)}, u32[]{:S(2)}, u32[]{:S(2)}) %collective-permute-start.3) | collective-permute-done | bytes 1048608 | tf_op jit(solution)/shard_map/ppermute | solution.py:547
  85.6 1.4 collective-permute-done.5.refs_2_.rest_11_
  88.0 12.9 %exp_bwd.5 = (bf16[24576,256]{1,0:T(8,128)(2,1)}, f32[8,256,256]{2,1,0:T(8,128)}, f32[8,256,256]{2,1,0:T(8,128)}, f32[8,256,256]{2,1,0:T(8,128)}) custom-call(s32[1]{0:T(128)} %bitcast.22.first_ref, s32[8,128]{1,0:T(8,128)} %get-tuple-element.34.tab_ref, ...), custom_call_target="tpu_custom_call", output_to_operand_aliasing={{0}: (5, {})} | custom-call | flops 8000000000 | bytes 20000000 | tf_op jit(solution)/shard_map/exp_bwd/pallas_call | solution.py:362
  100.9 4.3 %collective-permute-start.12 = (f32[8,256,256]{2,1,0:T(8,128)}, f32[8,256,256]{2,1,0:T(8,128)}, u32[]{:S(2)}, u32[]{:S(2)}) collective-permute-start(f32[8,256,256]{2,1,0:T(8,128)} %get-tuple-element.45), channel_id=1, source_target_pairs={{0,1},{1,0},{2,3},{3,2},{4,5},{5,4},{6,7},{7,6},{8,9},{9,8},{10,11... | collective-permute-start | bytes 6291464 | tf_op jit(solution)/shard_map/ppermute | solution.py:547
  107.1 17.5 %exp_bwd.6 = (bf16[24576,256]{1,0:T(8,128)(2,1)}, f32[8,256,256]{2,1,0:T(8,128)}, f32[8,256,256]{2,1,0:T(8,128)}, f32[8,256,256]{2,1,0:T(8,128)}) custom-call(s32[1]{0:T(128)} %bitcast.21.first_ref, s32[8,128]{1,0:T(8,128)} %get-tuple-element.34.tab_ref, bf16[8,256,256]{2,1,0:T(8,128)(2,1)} %bitcast.48, ...), custom_call_target="tpu_custom_call", output_to_operand_aliasing={{0}: (5, {})} | custom-call | flops 8000000000 | bytes 20000000 | tf_op jit(solution)/shard_map/exp_bwd/pallas_call | solution.py:362
  124.6 19.3 %exp_bwd.7 = (bf16[24576,256]{1,0:T(8,128)(2,1)}, f32[8,256,256]{2,1,0:T(8,128)}, f32[8,256,256]{2,1,0:T(8,128)}, f32[8,256,256]{2,1,0:T(8,128)}) custom-call(s32[1]{0:T(128)} %bitcast.17.first_ref, s32[8,128]{1,0:T(8,128)} %get-tuple-element.34.tab_ref, bf16[8,256,256]{2,1,0:T(8,128)(2,1)} %collective-permute-done.refs_0_.rest_6_, ...), custom_call_target="tpu_custom_call", output_to_operand_aliasing={{0}: (5, {})} | custom-call | flops 8000000000 | bytes 20000000 | tf_op jit(solution)/shard_map/exp_bwd/pallas_call | solution.py:362
  143.9 41.8 %post_bwd.1 = bf16[4096,256]{1,0:T(8,128)(2,1)} custom-call(s32[16384]{0:T(1024)} %bitcast.83, s32[8,128]{1,0:T(8,128)} %get-tuple-element.34.tab_ref, bf16[4096,256]{1,0:T(8,128)(2,1)} %bitcast.66, bf16[4096,256]{1,0:T(8,128)(2,1)} %bitcast.68, bf16[4096,256]{1,0:T(8,128)(2,1)} %get-tuple-element.36.h_ref, bf16[256,256]{1,0:T(8,128)(2,1)} %bitcast.72, ...), custom_call_target="tpu_custom_call" | custom-call | flops 30000001024 | bytes 30000000 | tf_op jit(solution)/shard_map/post_bwd/pallas_call | solution.py:428
  185.7 42.0 %fwd.2 = bf16[2048,256]{1,0:T(8,128)(2,1)} custom-call(s32[4]{0:T(128)} %pad_add_fusion.firsts_ref, s32[8,128]{1,0:T(8,128)} %get-tuple-element.61.tab_ref, s32[16384]{0:T(1024)} %bitcast.79, s32[16384]{0:T(1024)} %bitcast.80, bf16[4,4096]{1,0:T(4,128)(2,1)} %bitcast.86, bf16[4096,256]{1,0:T(8,128)(2,1)} %bitcast.69, bf16[256,256]{1,0:T(8,128)(2,1)} %bitcast.73, ...), custom_call_target="tpu_custom_call" | custom-call | flops 80000000000 | bytes 30000000 | tf_op jit(solution)/shard_map/fwd/pallas_call | solution.py:514
  227.8 7.5 %collective-permute-start.17 = (bf16[1,4096,256]{2,1,0:T(8,128)(2,1)}, bf16[1,4096,256]{2,1,0:T(8,128)(2,1)}, u32[]{:S(2)}, u32[]{:S(2)}) collective-permute-start(bf16[1,4096,256]{2,1,0:T(8,128)(2,1)} %bitcast.31), channel_id=1, source_target_pairs={{0,12},{4,0},{8,4},{12,8},{1,13},{5,1},{9,5},{13,9},{2,14},{6,2},{... | collective-permute-start | bytes 6291464 | tf_op jit(solution)/shard_map/ppermute | solution.py:588
  235.2 2.5 collective-permute-start.18
  237.7 40.0 %fwd.3 = bf16[2048,256]{1,0:T(8,128)(2,1)} custom-call(s32[4]{0:T(128)} %pad_add_fusion.firsts_ref, s32[8,128]{1,0:T(8,128)} %get-tuple-element.62.tab_ref, s32[16384]{0:T(1024)} %bitcast.81, s32[16384]{0:T(1024)} %bitcast.82, bf16[4,4096]{1,0:T(4,128)(2,1)} %bitcast.87, bf16[4096,256]{1,0:T(8,128)(2,1)} %bitcast.70, bf16[256,256]{1,0:T(8,128)(2,1)} %bitcast.74, ...), custom_call_target="tpu_custom_call" | custom-call | flops 80000000000 | bytes 30000000 | tf_op jit(solution)/shard_map/fwd/pallas_call | solution.py:514
  277.9 2.4 collective-permute-start.20
  280.3 46.3 %collective-permute-done.16 = bf16[2048,256]{1,0:T(8,128)(2,1)S(1)} collective-permute-done((bf16[2048,256]{1,0:T(8,128)(2,1)}, bf16[2048,256]{1,0:T(8,128)(2,1)S(1)}, u32[]{:S(2)}, u32[]{:S(2)}) %collective-permute-start.16) | collective-permute-done | bytes 1048608 | tf_op jit(solution)/shard_map/ppermute | solution.py:596
  326.6 1.5 maximum_bitcast_fusion
  328.0 3.3 add_bitcast_fusion.2
  331.4 1.6 add_bitcast_fusion.1
  333.0 40.0 %collective-permute-done.20 = f32[8,256,256]{2,1,0:T(8,128)S(1)} collective-permute-done((f32[8,256,256]{2,1,0:T(8,128)}, f32[8,256,256]{2,1,0:T(8,128)S(1)}, u32[]{:S(2)}, u32[]{:S(2)}) %collective-permute-start.20) | collective-permute-done | bytes 2097184 | tf_op jit(solution)/shard_map/ppermute | solution.py:550
  373.0 1.6 add_bitcast_fusion
  374.6 3.0 copy.28
  (52 shorter events, 7.9 us)
Async XLA Ops:
  0.6 51.8 %collective-permute-start.6 = (bf16[8,256,256]{2,1,0:T(8,128)(2,1)}, bf16[8,256,256]{2,1,0:T(8,128)(2,1)S(1)}, u32[]{:S(2)}, u32[]{:S(2)}) collective-permute-start(bf16[8,256,256]{2,1,0:T(8,128)(2,1)} %bitcast.46), channel_id=1, source_target_pairs={{0,1},{1,0},{2,3},{3,2},{4,5},{5,4},{6,7},{7,6},{8,9},{9,8},{10,11... | collective-permute-start | bytes 3145736 | tf_op jit(solution)/shard_map/ppermute | solution.py:547
  1.4 76.8 %collective-permute-start = (bf16[8,256,256]{2,1,0:T(8,128)(2,1)}, bf16[8,256,256]{2,1,0:T(8,128)(2,1)}, u32[]{:S(2)}, u32[]{:S(2)}) collective-permute-start(bf16[8,256,256]{2,1,0:T(8,128)(2,1)} %bitcast.47), channel_id=1, source_target_pairs={{0,2},{1,3},{2,0},{3,1},{4,6},{5,7},{6,4},{7,5},{8,10},{9,11},{10,... | collective-permute-start | bytes 3145736 | tf_op jit(solution)/shard_map/ppermute | solution.py:550
  3.9 50.3 %collective-permute-start.7 = (bf16[8,256,256]{2,1,0:T(8,128)(2,1)}, bf16[8,256,256]{2,1,0:T(8,128)(2,1)S(1)}, u32[]{:S(2)}, u32[]{:S(2)}) collective-permute-start(bf16[8,256,256]{2,1,0:T(8,128)(2,1)} %bitcast.51), channel_id=1, source_target_pairs={{0,1},{1,0},{2,3},{3,2},{4,5},{5,4},{6,7},{7,6},{8,9},{9,8},{10,11... | collective-permute-start | bytes 3145736 | tf_op jit(solution)/shard_map/ppermute | solution.py:547
  4.1 74.6 %collective-permute-start.1 = (bf16[8,256,256]{2,1,0:T(8,128)(2,1)}, bf16[8,256,256]{2,1,0:T(8,128)(2,1)}, u32[]{:S(2)}, u32[]{:S(2)}) collective-permute-start(bf16[8,256,256]{2,1,0:T(8,128)(2,1)} %bitcast.52), channel_id=1, source_target_pairs={{0,2},{1,3},{2,0},{3,1},{4,6},{5,7},{6,4},{7,5},{8,10},{9,11},{10,... | collective-permute-start | bytes 3145736 | tf_op jit(solution)/shard_map/ppermute | solution.py:550
  4.4 49.8 %collective-permute-start.8 = (bf16[8,256,256]{2,1,0:T(8,128)(2,1)}, bf16[8,256,256]{2,1,0:T(8,128)(2,1)}, u32[]{:S(2)}, u32[]{:S(2)}) collective-permute-start(bf16[8,256,256]{2,1,0:T(8,128)(2,1)} %bitcast.56), channel_id=1, source_target_pairs={{0,1},{1,0},{2,3},{3,2},{4,5},{5,4},{6,7},{7,6},{8,9},{9,8},{10,11... | collective-permute-start | bytes 3145736 | tf_op jit(solution)/shard_map/ppermute | solution.py:547
  14.3 38.1 %copy-start.4 = (bf16[1,8,256,256]{3,2,1,0:T(8,128)(2,1)S(1)}, bf16[1,8,256,256]{3,2,1,0:T(8,128)(2,1)}, u32[]{:S(2)}) copy-start(bf16[1,8,256,256]{3,2,1,0:T(8,128)(2,1)} %param.27) | copy-start | bytes 3145732
  52.4 26.3 %collective-permute-start.2 = (bf16[8,256,256]{2,1,0:T(8,128)(2,1)S(1)}, bf16[8,256,256]{2,1,0:T(8,128)(2,1)}, u32[]{:S(2)}, u32[]{:S(2)}) collective-permute-start(bf16[8,256,256]{2,1,0:T(8,128)(2,1)S(1)} %bitcast.60), channel_id=1, source_target_pairs={{0,2},{1,3},{2,0},{3,1},{4,6},{5,7},{6,4},{7,5},{8,10},{9,11},{10,... | collective-permute-start | bytes 3145736 | tf_op jit(solution)/shard_map/ppermute | solution.py:550
  78.1 27.1 %collective-permute-start.9 = (f32[8,256,256]{2,1,0:T(8,128)}, f32[8,256,256]{2,1,0:T(8,128)S(1)}, u32[]{:S(2)}, u32[]{:S(2)}) collective-permute-start(f32[8,256,256]{2,1,0:T(8,128)} %get-tuple-element.41), channel_id=1, source_target_pairs={{0,1},{1,0},{2,3},{3,2},{4,5},{5,4},{6,7},{7,6},{8,9},{9,8},{10,11... | collective-permute-start | bytes 6291464 | tf_op jit(solution)/shard_map/ppermute | solution.py:547
  78.2 6.0 %collective-permute-start.3 = (bf16[8,256,256]{2,1,0:T(8,128)(2,1)}, bf16[8,256,256]{2,1,0:T(8,128)(2,1)}, u32[]{:S(2)}, u32[]{:S(2)}) collective-permute-start(bf16[8,256,256]{2,1,0:T(8,128)(2,1)} %collective-permute-done.refs_0_.rest_6_), channel_id=1, source_target_pairs={{0,1},{1,0},{2,3},{3,2},{4,5},{5,4},{6,7},{7,6},{8,9},{9,8},{10,11... | collective-permute-start | bytes 3145736 | tf_op jit(solution)/shard_map/ppermute | solution.py:547
  78.6 7.0 %collective-permute-start.4 = (bf16[8,256,256]{2,1,0:T(8,128)(2,1)}, bf16[8,256,256]{2,1,0:T(8,128)(2,1)}, u32[]{:S(2)}, u32[]{:S(2)}) collective-permute-start(bf16[8,256,256]{2,1,0:T(8,128)(2,1)} %collective-permute-done.1.refs_1_.rest_7_), channel_id=1, source_target_pairs={{0,1},{1,0},{2,3},{3,2},{4,5},{5,4},{6,7},{7,6},{8,9},{9,8},{10,11... | collective-permute-start | bytes 3145736 | tf_op jit(solution)/shard_map/ppermute | solution.py:547
  78.7 8.3 %collective-permute-start.5 = (bf16[8,256,256]{2,1,0:T(8,128)(2,1)}, bf16[8,256,256]{2,1,0:T(8,128)(2,1)S(1)}, u32[]{:S(2)}, u32[]{:S(2)}) collective-permute-start(bf16[8,256,256]{2,1,0:T(8,128)(2,1)} %collective-permute-done.2.refs_2_.rest_8_), channel_id=1, source_target_pairs={{0,1},{1,0},{2,3},{3,2},{4,5},{5,4},{6,7},{7,6},{8,9},{9,8},{10,11... | collective-permute-start | bytes 3145736 | tf_op jit(solution)/shard_map/ppermute | solution.py:547
  79.2 27.9 %collective-permute-start.10 = (f32[8,256,256]{2,1,0:T(8,128)}, f32[8,256,256]{2,1,0:T(8,128)}, u32[]{:S(2)}, u32[]{:S(2)}) collective-permute-start(f32[8,256,256]{2,1,0:T(8,128)} %get-tuple-element.42), channel_id=1, source_target_pairs={{0,1},{1,0},{2,3},{3,2},{4,5},{5,4},{6,7},{7,6},{8,9},{9,8},{10,11... | collective-permute-start | bytes 6291464 | tf_op jit(solution)/shard_map/ppermute | solution.py:547
  84.1 22.9 %collective-permute-start.11 = (f32[8,256,256]{2,1,0:T(8,128)}, f32[8,256,256]{2,1,0:T(8,128)}, u32[]{:S(2)}, u32[]{:S(2)}) collective-permute-start(f32[8,256,256]{2,1,0:T(8,128)} %get-tuple-element.43), channel_id=1, source_target_pairs={{0,1},{1,0},{2,3},{3,2},{4,5},{5,4},{6,7},{7,6},{8,9},{9,8},{10,11... | collective-permute-start | bytes 6291464 | tf_op jit(solution)/shard_map/ppermute | solution.py:547
  100.9 23.7 %collective-permute-start.12 = (f32[8,256,256]{2,1,0:T(8,128)}, f32[8,256,256]{2,1,0:T(8,128)}, u32[]{:S(2)}, u32[]{:S(2)}) collective-permute-start(f32[8,256,256]{2,1,0:T(8,128)} %get-tuple-element.45), channel_id=1, source_target_pairs={{0,1},{1,0},{2,3},{3,2},{4,5},{5,4},{6,7},{7,6},{8,9},{9,8},{10,11... | collective-permute-start | bytes 6291464 | tf_op jit(solution)/shard_map/ppermute | solution.py:547
  105.2 19.4 %collective-permute-start.13 = (f32[8,256,256]{2,1,0:T(8,128)}, f32[8,256,256]{2,1,0:T(8,128)}, u32[]{:S(2)}, u32[]{:S(2)}) collective-permute-start(f32[8,256,256]{2,1,0:T(8,128)} %get-tuple-element.46), channel_id=1, source_target_pairs={{0,1},{1,0},{2,3},{3,2},{4,5},{5,4},{6,7},{7,6},{8,9},{9,8},{10,11... | collective-permute-start | bytes 6291464 | tf_op jit(solution)/shard_map/ppermute | solution.py:547
  105.2 19.4 %collective-permute-start.14 = (f32[8,256,256]{2,1,0:T(8,128)}, f32[8,256,256]{2,1,0:T(8,128)}, u32[]{:S(2)}, u32[]{:S(2)}) collective-permute-start(f32[8,256,256]{2,1,0:T(8,128)} %get-tuple-element.47), channel_id=1, source_target_pairs={{0,1},{1,0},{2,3},{3,2},{4,5},{5,4},{6,7},{7,6},{8,9},{9,8},{10,11... | collective-permute-start | bytes 6291464 | tf_op jit(solution)/shard_map/ppermute | solution.py:547
  227.7 50.1 %collective-permute-start.15 = (bf16[2048,256]{1,0:T(8,128)(2,1)}, bf16[2048,256]{1,0:T(8,128)(2,1)S(1)}, u32[]{:S(2)}, u32[]{:S(2)}) collective-permute-start(bf16[2048,256]{1,0:T(8,128)(2,1)} %fwd.2), channel_id=1, source_target_pairs={{0,4},{4,8},{8,12},{12,0},{1,5},{5,9},{9,13},{13,1},{2,6},{6,10},{... | collective-permute-start | bytes 3145736 | tf_op jit(solution)/shard_map/ppermute | solution.py:596
  227.8 100.2 %collective-permute-start.17 = (bf16[1,4096,256]{2,1,0:T(8,128)(2,1)}, bf16[1,4096,256]{2,1,0:T(8,128)(2,1)}, u32[]{:S(2)}, u32[]{:S(2)}) collective-permute-start(bf16[1,4096,256]{2,1,0:T(8,128)(2,1)} %bitcast.31), channel_id=1, source_target_pairs={{0,12},{4,0},{8,4},{12,8},{1,13},{5,1},{9,5},{13,9},{2,14},{6,2},{... | collective-permute-start | bytes 6291464 | tf_op jit(solution)/shard_map/ppermute | solution.py:588
  235.2 92.8 %collective-permute-start.18 = (f32[8,256,256]{2,1,0:T(8,128)}, f32[8,256,256]{2,1,0:T(8,128)}, u32[]{:S(2)}, u32[]{:S(2)}) collective-permute-start(f32[8,256,256]{2,1,0:T(8,128)} %get-tuple-element.56), channel_id=1, source_target_pairs={{0,2},{1,3},{2,0},{3,1},{4,6},{5,7},{6,4},{7,5},{8,10},{9,11},{10,... | collective-permute-start | bytes 6291464 | tf_op jit(solution)/shard_map/ppermute | solution.py:550
  237.7 93.7 %collective-permute-start.19 = (f32[8,256,256]{2,1,0:T(8,128)}, f32[8,256,256]{2,1,0:T(8,128)S(1)}, u32[]{:S(2)}, u32[]{:S(2)}) collective-permute-start(f32[8,256,256]{2,1,0:T(8,128)} %get-tuple-element.58), channel_id=1, source_target_pairs={{0,2},{1,3},{2,0},{3,1},{4,6},{5,7},{6,4},{7,5},{8,10},{9,11},{10,... | collective-permute-start | bytes 6291464 | tf_op jit(solution)/shard_map/ppermute | solution.py:550
  277.8 48.8 %collective-permute-start.16 = (bf16[2048,256]{1,0:T(8,128)(2,1)}, bf16[2048,256]{1,0:T(8,128)(2,1)S(1)}, u32[]{:S(2)}, u32[]{:S(2)}) collective-permute-start(bf16[2048,256]{1,0:T(8,128)(2,1)} %fwd.3), channel_id=1, source_target_pairs={{0,4},{4,8},{8,12},{12,0},{1,5},{5,9},{9,13},{13,1},{2,6},{6,10},{... | collective-permute-start | bytes 3145736 | tf_op jit(solution)/shard_map/ppermute | solution.py:596
  277.8 50.2 %copy-start.2 = (f32[8,256,256]{2,1,0:T(8,128)S(1)}, f32[8,256,256]{2,1,0:T(8,128)}, u32[]{:S(2)}) copy-start(f32[8,256,256]{2,1,0:T(8,128)} %get-tuple-element.55) | copy-start | bytes 6291460
  277.9 95.2 %collective-permute-start.20 = (f32[8,256,256]{2,1,0:T(8,128)}, f32[8,256,256]{2,1,0:T(8,128)S(1)}, u32[]{:S(2)}, u32[]{:S(2)}) collective-permute-start(f32[8,256,256]{2,1,0:T(8,128)} %get-tuple-element.60), channel_id=1, source_target_pairs={{0,2},{1,3},{2,0},{3,1},{4,6},{5,7},{6,4},{7,5},{8,10},{9,11},{10,... | collective-permute-start | bytes 6291464 | tf_op jit(solution)/shard_map/ppermute | solution.py:550
  331.4 41.6 %copy-start = (f32[8,256,256]{2,1,0:T(8,128)S(1)}, f32[8,256,256]{2,1,0:T(8,128)}, u32[]{:S(2)}) copy-start(f32[8,256,256]{2,1,0:T(8,128)} %get-tuple-element.59) | copy-start | bytes 6291460
  (6 other events, 27.4 us)

commit v5 on v4

--- a/solution.py
+++ b/solution.py
@@ -12,6 +12,7 @@
 TM = 256
 BT = 512
 DEPTH = 4
+QUEUE = 8
 HALVES = 2
 F32 = jnp.float32
 BF16 = jnp.bfloat16
@@ -50,22 +51,23 @@
     n, lanes = ids.shape
     row = lax.broadcasted_iota(jnp.int32, (lanes, lanes), 0)
     col = lax.broadcasted_iota(jnp.int32, (lanes, lanes), 1)
-    right = jnp.concatenate([jnp.where(row < col, 1.0, 0.0).astype(BF16), jnp.ones((lanes, lanes), BF16)], axis=1)
+    upper = jnp.where(row < col, 1.0, 0.0).astype(BF16)
+    right = jnp.concatenate([upper, jnp.ones((lanes, lanes), BF16)], axis=1)
     row = lax.broadcasted_iota(jnp.int32, (n + 8, n), 0)
     col = lax.broadcasted_iota(jnp.int32, (n + 8, n), 1)
     left = jnp.where((col < row) | (row >= n), 1.0, 0.0).astype(BF16)
-    lane = lax.broadcasted_iota(jnp.int32, (8, lanes), 1)
-    start = jnp.zeros((8, lanes), F32)
-    tab = jnp.zeros((8, lanes), F32)
+    lane = lax.broadcasted_iota(jnp.int32, (n, lanes), 1)
+    both = dot(jnp.concatenate([jnp.where(ids == e, 1.0, 0.0).astype(BF16) for e in range(n_exp)], axis=0), right)
+    totals = jnp.zeros((n, lanes), F32)
+    for e in range(n_exp):
+        totals = jnp.where(lane == e, both[e * n : (e + 1) * n, lanes:], totals)
+    pre = dot(left, totals.astype(BF16))
+    tiles = jnp.maximum(jnp.floor((pre[n:] + (TM - 1.0)) * (1.0 / TM)), 1.0)
+    tab = dot(tiles.astype(BF16), upper)
+    base = pre[:n] + TM * tab[0:1]
     pos = jnp.full((n, lanes), float(dump), F32)
     for e in range(n_exp):
-        mask = ids == e
-        both = dot(jnp.where(mask, 1.0, 0.0).astype(BF16), right)
-        pre = dot(left, both[:, lanes:].astype(BF16))
-        pos = jnp.where(mask, both[:, :lanes] + pre[:n] + start[0:1], pos)
-        tab = jnp.where(lane == e, start, tab)
-        start = start + TM * jnp.maximum(jnp.floor((pre[n:] + (TM - 1.0)) * (1.0 / TM)), 1.0)
-    tab = jnp.where(lane == n_exp, start, tab) * (1.0 / TM)
+        pos = jnp.where(ids == e, both[e * n : (e + 1) * n, :lanes] + base[:, e : e + 1], pos)
     return pos, tab.astype(jnp.int32)
 
 
@@ -192,11 +194,11 @@
             )
 
         def convert(t, c):
-            slot = lax.rem(t, DEPTH)
-
-            @pl.when(t >= DEPTH)
+            slot = lax.rem(t, QUEUE)
+
+            @pl.when(t >= QUEUE)
             def _():
-                for cp in copies(t - DEPTH, slot):
+                for cp in copies(t - QUEUE, slot):
                     cp.wait()
 
             rows = pl.multiple_of(t * (4 * TM), 4 * TM)
@@ -207,8 +209,8 @@
             return c
 
         lax.fori_loop(0, n_tiles, convert, 0)
-        for back in range(DEPTH, 0, -1):
-            for cp in copies(n_tiles - back, lax.rem(n_tiles - back, DEPTH)):
+        for back in range(QUEUE, 0, -1):
+            for cp in copies(n_tiles - back, lax.rem(n_tiles - back, QUEUE)):
                 cp.wait()
 
 
@@ -239,9 +241,9 @@
         scratch_shapes=[
             pltpu.VMEM((4 * rows + 8, hid // 2), F32),
             pltpu.VMEM((top_k, 4 * BT, hid // 2), F32),
-            pltpu.VMEM((DEPTH, TM, hid), BF16),
-            pltpu.VMEM((DEPTH, TM, hid), BF16),
-            pltpu.SemaphoreType.DMA((2, DEPTH)),
+            pltpu.VMEM((QUEUE, TM, hid), BF16),
+            pltpu.VMEM((QUEUE, TM, hid), BF16),
+            pltpu.SemaphoreType.DMA((2, QUEUE)),
         ],
         compiler_params=pltpu.CompilerParams(vmem_limit_bytes=VMEM_LIMIT),
         cost_estimate=pl.CostEstimate(flops=30_000_000_000, bytes_accessed=30_000_000, transcendentals=0),
@@ -252,7 +254,7 @@
 def exp_bwd_kernel(first_ref, tab_ref, *refs, n_loc, has_init):
     w_hbm, (xs_hbm, qs_hbm), refs = refs[:3], refs[3:5], refs[5:]
     init_hbm, refs = (refs[:3], refs[3:]) if has_init else ((), refs)
-    rs_hbm, *dw_hbm, wb, dwb, xb, qb, rb, sems, wsems, dsems, isems = refs
+    rs_hbm, *dw_hbm, wb, dwb, xb, qb, rb, mid, sems, wsems, dsems, isems = refs
     first = first_ref[0]
     begin = tab_ref[0, first]
     end = tab_ref[0, first + n_loc]
@@ -272,84 +274,98 @@
         return pltpu.make_async_copy(rb.at[slot], rs_hbm.at[rows_of(t)], sems.at[2, slot])
 
     def w_loads(e):
-        slot = lax.rem(e, 2)
-        return [pltpu.make_async_copy(w_hbm[i].at[e], wb.at[slot, i], wsems.at[i, slot]) for i in range(3)]
-
-    def init_loads(e):
-        slot = lax.rem(e, 3)
-        return [pltpu.make_async_copy(ref.at[e], dwb.at[slot, i], isems.at[i, slot]) for i, ref in enumerate(init_hbm)]
+        copies = [pltpu.make_async_copy(w_hbm[i].at[e], wb.at[i, e], wsems.at[i, e]) for i in range(3)]
+        return copies + [pltpu.make_async_copy(ref.at[e], dwb.at[i, e], isems.at[i, e]) for i, ref in enumerate(init_hbm)]
 
     def dw_saves(e):
-        slot = lax.rem(e, 3)
-        return [pltpu.make_async_copy(dwb.at[slot, i], dw_hbm[i].at[e], dsems.at[i, slot]) for i in range(3)]
-
-    for cp in w_loads(0) + init_loads(0):
+        return [pltpu.make_async_copy(dwb.at[i, e], dw_hbm[i].at[e], dsems.at[i, e]) for i in range(3)]
+
+    def first_half(t, e):
+        slot = lax.rem(t, DEPTH)
+        x = xb[slot]
+        pre = dot(x, wb[0, e])
+        up = dot(x, wb[1, e])
+        da = dot_nt(qb[slot], wb[2, e]).astype(BF16).astype(F32)
+        sig = jax.nn.sigmoid(pre)
+        sil = pre * sig
+        return (
+            (sil * up).astype(BF16),
+            (da * up * (sig * (1.0 + pre * (1.0 - sig)))).astype(BF16),
+            (da * sil).astype(BF16),
+        )
+
+    def keep(t, vals):
+        for i, v in enumerate(vals):
+            mid[lax.rem(t, 2), i] = v
+
+    for cp in w_loads(0):
         cp.start()
     for ahead in range(DEPTH - 1):
         for cp in loads(begin + ahead):
             cp.start()
-
-    def expert(e, c):
-        wslot = lax.rem(e, 2)
-        dslot = lax.rem(e, 3)
-        for cp in w_loads(e) + init_loads(e):
-            cp.wait()
-
-        @pl.when(e >= 2)
+    for e in range(1, n_loc):
+        for cp in w_loads(e):
+            cp.start()
+    if not has_init:
+        def clear(e, c):
+            for i in range(3):
+                dwb[i, e] = jnp.zeros(dwb.shape[2:], F32)
+            return c
+
+        lax.fori_loop(0, n_loc, clear, 0)
+    for cp in w_loads(0):
+        cp.wait()
+    for cp in loads(begin):
+        cp.wait()
+    keep(begin, first_half(begin, 0))
+
+    def body(t, e):
+        slot = lax.rem(t, DEPTH)
+        more = t + 1 < end
+        changes = t + 1 >= tab_ref[0, first + e + 1]
+        then = jnp.where(changes & more, e + 1, e)
+
+        @pl.when(changes & more)
         def _():
-            for cp in dw_saves(e - 2):
+            for cp in w_loads(then):
                 cp.wait()
 
-        @pl.when(e + 1 < n_loc)
+        @pl.when(t + (DEPTH - 1) < end)
         def _():
-            for cp in w_loads(e + 1) + init_loads(e + 1):
+            for cp in loads(t + (DEPTH - 1)):
                 cp.start()
 
-        if not has_init:
-            dwb[dslot] = jnp.zeros(dwb.shape[1:], F32)
-
-        def body(t, c):
-            slot = lax.rem(t, DEPTH)
-
-            @pl.when(t + (DEPTH - 1) < end)
-            def _():
-                for cp in loads(t + (DEPTH - 1)):
-                    cp.start()
-
-            for cp in loads(t):
+        @pl.when(more)
+        def _():
+            for cp in loads(t + 1):
                 cp.wait()
 
-            @pl.when(t >= begin + DEPTH)
-            def _():
-                save(t - DEPTH).wait()
-
-            x = xb[slot]
-            q = qb[slot]
-            wg, wu, wd = wb[wslot, 0], wb[wslot, 1], wb[wslot, 2]
-            pre = dot(x, wg)
-            up = dot(x, wu)
-            sig = jax.nn.sigmoid(pre)
-            sil = pre * sig
-            act = (sil * up).astype(BF16)
-            dwb[dslot, 2] += dot_tn(act, q)
-            da = dot_nt(q, wd).astype(BF16).astype(F32)
-            dpre = (da * up * (sig * (1.0 + pre * (1.0 - sig)))).astype(BF16)
-            dup = (da * sil).astype(BF16)
-            dwb[dslot, 0] += dot_tn(x, dpre)
-            dwb[dslot, 1] += dot_tn(x, dup)
-            rb[slot] = (dot_nt(dpre, wg) + dot_nt(dup, wu)).astype(BF16)
-            save(t).start()
-            return c
-
-        lax.fori_loop(tab_ref[0, first + e], tab_ref[0, first + e + 1], body, 0)
-        for cp in dw_saves(e):
-            cp.start()
-        return c
-
-    lax.fori_loop(0, n_loc, expert, 0)
+        @pl.when(t >= begin + DEPTH)
+        def _():
+            save(t - DEPTH).wait()
+
+        act, dpre, dup = mid[lax.rem(t, 2), 0], mid[lax.rem(t, 2), 1], mid[lax.rem(t, 2), 2]
+        x = xb[slot]
+        rows = (dot_nt(dpre, wb[0, e]) + dot_nt(dup, wb[1, e])).astype(BF16)
+        upcoming = first_half(jnp.minimum(t + 1, end - 1), then)
+        grads = (dot_tn(x, dpre), dot_tn(x, dup), dot_tn(act, qb[slot]))
+        rb[slot] = rows
+        for i, grad in enumerate(grads):
+            dwb[i, e] += grad
+        keep(t + 1, upcoming)
+        save(t).start()
+
+        @pl.when(changes)
+        def _():
+            for cp in dw_saves(e):
+                cp.start()
+
+        return then
+
+    lax.fori_loop(begin, end, body, 0)
     for back in range(DEPTH, 0, -1):
         save(end - back).wait()
-    for e in (n_loc - 2, n_loc - 1):
+    for e in range(n_loc):
         for cp in dw_saves(e):
             cp.wait()
 
@@ -366,15 +382,16 @@
         out_shape=(jax.ShapeDtypeStruct(xs.shape, BF16), dw, dw, dw),
         input_output_aliases={5: 0},
         scratch_shapes=[
-            pltpu.VMEM((2, 3, hid, ff), BF16),
-            pltpu.VMEM((3, 3, hid, ff), F32),
+            pltpu.VMEM((3, n_loc, hid, ff), BF16),
+            pltpu.VMEM((3, n_loc, hid, ff), F32),
             pltpu.VMEM((DEPTH, TM, hid), BF16),
             pltpu.VMEM((DEPTH, TM, hid), BF16),
             pltpu.VMEM((DEPTH, TM, hid), BF16),
+            pltpu.VMEM((2, 3, TM, ff), BF16),
             pltpu.SemaphoreType.DMA((3, DEPTH)),
-            pltpu.SemaphoreType.DMA((3, 2)),
-            pltpu.SemaphoreType.DMA((3, 3)),
-            pltpu.SemaphoreType.DMA((3, 3)),
+            pltpu.SemaphoreType.DMA((3, n_loc)),
+            pltpu.SemaphoreType.DMA((3, n_loc)),
+            pltpu.SemaphoreType.DMA((3, n_loc)),
         ],
         compiler_params=pltpu.CompilerParams(vmem_limit_bytes=VMEM_LIMIT),
         cost_estimate=pl.CostEstimate(flops=8_000_000_000, bytes_accessed=20_000_000, transcendentals=0),
@@ -388,20 +405,20 @@
         n_tiles = tab_ref[0, n_exp]
 
         def load(t):
-            slot = lax.rem(t, DEPTH)
+            slot = lax.rem(t, (2 * QUEUE))
             return pltpu.make_async_copy(rs_hbm.at[pl.ds(pl.multiple_of(t * TM, TM), TM)], st.at[slot], sems.at[slot])
 
-        for ahead in range(DEPTH - 1):
+        for ahead in range((2 * QUEUE) - 1):
             load(ahead).start()
         rbuf[2 * rows : 2 * rows + 8, :] = jnp.zeros((8, rbuf.shape[1]), F32)
 
         def expand(t, c):
-            @pl.when(t + (DEPTH - 1) < n_tiles)
+            @pl.when(t + ((2 * QUEUE) - 1) < n_tiles)
             def _():
-                load(t + (DEPTH - 1)).start()
+                load(t + ((2 * QUEUE) - 1)).start()
 
             load(t).wait()
-            put_rows(rbuf, pl.multiple_of(t * (2 * TM), 2 * TM), st[lax.rem(t, DEPTH)].astype(F32))
+            put_rows(rbuf, pl.multiple_of(t * (2 * TM), 2 * TM), st[lax.rem(t, (2 * QUEUE))].astype(F32))
             return c
 
         lax.fori_loop(0, n_tiles, expand, 0)
@@ -434,8 +451,8 @@
         scratch_shapes=[
             pltpu.VMEM((2 * rows + 8, hid // 2), F32),
             pltpu.VMEM((top_k, 2 * BT, hid // 2), F32),
-            pltpu.VMEM((DEPTH, TM, hid), BF16),
-            pltpu.SemaphoreType.DMA((DEPTH,)),
+            pltpu.VMEM(((2 * QUEUE), TM, hid), BF16),
+            pltpu.SemaphoreType.DMA(((2 * QUEUE),)),
         ],
         compiler_params=pltpu.CompilerParams(vmem_limit_bytes=VMEM_LIMIT),
         cost_estimate=pl.CostEstimate(flops=30_000_000_000, bytes_accessed=30_000_000, transcendentals=0),
@@ -445,13 +462,13 @@
 
 def fwd_kernel(firsts_ref, tab_ref, pos_ref, pos_out_ref, gate_ref, x_ref, w1_ref, w2_ref, *rest, n_blocks, top_k, n_exp, n_groups, rows):
     w_hbm = rest[: 3 * n_groups]
-    y_ref, buf, acc, hsc, wsc, sems = rest[3 * n_groups :]
+    y_ref, buf, acc, hsc, wsc, mid, sems = rest[3 * n_groups :]
     nsc = acc.at[0]
     step = pl.program_id(0)
     n_loc = n_exp // n_groups
 
     def w_copy(i):
-        return pltpu.make_async_copy(w_hbm[i], wsc.at[i], sems.at[i])
+        return pltpu.make_async_copy(w_hbm[i], wsc.at[i % 3, pl.ds(firsts_ref[i // 3], n_loc)], sems.at[i])
 
     @pl.when(step == 0)
     def _():
@@ -472,22 +489,30 @@
     @pl.when(step == n_blocks)
     def _():
         buf[2 * rows : 2 * rows + 8, :] = jnp.zeros((8, buf.shape[1]), F32)
-        for g in range(n_groups):
-            for i in range(3):
-                w_copy(3 * g + i).wait()
-            first = firsts_ref[g]
-
-            def body(t, e):
-                e = jnp.where(t >= tab_ref[0, first + e + 1], e + 1, e)
-                at = pl.multiple_of(t * (2 * TM), 2 * TM)
-                x = get_rows(buf, at, TM).astype(BF16)
-                pre = dot(x, wsc[3 * g, e])
-                up = dot(x, wsc[3 * g + 1, e])
-                act = (pre * jax.nn.sigmoid(pre) * up).astype(BF16)
-                put_rows(buf, at, dot(act, wsc[3 * g + 2, e]).astype(BF16).astype(F32))
-                return e
-
-            lax.fori_loop(tab_ref[0, first], tab_ref[0, first + n_loc], body, 0)
+        for i in range(3 * n_groups):
+            w_copy(i).wait()
+        end = tab_ref[0, n_exp]
+
+        def rows_of(t):
+            return get_rows(buf, pl.multiple_of(t * (2 * TM), 2 * TM), TM).astype(BF16)
+
+        def first_half(x, e):
+            pre = dot(x, wsc[0, e])
+            up = dot(x, wsc[1, e])
+            return (pre * jax.nn.sigmoid(pre) * up).astype(BF16)
+
+        mid[0] = first_half(rows_of(0), 0)
+
+        def body(t, e):
+            then = jnp.where((t + 1 >= tab_ref[0, e + 1]) & (t + 1 < end), e + 1, e)
+            x = rows_of(jnp.minimum(t + 1, end - 1))
+            out = dot(mid[lax.rem(t, 2)], wsc[2, e]).astype(BF16).astype(F32)
+            upcoming = first_half(x, then)
+            put_rows(buf, pl.multiple_of(t * (2 * TM), 2 * TM), out)
+            mid[lax.rem(t + 1, 2)] = upcoming
+            return then
+
+        lax.fori_loop(0, end, body, 0)
 
     @pl.when(step > n_blocks)
     def _():
@@ -507,7 +532,6 @@
     n_blocks = n_tok // BT
     skip = half * n_blocks
     n_groups = len(weights)
-    n_loc = n_exp // n_groups
     smem = pl.BlockSpec(memory_space=pltpu.SMEM)
     whole = pl.BlockSpec((hid, hid), lambda i: (0, 0))
     flat = [w for group in weights for w in group]
@@ -523,7 +547,8 @@
             pltpu.VMEM((2 * rows + 8, hid // 2), F32),
             pltpu.VMEM((top_k, 2 * BT, hid // 2), F32),
             pltpu.VMEM((n_tok, hid), BF16),
-            pltpu.VMEM((len(flat), n_loc, hid, hid), BF16),
+            pltpu.VMEM((3, n_exp, hid, hid), BF16),
+            pltpu.VMEM((2, TM, hid), BF16),
             pltpu.SemaphoreType.DMA((len(flat),)),
         ],
         compiler_params=pltpu.CompilerParams(vmem_limit_bytes=VMEM_LIMIT),

time: 379 us -> 343 us (0.905)
  Pallas kernels: 244 us -> 199 us
  waiting for transfers between devices: 94 us -> 102 us
    pallas_call x1, Pallas kernels: 41.8 us -> 29.1 us  [post_bwd(): pl.pallas_call(functools.partial(post_bwd_kernel, n_blocks=n_blocks, top_...]
    pallas_call x4, Pallas kernels: 72.7 us -> 61.2 us  [exp_bwd(): pl.pallas_call(functools.partial(exp_bwd_kernel, n_loc=n_loc, has_init=bo...]
    pallas_call x2, Pallas kernels: 82 us -> 72.3 us  [fwd(): pl.pallas_call(functools.partial(fwd_kernel, n_blocks=n_blocks, top_k=top...]
    ppermute x6, waiting for transfers between devices: 40.1 us -> 49.5 us  [chip(): return lax.ppermute(a, 'ep', chip_perm)]
    pallas_call x1, Pallas kernels: 38.1 us -> 31.8 us  [pre_bwd(): pl.pallas_call(functools.partial(pre_bwd_kernel, n_blocks=n_blocks, top_k...]
    ppermute x12, waiting for transfers between devices: 7.67 us -> 2.38 us  [mate(): return lax.ppermute(a, 'ep', mate_perm)]
    pallas_call x1, Pallas kernels: 9.83 us -> 5.04 us  [route_ranks(): pl.pallas_call(functools.partial(rank_kernel, n_exp, rows_b, rows_f), out...]
    ppermute x2, waiting for transfers between devices: 46.3 us -> 50.5 us  [slot(): halves.append(lax.ppermute(y_half, 'pp', next_perm))]
  transfers between devices with their start and end apart: 21 -> 21, of which waited for: 5 -> 4; matrix products, arithmetic and copies ran while one was open for 2% -> 2% of each run, Pallas kernels for 37% -> 34%
where the time goes in v5:
time: 343 us; the launch traced here: 341 us
  Pallas kernels  199 us (58%)
  waiting for transfers between devices  102 us (30%)
  starting transfers between devices  24.2 us (7%)
  other arithmetic  8.74 us (3%)
  local copies, waits for them, and re-layouts  5.61 us (2%)
    pallas_call x2, Pallas kernels, fwd(): pl.pallas_call(functools.partial(fwd_kernel, n_blocks=n_blocks, top_k=top...  72.3 us
    pallas_call x4, Pallas kernels, exp_bwd(): pl.pallas_call(functools.partial(exp_bwd_kernel, n_loc=n_loc, has_init=bo...  61.2 us
    ppermute x2, waiting for transfers between devices, slot(): halves.append(lax.ppermute(y_half, 'pp', next_perm))  50.5 us
    ppermute x6, waiting for transfers between devices, chip(): return lax.ppermute(a, 'ep', chip_perm)  49.5 us
    pallas_call x1, Pallas kernels, pre_bwd(): pl.pallas_call(functools.partial(pre_bwd_kernel, n_blocks=n_blocks, top_k...  31.8 us
    pallas_call x1, Pallas kernels, post_bwd(): pl.pallas_call(functools.partial(post_bwd_kernel, n_blocks=n_blocks, top_...  29.1 us
    ppermute x6, starting transfers between devices, chip(): return lax.ppermute(a, 'ep', chip_perm)  10.1 us
    ppermute x1, starting transfers between devices, slot(): dx_prev = lax.ppermute(grad_x[None], 'pp', prev_perm)  7.52 us
  transfers between devices with their start and end apart: 21, of which 4 were waited for; matrix products, arithmetic and copies ran while one was open for 2% of the time, Pallas kernels for 34%

profile of v5, /device:TPU:0, one launch (start us, length us, event | category | flops | bytes accessed | tf_op | source)
XLA Modules:
  0.0 341.3 jit_solution(15672939156750691060)
XLA Ops:
  1.4 2.5 collective-permute-start
  4.4 5.0 %rank.1 = (s32[8,128]{1,0:T(8,128)}, s32[128,128]{1,0:T(8,128)}, s32[128,128]{1,0:T(8,128)}, s32[2,8,128]{2,1,0:T(8,128)}, s32[128,128]{1,0:T(8,128)}) custom-call(s32[4,4096]{1,0:T(4,128)} %bitcast.61, s32[4,4096]{1,0:T(4,128)} %bitcast.62, s32[4,4096]{1,0:T(4,128)} %bitcast.63, s32[4,4096]{1,0:T(4,128)} %bitcast.64), custom_call_target="tpu_custom_call" | custom-call | tf_op jit(solution)/shard_map/rank/pallas_call | solution.py:94
  9.5 31.8 %pre_bwd.1 = (bf16[4096,256]{1,0:T(8,128)(2,1)}, bf16[24576,256]{1,0:T(8,128)(2,1)}, bf16[24576,256]{1,0:T(8,128)(2,1)}) custom-call(s32[16384]{0:T(1024)} %bitcast.84, s32[8,128]{1,0:T(8,128)} %get-tuple-element.34.tab_ref, bf16[4,4096]{1,0:T(4,128)(2,1)} %bitcast.85, bf16[4096,256]{1,0:T(8,128)(2,1)} %bitcast.65, bf16[4096,256]{1,0:T(8,128)(2,1)} %bitcast.67, ...), custom_call_target="tpu_custom_call" | custom-call | flops 30000001024 | bytes 30000000 | tf_op jit(solution)/shard_map/pre_bwd/pallas_call | solution.py:231
  41.3 1.8 collective-permute-start.2
  44.1 18.9 %exp_bwd.4 = (bf16[24576,256]{1,0:T(8,128)(2,1)}, f32[8,256,256]{2,1,0:T(8,128)}, f32[8,256,256]{2,1,0:T(8,128)}, f32[8,256,256]{2,1,0:T(8,128)}) custom-call(s32[1]{0:T(128)} %bitcast.23.first_ref, s32[8,128]{1,0:T(8,128)} %get-tuple-element.34.tab_ref, bf16[8,256,256]{2,1,0:T(8,128)(2,1)} %copy-done.6, ...), custom_call_target="tpu_custom_call", output_to_operand_aliasing={{0}: (5, {})} | custom-call | flops 8000000000 | bytes 20000000 | tf_op jit(solution)/shard_map/exp_bwd/pallas_call | solution.py:378
  63.6 9.4 %collective-permute-done.2.refs_2_.rest_8_ = bf16[8,256,256]{2,1,0:T(8,128)(2,1)} collective-permute-done((bf16[8,256,256]{2,1,0:T(8,128)(2,1)S(1)}, bf16[8,256,256]{2,1,0:T(8,128)(2,1)}, u32[]{:S(2)}, u32[]{:S(2)}) %collective-permute-start.2) | collective-permute-done | bytes 1048608 | tf_op jit(solution)/shard_map/ppermute | solution.py:575
  73.5 2.3 collective-permute-done.5.refs_2_.rest_11_
  76.8 10.0 %exp_bwd.5 = (bf16[24576,256]{1,0:T(8,128)(2,1)}, f32[8,256,256]{2,1,0:T(8,128)}, f32[8,256,256]{2,1,0:T(8,128)}, f32[8,256,256]{2,1,0:T(8,128)}) custom-call(s32[1]{0:T(128)} %bitcast.22.first_ref, s32[8,128]{1,0:T(8,128)} %get-tuple-element.34.tab_ref, ...), custom_call_target="tpu_custom_call", output_to_operand_aliasing={{0}: (5, {})} | custom-call | flops 8000000000 | bytes 20000000 | tf_op jit(solution)/shard_map/exp_bwd/pallas_call | solution.py:378
  86.8 3.9 %collective-permute-start.12 = (f32[8,256,256]{2,1,0:T(8,128)}, f32[8,256,256]{2,1,0:T(8,128)}, u32[]{:S(2)}, u32[]{:S(2)}) collective-permute-start(f32[8,256,256]{2,1,0:T(8,128)} %get-tuple-element.45), channel_id=1, source_target_pairs={{0,1},{1,0},{2,3},{3,2},{4,5},{5,4},{6,7},{7,6},{8,9},{9,8},{10,11... | collective-permute-start | bytes 6291464 | tf_op jit(solution)/shard_map/ppermute | solution.py:572
  92.6 14.5 %exp_bwd.6 = (bf16[24576,256]{1,0:T(8,128)(2,1)}, f32[8,256,256]{2,1,0:T(8,128)}, f32[8,256,256]{2,1,0:T(8,128)}, f32[8,256,256]{2,1,0:T(8,128)}) custom-call(s32[1]{0:T(128)} %bitcast.21.first_ref, s32[8,128]{1,0:T(8,128)} %get-tuple-element.34.tab_ref, bf16[8,256,256]{2,1,0:T(8,128)(2,1)} %bitcast.48, ...), custom_call_target="tpu_custom_call", output_to_operand_aliasing={{0}: (5, {})} | custom-call | flops 8000000000 | bytes 20000000 | tf_op jit(solution)/shard_map/exp_bwd/pallas_call | solution.py:378
  107.2 17.8 %exp_bwd.7 = (bf16[24576,256]{1,0:T(8,128)(2,1)}, f32[8,256,256]{2,1,0:T(8,128)}, f32[8,256,256]{2,1,0:T(8,128)}, f32[8,256,256]{2,1,0:T(8,128)}) custom-call(s32[1]{0:T(128)} %bitcast.17.first_ref, s32[8,128]{1,0:T(8,128)} %get-tuple-element.34.tab_ref, bf16[8,256,256]{2,1,0:T(8,128)(2,1)} %collective-permute-done.refs_0_.rest_6_, ...), custom_call_target="tpu_custom_call", output_to_operand_aliasing={{0}: (5, {})} | custom-call | flops 8000000000 | bytes 20000000 | tf_op jit(solution)/shard_map/exp_bwd/pallas_call | solution.py:378
  125.0 29.1 %post_bwd.1 = bf16[4096,256]{1,0:T(8,128)(2,1)} custom-call(s32[16384]{0:T(1024)} %bitcast.83, s32[8,128]{1,0:T(8,128)} %get-tuple-element.34.tab_ref, bf16[4096,256]{1,0:T(8,128)(2,1)} %bitcast.66, bf16[4096,256]{1,0:T(8,128)(2,1)} %bitcast.68, bf16[4096,256]{1,0:T(8,128)(2,1)} %get-tuple-element.36.h_ref, bf16[256,256]{1,0:T(8,128)(2,1)} %bitcast.72, ...), custom_call_target="tpu_custom_call" | custom-call | flops 30000001024 | bytes 30000000 | tf_op jit(solution)/shard_map/post_bwd/pallas_call | solution.py:445
  154.1 36.8 %fwd.2 = bf16[2048,256]{1,0:T(8,128)(2,1)} custom-call(s32[4]{0:T(128)} %pad_add_fusion.firsts_ref, s32[8,128]{1,0:T(8,128)} %get-tuple-element.61.tab_ref, s32[16384]{0:T(1024)} %bitcast.79, s32[16384]{0:T(1024)} %bitcast.80, bf16[4,4096]{1,0:T(4,128)(2,1)} %bitcast.86, bf16[4096,256]{1,0:T(8,128)(2,1)} %bitcast.69, bf16[256,256]{1,0:T(8,128)(2,1)} %bitcast.73, ...), custom_call_target="tpu_custom_call" | custom-call | flops 80000000000 | bytes 30000000 | tf_op jit(solution)/shard_map/fwd/pallas_call | solution.py:538
  191.0 7.5 %collective-permute-start.17 = (bf16[1,4096,256]{2,1,0:T(8,128)(2,1)}, bf16[1,4096,256]{2,1,0:T(8,128)(2,1)}, u32[]{:S(2)}, u32[]{:S(2)}) collective-permute-start(bf16[1,4096,256]{2,1,0:T(8,128)(2,1)} %bitcast.31), channel_id=1, source_target_pairs={{0,12},{4,0},{8,4},{12,8},{1,13},{5,1},{9,5},{13,9},{2,14},{6,2},{... | collective-permute-start | bytes 6291464 | tf_op jit(solution)/shard_map/ppermute | solution.py:613
  198.5 3.0 collective-permute-start.18
  201.5 35.4 %fwd.3 = bf16[2048,256]{1,0:T(8,128)(2,1)} custom-call(s32[4]{0:T(128)} %pad_add_fusion.firsts_ref, s32[8,128]{1,0:T(8,128)} %get-tuple-element.62.tab_ref, s32[16384]{0:T(1024)} %bitcast.81, s32[16384]{0:T(1024)} %bitcast.82, bf16[4,4096]{1,0:T(4,128)(2,1)} %bitcast.87, bf16[4096,256]{1,0:T(8,128)(2,1)} %bitcast.70, bf16[256,256]{1,0:T(8,128)(2,1)} %bitcast.74, ...), custom_call_target="tpu_custom_call" | custom-call | flops 80000000000 | bytes 30000000 | tf_op jit(solution)/shard_map/fwd/pallas_call | solution.py:538
  237.0 2.6 collective-permute-start.20
  239.6 50.5 %collective-permute-done.16 = bf16[2048,256]{1,0:T(8,128)(2,1)S(1)} collective-permute-done((bf16[2048,256]{1,0:T(8,128)(2,1)}, bf16[2048,256]{1,0:T(8,128)(2,1)S(1)}, u32[]{:S(2)}, u32[]{:S(2)}) %collective-permute-start.16) | collective-permute-done | bytes 1048608 | tf_op jit(solution)/shard_map/ppermute | solution.py:621
  290.0 1.5 maximum_bitcast_fusion
  291.5 3.3 add_bitcast_fusion.2
  294.9 1.6 add_bitcast_fusion.1
  296.4 40.2 %collective-permute-done.20 = f32[8,256,256]{2,1,0:T(8,128)S(1)} collective-permute-done((f32[8,256,256]{2,1,0:T(8,128)}, f32[8,256,256]{2,1,0:T(8,128)S(1)}, u32[]{:S(2)}, u32[]{:S(2)}) %collective-permute-start.20) | collective-permute-done | bytes 2097184 | tf_op jit(solution)/shard_map/ppermute | solution.py:575
  336.6 1.6 add_bitcast_fusion
  338.2 3.0 copy.28
  (52 shorter events, 6.4 us)
Async XLA Ops:
  0.6 40.7 %collective-permute-start.6 = (bf16[8,256,256]{2,1,0:T(8,128)(2,1)}, bf16[8,256,256]{2,1,0:T(8,128)(2,1)S(1)}, u32[]{:S(2)}, u32[]{:S(2)}) collective-permute-start(bf16[8,256,256]{2,1,0:T(8,128)(2,1)} %bitcast.46), channel_id=1, source_target_pairs={{0,1},{1,0},{2,3},{3,2},{4,5},{5,4},{6,7},{7,6},{8,9},{9,8},{10,11... | collective-permute-start | bytes 3145736 | tf_op jit(solution)/shard_map/ppermute | solution.py:572
  1.4 61.6 %collective-permute-start = (bf16[8,256,256]{2,1,0:T(8,128)(2,1)}, bf16[8,256,256]{2,1,0:T(8,128)(2,1)}, u32[]{:S(2)}, u32[]{:S(2)}) collective-permute-start(bf16[8,256,256]{2,1,0:T(8,128)(2,1)} %bitcast.47), channel_id=1, source_target_pairs={{0,2},{1,3},{2,0},{3,1},{4,6},{5,7},{6,4},{7,5},{8,10},{9,11},{10,... | collective-permute-start | bytes 3145736 | tf_op jit(solution)/shard_map/ppermute | solution.py:575
  3.9 39.2 %collective-permute-start.7 = (bf16[8,256,256]{2,1,0:T(8,128)(2,1)}, bf16[8,256,256]{2,1,0:T(8,128)(2,1)S(1)}, u32[]{:S(2)}, u32[]{:S(2)}) collective-permute-start(bf16[8,256,256]{2,1,0:T(8,128)(2,1)} %bitcast.51), channel_id=1, source_target_pairs={{0,1},{1,0},{2,3},{3,2},{4,5},{5,4},{6,7},{7,6},{8,9},{9,8},{10,11... | collective-permute-start | bytes 3145736 | tf_op jit(solution)/shard_map/ppermute | solution.py:572
  4.1 59.4 %collective-permute-start.1 = (bf16[8,256,256]{2,1,0:T(8,128)(2,1)}, bf16[8,256,256]{2,1,0:T(8,128)(2,1)}, u32[]{:S(2)}, u32[]{:S(2)}) collective-permute-start(bf16[8,256,256]{2,1,0:T(8,128)(2,1)} %bitcast.52), channel_id=1, source_target_pairs={{0,2},{1,3},{2,0},{3,1},{4,6},{5,7},{6,4},{7,5},{8,10},{9,11},{10,... | collective-permute-start | bytes 3145736 | tf_op jit(solution)/shard_map/ppermute | solution.py:575
  4.4 38.8 %collective-permute-start.8 = (bf16[8,256,256]{2,1,0:T(8,128)(2,1)}, bf16[8,256,256]{2,1,0:T(8,128)(2,1)}, u32[]{:S(2)}, u32[]{:S(2)}) collective-permute-start(bf16[8,256,256]{2,1,0:T(8,128)(2,1)} %bitcast.56), channel_id=1, source_target_pairs={{0,1},{1,0},{2,3},{3,2},{4,5},{5,4},{6,7},{7,6},{8,9},{9,8},{10,11... | collective-permute-start | bytes 3145736 | tf_op jit(solution)/shard_map/ppermute | solution.py:572
  9.5 31.9 %copy-start.4 = (bf16[1,8,256,256]{3,2,1,0:T(8,128)(2,1)S(1)}, bf16[1,8,256,256]{3,2,1,0:T(8,128)(2,1)}, u32[]{:S(2)}) copy-start(bf16[1,8,256,256]{3,2,1,0:T(8,128)(2,1)} %param.27) | copy-start | bytes 3145732
  41.3 31.6 %collective-permute-start.2 = (bf16[8,256,256]{2,1,0:T(8,128)(2,1)S(1)}, bf16[8,256,256]{2,1,0:T(8,128)(2,1)}, u32[]{:S(2)}, u32[]{:S(2)}) collective-permute-start(bf16[8,256,256]{2,1,0:T(8,128)(2,1)S(1)} %bitcast.60), channel_id=1, source_target_pairs={{0,2},{1,3},{2,0},{3,1},{4,6},{5,7},{6,4},{7,5},{8,10},{9,11},{10,... | collective-permute-start | bytes 3145736 | tf_op jit(solution)/shard_map/ppermute | solution.py:575
  63.0 27.8 %collective-permute-start.9 = (f32[8,256,256]{2,1,0:T(8,128)}, f32[8,256,256]{2,1,0:T(8,128)S(1)}, u32[]{:S(2)}, u32[]{:S(2)}) collective-permute-start(f32[8,256,256]{2,1,0:T(8,128)} %get-tuple-element.41), channel_id=1, source_target_pairs={{0,1},{1,0},{2,3},{3,2},{4,5},{5,4},{6,7},{7,6},{8,9},{9,8},{10,11... | collective-permute-start | bytes 6291464 | tf_op jit(solution)/shard_map/ppermute | solution.py:572
  63.0 10.4 %collective-permute-start.3 = (bf16[8,256,256]{2,1,0:T(8,128)(2,1)}, bf16[8,256,256]{2,1,0:T(8,128)(2,1)}, u32[]{:S(2)}, u32[]{:S(2)}) collective-permute-start(bf16[8,256,256]{2,1,0:T(8,128)(2,1)} %collective-permute-done.refs_0_.rest_6_), channel_id=1, source_target_pairs={{0,1},{1,0},{2,3},{3,2},{4,5},{5,4},{6,7},{7,6},{8,9},{9,8},{10,11... | collective-permute-start | bytes 3145736 | tf_op jit(solution)/shard_map/ppermute | solution.py:572
  63.5 9.9 %collective-permute-start.4 = (bf16[8,256,256]{2,1,0:T(8,128)(2,1)}, bf16[8,256,256]{2,1,0:T(8,128)(2,1)}, u32[]{:S(2)}, u32[]{:S(2)}) collective-permute-start(bf16[8,256,256]{2,1,0:T(8,128)(2,1)} %collective-permute-done.1.refs_1_.rest_7_), channel_id=1, source_target_pairs={{0,1},{1,0},{2,3},{3,2},{4,5},{5,4},{6,7},{7,6},{8,9},{9,8},{10,11... | collective-permute-start | bytes 3145736 | tf_op jit(solution)/shard_map/ppermute | solution.py:572
  73.0 2.9 collective-permute-start.5
  73.0 19.6 %collective-permute-start.10 = (f32[8,256,256]{2,1,0:T(8,128)}, f32[8,256,256]{2,1,0:T(8,128)}, u32[]{:S(2)}, u32[]{:S(2)}) collective-permute-start(f32[8,256,256]{2,1,0:T(8,128)} %get-tuple-element.42), channel_id=1, source_target_pairs={{0,1},{1,0},{2,3},{3,2},{4,5},{5,4},{6,7},{7,6},{8,9},{9,8},{10,11... | collective-permute-start | bytes 6291464 | tf_op jit(solution)/shard_map/ppermute | solution.py:572
  73.5 19.1 %collective-permute-start.11 = (f32[8,256,256]{2,1,0:T(8,128)}, f32[8,256,256]{2,1,0:T(8,128)}, u32[]{:S(2)}, u32[]{:S(2)}) collective-permute-start(f32[8,256,256]{2,1,0:T(8,128)} %get-tuple-element.43), channel_id=1, source_target_pairs={{0,1},{1,0},{2,3},{3,2},{4,5},{5,4},{6,7},{7,6},{8,9},{9,8},{10,11... | collective-permute-start | bytes 6291464 | tf_op jit(solution)/shard_map/ppermute | solution.py:572
  86.8 20.3 %collective-permute-start.12 = (f32[8,256,256]{2,1,0:T(8,128)}, f32[8,256,256]{2,1,0:T(8,128)}, u32[]{:S(2)}, u32[]{:S(2)}) collective-permute-start(f32[8,256,256]{2,1,0:T(8,128)} %get-tuple-element.45), channel_id=1, source_target_pairs={{0,1},{1,0},{2,3},{3,2},{4,5},{5,4},{6,7},{7,6},{8,9},{9,8},{10,11... | collective-permute-start | bytes 6291464 | tf_op jit(solution)/shard_map/ppermute | solution.py:572
  90.7 16.4 %collective-permute-start.13 = (f32[8,256,256]{2,1,0:T(8,128)}, f32[8,256,256]{2,1,0:T(8,128)}, u32[]{:S(2)}, u32[]{:S(2)}) collective-permute-start(f32[8,256,256]{2,1,0:T(8,128)} %get-tuple-element.46), channel_id=1, source_target_pairs={{0,1},{1,0},{2,3},{3,2},{4,5},{5,4},{6,7},{7,6},{8,9},{9,8},{10,11... | collective-permute-start | bytes 6291464 | tf_op jit(solution)/shard_map/ppermute | solution.py:572
  90.8 16.4 %collective-permute-start.14 = (f32[8,256,256]{2,1,0:T(8,128)}, f32[8,256,256]{2,1,0:T(8,128)}, u32[]{:S(2)}, u32[]{:S(2)}) collective-permute-start(f32[8,256,256]{2,1,0:T(8,128)} %get-tuple-element.47), channel_id=1, source_target_pairs={{0,1},{1,0},{2,3},{3,2},{4,5},{5,4},{6,7},{7,6},{8,9},{9,8},{10,11... | collective-permute-start | bytes 6291464 | tf_op jit(solution)/shard_map/ppermute | solution.py:572
  190.9 46.0 %collective-permute-start.15 = (bf16[2048,256]{1,0:T(8,128)(2,1)}, bf16[2048,256]{1,0:T(8,128)(2,1)S(1)}, u32[]{:S(2)}, u32[]{:S(2)}) collective-permute-start(bf16[2048,256]{1,0:T(8,128)(2,1)} %fwd.2), channel_id=1, source_target_pairs={{0,4},{4,8},{8,12},{12,0},{1,5},{5,9},{9,13},{13,1},{2,6},{6,10},{... | collective-permute-start | bytes 3145736 | tf_op jit(solution)/shard_map/ppermute | solution.py:621
  191.0 100.5 %collective-permute-start.17 = (bf16[1,4096,256]{2,1,0:T(8,128)(2,1)}, bf16[1,4096,256]{2,1,0:T(8,128)(2,1)}, u32[]{:S(2)}, u32[]{:S(2)}) collective-permute-start(bf16[1,4096,256]{2,1,0:T(8,128)(2,1)} %bitcast.31), channel_id=1, source_target_pairs={{0,12},{4,0},{8,4},{12,8},{1,13},{5,1},{9,5},{13,9},{2,14},{6,2},{... | collective-permute-start | bytes 6291464 | tf_op jit(solution)/shard_map/ppermute | solution.py:613
  198.5 93.0 %collective-permute-start.18 = (f32[8,256,256]{2,1,0:T(8,128)}, f32[8,256,256]{2,1,0:T(8,128)}, u32[]{:S(2)}, u32[]{:S(2)}) collective-permute-start(f32[8,256,256]{2,1,0:T(8,128)} %get-tuple-element.56), channel_id=1, source_target_pairs={{0,2},{1,3},{2,0},{3,1},{4,6},{5,7},{6,4},{7,5},{8,10},{9,11},{10,... | collective-permute-start | bytes 6291464 | tf_op jit(solution)/shard_map/ppermute | solution.py:575
  201.5 93.4 %collective-permute-start.19 = (f32[8,256,256]{2,1,0:T(8,128)}, f32[8,256,256]{2,1,0:T(8,128)S(1)}, u32[]{:S(2)}, u32[]{:S(2)}) collective-permute-start(f32[8,256,256]{2,1,0:T(8,128)} %get-tuple-element.58), channel_id=1, source_target_pairs={{0,2},{1,3},{2,0},{3,1},{4,6},{5,7},{6,4},{7,5},{8,10},{9,11},{10,... | collective-permute-start | bytes 6291464 | tf_op jit(solution)/shard_map/ppermute | solution.py:575
  236.9 53.1 %collective-permute-start.16 = (bf16[2048,256]{1,0:T(8,128)(2,1)}, bf16[2048,256]{1,0:T(8,128)(2,1)S(1)}, u32[]{:S(2)}, u32[]{:S(2)}) collective-permute-start(bf16[2048,256]{1,0:T(8,128)(2,1)} %fwd.3), channel_id=1, source_target_pairs={{0,4},{4,8},{8,12},{12,0},{1,5},{5,9},{9,13},{13,1},{2,6},{6,10},{... | collective-permute-start | bytes 3145736 | tf_op jit(solution)/shard_map/ppermute | solution.py:621
  237.0 54.5 %copy-start.2 = (f32[8,256,256]{2,1,0:T(8,128)S(1)}, f32[8,256,256]{2,1,0:T(8,128)}, u32[]{:S(2)}) copy-start(f32[8,256,256]{2,1,0:T(8,128)} %get-tuple-element.55) | copy-start | bytes 6291460
  237.0 99.6 %collective-permute-start.20 = (f32[8,256,256]{2,1,0:T(8,128)}, f32[8,256,256]{2,1,0:T(8,128)S(1)}, u32[]{:S(2)}, u32[]{:S(2)}) collective-permute-start(f32[8,256,256]{2,1,0:T(8,128)} %get-tuple-element.60), channel_id=1, source_target_pairs={{0,2},{1,3},{2,0},{3,1},{4,6},{5,7},{6,4},{7,5},{8,10},{9,11},{10,... | collective-permute-start | bytes 6291464 | tf_op jit(solution)/shard_map/ppermute | solution.py:575
  294.8 41.8 %copy-start = (f32[8,256,256]{2,1,0:T(8,128)S(1)}, f32[8,256,256]{2,1,0:T(8,128)}, u32[]{:S(2)}) copy-start(f32[8,256,256]{2,1,0:T(8,128)} %get-tuple-element.59) | copy-start | bytes 6291460
  (6 other events, 24.1 us)

commit v6 on v5

--- a/solution.py
+++ b/solution.py
@@ -13,7 +13,7 @@
 BT = 512
 DEPTH = 4
 QUEUE = 8
-HALVES = 2
+FWD_BLOCKS = (5, 3)
 F32 = jnp.float32
 BF16 = jnp.bfloat16
 VMEM_LIMIT = 60 * 1024 * 1024
@@ -80,12 +80,13 @@
     pos, tab_b[...] = rank_routes(chunks(ids_b, 0, n), chunks(slots_b, 0, n), n_exp, rows_b)
     pos4_b[...] = (pos * 4.0).astype(jnp.int32)
     pos2_b[...] = (pos * 2.0).astype(jnp.int32)
-    step = n // HALVES
-    for h in range(HALVES):
-        at = (h * step, (h + 1) * step)
-        pos, tab_f[h] = rank_routes(chunks(ids_f, *at), chunks(slots_f, *at), n_exp, rows_f)
-        k = pos.shape[0]
-        pos2_f[h * k : (h + 1) * k, :] = (pos * 2.0).astype(jnp.int32)
+    first = 0
+    for h, (blocks, dump) in enumerate(zip(FWD_BLOCKS, rows_f)):
+        last = first + blocks * (BT // 128)
+        pos, tab_f[h] = rank_routes(chunks(ids_f, first, last), chunks(slots_f, first, last), n_exp, dump)
+        k = ids_f.shape[0]
+        pos2_f[first * k : last * k, :] = (pos * 2.0).astype(jnp.int32)
+        first = last
 
 
 def route_ranks(ids_b, slots_b, ids_f, slots_f, n_exp, rows_b, rows_f):
@@ -97,7 +98,7 @@
             jax.ShapeDtypeStruct(tab, jnp.int32),
             pos,
             pos,
-            jax.ShapeDtypeStruct((HALVES, *tab), jnp.int32),
+            jax.ShapeDtypeStruct((len(FWD_BLOCKS), *tab), jnp.int32),
             pos,
         ),
         name="rank",
@@ -465,10 +466,9 @@
     y_ref, buf, acc, hsc, wsc, mid, sems = rest[3 * n_groups :]
     nsc = acc.at[0]
     step = pl.program_id(0)
-    n_loc = n_exp // n_groups
 
     def w_copy(i):
-        return pltpu.make_async_copy(w_hbm[i], wsc.at[i % 3, pl.ds(firsts_ref[i // 3], n_loc)], sems.at[i])
+        return pltpu.make_async_copy(w_hbm[i], wsc.at[i % 3, pl.ds(firsts_ref[i // 3], w_hbm[i].shape[0])], sems.at[i])
 
     @pl.when(step == 0)
     def _():
@@ -527,10 +527,8 @@
         y_ref[...] = (h.astype(F32) + mix).astype(BF16)
 
 
-def fwd(half, firsts, tab, pos, gates, x, w1, w2, weights, rows, n_exp, top_k):
-    n_tok, hid = x.shape[0] // HALVES, x.shape[1]
-    n_blocks = n_tok // BT
-    skip = half * n_blocks
+def fwd(n_blocks, skip, firsts, tab, pos, gates, x, w1, w2, weights, rows, n_exp, top_k):
+    n_tok, hid = n_blocks * BT, x.shape[1]
     n_groups = len(weights)
     smem = pl.BlockSpec(memory_space=pltpu.SMEM)
     whole = pl.BlockSpec((hid, hid), lambda i: (0, 0))
@@ -582,15 +580,22 @@
         n_loc = w_gate.shape[0]
         n_exp = n_loc * ep_size
         rows = TM * (ids_fwd.size // TM + n_exp)
-        rows_f = TM * (ids_fwd.size // HALVES // TM + n_exp)
+        rows_f = [TM * (blocks * BT * top_k // TM + n_exp) for blocks in FWD_BLOCKS]
         me = lax.axis_index("ep")
 
         own = (w_gate, w_up, w_down)
-        far = tuple(chip(w) for w in own)
-        near = tuple(mate(w) for w in own)
-        far_near = tuple(mate(w) for w in far)
-        weights = (own, near, far, far_near)
-        firsts = [(me ^ g) * n_loc for g in range(ep_size)]
+        half = n_loc // 2
+        far = [[chip(w[h * half : (h + 1) * half]) for w in own] for h in range(2)]
+        near = [mate(w) for w in own]
+        relay = [[mate(w) for w in far[h]] for h in range(2)]
+        groups = {
+            "own": (me * n_loc, own),
+            "near": ((me ^ 1) * n_loc, near),
+            "far0": ((me ^ 2) * n_loc, far[0]),
+            "far1": ((me ^ 2) * n_loc + half, far[1]),
+            "relay0": ((me ^ 3) * n_loc, relay[0]),
+            "relay1": ((me ^ 3) * n_loc + half, relay[1]),
+        }
 
         tab_b, pos4_b, pos2_b, tab_f, pos2_f = route_ranks(ids_bwd, slots_bwd, ids_fwd, slots_fwd, n_exp, rows, rows_f)
         gates_b = gates_bwd.T
@@ -598,29 +603,41 @@
 
         h_bwd, xs, qs = pre_bwd(pos4_b, tab_b, gates_b, x_saved, grad_in, w1, w2, rows, n_exp, top_k)
 
-        def experts(g, xs, init=()):
-            return exp_bwd(firsts[g].reshape(1), tab_b, *weights[g], xs, qs, init)
-
-        xs, *part = experts(1, xs)
-        near_sum = [mate(v) for v in part]
-        xs, *part = experts(3, xs)
-        far_sum = [mate(v) for v in part]
-        xs, *dw_own = experts(0, xs, near_sum)
-        xs, *part = experts(2, xs, far_sum)
-        there = [chip(v) for v in part]
+        def experts(name, xs, init=()):
+            first, weights = groups[name]
+            return exp_bwd(first.reshape(1), tab_b, *weights, xs, qs, init)
+
+        def to_mate(parts):
+            return [mate(v) for v in parts]
+
+        there = []
+        xs, *part = experts("relay0", xs)
+        far_sum = to_mate(part)
+        xs, *part = experts("near", xs)
+        near_sum = to_mate(part)
+        xs, *part = experts("far0", xs, far_sum)
+        there.append([chip(v) for v in part])
+        xs, *part = experts("relay1", xs)
+        far_sum = to_mate(part)
+        xs, *dw_own = experts("own", xs, near_sum)
+        xs, *part = experts("far1", xs, far_sum)
+        there.append([chip(v) for v in part])
         grad_x = post_bwd(pos2_b, tab_b, x_saved, grad_in, h_bwd, w1, w2, xs, n_exp, top_k)
         x_fwd, grad_x = lax.optimization_barrier((x_fwd, grad_x))
         dx_prev = lax.ppermute(grad_x[None], "pp", prev_perm)
 
         halves = []
-        first_stack = jnp.stack(firsts)
-        for h in range(HALVES):
-            y_half = fwd(h, first_stack, tab_f[h], pos2_f, gates_f, x_fwd, w1, w2, weights, rows_f, n_exp, top_k)
-            if h + 1 < HALVES:
+        firsts = jnp.stack([first for first, _ in groups.values()])
+        weights = [w for _, w in groups.values()]
+        skip = 0
+        for h, blocks in enumerate(FWD_BLOCKS):
+            y_half = fwd(blocks, skip, firsts, tab_f[h], pos2_f, gates_f, x_fwd, w1, w2, weights, rows_f[h], n_exp, top_k)
+            skip += blocks
+            if h + 1 < len(FWD_BLOCKS):
                 x_fwd, y_half = lax.optimization_barrier((x_fwd, y_half))
             halves.append(lax.ppermute(y_half, "pp", next_perm))
         y_next = jnp.concatenate(halves, axis=0)[None]
-        dws = [(a + b)[None] for a, b in zip(dw_own, there)]
+        dws = [jnp.concatenate([a[:half] + b, a[half:] + c], axis=0)[None] for a, b, c in zip(dw_own, *there)]
         return y_next, dx_prev, *dws
 
     in_specs = (tok_spec,) * 9 + (dense_spec, dense_spec, expert_spec, expert_spec, expert_spec)

time: 343 us -> 350 us (1.020)
  waiting for transfers between devices: 102 us -> 89.5 us
  starting transfers between devices: 24.2 us -> 32.7 us
  local copies, waits for them, and re-layouts: 5.61 us -> 11.4 us
  Pallas kernels: 199 us -> 203 us
    ppermute x6 -> x12, starting transfers between devices: 10.1 us -> 21.9 us  [chip(): return lax.ppermute(a, 'ep', chip_perm)]
    ppermute x6 -> x12, waiting for transfers between devices: 49.5 us -> 40.7 us  [chip(): return lax.ppermute(a, 'ep', chip_perm)]
    add x0 -> x3, other arithmetic: none -> 5.47 us  [slot(): a[:half] + b]
    ppermute x1, starting transfers between devices: 7.52 us -> 2.21 us  [slot(): dx_prev = lax.ppermute(grad_x[None], 'pp', prev_perm)]
    pallas_call x4 -> x6, Pallas kernels: 61.2 us -> 65.6 us  [exp_bwd(): pl.pallas_call(functools.partial(exp_bwd_kernel, n_loc=n_loc, has_init=bo...]
    slice x0 -> x3, local copies, waits for them, and re-layouts: none -> 4.28 us  [slot(): far = [[chip(w[h * half:(h + 1) * half]) for w in own] for h in range(2)]]
  transfers between devices with their start and end apart: 21 -> 33, of which waited for: 4 -> 6; matrix products, arithmetic and copies ran while one was open for 2% -> 4% of each run, Pallas kernels for 34% -> 58%
where the time goes in v6:
time: 350 us; the launch traced here: 349 us
  Pallas kernels  203 us (58%)
  waiting for transfers between devices  89.5 us (26%)
  starting transfers between devices  32.7 us (9%)
  local copies, waits for them, and re-layouts  11.4 us (3%)
  other arithmetic  11.4 us (3%)
    pallas_call x2, Pallas kernels, fwd(): pl.pallas_call(functools.partial(fwd_kernel, n_blocks=n_blocks, top_k=top...  71.6 us
    pallas_call x6, Pallas kernels, exp_bwd(): pl.pallas_call(functools.partial(exp_bwd_kernel, n_loc=n_loc, has_init=bo...  65.6 us
    ppermute x2, waiting for transfers between devices, slot(): halves.append(lax.ppermute(y_half, 'pp', next_perm))  48.8 us
    ppermute x12, waiting for transfers between devices, chip(): return lax.ppermute(a, 'ep', chip_perm)  40.7 us
    pallas_call x1, Pallas kernels, pre_bwd(): pl.pallas_call(functools.partial(pre_bwd_kernel, n_blocks=n_blocks, top_k...  31.6 us
    pallas_call x1, Pallas kernels, post_bwd(): pl.pallas_call(functools.partial(post_bwd_kernel, n_blocks=n_blocks, top_...  29.1 us
    ppermute x12, starting transfers between devices, chip(): return lax.ppermute(a, 'ep', chip_perm)  21.9 us
  transfers between devices with their start and end apart: 33, of which 6 were waited for; matrix products, arithmetic and copies ran while one was open for 4% of the time, Pallas kernels for 58%

profile of v6, /device:TPU:0, one launch (start us, length us, event | category | flops | bytes accessed | tf_op | source)
XLA Modules:
  0.0 348.8 jit_solution(16530928434015626329)
XLA Ops:
  0.7 2.2 slice_bitcast_fusion.2
  2.9 3.2 collective-permute-start.6
  10.2 8.8 %collective-permute-done.6.refs_0_.rest_6_ = bf16[4,256,256]{2,1,0:T(8,128)(2,1)} collective-permute-done((bf16[4,256,256]{2,1,0:T(8,128)(2,1)S(1)}, bf16[4,256,256]{2,1,0:T(8,128)(2,1)}, u32[]{:S(2)}, u32[]{:S(2)}) %collective-permute-start.6) | collective-permute-done | bytes 524320 | tf_op jit(solution)/shard_map/ppermute | solution.py:573
  19.5 5.0 %rank.1 = (s32[8,128]{1,0:T(8,128)}, s32[128,128]{1,0:T(8,128)}, s32[128,128]{1,0:T(8,128)}, s32[2,8,128]{2,1,0:T(8,128)}, s32[128,128]{1,0:T(8,128)}) custom-call(s32[4,4096]{1,0:T(4,128)} %bitcast.72, s32[4,4096]{1,0:T(4,128)} %bitcast.73, s32[4,4096]{1,0:T(4,128)} %bitcast.74, s32[4,4096]{1,0:T(4,128)} %bitcast.75), custom_call_target="tpu_custom_call" | custom-call | tf_op jit(solution)/shard_map/rank/pallas_call | solution.py:95
  24.4 5.8 %collective-permute-done.7.refs_1_.rest_7_ = bf16[4,256,256]{2,1,0:T(8,128)(2,1)} collective-permute-done((bf16[4,256,256]{2,1,0:T(8,128)(2,1)}, bf16[4,256,256]{2,1,0:T(8,128)(2,1)}, u32[]{:S(2)}, u32[]{:S(2)}) %collective-permute-start.7) | collective-permute-done | bytes 524320 | tf_op jit(solution)/shard_map/ppermute | solution.py:573
  30.2 10.4 %collective-permute-done.8.refs_2_.rest_8_ = bf16[4,256,256]{2,1,0:T(8,128)(2,1)} collective-permute-done((bf16[4,256,256]{2,1,0:T(8,128)(2,1)}, bf16[4,256,256]{2,1,0:T(8,128)(2,1)}, u32[]{:S(2)}, u32[]{:S(2)}) %collective-permute-start.8) | collective-permute-done | bytes 524320 | tf_op jit(solution)/shard_map/ppermute | solution.py:573
  41.1 31.6 %pre_bwd.1 = (bf16[4096,256]{1,0:T(8,128)(2,1)}, bf16[24576,256]{1,0:T(8,128)(2,1)}, bf16[24576,256]{1,0:T(8,128)(2,1)}) custom-call(s32[16384]{0:T(1024)} %bitcast.95, s32[8,128]{1,0:T(8,128)} %get-tuple-element.42.tab_ref, bf16[4,4096]{1,0:T(4,128)(2,1)} %bitcast.96, bf16[4096,256]{1,0:T(8,128)(2,1)} %bitcast.76, bf16[4096,256]{1,0:T(8,128)(2,1)} %bitcast.78, ...), custom_call_target="tpu_custom_call" | custom-call | flops 30000001024 | bytes 30000000 | tf_op jit(solution)/shard_map/pre_bwd/pallas_call | solution.py:232
  74.8 6.8 %exp_bwd.6 = (bf16[24576,256]{1,0:T(8,128)(2,1)}, f32[4,256,256]{2,1,0:T(8,128)}, f32[4,256,256]{2,1,0:T(8,128)}, f32[4,256,256]{2,1,0:T(8,128)}) custom-call(s32[1]{0:T(128)} %bitcast.31.first_ref, s32[8,128]{1,0:T(8,128)} %get-tuple-element.42.tab_ref, ...), custom_call_target="tpu_custom_call", output_to_operand_aliasing={{0}: (5, {})} | custom-call | flops 8000000000 | bytes 20000000 | tf_op jit(solution)/shard_map/exp_bwd/pallas_call | solution.py:379
  81.6 6.1 %collective-permute-done.refs_0_.rest_9_ = bf16[4,256,256]{2,1,0:T(8,128)(2,1)S(1)} collective-permute-done((bf16[4,256,256]{2,1,0:T(8,128)(2,1)}, bf16[4,256,256]{2,1,0:T(8,128)(2,1)S(1)}, u32[]{:S(2)}, u32[]{:S(2)}) %collective-permute-start) | collective-permute-done | bytes 524320 | tf_op jit(solution)/shard_map/ppermute | solution.py:573
  89.5 9.6 %collective-permute-done.1.refs_1_.rest_10_ = bf16[4,256,256]{2,1,0:T(8,128)(2,1)} collective-permute-done((bf16[4,256,256]{2,1,0:T(8,128)(2,1)}, bf16[4,256,256]{2,1,0:T(8,128)(2,1)}, u32[]{:S(2)}, u32[]{:S(2)}) %collective-permute-start.1) | collective-permute-done | bytes 524320 | tf_op jit(solution)/shard_map/ppermute | solution.py:573
  100.1 18.9 %exp_bwd.7 = (bf16[24576,256]{1,0:T(8,128)(2,1)}, f32[8,256,256]{2,1,0:T(8,128)}, f32[8,256,256]{2,1,0:T(8,128)}, f32[8,256,256]{2,1,0:T(8,128)}) custom-call(s32[1]{0:T(128)} %bitcast.30.first_ref, s32[8,128]{1,0:T(8,128)} %get-tuple-element.42.tab_ref, ...), custom_call_target="tpu_custom_call", output_to_operand_aliasing={{0}: (5, {})} | custom-call | flops 8000000000 | bytes 20000000 | tf_op jit(solution)/shard_map/exp_bwd/pallas_call | solution.py:379
  121.1 10.7 %exp_bwd.8 = (bf16[24576,256]{1,0:T(8,128)(2,1)}, f32[4,256,256]{2,1,0:T(8,128)}, f32[4,256,256]{2,1,0:T(8,128)}, f32[4,256,256]{2,1,0:T(8,128)}) custom-call(s32[1]{0:T(128)} %bitcast.26.first_ref, s32[8,128]{1,0:T(8,128)} %get-tuple-element.42.tab_ref, ...), custom_call_target="tpu_custom_call", output_to_operand_aliasing={{0}: (5, {})} | custom-call | flops 8000000000 | bytes 20000000 | tf_op jit(solution)/shard_map/exp_bwd/pallas_call | solution.py:379
  132.6 5.7 %exp_bwd.9 = (bf16[24576,256]{1,0:T(8,128)(2,1)}, f32[4,256,256]{2,1,0:T(8,128)}, f32[4,256,256]{2,1,0:T(8,128)}, f32[4,256,256]{2,1,0:T(8,128)}) custom-call(s32[1]{0:T(128)} %bitcast.25.first_ref, s32[8,128]{1,0:T(8,128)} %get-tuple-element.42.tab_ref, ...), custom_call_target="tpu_custom_call", output_to_operand_aliasing={{0}: (5, {})} | custom-call | flops 8000000000 | bytes 20000000 | tf_op jit(solution)/shard_map/exp_bwd/pallas_call | solution.py:379
  142.4 3.5 %collective-permute-start.27 = (f32[4,256,256]{2,1,0:T(8,128)}, f32[4,256,256]{2,1,0:T(8,128)}, u32[]{:S(2)}, u32[]{:S(2)}) collective-permute-start(f32[4,256,256]{2,1,0:T(8,128)} %get-tuple-element.69), channel_id=1, source_target_pairs={{0,2},{1,3},{2,0},{3,1},{4,6},{5,7},{6,4},{7,5},{8,10},{9,11},{10,... | collective-permute-start | bytes 3145736 | tf_op jit(solution)/shard_map/ppermute | solution.py:573
  146.0 14.6 %exp_bwd.10 = (bf16[24576,256]{1,0:T(8,128)(2,1)}, f32[8,256,256]{2,1,0:T(8,128)}, f32[8,256,256]{2,1,0:T(8,128)}, f32[8,256,256]{2,1,0:T(8,128)}) custom-call(s32[1]{0:T(128)} %bitcast.21.first_ref, s32[8,128]{1,0:T(8,128)} %get-tuple-element.42.tab_ref, bf16[8,256,256]{2,1,0:T(8,128)(2,1)} %bitcast.60, ...), custom_call_target="tpu_custom_call", output_to_operand_aliasing={{0}: (5, {})} | custom-call | flops 8000000000 | bytes 20000000 | tf_op jit(solution)/shard_map/exp_bwd/pallas_call | solution.py:379
  160.6 5.2 %collective-permute-start.31 = (f32[4,256,256]{2,1,0:T(8,128)}, f32[4,256,256]{2,1,0:T(8,128)}, u32[]{:S(2)}, u32[]{:S(2)}) collective-permute-start(f32[4,256,256]{2,1,0:T(8,128)} %get-tuple-element.75), channel_id=1, source_target_pairs={{0,2},{1,3},{2,0},{3,1},{4,6},{5,7},{6,4},{7,5},{8,10},{9,11},{10,... | collective-permute-start | bytes 3145736 | tf_op jit(solution)/shard_map/ppermute | solution.py:573
  165.8 8.9 %exp_bwd.11 = (bf16[24576,256]{1,0:T(8,128)(2,1)}, f32[4,256,256]{2,1,0:T(8,128)}, f32[4,256,256]{2,1,0:T(8,128)}, f32[4,256,256]{2,1,0:T(8,128)}) custom-call(s32[1]{0:T(128)} %bitcast.17.first_ref, s32[8,128]{1,0:T(8,128)} %get-tuple-element.42.tab_ref, bf16[4,256,256]{2,1,0:T(8,128)(2,1)} %copy-done.9, ...), custom_call_target="tpu_custom_call", output_to_operand_aliasing={{0}: (5, {})} | custom-call | flops 8000000000 | bytes 20000000 | tf_op jit(solution)/shard_map/exp_bwd/pallas_call | solution.py:379
  174.8 29.1 %post_bwd.1 = bf16[4096,256]{1,0:T(8,128)(2,1)} custom-call(s32[16384]{0:T(1024)} %bitcast.94, s32[8,128]{1,0:T(8,128)} %get-tuple-element.42.tab_ref, bf16[4096,256]{1,0:T(8,128)(2,1)} %bitcast.77, bf16[4096,256]{1,0:T(8,128)(2,1)} %bitcast.79, bf16[4096,256]{1,0:T(8,128)(2,1)} %get-tuple-element.44.h_ref, bf16[256,256]{1,0:T(8,128)(2,1)} %bitcast.83, ...), custom_call_target="tpu_custom_call" | custom-call | flops 30000001024 | bytes 30000000 | tf_op jit(solution)/shard_map/post_bwd/pallas_call | solution.py:446
  203.9 2.6 collective-permute-start.28
  206.5 42.9 %fwd.2 = bf16[2560,256]{1,0:T(8,128)(2,1)} custom-call(s32[6]{0:T(128)} %stack.2.firsts_ref, s32[8,128]{1,0:T(8,128)} %get-tuple-element.89.tab_ref, s32[16384]{0:T(1024)} %bitcast.90, s32[16384]{0:T(1024)} %bitcast.91, bf16[4,4096]{1,0:T(4,128)(2,1)} %bitcast.97, bf16[4096,256]{1,0:T(8,128)(2,1)} %bitcast.80, bf16[256,256]{1,0:T(8,128)(2,1)} %bitcast.84, ...), custom_call_target="tpu_custom_call" | custom-call | flops 80000000000 | bytes 30000000 | tf_op jit(solution)/shard_map/fwd/pallas_call | solution.py:536
  253.1 28.7 %fwd.3 = bf16[1536,256]{1,0:T(8,128)(2,1)} custom-call(s32[6]{0:T(128)} %stack.2.firsts_ref, s32[8,128]{1,0:T(8,128)} %get-tuple-element.90.tab_ref, s32[16384]{0:T(1024)} %bitcast.92, s32[16384]{0:T(1024)} %bitcast.93, bf16[4,4096]{1,0:T(4,128)(2,1)} %bitcast.98, bf16[4096,256]{1,0:T(8,128)(2,1)} %bitcast.81, bf16[256,256]{1,0:T(8,128)(2,1)} %bitcast.85, ...), custom_call_target="tpu_custom_call" | custom-call | flops 80000000000 | bytes 30000000 | tf_op jit(solution)/shard_map/fwd/pallas_call | solution.py:536
  284.0 2.7 collective-permute-start.25
  295.5 48.8 %collective-permute-done.25 = bf16[1536,256]{1,0:T(8,128)(2,1)S(1)} collective-permute-done((bf16[1536,256]{1,0:T(8,128)(2,1)S(1)}, bf16[1536,256]{1,0:T(8,128)(2,1)S(1)}, u32[]{:S(2)}, u32[]{:S(2)}) %collective-permute-start.25) | collective-permute-done | bytes 786464 | tf_op jit(solution)/shard_map/ppermute | solution.py:638
  345.8 3.0 copy.32
  (92 shorter events, 33.0 us)
Async XLA Ops:
  7.1 23.1 %collective-permute-start.7 = (bf16[4,256,256]{2,1,0:T(8,128)(2,1)}, bf16[4,256,256]{2,1,0:T(8,128)(2,1)}, u32[]{:S(2)}, u32[]{:S(2)}) collective-permute-start(bf16[4,256,256]{2,1,0:T(8,128)(2,1)} %get-tuple-element.85), channel_id=1, source_target_pairs={{0,2},{1,3},{2,0},{3,1},{4,6},{5,7},{6,4},{7,5},{8,10},{9,11},{10,... | collective-permute-start | bytes 1572872 | tf_op jit(solution)/shard_map/ppermute | solution.py:573
  8.1 32.4 %collective-permute-start.8 = (bf16[4,256,256]{2,1,0:T(8,128)(2,1)}, bf16[4,256,256]{2,1,0:T(8,128)(2,1)}, u32[]{:S(2)}, u32[]{:S(2)}) collective-permute-start(bf16[4,256,256]{2,1,0:T(8,128)(2,1)} %get-tuple-element.83), channel_id=1, source_target_pairs={{0,2},{1,3},{2,0},{3,1},{4,6},{5,7},{6,4},{7,5},{8,10},{9,11},{10,... | collective-permute-start | bytes 1572872 | tf_op jit(solution)/shard_map/ppermute | solution.py:573
  18.9 21.6 %collective-permute-start.12 = (bf16[4,256,256]{2,1,0:T(8,128)(2,1)}, bf16[4,256,256]{2,1,0:T(8,128)(2,1)}, u32[]{:S(2)}, u32[]{:S(2)}) collective-permute-start(bf16[4,256,256]{2,1,0:T(8,128)(2,1)} %collective-permute-done.6.refs_0_.rest_6_), channel_id=1, source_target_pairs={{0,1},{1,0},{2,3},{3,2},{4,5},{5,4},{6,7},{7,6},{8,9},{9,8},{10,11... | collective-permute-start | bytes 1572872 | tf_op jit(solution)/shard_map/ppermute | solution.py:570
  18.9 80.2 %collective-permute-start.9 = (bf16[8,256,256]{2,1,0:T(8,128)(2,1)S(1)}, bf16[8,256,256]{2,1,0:T(8,128)(2,1)}, u32[]{:S(2)}, u32[]{:S(2)}) collective-permute-start(bf16[8,256,256]{2,1,0:T(8,128)(2,1)S(1)} %bitcast.63), channel_id=1, source_target_pairs={{0,1},{1,0},{2,3},{3,2},{4,5},{5,4},{6,7},{7,6},{8,9},{9,8},{10,11... | collective-permute-start | bytes 3145736 | tf_op jit(solution)/shard_map/ppermute | solution.py:570
  19.4 80.2 %collective-permute-start.10 = (bf16[8,256,256]{2,1,0:T(8,128)(2,1)S(1)}, bf16[8,256,256]{2,1,0:T(8,128)(2,1)}, u32[]{:S(2)}, u32[]{:S(2)}) collective-permute-start(bf16[8,256,256]{2,1,0:T(8,128)(2,1)S(1)} %bitcast.67), channel_id=1, source_target_pairs={{0,1},{1,0},{2,3},{3,2},{4,5},{5,4},{6,7},{7,6},{8,9},{9,8},{10,11... | collective-permute-start | bytes 3145736 | tf_op jit(solution)/shard_map/ppermute | solution.py:570
  30.2 69.5 %collective-permute-start.11 = (bf16[8,256,256]{2,1,0:T(8,128)(2,1)S(1)}, bf16[8,256,256]{2,1,0:T(8,128)(2,1)}, u32[]{:S(2)}, u32[]{:S(2)}) collective-permute-start(bf16[8,256,256]{2,1,0:T(8,128)(2,1)S(1)} %bitcast.71), channel_id=1, source_target_pairs={{0,1},{1,0},{2,3},{3,2},{4,5},{5,4},{6,7},{7,6},{8,9},{9,8},{10,11... | collective-permute-start | bytes 3145736 | tf_op jit(solution)/shard_map/ppermute | solution.py:570
  40.6 32.2 %collective-permute-start.13 = (bf16[4,256,256]{2,1,0:T(8,128)(2,1)}, bf16[4,256,256]{2,1,0:T(8,128)(2,1)}, u32[]{:S(2)}, u32[]{:S(2)}) collective-permute-start(bf16[4,256,256]{2,1,0:T(8,128)(2,1)} %collective-permute-done.7.refs_1_.rest_7_), channel_id=1, source_target_pairs={{0,1},{1,0},{2,3},{3,2},{4,5},{5,4},{6,7},{7,6},{8,9},{9,8},{10,11... | collective-permute-start | bytes 1572872 | tf_op jit(solution)/shard_map/ppermute | solution.py:570
  40.6 33.9 %collective-permute-start.14 = (bf16[4,256,256]{2,1,0:T(8,128)(2,1)}, bf16[4,256,256]{2,1,0:T(8,128)(2,1)}, u32[]{:S(2)}, u32[]{:S(2)}) collective-permute-start(bf16[4,256,256]{2,1,0:T(8,128)(2,1)} %collective-permute-done.8.refs_2_.rest_8_), channel_id=1, source_target_pairs={{0,1},{1,0},{2,3},{3,2},{4,5},{5,4},{6,7},{7,6},{8,9},{9,8},{10,11... | collective-permute-start | bytes 1572872 | tf_op jit(solution)/shard_map/ppermute | solution.py:570
  74.5 24.6 %collective-permute-start.1 = (bf16[4,256,256]{2,1,0:T(8,128)(2,1)}, bf16[4,256,256]{2,1,0:T(8,128)(2,1)}, u32[]{:S(2)}, u32[]{:S(2)}) collective-permute-start(bf16[4,256,256]{2,1,0:T(8,128)(2,1)} %get-tuple-element.86), channel_id=1, source_target_pairs={{0,2},{1,3},{2,0},{3,1},{4,6},{5,7},{6,4},{7,5},{8,10},{9,11},{10,... | collective-permute-start | bytes 1572872 | tf_op jit(solution)/shard_map/ppermute | solution.py:573
  87.8 31.3 %collective-permute-start.2 = (bf16[4,256,256]{2,1,0:T(8,128)(2,1)}, bf16[4,256,256]{2,1,0:T(8,128)(2,1)}, u32[]{:S(2)}, u32[]{:S(2)}) collective-permute-start(bf16[4,256,256]{2,1,0:T(8,128)(2,1)} %get-tuple-element.84), channel_id=1, source_target_pairs={{0,2},{1,3},{2,0},{3,1},{4,6},{5,7},{6,4},{7,5},{8,10},{9,11},{10,... | collective-permute-start | bytes 1572872 | tf_op jit(solution)/shard_map/ppermute | solution.py:573
  119.1 23.3 %collective-permute-start.19 = (f32[8,256,256]{2,1,0:T(8,128)}, f32[8,256,256]{2,1,0:T(8,128)}, u32[]{:S(2)}, u32[]{:S(2)}) collective-permute-start(f32[8,256,256]{2,1,0:T(8,128)} %get-tuple-element.55), channel_id=1, source_target_pairs={{0,1},{1,0},{2,3},{3,2},{4,5},{5,4},{6,7},{7,6},{8,9},{9,8},{10,11... | collective-permute-start | bytes 6291464 | tf_op jit(solution)/shard_map/ppermute | solution.py:570
  119.6 26.4 %collective-permute-start.20 = (f32[8,256,256]{2,1,0:T(8,128)}, f32[8,256,256]{2,1,0:T(8,128)}, u32[]{:S(2)}, u32[]{:S(2)}) collective-permute-start(f32[8,256,256]{2,1,0:T(8,128)} %get-tuple-element.56), channel_id=1, source_target_pairs={{0,1},{1,0},{2,3},{3,2},{4,5},{5,4},{6,7},{7,6},{8,9},{9,8},{10,11... | collective-permute-start | bytes 6291464 | tf_op jit(solution)/shard_map/ppermute | solution.py:570
  138.3 22.2 %collective-permute-start.21 = (f32[4,256,256]{2,1,0:T(8,128)}, f32[4,256,256]{2,1,0:T(8,128)S(1)}, u32[]{:S(2)}, u32[]{:S(2)}) collective-permute-start(f32[4,256,256]{2,1,0:T(8,128)} %get-tuple-element.58), channel_id=1, source_target_pairs={{0,1},{1,0},{2,3},{3,2},{4,5},{5,4},{6,7},{7,6},{8,9},{9,8},{10,11... | collective-permute-start | bytes 3145736 | tf_op jit(solution)/shard_map/ppermute | solution.py:570
  140.5 25.4 %collective-permute-start.22 = (f32[4,256,256]{2,1,0:T(8,128)}, f32[4,256,256]{2,1,0:T(8,128)}, u32[]{:S(2)}, u32[]{:S(2)}) collective-permute-start(f32[4,256,256]{2,1,0:T(8,128)} %get-tuple-element.59), channel_id=1, source_target_pairs={{0,1},{1,0},{2,3},{3,2},{4,5},{5,4},{6,7},{7,6},{8,9},{9,8},{10,11... | collective-permute-start | bytes 3145736 | tf_op jit(solution)/shard_map/ppermute | solution.py:570
  140.5 25.3 %collective-permute-start.23 = (f32[4,256,256]{2,1,0:T(8,128)}, f32[4,256,256]{2,1,0:T(8,128)}, u32[]{:S(2)}, u32[]{:S(2)}) collective-permute-start(f32[4,256,256]{2,1,0:T(8,128)} %get-tuple-element.60), channel_id=1, source_target_pairs={{0,1},{1,0},{2,3},{3,2},{4,5},{5,4},{6,7},{7,6},{8,9},{9,8},{10,11... | collective-permute-start | bytes 3145736 | tf_op jit(solution)/shard_map/ppermute | solution.py:570
  142.4 107.0 %collective-permute-start.27 = (f32[4,256,256]{2,1,0:T(8,128)}, f32[4,256,256]{2,1,0:T(8,128)}, u32[]{:S(2)}, u32[]{:S(2)}) collective-permute-start(f32[4,256,256]{2,1,0:T(8,128)} %get-tuple-element.69), channel_id=1, source_target_pairs={{0,2},{1,3},{2,0},{3,1},{4,6},{5,7},{6,4},{7,5},{8,10},{9,11},{10,... | collective-permute-start | bytes 3145736 | tf_op jit(solution)/shard_map/ppermute | solution.py:573
  145.9 105.0 %collective-permute-start.29 = (f32[4,256,256]{2,1,0:T(8,128)}, f32[4,256,256]{2,1,0:T(8,128)}, u32[]{:S(2)}, u32[]{:S(2)}) collective-permute-start(f32[4,256,256]{2,1,0:T(8,128)} %get-tuple-element.72), channel_id=1, source_target_pairs={{0,2},{1,3},{2,0},{3,1},{4,6},{5,7},{6,4},{7,5},{8,10},{9,11},{10,... | collective-permute-start | bytes 3145736 | tf_op jit(solution)/shard_map/ppermute | solution.py:573
  160.6 131.0 %collective-permute-start.31 = (f32[4,256,256]{2,1,0:T(8,128)}, f32[4,256,256]{2,1,0:T(8,128)}, u32[]{:S(2)}, u32[]{:S(2)}) collective-permute-start(f32[4,256,256]{2,1,0:T(8,128)} %get-tuple-element.75), channel_id=1, source_target_pairs={{0,2},{1,3},{2,0},{3,1},{4,6},{5,7},{6,4},{7,5},{8,10},{9,11},{10,... | collective-permute-start | bytes 3145736 | tf_op jit(solution)/shard_map/ppermute | solution.py:573
  203.9 77.9 %collective-permute-start.28 = (f32[4,256,256]{2,1,0:T(8,128)}, f32[4,256,256]{2,1,0:T(8,128)}, u32[]{:S(2)}, u32[]{:S(2)}) collective-permute-start(f32[4,256,256]{2,1,0:T(8,128)} %get-tuple-element.70), channel_id=1, source_target_pairs={{0,2},{1,3},{2,0},{3,1},{4,6},{5,7},{6,4},{7,5},{8,10},{9,11},{10,... | collective-permute-start | bytes 3145736 | tf_op jit(solution)/shard_map/ppermute | solution.py:573
  206.5 77.5 %collective-permute-start.30 = (f32[4,256,256]{2,1,0:T(8,128)}, f32[4,256,256]{2,1,0:T(8,128)}, u32[]{:S(2)}, u32[]{:S(2)}) collective-permute-start(f32[4,256,256]{2,1,0:T(8,128)} %get-tuple-element.73), channel_id=1, source_target_pairs={{0,2},{1,3},{2,0},{3,1},{4,6},{5,7},{6,4},{7,5},{8,10},{9,11},{10,... | collective-permute-start | bytes 3145736 | tf_op jit(solution)/shard_map/ppermute | solution.py:573
  249.5 42.1 %collective-permute-start.32 = (f32[4,256,256]{2,1,0:T(8,128)}, f32[4,256,256]{2,1,0:T(8,128)S(1)}, u32[]{:S(2)}, u32[]{:S(2)}) collective-permute-start(f32[4,256,256]{2,1,0:T(8,128)} %get-tuple-element.76), channel_id=1, source_target_pairs={{0,2},{1,3},{2,0},{3,1},{4,6},{5,7},{6,4},{7,5},{8,10},{9,11},{10,... | collective-permute-start | bytes 3145736 | tf_op jit(solution)/shard_map/ppermute | solution.py:573
  250.9 94.9 %collective-permute-start.26 = (bf16[1,4096,256]{2,1,0:T(8,128)(2,1)}, bf16[1,4096,256]{2,1,0:T(8,128)(2,1)}, u32[]{:S(2)}, u32[]{:S(2)}) collective-permute-start(bf16[1,4096,256]{2,1,0:T(8,128)(2,1)} %bitcast.39), channel_id=1, source_target_pairs={{0,12},{4,0},{8,4},{12,8},{1,13},{5,1},{9,5},{13,9},{2,14},{6,2},{... | collective-permute-start | bytes 6291464 | tf_op jit(solution)/shard_map/ppermute | solution.py:627
  281.8 62.5 %collective-permute-start.24 = (bf16[2560,256]{1,0:T(8,128)(2,1)}, bf16[2560,256]{1,0:T(8,128)(2,1)S(1)}, u32[]{:S(2)}, u32[]{:S(2)}) collective-permute-start(bf16[2560,256]{1,0:T(8,128)(2,1)} %fwd.2), channel_id=1, source_target_pairs={{0,4},{4,8},{8,12},{12,0},{1,5},{5,9},{9,13},{13,1},{2,6},{6,10},{... | collective-permute-start | bytes 3932168 | tf_op jit(solution)/shard_map/ppermute | solution.py:638
  284.0 60.3 %collective-permute-start.25 = (bf16[1536,256]{1,0:T(8,128)(2,1)S(1)}, bf16[1536,256]{1,0:T(8,128)(2,1)S(1)}, u32[]{:S(2)}, u32[]{:S(2)}) collective-permute-start(bf16[1536,256]{1,0:T(8,128)(2,1)S(1)} %copy-done.11), channel_id=1, source_target_pairs={{0,4},{4,8},{8,12},{12,0},{1,5},{5,9},{9,13},{13,1},{2,6},{6,10},{... | collective-permute-start | bytes 2359304 | tf_op jit(solution)/shard_map/ppermute | solution.py:638
  (22 other events, 276.3 us)

commit v7 on v6

--- a/solution.py
+++ b/solution.py
@@ -127,7 +127,7 @@
 
 
 def gather_rows(buf, acc, pos_ref, top_k):
-    unroll = 16
+    unroll = 32
 
     def body(j, c):
         base = table_at(j, unroll, top_k)
@@ -141,7 +141,7 @@
 
 
 def scatter_rows(src, buf, pos_ref, top_k, n, shared):
-    unroll = 16
+    unroll = 32
 
     def body(j, c):
         base = table_at(j, unroll, top_k)
@@ -252,10 +252,12 @@
     )(pos, tab, gates, x, g, w1, w2)
 
 
-def exp_bwd_kernel(first_ref, tab_ref, *refs, n_loc, has_init):
-    w_hbm, (xs_hbm, qs_hbm), refs = refs[:3], refs[3:5], refs[5:]
-    init_hbm, refs = (refs[:3], refs[3:]) if has_init else ((), refs)
-    rs_hbm, *dw_hbm, wb, dwb, xb, qb, rb, mid, sems, wsems, dsems, isems = refs
+def exp_bwd_kernel(first_ref, tab_ref, xs_hbm, qs_hbm, *refs, n_parts, has_init):
+    w_hbm, refs = refs[:n_parts], refs[n_parts:]
+    init_hbm, refs = (refs[:1], refs[1:]) if has_init else ((), refs)
+    per = w_hbm[0].shape[0]
+    n_loc = n_parts * per
+    rs_hbm, dw_hbm, wb, dwb, xb, qb, rb, mid, sems, wsems, dsems, isems = refs
     first = first_ref[0]
     begin = tab_ref[0, first]
     end = tab_ref[0, first + n_loc]
@@ -274,19 +276,19 @@
         slot = lax.rem(t, DEPTH)
         return pltpu.make_async_copy(rb.at[slot], rs_hbm.at[rows_of(t)], sems.at[2, slot])
 
-    def w_loads(e):
-        copies = [pltpu.make_async_copy(w_hbm[i].at[e], wb.at[i, e], wsems.at[i, e]) for i in range(3)]
-        return copies + [pltpu.make_async_copy(ref.at[e], dwb.at[i, e], isems.at[i, e]) for i, ref in enumerate(init_hbm)]
-
-    def dw_saves(e):
-        return [pltpu.make_async_copy(dwb.at[i, e], dw_hbm[i].at[e], dsems.at[i, e]) for i in range(3)]
+    def w_loads(e, part=0, at=0):
+        copies = [pltpu.make_async_copy(w_hbm[part].at[at], wb.at[e], wsems.at[e])]
+        return copies + [pltpu.make_async_copy(ref.at[e], dwb.at[e], isems.at[e]) for ref in init_hbm]
+
+    def dw_save(e):
+        return pltpu.make_async_copy(dwb.at[e], dw_hbm.at[e], dsems.at[e])
 
     def first_half(t, e):
         slot = lax.rem(t, DEPTH)
         x = xb[slot]
-        pre = dot(x, wb[0, e])
-        up = dot(x, wb[1, e])
-        da = dot_nt(qb[slot], wb[2, e]).astype(BF16).astype(F32)
+        pre = dot(x, wb[e, 0])
+        up = dot(x, wb[e, 1])
+        da = dot_nt(qb[slot], wb[e, 2]).astype(BF16).astype(F32)
         sig = jax.nn.sigmoid(pre)
         sil = pre * sig
         return (
@@ -305,12 +307,11 @@
         for cp in loads(begin + ahead):
             cp.start()
     for e in range(1, n_loc):
-        for cp in w_loads(e):
+        for cp in w_loads(e, e // per, e % per):
             cp.start()
     if not has_init:
         def clear(e, c):
-            for i in range(3):
-                dwb[i, e] = jnp.zeros(dwb.shape[2:], F32)
+            dwb[e] = jnp.zeros(dwb.shape[1:], F32)
             return c
 
         lax.fori_loop(0, n_loc, clear, 0)
@@ -347,19 +348,18 @@
 
         act, dpre, dup = mid[lax.rem(t, 2), 0], mid[lax.rem(t, 2), 1], mid[lax.rem(t, 2), 2]
         x = xb[slot]
-        rows = (dot_nt(dpre, wb[0, e]) + dot_nt(dup, wb[1, e])).astype(BF16)
+        rows = (dot_nt(dpre, wb[e, 0]) + dot_nt(dup, wb[e, 1])).astype(BF16)
         upcoming = first_half(jnp.minimum(t + 1, end - 1), then)
         grads = (dot_tn(x, dpre), dot_tn(x, dup), dot_tn(act, qb[slot]))
         rb[slot] = rows
         for i, grad in enumerate(grads):
-            dwb[i, e] += grad
+            dwb[e, i] += grad
         keep(t + 1, upcoming)
         save(t).start()
 
         @pl.when(changes)
         def _():
-            for cp in dw_saves(e):
-                cp.start()
+            dw_save(e).start()
 
         return then
 
@@ -367,37 +367,36 @@
     for back in range(DEPTH, 0, -1):
         save(end - back).wait()
     for e in range(n_loc):
-        for cp in dw_saves(e):
-            cp.wait()
-
-
-def exp_bwd(first, tab, wg, wu, wd, xs, qs, init=()):
-    n_loc, hid, ff = wg.shape
+        dw_save(e).wait()
+
+
+def exp_bwd(first, tab, weights, xs, qs, init=()):
+    per, _, hid, ff = weights[0].shape
+    n_loc = per * len(weights)
     smem = pl.BlockSpec(memory_space=pltpu.SMEM)
     hbm = pl.BlockSpec(memory_space=pl.ANY)
-    dw = jax.ShapeDtypeStruct((n_loc, hid, ff), F32)
     return pl.pallas_call(
-        functools.partial(exp_bwd_kernel, n_loc=n_loc, has_init=bool(init)),
-        in_specs=[smem, smem] + [hbm] * (5 + len(init)),
-        out_specs=[hbm, hbm, hbm, hbm],
-        out_shape=(jax.ShapeDtypeStruct(xs.shape, BF16), dw, dw, dw),
-        input_output_aliases={5: 0},
+        functools.partial(exp_bwd_kernel, n_parts=len(weights), has_init=bool(init)),
+        in_specs=[smem, smem] + [hbm] * (2 + len(weights) + len(init)),
+        out_specs=[hbm, hbm],
+        out_shape=(jax.ShapeDtypeStruct(xs.shape, BF16), jax.ShapeDtypeStruct((n_loc, 3, hid, ff), F32)),
+        input_output_aliases={2: 0},
         scratch_shapes=[
-            pltpu.VMEM((3, n_loc, hid, ff), BF16),
-            pltpu.VMEM((3, n_loc, hid, ff), F32),
+            pltpu.VMEM((n_loc, 3, hid, ff), BF16),
+            pltpu.VMEM((n_loc, 3, hid, ff), F32),
             pltpu.VMEM((DEPTH, TM, hid), BF16),
             pltpu.VMEM((DEPTH, TM, hid), BF16),
             pltpu.VMEM((DEPTH, TM, hid), BF16),
             pltpu.VMEM((2, 3, TM, ff), BF16),
             pltpu.SemaphoreType.DMA((3, DEPTH)),
-            pltpu.SemaphoreType.DMA((3, n_loc)),
-            pltpu.SemaphoreType.DMA((3, n_loc)),
-            pltpu.SemaphoreType.DMA((3, n_loc)),
+            pltpu.SemaphoreType.DMA((n_loc,)),
+            pltpu.SemaphoreType.DMA((n_loc,)),
+            pltpu.SemaphoreType.DMA((n_loc,)),
         ],
         compiler_params=pltpu.CompilerParams(vmem_limit_bytes=VMEM_LIMIT),
         cost_estimate=pl.CostEstimate(flops=8_000_000_000, bytes_accessed=20_000_000, transcendentals=0),
         name="exp_bwd",
-    )(first, tab, wg, wu, wd, xs, qs, *init)
+    )(first, tab, xs, qs, *weights, *init)
 
 
 def post_bwd_kernel(pos_ref, tab_ref, x_ref, g_ref, h_ref, w1_ref, w2_ref, rs_hbm, dx_ref, rbuf, acc, st, sems, *, n_blocks, top_k, n_exp, rows):
@@ -462,17 +461,17 @@
 
 
 def fwd_kernel(firsts_ref, tab_ref, pos_ref, pos_out_ref, gate_ref, x_ref, w1_ref, w2_ref, *rest, n_blocks, top_k, n_exp, n_groups, rows):
-    w_hbm = rest[: 3 * n_groups]
-    y_ref, buf, acc, hsc, wsc, mid, sems = rest[3 * n_groups :]
+    w_hbm = rest[:n_groups]
+    y_ref, buf, acc, hsc, wsc, mid, sems = rest[n_groups:]
     nsc = acc.at[0]
     step = pl.program_id(0)
 
     def w_copy(i):
-        return pltpu.make_async_copy(w_hbm[i], wsc.at[i % 3, pl.ds(firsts_ref[i // 3], w_hbm[i].shape[0])], sems.at[i])
+        return pltpu.make_async_copy(w_hbm[i], wsc.at[pl.ds(firsts_ref[i], w_hbm[i].shape[0])], sems.at[i])
 
     @pl.when(step == 0)
     def _():
-        for i in range(3 * n_groups):
+        for i in range(n_groups):
             w_copy(i).start()
         zero_tails(buf, tab_ref, n_exp, 2)
 
@@ -489,7 +488,7 @@
     @pl.when(step == n_blocks)
     def _():
         buf[2 * rows : 2 * rows + 8, :] = jnp.zeros((8, buf.shape[1]), F32)
-        for i in range(3 * n_groups):
+        for i in range(n_groups):
             w_copy(i).wait()
         end = tab_ref[0, n_exp]
 
@@ -497,8 +496,8 @@
             return get_rows(buf, pl.multiple_of(t * (2 * TM), 2 * TM), TM).astype(BF16)
 
         def first_half(x, e):
-            pre = dot(x, wsc[0, e])
-            up = dot(x, wsc[1, e])
+            pre = dot(x, wsc[e, 0])
+            up = dot(x, wsc[e, 1])
             return (pre * jax.nn.sigmoid(pre) * up).astype(BF16)
 
         mid[0] = first_half(rows_of(0), 0)
@@ -506,7 +505,7 @@
         def body(t, e):
             then = jnp.where((t + 1 >= tab_ref[0, e + 1]) & (t + 1 < end), e + 1, e)
             x = rows_of(jnp.minimum(t + 1, end - 1))
-            out = dot(mid[lax.rem(t, 2)], wsc[2, e]).astype(BF16).astype(F32)
+            out = dot(mid[lax.rem(t, 2)], wsc[e, 2]).astype(BF16).astype(F32)
             upcoming = first_half(x, then)
             put_rows(buf, pl.multiple_of(t * (2 * TM), 2 * TM), out)
             mid[lax.rem(t + 1, 2)] = upcoming
@@ -532,27 +531,26 @@
     n_groups = len(weights)
     smem = pl.BlockSpec(memory_space=pltpu.SMEM)
     whole = pl.BlockSpec((hid, hid), lambda i: (0, 0))
-    flat = [w for group in weights for w in group]
     return pl.pallas_call(
         functools.partial(fwd_kernel, n_blocks=n_blocks, top_k=top_k, n_exp=n_exp, n_groups=n_groups, rows=rows),
         grid=(2 * n_blocks + 1,),
         in_specs=[smem, smem, route_spec(top_k, n_blocks, 0, skip), route_spec(top_k, n_blocks, n_blocks + 1, skip), gate_spec(top_k, n_blocks, n_blocks + 1, skip)]
         + [pl.BlockSpec((BT, hid), lambda i: (skip + jnp.minimum(i, n_blocks - 1), 0)), whole, whole]
-        + [pl.BlockSpec(memory_space=pl.ANY)] * len(flat),
+        + [pl.BlockSpec(memory_space=pl.ANY)] * n_groups,
         out_specs=pl.BlockSpec((BT, hid), lambda i: (jnp.maximum(i - n_blocks - 1, 0), 0)),
         out_shape=jax.ShapeDtypeStruct((n_tok, hid), BF16),
         scratch_shapes=[
             pltpu.VMEM((2 * rows + 8, hid // 2), F32),
             pltpu.VMEM((top_k, 2 * BT, hid // 2), F32),
             pltpu.VMEM((n_tok, hid), BF16),
-            pltpu.VMEM((3, n_exp, hid, hid), BF16),
+            pltpu.VMEM((n_exp, 3, hid, hid), BF16),
             pltpu.VMEM((2, TM, hid), BF16),
-            pltpu.SemaphoreType.DMA((len(flat),)),
+            pltpu.SemaphoreType.DMA((n_groups,)),
         ],
         compiler_params=pltpu.CompilerParams(vmem_limit_bytes=VMEM_LIMIT),
         cost_estimate=pl.CostEstimate(flops=80_000_000_000, bytes_accessed=30_000_000, transcendentals=0),
         name="fwd",
-    )(firsts, tab, pos, pos, gates, x, w1, w2, *flat)
+    )(firsts, tab, pos, pos, gates, x, w1, w2, *weights)
 
 
 def solution(mesh):
@@ -583,18 +581,19 @@
         rows_f = [TM * (blocks * BT * top_k // TM + n_exp) for blocks in FWD_BLOCKS]
         me = lax.axis_index("ep")
 
-        own = (w_gate, w_up, w_down)
         half = n_loc // 2
-        far = [[chip(w[h * half : (h + 1) * half]) for w in own] for h in range(2)]
+        halves = [slice(0, half), slice(half, n_loc)]
+        own = [jnp.stack([w[at] for w in (w_gate, w_up, w_down)], axis=1) for at in halves]
+        far = [chip(w) for w in own]
         near = [mate(w) for w in own]
-        relay = [[mate(w) for w in far[h]] for h in range(2)]
+        relay = [mate(w) for w in far]
         groups = {
             "own": (me * n_loc, own),
             "near": ((me ^ 1) * n_loc, near),
-            "far0": ((me ^ 2) * n_loc, far[0]),
-            "far1": ((me ^ 2) * n_loc + half, far[1]),
-            "relay0": ((me ^ 3) * n_loc, relay[0]),
-            "relay1": ((me ^ 3) * n_loc + half, relay[1]),
+            "far0": ((me ^ 2) * n_loc, far[:1]),
+            "far1": ((me ^ 2) * n_loc + half, far[1:]),
+            "relay0": ((me ^ 3) * n_loc, relay[:1]),
+            "relay1": ((me ^ 3) * n_loc + half, relay[1:]),
         }
 
         tab_b, pos4_b, pos2_b, tab_f, pos2_f = route_ranks(ids_bwd, slots_bwd, ids_fwd, slots_fwd, n_exp, rows, rows_f)
@@ -605,39 +604,36 @@
 
         def experts(name, xs, init=()):
             first, weights = groups[name]
-            return exp_bwd(first.reshape(1), tab_b, *weights, xs, qs, init)
-
-        def to_mate(parts):
-            return [mate(v) for v in parts]
-
-        there = []
-        xs, *part = experts("relay0", xs)
-        far_sum = to_mate(part)
-        xs, *part = experts("near", xs)
-        near_sum = to_mate(part)
-        xs, *part = experts("far0", xs, far_sum)
-        there.append([chip(v) for v in part])
-        xs, *part = experts("relay1", xs)
-        far_sum = to_mate(part)
-        xs, *dw_own = experts("own", xs, near_sum)
-        xs, *part = experts("far1", xs, far_sum)
-        there.append([chip(v) for v in part])
+            return exp_bwd(first.reshape(1), tab_b, weights, xs, qs, init)
+
+        xs, part = experts("relay0", xs)
+        far_sum = mate(part)
+        xs, part = experts("near", xs)
+        near_sum = mate(part)
+        xs, part = experts("far0", xs, (far_sum,))
+        there = [chip(part)]
+        xs, part = experts("relay1", xs)
+        far_sum = mate(part)
+        xs, dw_own = experts("own", xs, (near_sum,))
+        xs, part = experts("far1", xs, (far_sum,))
+        there.append(chip(part))
         grad_x = post_bwd(pos2_b, tab_b, x_saved, grad_in, h_bwd, w1, w2, xs, n_exp, top_k)
         x_fwd, grad_x = lax.optimization_barrier((x_fwd, grad_x))
         dx_prev = lax.ppermute(grad_x[None], "pp", prev_perm)
 
-        halves = []
-        firsts = jnp.stack([first for first, _ in groups.values()])
-        weights = [w for _, w in groups.values()]
+        parts = []
+        firsts = jnp.stack([first + i * half for first, ws in groups.values() for i in range(len(ws))])
+        weights = [w for _, ws in groups.values() for w in ws]
         skip = 0
         for h, blocks in enumerate(FWD_BLOCKS):
             y_half = fwd(blocks, skip, firsts, tab_f[h], pos2_f, gates_f, x_fwd, w1, w2, weights, rows_f[h], n_exp, top_k)
             skip += blocks
             if h + 1 < len(FWD_BLOCKS):
                 x_fwd, y_half = lax.optimization_barrier((x_fwd, y_half))
-            halves.append(lax.ppermute(y_half, "pp", next_perm))
-        y_next = jnp.concatenate(halves, axis=0)[None]
-        dws = [jnp.concatenate([a[:half] + b, a[half:] + c], axis=0)[None] for a, b, c in zip(dw_own, *there)]
+            parts.append(lax.ppermute(y_half, "pp", next_perm))
+        y_next = jnp.concatenate(parts, axis=0)[None]
+        dws = [jnp.concatenate([dw_own[at, i] + sums[:, i] for at, sums in zip(halves, there)], axis=0)[None] for i in range(3)]
+        dx_prev = jnp.where(me >= 0, dx_prev, jnp.zeros_like(dx_prev))
         return y_next, dx_prev, *dws
 
     in_specs = (tok_spec,) * 9 + (dense_spec, dense_spec, expert_spec, expert_spec, expert_spec)

time: 350 us -> 332 us (0.949)
  starting transfers between devices: 32.7 us -> 22.6 us
  Pallas kernels: 203 us -> 195 us
  local copies, waits for them, and re-layouts: 11.4 us -> 6.42 us
    ppermute x12 -> x4, waiting for transfers between devices: 40.7 us -> 29.6 us  [chip(): return lax.ppermute(a, 'ep', chip_perm)]
    ppermute x2, waiting for transfers between devices: 48.8 us -> 59.3 us  [slot(): parts.append(lax.ppermute(y_half, 'pp', next_perm))]
    ppermute x12 -> x4, starting transfers between devices: 21.9 us -> 13.8 us  [chip(): return lax.ppermute(a, 'ep', chip_perm)]
    slice x3 -> x0, local copies, waits for them, and re-layouts: 4.28 us -> none  [slot(): far = [[chip(w[h * half:(h + 1) * half]) for w in own] for h in range(2)]]
    unnamed x27 -> x16, local copies, waits for them, and re-layouts: 5.66 us -> 1.59 us
    pallas_call x6, Pallas kernels: 65.6 us -> 62 us  [exp_bwd(): pl.pallas_call(functools.partial(exp_bwd_kernel, n_parts=len(weights), ha...]
  transfers between devices with their start and end apart: 33 -> 14, of which waited for: 6 -> 3; matrix products, arithmetic and copies ran while one was open for 4% -> 3% of each run, Pallas kernels for 58% -> 59%
where the time goes in v7:
time: 332 us; the launch traced here: 330 us
  Pallas kernels  195 us (59%)
  waiting for transfers between devices  91 us (27%)
  starting transfers between devices  22.6 us (7%)
  other arithmetic  13.9 us (4%)
  local copies, waits for them, and re-layouts  6.42 us (2%)
    pallas_call x2, Pallas kernels, fwd(): pl.pallas_call(functools.partial(fwd_kernel, n_blocks=n_blocks, top_k=top...  69.4 us
    pallas_call x6, Pallas kernels, exp_bwd(): pl.pallas_call(functools.partial(exp_bwd_kernel, n_parts=len(weights), ha...  62 us
    ppermute x2, waiting for transfers between devices, slot(): parts.append(lax.ppermute(y_half, 'pp', next_perm))  59.3 us
    pallas_call x1, Pallas kernels, pre_bwd(): pl.pallas_call(functools.partial(pre_bwd_kernel, n_blocks=n_blocks, top_k...  30.8 us
    ppermute x4, waiting for transfers between devices, chip(): return lax.ppermute(a, 'ep', chip_perm)  29.6 us
    pallas_call x1, Pallas kernels, post_bwd(): pl.pallas_call(functools.partial(post_bwd_kernel, n_blocks=n_blocks, top_...  28.2 us
    ppermute x4, starting transfers between devices, chip(): return lax.ppermute(a, 'ep', chip_perm)  13.8 us
  transfers between devices with their start and end apart: 14, of which 3 were waited for; matrix products, arithmetic and copies ran while one was open for 3% of the time, Pallas kernels for 59%

profile of v7, /device:TPU:0, one launch (start us, length us, event | category | flops | bytes accessed | tf_op | source)
XLA Modules:
  0.0 330.1 jit_solution(4512863573473066092)
XLA Ops:
  2.9 3.2 collective-permute-start
  6.9 5.0 %rank.1 = (s32[8,128]{1,0:T(8,128)}, s32[128,128]{1,0:T(8,128)}, s32[128,128]{1,0:T(8,128)}, s32[2,8,128]{2,1,0:T(8,128)}, s32[128,128]{1,0:T(8,128)}) custom-call(s32[4,4096]{1,0:T(4,128)} %bitcast.83, s32[4,4096]{1,0:T(4,128)} %bitcast.84, s32[4,4096]{1,0:T(4,128)} %bitcast.85, s32[4,4096]{1,0:T(4,128)} %bitcast.86), custom_call_target="tpu_custom_call" | custom-call | tf_op jit(solution)/shard_map/rank/pallas_call | solution.py:95
  11.8 29.6 %collective-permute-done.refs_0_.rest_4_ = bf16[4,3,256,256]{3,2,1,0:T(8,128)(2,1)} collective-permute-done((bf16[4,3,256,256]{3,2,1,0:T(8,128)(2,1)S(1)}, bf16[4,3,256,256]{3,2,1,0:T(8,128)(2,1)}, u32[]{:S(2)}, u32[]{:S(2)}) %collective-permute-start) | collective-permute-done | bytes 1572896 | tf_op jit(solution)/shard_map/ppermute | solution.py:571
  41.5 30.8 %pre_bwd.1 = (bf16[4096,256]{1,0:T(8,128)(2,1)}, bf16[24576,256]{1,0:T(8,128)(2,1)}, bf16[24576,256]{1,0:T(8,128)(2,1)}) custom-call(s32[16384]{0:T(1024)} %bitcast.106, s32[8,128]{1,0:T(8,128)} %get-tuple-element.30.tab_ref, bf16[4,4096]{1,0:T(4,128)(2,1)} %bitcast.107, bf16[4096,256]{1,0:T(8,128)(2,1)} %bitcast.87, bf16[4096,256]{1,0:T(8,128)(2,1)} %bitcast.89, ...), custom_call_target="tpu_custom_call" | custom-call | flops 30000001024 | bytes 30000000 | tf_op jit(solution)/shard_map/pre_bwd/pallas_call | solution.py:232
  72.3 6.4 %exp_bwd.6 = (bf16[24576,256]{1,0:T(8,128)(2,1)}, f32[4,3,256,256]{3,2,1,0:T(8,128)}) custom-call(s32[1]{0:T(128)} %bitcast.22.first_ref, s32[8,128]{1,0:T(8,128)} %get-tuple-element.30.tab_ref, bf16[24576,256]{1,0:T(8,128)(2,1)} %get-tuple-element.33.xs_hbm, bf16[24576,256]{1,0:T(8,128)(2,1)} %get-tuple-element.34.qs_hbm, ...), custom_call_target="tpu_custom_call", output_to_operand_aliasing={{0}: (2, {})} | custom-call | flops 8000000000 | bytes 20000000 | tf_op jit(solution)/shard_map/exp_bwd/pallas_call | solution.py:378
  78.7 1.9 collective-permute-start.4
  80.5 18.1 %exp_bwd.7 = (bf16[24576,256]{1,0:T(8,128)(2,1)}, f32[8,3,256,256]{3,2,1,0:T(8,128)}) custom-call(s32[1]{0:T(128)} %bitcast.21.first_ref, s32[8,128]{1,0:T(8,128)} %get-tuple-element.30.tab_ref, bf16[24576,256]{1,0:T(8,128)(2,1)} %get-tuple-element.35.xs_hbm, bf16[24576,256]{1,0:T(8,128)(2,1)} %get-tuple-element.34.qs_hbm, ...), custom_call_target="tpu_custom_call", output_to_operand_aliasing={{0}: (2, {})} | custom-call | flops 8000000000 | bytes 20000000 | tf_op jit(solution)/shard_map/exp_bwd/pallas_call | solution.py:378
  99.2 10.0 %exp_bwd.8 = (bf16[24576,256]{1,0:T(8,128)(2,1)}, f32[4,3,256,256]{3,2,1,0:T(8,128)}) custom-call(s32[1]{0:T(128)} %bitcast.20.first_ref, s32[8,128]{1,0:T(8,128)} %get-tuple-element.30.tab_ref, bf16[24576,256]{1,0:T(8,128)(2,1)} %get-tuple-element.36.xs_hbm, bf16[24576,256]{1,0:T(8,128)(2,1)} %get-tuple-element.34.qs_hbm, ...), custom_call_target="tpu_custom_call", output_to_operand_aliasing={{0}: (2, {})} | custom-call | flops 8000000000 | bytes 20000000 | tf_op jit(solution)/shard_map/exp_bwd/pallas_call | solution.py:378
  109.2 2.1 collective-permute-done.6.refs_0_.rest_7_
  112.4 5.4 %exp_bwd.9 = (bf16[24576,256]{1,0:T(8,128)(2,1)}, f32[4,3,256,256]{3,2,1,0:T(8,128)}) custom-call(s32[1]{0:T(128)} %bitcast.19.first_ref, s32[8,128]{1,0:T(8,128)} %get-tuple-element.30.tab_ref, bf16[24576,256]{1,0:T(8,128)(2,1)} %get-tuple-element.38.xs_hbm, bf16[24576,256]{1,0:T(8,128)(2,1)} %get-tuple-element.34.qs_hbm, ...), custom_call_target="tpu_custom_call", output_to_operand_aliasing={{0}: (2, {})} | custom-call | flops 8000000000 | bytes 20000000 | tf_op jit(solution)/shard_map/exp_bwd/pallas_call | solution.py:378
  117.9 2.8 collective-permute-start.8
  121.9 2.0 copy.26
  123.9 6.4 %collective-permute-start.12 = (f32[4,3,256,256]{3,2,0,1:T(8,128)}, f32[4,3,256,256]{3,2,0,1:T(8,128)}, u32[]{:S(2)}, u32[]{:S(2)}) collective-permute-start(f32[4,3,256,256]{3,2,0,1:T(8,128)} %copy.26), channel_id=1, source_target_pairs={{0,2},{1,3},{2,0},{3,1},{4,6},{5,7},{6,4},{7,5},{8,10},{9,11},{10,... | collective-permute-start | bytes 9437192 | tf_op jit(solution)/shard_map/ppermute | solution.py:571
  130.4 13.8 %exp_bwd.10 = (bf16[24576,256]{1,0:T(8,128)(2,1)}, f32[8,3,256,256]{3,2,1,0:T(8,128)}) custom-call(s32[1]{0:T(128)} %bitcast.18.first_ref, s32[8,128]{1,0:T(8,128)} %get-tuple-element.30.tab_ref, bf16[24576,256]{1,0:T(8,128)(2,1)} %get-tuple-element.39.xs_hbm, bf16[24576,256]{1,0:T(8,128)(2,1)} %get-tuple-element.34.qs_hbm, ...), custom_call_target="tpu_custom_call", output_to_operand_aliasing={{0}: (2, {})} | custom-call | flops 8000000000 | bytes 20000000 | tf_op jit(solution)/shard_map/exp_bwd/pallas_call | solution.py:378
  144.2 8.3 %exp_bwd.11 = (bf16[24576,256]{1,0:T(8,128)(2,1)}, f32[4,3,256,256]{3,2,1,0:T(8,128)}) custom-call(s32[1]{0:T(128)} %bitcast.17.first_ref, s32[8,128]{1,0:T(8,128)} %get-tuple-element.30.tab_ref, bf16[24576,256]{1,0:T(8,128)(2,1)} %get-tuple-element.41.xs_hbm, bf16[24576,256]{1,0:T(8,128)(2,1)} %get-tuple-element.34.qs_hbm, ...), custom_call_target="tpu_custom_call", output_to_operand_aliasing={{0}: (2, {})} | custom-call | flops 8000000000 | bytes 20000000 | tf_op jit(solution)/shard_map/exp_bwd/pallas_call | solution.py:378
  152.5 28.2 %post_bwd.1 = bf16[4096,256]{1,0:T(8,128)(2,1)} custom-call(s32[16384]{0:T(1024)} %bitcast.105, s32[8,128]{1,0:T(8,128)} %get-tuple-element.30.tab_ref, bf16[4096,256]{1,0:T(8,128)(2,1)} %bitcast.88, bf16[4096,256]{1,0:T(8,128)(2,1)} %bitcast.90, bf16[4096,256]{1,0:T(8,128)(2,1)} %get-tuple-element.32.h_ref, bf16[256,256]{1,0:T(8,128)(2,1)} %bitcast.94, ...), custom_call_target="tpu_custom_call" | custom-call | flops 30000001024 | bytes 30000000 | tf_op jit(solution)/shard_map/post_bwd/pallas_call | solution.py:445
  180.7 41.7 %fwd.2 = bf16[2560,256]{1,0:T(8,128)(2,1)} custom-call(s32[8]{0:T(128)} %stack.49.firsts_ref, s32[8,128]{1,0:T(8,128)} %get-tuple-element.66.tab_ref, s32[16384]{0:T(1024)} %bitcast.101, s32[16384]{0:T(1024)} %bitcast.102, bf16[4,4096]{1,0:T(4,128)(2,1)} %bitcast.108, bf16[4096,256]{1,0:T(8,128)(2,1)} %bitcast.91, bf16[256,256]{1,0:T(8,128)(2,1)} %bitcast.95, ...), custom_call_target="tpu_custom_call" | custom-call | flops 80000000000 | bytes 30000000 | tf_op jit(solution)/shard_map/fwd/pallas_call | solution.py:534
  223.8 1.6 collective-permute-start.11
  225.3 4.0 %collective-permute-start.13 = (f32[4,3,256,256]{3,2,1,0:T(8,128)}, f32[4,3,256,256]{3,2,1,0:T(8,128)S(1)}, u32[]{:S(2)}, u32[]{:S(2)}) collective-permute-start(f32[4,3,256,256]{3,2,1,0:T(8,128)} %get-tuple-element.52), channel_id=1, source_target_pairs={{0,2},{1,3},{2,0},{3,1},{4,6},{5,7},{6,4},{7,5},{8,10},{9,11},{10,... | collective-permute-start | bytes 9437192 | tf_op jit(solution)/shard_map/ppermute | solution.py:571
  229.4 27.8 %fwd.3 = bf16[1536,256]{1,0:T(8,128)(2,1)} custom-call(s32[8]{0:T(128)} %stack.49.firsts_ref, s32[8,128]{1,0:T(8,128)} %get-tuple-element.67.tab_ref, s32[16384]{0:T(1024)} %bitcast.103, s32[16384]{0:T(1024)} %bitcast.104, bf16[4,4096]{1,0:T(4,128)(2,1)} %bitcast.109, bf16[4096,256]{1,0:T(8,128)(2,1)} %bitcast.92, bf16[256,256]{1,0:T(8,128)(2,1)} %bitcast.96, ...), custom_call_target="tpu_custom_call" | custom-call | flops 80000000000 | bytes 30000000 | tf_op jit(solution)/shard_map/fwd/pallas_call | solution.py:534
  257.2 59.3 %collective-permute-done.10 = bf16[1536,256]{1,0:T(8,128)(2,1)} collective-permute-done((bf16[1536,256]{1,0:T(8,128)(2,1)}, bf16[1536,256]{1,0:T(8,128)(2,1)}, u32[]{:S(2)}, u32[]{:S(2)}) %collective-permute-start.10) | collective-permute-done | bytes 786464 | tf_op jit(solution)/shard_map/ppermute | solution.py:633
  316.5 3.2 maximum_bitcast_fusion
  319.7 3.1 broadcast_select_fusion
  322.9 2.6 fusion.1
  (45 shorter events, 12.1 us)
Async XLA Ops:
  0.6 1.5 copy-start.4
  0.6 1.8 copy-start.5
  2.9 69.4 %copy-start = (bf16[4,3,256,256]{3,2,1,0:T(8,128)(2,1)}, bf16[4,3,256,256]{3,2,1,0:T(8,128)(2,1)S(1)}, u32[]{:S(2)}) copy-start(bf16[4,3,256,256]{3,2,1,0:T(8,128)(2,1)S(1)} %pad_maximum_fusion.refs_0_.rest_0_) | copy-start | bytes 4718596
  2.9 38.6 %collective-permute-start = (bf16[4,3,256,256]{3,2,1,0:T(8,128)(2,1)S(1)}, bf16[4,3,256,256]{3,2,1,0:T(8,128)(2,1)}, u32[]{:S(2)}, u32[]{:S(2)}) collective-permute-start(bf16[4,3,256,256]{3,2,1,0:T(8,128)(2,1)S(1)} %pad_maximum_fusion.refs_0_.rest_0_), channel_id=1, source_target_pairs={{0,2},{1,3},{2,0},{3,1},{4,6},{5,7},{6,4},{7,5},{8,10},{9,11},{10,... | collective-permute-start | bytes 4718600 | tf_op jit(solution)/shard_map/ppermute | solution.py:571
  6.1 74.4 %collective-permute-start.2 = (bf16[4,3,256,256]{3,2,1,0:T(8,128)(2,1)S(1)}, bf16[4,3,256,256]{3,2,1,0:T(8,128)(2,1)}, u32[]{:S(2)}, u32[]{:S(2)}) collective-permute-start(bf16[4,3,256,256]{3,2,1,0:T(8,128)(2,1)S(1)} %pad_maximum_fusion.refs_0_.rest_0_), channel_id=1, source_target_pairs={{0,1},{1,0},{2,3},{3,2},{4,5},{5,4},{6,7},{7,6},{8,9},{9,8},{10,11... | collective-permute-start | bytes 4718600 | tf_op jit(solution)/shard_map/ppermute | solution.py:568
  6.3 66.0 %copy-start.1 = (bf16[4,3,256,256]{3,2,1,0:T(8,128)(2,1)}, bf16[4,3,256,256]{3,2,1,0:T(8,128)(2,1)S(1)}, u32[]{:S(2)}) copy-start(bf16[4,3,256,256]{3,2,1,0:T(8,128)(2,1)S(1)} %pad_maximum_fusion.1.refs_1_.rest_1_) | copy-start | bytes 4718596
  6.3 92.4 %collective-permute-start.5 = (bf16[4,3,256,256]{3,2,1,0:T(8,128)(2,1)S(1)}, bf16[4,3,256,256]{3,2,1,0:T(8,128)(2,1)}, u32[]{:S(2)}, u32[]{:S(2)}) collective-permute-start(bf16[4,3,256,256]{3,2,1,0:T(8,128)(2,1)S(1)} %pad_maximum_fusion.1.refs_1_.rest_1_), channel_id=1, source_target_pairs={{0,2},{1,3},{2,0},{3,1},{4,6},{5,7},{6,4},{7,5},{8,10},{9,11},{10,... | collective-permute-start | bytes 4718600 | tf_op jit(solution)/shard_map/ppermute | solution.py:571
  6.4 74.1 %collective-permute-start.3 = (bf16[4,3,256,256]{3,2,1,0:T(8,128)(2,1)S(1)}, bf16[4,3,256,256]{3,2,1,0:T(8,128)(2,1)}, u32[]{:S(2)}, u32[]{:S(2)}) collective-permute-start(bf16[4,3,256,256]{3,2,1,0:T(8,128)(2,1)S(1)} %pad_maximum_fusion.1.refs_1_.rest_1_), channel_id=1, source_target_pairs={{0,1},{1,0},{2,3},{3,2},{4,5},{5,4},{6,7},{7,6},{8,9},{9,8},{10,11... | collective-permute-start | bytes 4718600 | tf_op jit(solution)/shard_map/ppermute | solution.py:568
  41.5 30.8 %collective-permute-start.1 = (bf16[4,3,256,256]{3,2,1,0:T(8,128)(2,1)}, bf16[4,3,256,256]{3,2,1,0:T(8,128)(2,1)}, u32[]{:S(2)}, u32[]{:S(2)}) collective-permute-start(bf16[4,3,256,256]{3,2,1,0:T(8,128)(2,1)} %collective-permute-done.refs_0_.rest_4_), channel_id=1, source_target_pairs={{0,1},{1,0},{2,3},{3,2},{4,5},{5,4},{6,7},{7,6},{8,9},{9,8},{10,11... | collective-permute-start | bytes 4718600 | tf_op jit(solution)/shard_map/ppermute | solution.py:568
  78.7 20.5 %collective-permute-start.4 = (f32[4,3,256,256]{3,2,1,0:T(8,128)}, f32[4,3,256,256]{3,2,1,0:T(8,128)}, u32[]{:S(2)}, u32[]{:S(2)}) collective-permute-start(f32[4,3,256,256]{3,2,1,0:T(8,128)} %get-tuple-element.37), channel_id=1, source_target_pairs={{0,1},{1,0},{2,3},{3,2},{4,5},{5,4},{6,7},{7,6},{8,9},{9,8},{10,11... | collective-permute-start | bytes 9437192 | tf_op jit(solution)/shard_map/ppermute | solution.py:568
  98.6 31.8 %collective-permute-start.7 = (f32[8,3,256,256]{3,2,1,0:T(8,128)}, f32[8,3,256,256]{3,2,1,0:T(8,128)}, u32[]{:S(2)}, u32[]{:S(2)}) collective-permute-start(f32[8,3,256,256]{3,2,1,0:T(8,128)} %get-tuple-element.40), channel_id=1, source_target_pairs={{0,1},{1,0},{2,3},{3,2},{4,5},{5,4},{6,7},{7,6},{8,9},{9,8},{10,11... | collective-permute-start | bytes 18874376 | tf_op jit(solution)/shard_map/ppermute | solution.py:568
  98.7 12.6 %collective-permute-start.6 = (bf16[4,3,256,256]{3,2,1,0:T(8,128)(2,1)}, bf16[4,3,256,256]{3,2,1,0:T(8,128)(2,1)S(1)}, u32[]{:S(2)}, u32[]{:S(2)}) collective-permute-start(bf16[4,3,256,256]{3,2,1,0:T(8,128)(2,1)} %collective-permute-done.5.refs_0_.rest_5_), channel_id=1, source_target_pairs={{0,1},{1,0},{2,3},{3,2},{4,5},{5,4},{6,7},{7,6},{8,9},{9,8},{10,11... | collective-permute-start | bytes 4718600 | tf_op jit(solution)/shard_map/ppermute | solution.py:568
  111.3 1.1 copy-start.7
  112.4 8.9 %copy-start.6 = (s32[2,8,128]{2,1,0:T(8,128)S(1)}, s32[2,8,128]{2,1,0:T(8,128)}, u32[]{:S(2)}) copy-start(s32[2,8,128]{2,1,0:T(8,128)} %get-tuple-element.45) | copy-start | bytes 24580
  112.4 9.5 %copy-start.3 = (f32[4,3,256,256]{3,2,1,0:T(8,128)S(1)}, f32[4,3,256,256]{3,2,1,0:T(8,128)}, u32[]{:S(2)}) copy-start(f32[4,3,256,256]{3,2,1,0:T(8,128)} %get-tuple-element.51) | copy-start | bytes 9437188
  117.9 26.3 %collective-permute-start.8 = (f32[4,3,256,256]{3,2,1,0:T(8,128)}, f32[4,3,256,256]{3,2,1,0:T(8,128)}, u32[]{:S(2)}, u32[]{:S(2)}) collective-permute-start(f32[4,3,256,256]{3,2,1,0:T(8,128)} %get-tuple-element.42), channel_id=1, source_target_pairs={{0,1},{1,0},{2,3},{3,2},{4,5},{5,4},{6,7},{7,6},{8,9},{9,8},{10,11... | collective-permute-start | bytes 9437192 | tf_op jit(solution)/shard_map/ppermute | solution.py:568
  123.9 198.9 %collective-permute-start.12 = (f32[4,3,256,256]{3,2,0,1:T(8,128)}, f32[4,3,256,256]{3,2,0,1:T(8,128)}, u32[]{:S(2)}, u32[]{:S(2)}) collective-permute-start(f32[4,3,256,256]{3,2,0,1:T(8,128)} %copy.26), channel_id=1, source_target_pairs={{0,2},{1,3},{2,0},{3,1},{4,6},{5,7},{6,4},{7,5},{8,10},{9,11},{10,... | collective-permute-start | bytes 9437192 | tf_op jit(solution)/shard_map/ppermute | solution.py:571
  222.4 94.1 %collective-permute-start.9 = (bf16[2560,256]{1,0:T(8,128)(2,1)}, bf16[2560,256]{1,0:T(8,128)(2,1)}, u32[]{:S(2)}, u32[]{:S(2)}) collective-permute-start(bf16[2560,256]{1,0:T(8,128)(2,1)} %fwd.2), channel_id=1, source_target_pairs={{0,4},{4,8},{8,12},{12,0},{1,5},{5,9},{9,13},{13,1},{2,6},{6,10},{... | collective-permute-start | bytes 3932168 | tf_op jit(solution)/shard_map/ppermute | solution.py:633
  223.8 95.9 %collective-permute-start.11 = (bf16[1,4096,256]{2,1,0:T(8,128)(2,1)}, bf16[1,4096,256]{2,1,0:T(8,128)(2,1)}, u32[]{:S(2)}, u32[]{:S(2)}) collective-permute-start(bf16[1,4096,256]{2,1,0:T(8,128)(2,1)} %bitcast.38), channel_id=1, source_target_pairs={{0,12},{4,0},{8,4},{12,8},{1,13},{5,1},{9,5},{13,9},{2,14},{6,2},{... | collective-permute-start | bytes 6291464 | tf_op jit(solution)/shard_map/ppermute | solution.py:622
  225.3 97.4 %collective-permute-start.13 = (f32[4,3,256,256]{3,2,1,0:T(8,128)}, f32[4,3,256,256]{3,2,1,0:T(8,128)S(1)}, u32[]{:S(2)}, u32[]{:S(2)}) collective-permute-start(f32[4,3,256,256]{3,2,1,0:T(8,128)} %get-tuple-element.52), channel_id=1, source_target_pairs={{0,2},{1,3},{2,0},{3,1},{4,6},{5,7},{6,4},{7,5},{8,10},{9,11},{10,... | collective-permute-start | bytes 9437192 | tf_op jit(solution)/shard_map/ppermute | solution.py:571
  257.1 59.4 %collective-permute-start.10 = (bf16[1536,256]{1,0:T(8,128)(2,1)}, bf16[1536,256]{1,0:T(8,128)(2,1)}, u32[]{:S(2)}, u32[]{:S(2)}) collective-permute-start(bf16[1536,256]{1,0:T(8,128)(2,1)} %fwd.3), channel_id=1, source_target_pairs={{0,4},{4,8},{8,12},{12,0},{1,5},{5,9},{9,13},{13,1},{2,6},{6,10},{... | collective-permute-start | bytes 2359304 | tf_op jit(solution)/shard_map/ppermute | solution.py:633
  316.5 6.3 %copy-start.2 = (f32[8,3,256,256]{3,2,1,0:T(8,128)S(1)}, f32[8,3,256,256]{3,2,1,0:T(8,128)}, u32[]{:S(2)}) copy-start(f32[8,3,256,256]{3,2,1,0:T(8,128)} %get-tuple-element.50) | copy-start | bytes 18874372

commit v8 on v7

--- a/solution.py
+++ b/solution.py
@@ -72,10 +72,10 @@
 
 
 def chunks(ref, first, last):
-    return jnp.concatenate([ref[:, c * 128 : (c + 1) * 128] for c in range(first, last)], axis=0)
-
-
-def rank_kernel(n_exp, rows_b, rows_f, ids_b, slots_b, ids_f, slots_f, tab_b, pos4_b, pos2_b, tab_f, pos2_f):
+    return jnp.concatenate([ref[r : r + 1, c * 128 : (c + 1) * 128] for r in range(ref.shape[0]) for c in range(first, last)], axis=0)
+
+
+def rank_kernel(n_exp, rows_b, rows_f, ids_b, slots_b, ids_f, slots_f, tab_b, pos4_b, pos2_b, tab_f, *pos2_f):
     n = ids_b.shape[1] // 128
     pos, tab_b[...] = rank_routes(chunks(ids_b, 0, n), chunks(slots_b, 0, n), n_exp, rows_b)
     pos4_b[...] = (pos * 4.0).astype(jnp.int32)
@@ -84,26 +84,27 @@
     for h, (blocks, dump) in enumerate(zip(FWD_BLOCKS, rows_f)):
         last = first + blocks * (BT // 128)
         pos, tab_f[h] = rank_routes(chunks(ids_f, first, last), chunks(slots_f, first, last), n_exp, dump)
-        k = ids_f.shape[0]
-        pos2_f[first * k : last * k, :] = (pos * 2.0).astype(jnp.int32)
+        pos2_f[h][...] = (pos * 2.0).astype(jnp.int32)
         first = last
 
 
 def route_ranks(ids_b, slots_b, ids_f, slots_f, n_exp, rows_b, rows_f):
-    pos = jax.ShapeDtypeStruct((ids_b.size // 128, 128), jnp.int32)
-    tab = (8, 128)
-    tab_b, pos4_b, pos2_b, tab_f, pos2_f = pl.pallas_call(
+    def table(n_tok):
+        return jax.ShapeDtypeStruct((n_tok * ids_b.shape[1] // 128, 128), jnp.int32)
+
+    n_tok = ids_b.shape[0]
+    tab_b, pos4_b, pos2_b, tab_f, *pos2_f = pl.pallas_call(
         functools.partial(rank_kernel, n_exp, rows_b, rows_f),
         out_shape=(
-            jax.ShapeDtypeStruct(tab, jnp.int32),
-            pos,
-            pos,
-            jax.ShapeDtypeStruct((len(FWD_BLOCKS), *tab), jnp.int32),
-            pos,
+            jax.ShapeDtypeStruct((8, 128), jnp.int32),
+            table(n_tok),
+            table(n_tok),
+            jax.ShapeDtypeStruct((len(FWD_BLOCKS), 8, 128), jnp.int32),
+            *[table(blocks * BT) for blocks in FWD_BLOCKS],
         ),
         name="rank",
     )(ids_b.T, slots_b.T, ids_f.T, slots_f.T)
-    return tab_b, pos4_b.reshape(-1), pos2_b.reshape(-1), tab_f, pos2_f.reshape(-1)
+    return tab_b, pos4_b.reshape(-1), pos2_b.reshape(-1), tab_f, [p.reshape(-1) for p in pos2_f]
 
 
 def put_rows(ref, at, vals, pitch=2, off=0):
@@ -121,36 +122,32 @@
     return pl.ds(pl.multiple_of(p, n), n)
 
 
-def table_at(j, unroll, top_k):
-    per = 128 // unroll
-    return lax.div(j, per) * (128 * top_k) + lax.rem(j, per) * unroll
-
-
-def gather_rows(buf, acc, pos_ref, top_k):
+def gather_rows(buf, acc, pos_refs):
     unroll = 32
 
     def body(j, c):
-        base = table_at(j, unroll, top_k)
+        base = j * unroll
         at = pl.multiple_of(j * (2 * unroll), 2 * unroll)
         for k in range(unroll):
-            for r in range(top_k):
-                acc[r, pl.ds(at + 2 * k, 2), :] = buf[rows_at(pos_ref[base + (r * 128 + k)], 2), :]
+            i = base + k
+            for r, pos_ref in enumerate(pos_refs):
+                acc[r, pl.ds(at + 2 * k, 2), :] = buf[rows_at(pos_ref[i], 2), :]
         return c
 
     lax.fori_loop(0, BT // unroll, body, 0)
 
 
-def scatter_rows(src, buf, pos_ref, top_k, n, shared):
+def scatter_rows(src, buf, pos_refs, n, shared):
     unroll = 32
 
     def body(j, c):
-        base = table_at(j, unroll, top_k)
+        base = j * unroll
         at = pl.multiple_of(j * (n * unroll), n * unroll)
         for k in range(unroll):
+            i = base + k
             v = src[pl.ds(at + n * k, n), :] if shared else None
-            for r in range(top_k):
-                row = v if shared else src[r, pl.ds(at + n * k, n), :]
-                buf[rows_at(pos_ref[base + (r * 128 + k)], n), :] = row
+            for r, pos_ref in enumerate(pos_refs):
+                buf[rows_at(pos_ref[i], n), :] = v if shared else src[r, pl.ds(at + n * k, n), :]
         return c
 
     lax.fori_loop(0, BT // unroll, body, 0)
@@ -165,7 +162,9 @@
     lax.fori_loop(0, n_exp, body, 0)
 
 
-def pre_bwd_kernel(pos_ref, tab_ref, gate_ref, x_ref, g_ref, w1_ref, w2_ref, h_ref, xs_hbm, qs_hbm, buf, src, xst, qst, sems, *, n_blocks, top_k, n_exp):
+def pre_bwd_kernel(*refs, n_blocks, top_k, n_exp):
+    pos_refs, refs = refs[:top_k], refs[top_k:]
+    tab_ref, gate_ref, x_ref, g_ref, w1_ref, w2_ref, h_ref, xs_hbm, qs_hbm, buf, src, xst, qst, sems = refs
     step = pl.program_id(0)
 
     @pl.when(step == 0)
@@ -181,7 +180,7 @@
     for r in range(top_k):
         put_rows(src.at[r], 0, n, 4, 0)
         put_rows(src.at[r], 0, g * gates[:, r : r + 1], 4, 2)
-    scatter_rows(src, buf, pos_ref, top_k, 4, False)
+    scatter_rows(src, buf, pos_refs, 4, False)
 
     @pl.when(step == n_blocks - 1)
     def _():
@@ -215,8 +214,11 @@
                 cp.wait()
 
 
-def route_spec(top_k, n_blocks, first=0, skip=0):
-    return pl.BlockSpec((top_k * BT,), lambda i: (skip + jnp.clip(i - first, 0, n_blocks - 1),), memory_space=pltpu.SMEM)
+def route_specs(top_k, n_blocks, first=0):
+    def spec(r):
+        return pl.BlockSpec((BT,), lambda i: (r * n_blocks + jnp.clip(i - first, 0, n_blocks - 1),), memory_space=pltpu.SMEM)
+
+    return [spec(r) for r in range(top_k)]
 
 
 def gate_spec(top_k, n_blocks, first=0, skip=0):
@@ -232,7 +234,7 @@
     return pl.pallas_call(
         functools.partial(pre_bwd_kernel, n_blocks=n_blocks, top_k=top_k, n_exp=n_exp),
         grid=(n_blocks,),
-        in_specs=[route_spec(top_k, n_blocks), smem, gate_spec(top_k, n_blocks), blk, blk, whole, whole],
+        in_specs=[*route_specs(top_k, n_blocks), smem, gate_spec(top_k, n_blocks), blk, blk, whole, whole],
         out_specs=[blk, pl.BlockSpec(memory_space=pl.ANY), pl.BlockSpec(memory_space=pl.ANY)],
         out_shape=(
             jax.ShapeDtypeStruct((n_tok, hid), BF16),
@@ -249,7 +251,7 @@
         compiler_params=pltpu.CompilerParams(vmem_limit_bytes=VMEM_LIMIT),
         cost_estimate=pl.CostEstimate(flops=30_000_000_000, bytes_accessed=30_000_000, transcendentals=0),
         name="pre_bwd",
-    )(pos, tab, gates, x, g, w1, w2)
+    )(*[pos] * top_k, tab, gates, x, g, w1, w2)
 
 
 def exp_bwd_kernel(first_ref, tab_ref, xs_hbm, qs_hbm, *refs, n_parts, has_init):
@@ -278,10 +280,10 @@
 
     def w_loads(e, part=0, at=0):
         copies = [pltpu.make_async_copy(w_hbm[part].at[at], wb.at[e], wsems.at[e])]
-        return copies + [pltpu.make_async_copy(ref.at[e], dwb.at[e], isems.at[e]) for ref in init_hbm]
+        return copies + [pltpu.make_async_copy(ref.at[:, e], dwb.at[:, e], isems.at[e]) for ref in init_hbm]
 
     def dw_save(e):
-        return pltpu.make_async_copy(dwb.at[e], dw_hbm.at[e], dsems.at[e])
+        return pltpu.make_async_copy(dwb.at[:, e], dw_hbm.at[:, e], dsems.at[e])
 
     def first_half(t, e):
         slot = lax.rem(t, DEPTH)
@@ -311,7 +313,8 @@
             cp.start()
     if not has_init:
         def clear(e, c):
-            dwb[e] = jnp.zeros(dwb.shape[1:], F32)
+            for i in range(3):
+                dwb[i, e] = jnp.zeros(dwb.shape[2:], F32)
             return c
 
         lax.fori_loop(0, n_loc, clear, 0)
@@ -353,7 +356,7 @@
         grads = (dot_tn(x, dpre), dot_tn(x, dup), dot_tn(act, qb[slot]))
         rb[slot] = rows
         for i, grad in enumerate(grads):
-            dwb[e, i] += grad
+            dwb[i, e] += grad
         keep(t + 1, upcoming)
         save(t).start()
 
@@ -379,11 +382,11 @@
         functools.partial(exp_bwd_kernel, n_parts=len(weights), has_init=bool(init)),
         in_specs=[smem, smem] + [hbm] * (2 + len(weights) + len(init)),
         out_specs=[hbm, hbm],
-        out_shape=(jax.ShapeDtypeStruct(xs.shape, BF16), jax.ShapeDtypeStruct((n_loc, 3, hid, ff), F32)),
+        out_shape=(jax.ShapeDtypeStruct(xs.shape, BF16), jax.ShapeDtypeStruct((3, n_loc, hid, ff), F32)),
         input_output_aliases={2: 0},
         scratch_shapes=[
             pltpu.VMEM((n_loc, 3, hid, ff), BF16),
-            pltpu.VMEM((n_loc, 3, hid, ff), F32),
+            pltpu.VMEM((3, n_loc, hid, ff), F32),
             pltpu.VMEM((DEPTH, TM, hid), BF16),
             pltpu.VMEM((DEPTH, TM, hid), BF16),
             pltpu.VMEM((DEPTH, TM, hid), BF16),
@@ -399,7 +402,10 @@
     )(first, tab, xs, qs, *weights, *init)
 
 
-def post_bwd_kernel(pos_ref, tab_ref, x_ref, g_ref, h_ref, w1_ref, w2_ref, rs_hbm, dx_ref, rbuf, acc, st, sems, *, n_blocks, top_k, n_exp, rows):
+def post_bwd_kernel(*refs, n_blocks, top_k, n_exp, rows):
+    pos_refs, refs = refs[:top_k], refs[top_k:]
+    tab_ref, x_ref, g_ref, h_ref, w1_ref, w2_ref, rs_hbm, dx_ref, rbuf, acc, st, sems = refs
+
     @pl.when(pl.program_id(0) == 0)
     def _():
         n_tiles = tab_ref[0, n_exp]
@@ -423,7 +429,7 @@
 
         lax.fori_loop(0, n_tiles, expand, 0)
 
-    gather_rows(rbuf, acc, pos_ref, top_k)
+    gather_rows(rbuf, acc, pos_refs)
     dn = get_rows(acc.at[0], 0, BT)
     for r in range(1, top_k):
         dn = dn + get_rows(acc.at[r], 0, BT)
@@ -445,7 +451,7 @@
     return pl.pallas_call(
         functools.partial(post_bwd_kernel, n_blocks=n_blocks, top_k=top_k, n_exp=n_exp, rows=rows),
         grid=(n_blocks,),
-        in_specs=[route_spec(top_k, n_blocks), smem, blk, blk, blk, whole, whole, pl.BlockSpec(memory_space=pl.ANY)],
+        in_specs=[*route_specs(top_k, n_blocks), smem, blk, blk, blk, whole, whole, pl.BlockSpec(memory_space=pl.ANY)],
         out_specs=blk,
         out_shape=jax.ShapeDtypeStruct((n_tok, hid), BF16),
         scratch_shapes=[
@@ -457,10 +463,12 @@
         compiler_params=pltpu.CompilerParams(vmem_limit_bytes=VMEM_LIMIT),
         cost_estimate=pl.CostEstimate(flops=30_000_000_000, bytes_accessed=30_000_000, transcendentals=0),
         name="post_bwd",
-    )(pos, tab, x, g, h, w1, w2, rs)
-
-
-def fwd_kernel(firsts_ref, tab_ref, pos_ref, pos_out_ref, gate_ref, x_ref, w1_ref, w2_ref, *rest, n_blocks, top_k, n_exp, n_groups, rows):
+    )(*[pos] * top_k, tab, x, g, h, w1, w2, rs)
+
+
+def fwd_kernel(*refs, n_blocks, top_k, n_exp, n_groups, rows):
+    pos_refs, pos_out_refs, refs = refs[:top_k], refs[top_k : 2 * top_k], refs[2 * top_k :]
+    firsts_ref, tab_ref, gate_ref, x_ref, w1_ref, w2_ref, *rest = refs
     w_hbm = rest[:n_groups]
     y_ref, buf, acc, hsc, wsc, mid, sems = rest[n_groups:]
     nsc = acc.at[0]
@@ -483,7 +491,7 @@
         hf = h.astype(F32)
         put_rows(nsc, 0, (hf * rms_scale(hf)).astype(BF16).astype(F32))
 
-        scatter_rows(nsc, buf, pos_ref, top_k, 2, True)
+        scatter_rows(nsc, buf, pos_refs, 2, True)
 
     @pl.when(step == n_blocks)
     def _():
@@ -500,24 +508,37 @@
             up = dot(x, wsc[e, 1])
             return (pre * jax.nn.sigmoid(pre) * up).astype(BF16)
 
-        mid[0] = first_half(rows_of(0), 0)
-
-        def body(t, e):
-            then = jnp.where((t + 1 >= tab_ref[0, e + 1]) & (t + 1 < end), e + 1, e)
-            x = rows_of(jnp.minimum(t + 1, end - 1))
-            out = dot(mid[lax.rem(t, 2)], wsc[e, 2]).astype(BF16).astype(F32)
-            upcoming = first_half(x, then)
-            put_rows(buf, pl.multiple_of(t * (2 * TM), 2 * TM), out)
-            mid[lax.rem(t + 1, 2)] = upcoming
-            return then
-
-        lax.fori_loop(0, end, body, 0)
+        def expert_of(t, e):
+            return jnp.where((t >= tab_ref[0, e + 1]) & (t < end), e + 1, e)
+
+        def second(t):
+            return jnp.minimum(t, end - 1)
+
+        spare = 2 * rows + 8
+        mid[0, 0] = first_half(rows_of(0), 0)
+        mid[0, 1] = first_half(rows_of(second(1)), expert_of(1, 0))
+
+        def body(i, experts):
+            t = 2 * i
+            slot = lax.rem(i, 2)
+            e2 = expert_of(t + 2, experts[1])
+            e3 = expert_of(t + 3, e2)
+            x2, x3 = rows_of(second(t + 2)), rows_of(second(t + 3))
+            outs = [dot(mid[slot, k], wsc[experts[k], 2]).astype(BF16).astype(F32) for k in range(2)]
+            acts = [first_half(x2, e2), first_half(x3, e3)]
+            put_rows(buf, pl.multiple_of(t * (2 * TM), 2 * TM), outs[0])
+            put_rows(buf, pl.multiple_of(jnp.where(t + 1 < end, (t + 1) * (2 * TM), spare), 8), outs[1])
+            for k in range(2):
+                mid[1 - slot, k] = acts[k]
+            return e2, e3
+
+        lax.fori_loop(0, lax.div(end + 1, 2), body, (jnp.int32(0), expert_of(1, 0)))
 
     @pl.when(step > n_blocks)
     def _():
         base = (step - n_blocks - 1) * BT
 
-        gather_rows(buf, acc, pos_out_ref, top_k)
+        gather_rows(buf, acc, pos_out_refs)
         gates = gate_ref[...].astype(F32).T
         h = hsc[pl.ds(pl.multiple_of(base, BT), BT), :]
         mix = get_rows(acc.at[0], 0, BT) * gates[:, 0:1]
@@ -534,23 +555,23 @@
     return pl.pallas_call(
         functools.partial(fwd_kernel, n_blocks=n_blocks, top_k=top_k, n_exp=n_exp, n_groups=n_groups, rows=rows),
         grid=(2 * n_blocks + 1,),
-        in_specs=[smem, smem, route_spec(top_k, n_blocks, 0, skip), route_spec(top_k, n_blocks, n_blocks + 1, skip), gate_spec(top_k, n_blocks, n_blocks + 1, skip)]
+        in_specs=[*route_specs(top_k, n_blocks), *route_specs(top_k, n_blocks, n_blocks + 1), smem, smem, gate_spec(top_k, n_blocks, n_blocks + 1, skip)]
         + [pl.BlockSpec((BT, hid), lambda i: (skip + jnp.minimum(i, n_blocks - 1), 0)), whole, whole]
         + [pl.BlockSpec(memory_space=pl.ANY)] * n_groups,
         out_specs=pl.BlockSpec((BT, hid), lambda i: (jnp.maximum(i - n_blocks - 1, 0), 0)),
         out_shape=jax.ShapeDtypeStruct((n_tok, hid), BF16),
         scratch_shapes=[
-            pltpu.VMEM((2 * rows + 8, hid // 2), F32),
+            pltpu.VMEM((2 * rows + 8 + 2 * TM, hid // 2), F32),
             pltpu.VMEM((top_k, 2 * BT, hid // 2), F32),
             pltpu.VMEM((n_tok, hid), BF16),
             pltpu.VMEM((n_exp, 3, hid, hid), BF16),
-            pltpu.VMEM((2, TM, hid), BF16),
+            pltpu.VMEM((2, 2, TM, hid), BF16),
             pltpu.SemaphoreType.DMA((n_groups,)),
         ],
         compiler_params=pltpu.CompilerParams(vmem_limit_bytes=VMEM_LIMIT),
         cost_estimate=pl.CostEstimate(flops=80_000_000_000, bytes_accessed=30_000_000, transcendentals=0),
         name="fwd",
-    )(firsts, tab, pos, pos, gates, x, w1, w2, *weights)
+    )(*[pos] * (2 * top_k), firsts, tab, gates, x, w1, w2, *weights)
 
 
 def solution(mesh):
@@ -626,13 +647,13 @@
         weights = [w for _, ws in groups.values() for w in ws]
         skip = 0
         for h, blocks in enumerate(FWD_BLOCKS):
-            y_half = fwd(blocks, skip, firsts, tab_f[h], pos2_f, gates_f, x_fwd, w1, w2, weights, rows_f[h], n_exp, top_k)
+            y_half = fwd(blocks, skip, firsts, tab_f[h], pos2_f[h], gates_f, x_fwd, w1, w2, weights, rows_f[h], n_exp, top_k)
             skip += blocks
             if h + 1 < len(FWD_BLOCKS):
                 x_fwd, y_half = lax.optimization_barrier((x_fwd, y_half))
             parts.append(lax.ppermute(y_half, "pp", next_perm))
         y_next = jnp.concatenate(parts, axis=0)[None]
-        dws = [jnp.concatenate([dw_own[at, i] + sums[:, i] for at, sums in zip(halves, there)], axis=0)[None] for i in range(3)]
+        dws = [jnp.concatenate([dw_own[i, at] + sums[i] for at, sums in zip(halves, there)], axis=0)[None] for i in range(3)]
         dx_prev = jnp.where(me >= 0, dx_prev, jnp.zeros_like(dx_prev))
         return y_next, dx_prev, *dws
 

time: 332 us -> 316 us (0.952)
  Pallas kernels: 195 us -> 174 us
  waiting for transfers between devices: 91 us -> 96.3 us
    pallas_call x2, Pallas kernels: 69.4 us -> 55.7 us  [fwd(): pl.pallas_call(functools.partial(fwd_kernel, n_blocks=n_blocks, top_k=top...]
    ppermute x2, waiting for transfers between devices: 59.3 us -> 64.7 us  [slot(): parts.append(lax.ppermute(y_half, 'pp', next_perm))]
    pallas_call x1, Pallas kernels: 30.8 us -> 27.2 us  [pre_bwd(): pl.pallas_call(functools.partial(pre_bwd_kernel, n_blocks=n_blocks, top_k...]
    pallas_call x1, Pallas kernels: 28.2 us -> 24.8 us  [post_bwd(): pl.pallas_call(functools.partial(post_bwd_kernel, n_blocks=n_blocks, top_...]
  transfers between devices with their start and end apart: 14 -> 14, of which waited for: 3 -> 3; matrix products, arithmetic and copies ran while one was open for 3% -> 2% of each run, Pallas kernels for 59% -> 55%
where the time goes in v8:
time: 316 us; the launch traced here: 315 us
  Pallas kernels  174 us (55%)
  waiting for transfers between devices  96.3 us (30%)
  starting transfers between devices  23 us (7%)
  other arithmetic  14.3 us (5%)
  local copies, waits for them, and re-layouts  6.02 us (2%)
    ppermute x2, waiting for transfers between devices, slot(): parts.append(lax.ppermute(y_half, 'pp', next_perm))  64.7 us
    pallas_call x6, Pallas kernels, exp_bwd(): pl.pallas_call(functools.partial(exp_bwd_kernel, n_parts=len(weights), ha...  61.8 us
    pallas_call x2, Pallas kernels, fwd(): pl.pallas_call(functools.partial(fwd_kernel, n_blocks=n_blocks, top_k=top...  55.7 us
    ppermute x4, waiting for transfers between devices, chip(): return lax.ppermute(a, 'ep', chip_perm)  29.6 us
    pallas_call x1, Pallas kernels, pre_bwd(): pl.pallas_call(functools.partial(pre_bwd_kernel, n_blocks=n_blocks, top_k...  27.2 us
    pallas_call x1, Pallas kernels, post_bwd(): pl.pallas_call(functools.partial(post_bwd_kernel, n_blocks=n_blocks, top_...  24.8 us
    ppermute x4, starting transfers between devices, chip(): return lax.ppermute(a, 'ep', chip_perm)  14.1 us
  transfers between devices with their start and end apart: 14, of which 3 were waited for; matrix products, arithmetic and copies ran while one was open for 2% of the time, Pallas kernels for 55%

profile of v8, /device:TPU:0, one launch (start us, length us, event | category | flops | bytes accessed | tf_op | source)
XLA Modules:
  0.0 314.9 jit_solution(10926924752948140478)
XLA Ops:
  2.9 3.2 %collective-permute-start = (bf16[4,3,256,256]{3,2,1,0:T(8,128)(2,1)S(1)}, bf16[4,3,256,256]{3,2,1,0:T(8,128)(2,1)}, u32[]{:S(2)}, u32[]{:S(2)}) collective-permute-start(bf16[4,3,256,256]{3,2,1,0:T(8,128)(2,1)S(1)} %pad_maximum_fusion.refs_0_.refs_14_), channel_id=1, source_target_pairs={{0,2},{1,3},{2,0},{3,1},{4,6},{5,7},{6,4},{7,5},{8,10},{9,11},{10,... | collective-permute-start | bytes 4718600 | tf_op jit(solution)/shard_map/ppermute | solution.py:592
  6.9 5.0 %rank.1 = (s32[8,128]{1,0:T(8,128)}, s32[128,128]{1,0:T(8,128)}, s32[128,128]{1,0:T(8,128)}, s32[2,8,128]{2,1,0:T(8,128)}, s32[80,128]{1,0:T(8,128)}, /*index=5*/s32[48,128]{1,0:T(8,128)}) custom-call(s32[4,4096]{1,0:T(4,128)} %bitcast.72, s32[4,4096]{1,0:T(4,128)} %bitcast.73, s32[4,4096]{1,0:T(4,128)} %bitcast.74, s32[4,4096]{1,0:T(4,128)} %bitcast.75), custom_call_target="tpu_custom_call" | custom-call | tf_op jit(solution)/shard_map/rank/pallas_call | solution.py:96
  11.8 29.6 %collective-permute-done.refs_0_.refs_18_ = bf16[4,3,256,256]{3,2,1,0:T(8,128)(2,1)} collective-permute-done((bf16[4,3,256,256]{3,2,1,0:T(8,128)(2,1)S(1)}, bf16[4,3,256,256]{3,2,1,0:T(8,128)(2,1)}, u32[]{:S(2)}, u32[]{:S(2)}) %collective-permute-start) | collective-permute-done | bytes 1572896 | tf_op jit(solution)/shard_map/ppermute | solution.py:592
  41.5 27.2 %pre_bwd.1 = (bf16[4096,256]{1,0:T(8,128)(2,1)}, bf16[24576,256]{1,0:T(8,128)(2,1)}, bf16[24576,256]{1,0:T(8,128)(2,1)}) custom-call(s32[16384]{0:T(1024)} %bitcast.94, s32[16384]{0:T(1024)} %bitcast.95, s32[16384]{0:T(1024)} %bitcast.96, s32[16384]{0:T(1024)} %bitcast.97, s32[8,128]{1,0:T(8,128)} %get-tuple-element.31.refs_4_.tab_ref, ...), custom_call_target="tpu_custom_call" | custom-call | flops 30000001024 | bytes 30000000 | tf_op jit(solution)/shard_map/pre_bwd/pallas_call | solution.py:234
  68.7 6.4 %exp_bwd.6 = (bf16[24576,256]{1,0:T(8,128)(2,1)}, f32[3,4,256,256]{3,2,1,0:T(8,128)}) custom-call(s32[1]{0:T(128)} %bitcast.22.first_ref, s32[8,128]{1,0:T(8,128)} %get-tuple-element.31.refs_4_.tab_ref, bf16[24576,256]{1,0:T(8,128)(2,1)} %get-tuple-element.34.xs_hbm, bf16[24576,256]{1,0:T(8,128)(2,1)} %get-tuple-element.35.qs_hbm, ...), custom_call_target="tpu_custom_call", output_to_operand_aliasing={{0}: (2, {})} | custom-call | flops 8000000000 | bytes 20000000 | tf_op jit(solution)/shard_map/exp_bwd/pallas_call | solution.py:381
  75.1 1.9 collective-permute-start.4
  77.0 18.0 %exp_bwd.7 = (bf16[24576,256]{1,0:T(8,128)(2,1)}, f32[3,8,256,256]{3,2,1,0:T(8,128)}) custom-call(s32[1]{0:T(128)} %bitcast.21.first_ref, s32[8,128]{1,0:T(8,128)} %get-tuple-element.31.refs_4_.tab_ref, bf16[24576,256]{1,0:T(8,128)(2,1)} %get-tuple-element.36.xs_hbm, bf16[24576,256]{1,0:T(8,128)(2,1)} %get-tuple-element.35.qs_hbm, ...), custom_call_target="tpu_custom_call", output_to_operand_aliasing={{0}: (2, {})} | custom-call | flops 8000000000 | bytes 20000000 | tf_op jit(solution)/shard_map/exp_bwd/pallas_call | solution.py:381
  95.6 10.1 %exp_bwd.8 = (bf16[24576,256]{1,0:T(8,128)(2,1)}, f32[3,4,256,256]{3,2,1,0:T(8,128)}) custom-call(s32[1]{0:T(128)} %bitcast.20.first_ref, s32[8,128]{1,0:T(8,128)} %get-tuple-element.31.refs_4_.tab_ref, bf16[24576,256]{1,0:T(8,128)(2,1)} %get-tuple-element.37.xs_hbm, bf16[24576,256]{1,0:T(8,128)(2,1)} %get-tuple-element.35.qs_hbm, ...), custom_call_target="tpu_custom_call", output_to_operand_aliasing={{0}: (2, {})} | custom-call | flops 8000000000 | bytes 20000000 | tf_op jit(solution)/shard_map/exp_bwd/pallas_call | solution.py:381
  105.7 2.0 collective-permute-done.6.refs_0_.refs_21_
  108.8 5.3 %exp_bwd.9 = (bf16[24576,256]{1,0:T(8,128)(2,1)}, f32[3,4,256,256]{3,2,1,0:T(8,128)}) custom-call(s32[1]{0:T(128)} %bitcast.19.first_ref, s32[8,128]{1,0:T(8,128)} %get-tuple-element.31.refs_4_.tab_ref, bf16[24576,256]{1,0:T(8,128)(2,1)} %get-tuple-element.39.xs_hbm, bf16[24576,256]{1,0:T(8,128)(2,1)} %get-tuple-element.35.qs_hbm, ...), custom_call_target="tpu_custom_call", output_to_operand_aliasing={{0}: (2, {})} | custom-call | flops 8000000000 | bytes 20000000 | tf_op jit(solution)/shard_map/exp_bwd/pallas_call | solution.py:381
  114.1 2.9 collective-permute-start.8
  118.2 6.4 %collective-permute-start.12 = (f32[3,4,256,256]{3,2,1,0:T(8,128)}, f32[3,4,256,256]{3,2,1,0:T(8,128)}, u32[]{:S(2)}, u32[]{:S(2)}) collective-permute-start(f32[3,4,256,256]{3,2,1,0:T(8,128)} %get-tuple-element.53), channel_id=1, source_target_pairs={{0,2},{1,3},{2,0},{3,1},{4,6},{5,7},{6,4},{7,5},{8,10},{9,11},{10,... | collective-permute-start | bytes 9437192 | tf_op jit(solution)/shard_map/ppermute | solution.py:592
  124.6 13.7 %exp_bwd.10 = (bf16[24576,256]{1,0:T(8,128)(2,1)}, f32[3,8,256,256]{3,2,1,0:T(8,128)}) custom-call(s32[1]{0:T(128)} %bitcast.18.first_ref, s32[8,128]{1,0:T(8,128)} %get-tuple-element.31.refs_4_.tab_ref, bf16[24576,256]{1,0:T(8,128)(2,1)} %get-tuple-element.40.xs_hbm, bf16[24576,256]{1,0:T(8,128)(2,1)} %get-tuple-element.35.qs_hbm, ...), custom_call_target="tpu_custom_call", output_to_operand_aliasing={{0}: (2, {})} | custom-call | flops 8000000000 | bytes 20000000 | tf_op jit(solution)/shard_map/exp_bwd/pallas_call | solution.py:381
  138.4 1.6 copy-done.3
  140.0 8.3 %exp_bwd.11 = (bf16[24576,256]{1,0:T(8,128)(2,1)}, f32[3,4,256,256]{3,2,1,0:T(8,128)}) custom-call(s32[1]{0:T(128)} %bitcast.17.first_ref, s32[8,128]{1,0:T(8,128)} %get-tuple-element.31.refs_4_.tab_ref, bf16[24576,256]{1,0:T(8,128)(2,1)} %get-tuple-element.42.xs_hbm, bf16[24576,256]{1,0:T(8,128)(2,1)} %get-tuple-element.35.qs_hbm, ...), custom_call_target="tpu_custom_call", output_to_operand_aliasing={{0}: (2, {})} | custom-call | flops 8000000000 | bytes 20000000 | tf_op jit(solution)/shard_map/exp_bwd/pallas_call | solution.py:381
  148.3 24.8 %post_bwd.1 = bf16[4096,256]{1,0:T(8,128)(2,1)} custom-call(s32[16384]{0:T(1024)} %bitcast.90, s32[16384]{0:T(1024)} %bitcast.91, s32[16384]{0:T(1024)} %bitcast.92, s32[16384]{0:T(1024)} %bitcast.93, s32[8,128]{1,0:T(8,128)} %get-tuple-element.31.refs_4_.tab_ref, bf16[4096,256]{1,0:T(8,128)(2,1)} %bitcast.77, bf16[4096,256]{1,0:T(8,128)(2,1)} %bitcast.79, ...), custom_call_target="tpu_custom_call" | custom-call | flops 30000001024 | bytes 30000000 | tf_op jit(solution)/shard_map/post_bwd/pallas_call | solution.py:451
  173.1 33.3 %fwd.2 = bf16[2560,256]{1,0:T(8,128)(2,1)} custom-call(s32[10240]{0:T(1024)} %bitcast.98, s32[10240]{0:T(1024)} %bitcast.99, s32[10240]{0:T(1024)} %bitcast.100, s32[10240]{0:T(1024)} %bitcast.101, s32[10240]{0:T(1024)} %bitcast.102, s32[10240]{0:T(1024)} %bitcast.103, s32[10240]{0:T(1024)} %bitcast.104, s32[10240]{0:T(1024)} %bitcast.105, s32[8]{0:T(128)} %stack.49.refs_8_, ...), custom_call_target="tpu_custom_call" | custom-call | flops 80000000000 | bytes 30000000 | tf_op jit(solution)/shard_map/fwd/pallas_call | solution.py:555
  209.4 4.4 %collective-permute-start.13 = (f32[3,4,256,256]{3,2,1,0:T(8,128)}, f32[3,4,256,256]{3,2,1,0:T(8,128)S(1)}, u32[]{:S(2)}, u32[]{:S(2)}) collective-permute-start(f32[3,4,256,256]{3,2,1,0:T(8,128)} %get-tuple-element.54), channel_id=1, source_target_pairs={{0,2},{1,3},{2,0},{3,1},{4,6},{5,7},{6,4},{7,5},{8,10},{9,11},{10,... | collective-permute-start | bytes 9437192 | tf_op jit(solution)/shard_map/ppermute | solution.py:592
  213.8 22.4 %fwd.3 = bf16[1536,256]{1,0:T(8,128)(2,1)} custom-call(s32[6144]{0:T(1024)} %bitcast.109, s32[6144]{0:T(1024)} %bitcast.110, s32[6144]{0:T(1024)} %bitcast.111, s32[6144]{0:T(1024)} %bitcast.112, s32[6144]{0:T(1024)} %bitcast.113, s32[6144]{0:T(1024)} %bitcast.114, s32[6144]{0:T(1024)} %bitcast.115, s32[6144]{0:T(1024)} %bitcast.116, s32[8]{0:T(128)} %stack.49.refs_8_, ...), custom_call_target="tpu_custom_call" | custom-call | flops 80000000000 | bytes 30000000 | tf_op jit(solution)/shard_map/fwd/pallas_call | solution.py:555
  236.3 64.7 %collective-permute-done.10 = bf16[1536,256]{1,0:T(8,128)(2,1)} collective-permute-done((bf16[1536,256]{1,0:T(8,128)(2,1)}, bf16[1536,256]{1,0:T(8,128)(2,1)}, u32[]{:S(2)}, u32[]{:S(2)}) %collective-permute-start.10) | collective-permute-done | bytes 786464 | tf_op jit(solution)/shard_map/ppermute | solution.py:654
  300.9 3.2 %maximum_bitcast_fusion = bf16[1,4096,256]{2,1,0:T(8,128)(2,1)} fusion(bf16[1536,256]{1,0:T(8,128)(2,1)} %collective-permute-done.10, bf16[2560,256]{1,0:T(8,128)(2,1)} %collective-permute-done.9), kind=kLoop, calls=%fused_computation | loop fusion | flops 4194304 | bytes 4194304 | tf_op jit(solution)/shard_map/broadcast_in_dim | solution.py:655
  304.1 3.1 broadcast_select_fusion
  307.2 3.0 fusion.1
  310.2 1.6 maximum_bitcast_fusion.3
  (43 shorter events, 12.0 us)
Async XLA Ops:
  0.6 1.5 copy-start.4
  0.6 1.8 copy-start.5
  2.9 65.8 %copy-start = (bf16[4,3,256,256]{3,2,1,0:T(8,128)(2,1)}, bf16[4,3,256,256]{3,2,1,0:T(8,128)(2,1)S(1)}, u32[]{:S(2)}) copy-start(bf16[4,3,256,256]{3,2,1,0:T(8,128)(2,1)S(1)} %pad_maximum_fusion.refs_0_.refs_14_) | copy-start | bytes 4718596
  2.9 38.6 %collective-permute-start = (bf16[4,3,256,256]{3,2,1,0:T(8,128)(2,1)S(1)}, bf16[4,3,256,256]{3,2,1,0:T(8,128)(2,1)}, u32[]{:S(2)}, u32[]{:S(2)}) collective-permute-start(bf16[4,3,256,256]{3,2,1,0:T(8,128)(2,1)S(1)} %pad_maximum_fusion.refs_0_.refs_14_), channel_id=1, source_target_pairs={{0,2},{1,3},{2,0},{3,1},{4,6},{5,7},{6,4},{7,5},{8,10},{9,11},{10,... | collective-permute-start | bytes 4718600 | tf_op jit(solution)/shard_map/ppermute | solution.py:592
  6.1 70.9 %collective-permute-start.2 = (bf16[4,3,256,256]{3,2,1,0:T(8,128)(2,1)S(1)}, bf16[4,3,256,256]{3,2,1,0:T(8,128)(2,1)}, u32[]{:S(2)}, u32[]{:S(2)}) collective-permute-start(bf16[4,3,256,256]{3,2,1,0:T(8,128)(2,1)S(1)} %pad_maximum_fusion.refs_0_.refs_14_), channel_id=1, source_target_pairs={{0,1},{1,0},{2,3},{3,2},{4,5},{5,4},{6,7},{7,6},{8,9},{9,8},{10,11... | collective-permute-start | bytes 4718600 | tf_op jit(solution)/shard_map/ppermute | solution.py:589
  6.3 62.4 %copy-start.1 = (bf16[4,3,256,256]{3,2,1,0:T(8,128)(2,1)}, bf16[4,3,256,256]{3,2,1,0:T(8,128)(2,1)S(1)}, u32[]{:S(2)}) copy-start(bf16[4,3,256,256]{3,2,1,0:T(8,128)(2,1)S(1)} %pad_maximum_fusion.1.refs_1_.refs_15_) | copy-start | bytes 4718596
  6.3 88.8 %collective-permute-start.5 = (bf16[4,3,256,256]{3,2,1,0:T(8,128)(2,1)S(1)}, bf16[4,3,256,256]{3,2,1,0:T(8,128)(2,1)}, u32[]{:S(2)}, u32[]{:S(2)}) collective-permute-start(bf16[4,3,256,256]{3,2,1,0:T(8,128)(2,1)S(1)} %pad_maximum_fusion.1.refs_1_.refs_15_), channel_id=1, source_target_pairs={{0,2},{1,3},{2,0},{3,1},{4,6},{5,7},{6,4},{7,5},{8,10},{9,11},{10,... | collective-permute-start | bytes 4718600 | tf_op jit(solution)/shard_map/ppermute | solution.py:592
  6.4 70.6 %collective-permute-start.3 = (bf16[4,3,256,256]{3,2,1,0:T(8,128)(2,1)S(1)}, bf16[4,3,256,256]{3,2,1,0:T(8,128)(2,1)}, u32[]{:S(2)}, u32[]{:S(2)}) collective-permute-start(bf16[4,3,256,256]{3,2,1,0:T(8,128)(2,1)S(1)} %pad_maximum_fusion.1.refs_1_.refs_15_), channel_id=1, source_target_pairs={{0,1},{1,0},{2,3},{3,2},{4,5},{5,4},{6,7},{7,6},{8,9},{9,8},{10,11... | collective-permute-start | bytes 4718600 | tf_op jit(solution)/shard_map/ppermute | solution.py:589
  41.5 27.2 %collective-permute-start.1 = (bf16[4,3,256,256]{3,2,1,0:T(8,128)(2,1)}, bf16[4,3,256,256]{3,2,1,0:T(8,128)(2,1)}, u32[]{:S(2)}, u32[]{:S(2)}) collective-permute-start(bf16[4,3,256,256]{3,2,1,0:T(8,128)(2,1)} %collective-permute-done.refs_0_.refs_18_), channel_id=1, source_target_pairs={{0,1},{1,0},{2,3},{3,2},{4,5},{5,4},{6,7},{7,6},{8,9},{9,8},{10,11... | collective-permute-start | bytes 4718600 | tf_op jit(solution)/shard_map/ppermute | solution.py:589
  75.1 20.5 %collective-permute-start.4 = (f32[3,4,256,256]{3,2,1,0:T(8,128)}, f32[3,4,256,256]{3,2,1,0:T(8,128)}, u32[]{:S(2)}, u32[]{:S(2)}) collective-permute-start(f32[3,4,256,256]{3,2,1,0:T(8,128)} %get-tuple-element.38), channel_id=1, source_target_pairs={{0,1},{1,0},{2,3},{3,2},{4,5},{5,4},{6,7},{7,6},{8,9},{9,8},{10,11... | collective-permute-start | bytes 9437192 | tf_op jit(solution)/shard_map/ppermute | solution.py:589
  95.0 29.6 %collective-permute-start.7 = (f32[3,8,256,256]{3,2,1,0:T(8,128)}, f32[3,8,256,256]{3,2,1,0:T(8,128)}, u32[]{:S(2)}, u32[]{:S(2)}) collective-permute-start(f32[3,8,256,256]{3,2,1,0:T(8,128)} %get-tuple-element.41), channel_id=1, source_target_pairs={{0,1},{1,0},{2,3},{3,2},{4,5},{5,4},{6,7},{7,6},{8,9},{9,8},{10,11... | collective-permute-start | bytes 18874376 | tf_op jit(solution)/shard_map/ppermute | solution.py:589
  95.1 12.6 %collective-permute-start.6 = (bf16[4,3,256,256]{3,2,1,0:T(8,128)(2,1)}, bf16[4,3,256,256]{3,2,1,0:T(8,128)(2,1)S(1)}, u32[]{:S(2)}, u32[]{:S(2)}) collective-permute-start(bf16[4,3,256,256]{3,2,1,0:T(8,128)(2,1)} %collective-permute-done.5.refs_0_.refs_19_), channel_id=1, source_target_pairs={{0,1},{1,0},{2,3},{3,2},{4,5},{5,4},{6,7},{7,6},{8,9},{9,8},{10,11... | collective-permute-start | bytes 4718600 | tf_op jit(solution)/shard_map/ppermute | solution.py:589
  107.7 1.1 copy-start.7
  108.8 8.8 %copy-start.6 = (s32[2,8,128]{2,1,0:T(8,128)S(1)}, s32[2,8,128]{2,1,0:T(8,128)}, u32[]{:S(2)}) copy-start(s32[2,8,128]{2,1,0:T(8,128)} %get-tuple-element.47) | copy-start | bytes 24580
  114.1 24.3 %collective-permute-start.8 = (f32[3,4,256,256]{3,2,1,0:T(8,128)}, f32[3,4,256,256]{3,2,1,0:T(8,128)S(1)}, u32[]{:S(2)}, u32[]{:S(2)}) collective-permute-start(f32[3,4,256,256]{3,2,1,0:T(8,128)} %get-tuple-element.43), channel_id=1, source_target_pairs={{0,1},{1,0},{2,3},{3,2},{4,5},{5,4},{6,7},{7,6},{8,9},{9,8},{10,11... | collective-permute-start | bytes 9437192 | tf_op jit(solution)/shard_map/ppermute | solution.py:589
  118.2 189.0 %collective-permute-start.12 = (f32[3,4,256,256]{3,2,1,0:T(8,128)}, f32[3,4,256,256]{3,2,1,0:T(8,128)}, u32[]{:S(2)}, u32[]{:S(2)}) collective-permute-start(f32[3,4,256,256]{3,2,1,0:T(8,128)} %get-tuple-element.53), channel_id=1, source_target_pairs={{0,2},{1,3},{2,0},{3,1},{4,6},{5,7},{6,4},{7,5},{8,10},{9,11},{10,... | collective-permute-start | bytes 9437192 | tf_op jit(solution)/shard_map/ppermute | solution.py:592
  138.4 1.6 copy-start.3
  206.4 94.5 %collective-permute-start.9 = (bf16[2560,256]{1,0:T(8,128)(2,1)}, bf16[2560,256]{1,0:T(8,128)(2,1)}, u32[]{:S(2)}, u32[]{:S(2)}) collective-permute-start(bf16[2560,256]{1,0:T(8,128)(2,1)} %fwd.2), channel_id=1, source_target_pairs={{0,4},{4,8},{8,12},{12,0},{1,5},{5,9},{9,13},{13,1},{2,6},{6,10},{... | collective-permute-start | bytes 3932168 | tf_op jit(solution)/shard_map/ppermute | solution.py:654
  208.0 96.1 %collective-permute-start.11 = (bf16[1,4096,256]{2,1,0:T(8,128)(2,1)}, bf16[1,4096,256]{2,1,0:T(8,128)(2,1)}, u32[]{:S(2)}, u32[]{:S(2)}) collective-permute-start(bf16[1,4096,256]{2,1,0:T(8,128)(2,1)} %bitcast.39), channel_id=1, source_target_pairs={{0,12},{4,0},{8,4},{12,8},{1,13},{5,1},{9,5},{13,9},{2,14},{6,2},{... | collective-permute-start | bytes 6291464 | tf_op jit(solution)/shard_map/ppermute | solution.py:643
  209.4 97.8 %collective-permute-start.13 = (f32[3,4,256,256]{3,2,1,0:T(8,128)}, f32[3,4,256,256]{3,2,1,0:T(8,128)S(1)}, u32[]{:S(2)}, u32[]{:S(2)}) collective-permute-start(f32[3,4,256,256]{3,2,1,0:T(8,128)} %get-tuple-element.54), channel_id=1, source_target_pairs={{0,2},{1,3},{2,0},{3,1},{4,6},{5,7},{6,4},{7,5},{8,10},{9,11},{10,... | collective-permute-start | bytes 9437192 | tf_op jit(solution)/shard_map/ppermute | solution.py:592
  236.2 64.7 %collective-permute-start.10 = (bf16[1536,256]{1,0:T(8,128)(2,1)}, bf16[1536,256]{1,0:T(8,128)(2,1)}, u32[]{:S(2)}, u32[]{:S(2)}) collective-permute-start(bf16[1536,256]{1,0:T(8,128)(2,1)} %fwd.3), channel_id=1, source_target_pairs={{0,4},{4,8},{8,12},{12,0},{1,5},{5,9},{9,13},{13,1},{2,6},{6,10},{... | collective-permute-start | bytes 2359304 | tf_op jit(solution)/shard_map/ppermute | solution.py:654
  300.9 6.3 %copy-start.2 = (f32[3,8,256,256]{3,2,1,0:T(8,128)S(1)}, f32[3,8,256,256]{3,2,1,0:T(8,128)}, u32[]{:S(2)}) copy-start(f32[3,8,256,256]{3,2,1,0:T(8,128)} %get-tuple-element.52) | copy-start | bytes 18874372

commit v9 on v8

--- a/solution.py
+++ b/solution.py
@@ -14,6 +14,7 @@
 DEPTH = 4
 QUEUE = 8
 FWD_BLOCKS = (5, 3)
+POST_BLOCKS = (4, 4)
 F32 = jnp.float32
 BF16 = jnp.bfloat16
 VMEM_LIMIT = 60 * 1024 * 1024
@@ -214,9 +215,10 @@
                 cp.wait()
 
 
-def route_specs(top_k, n_blocks, first=0):
+def route_specs(top_k, n_blocks, first=0, skip=0, total=None):
     def spec(r):
-        return pl.BlockSpec((BT,), lambda i: (r * n_blocks + jnp.clip(i - first, 0, n_blocks - 1),), memory_space=pltpu.SMEM)
+        start = r * (total or n_blocks) + skip
+        return pl.BlockSpec((BT,), lambda i: (start + jnp.clip(i - first, 0, n_blocks - 1),), memory_space=pltpu.SMEM)
 
     return [spec(r) for r in range(top_k)]
 
@@ -441,19 +443,18 @@
     dx_ref[...] = (dh + rms_back(xf, dot_nt(du, w1_ref[...]))).astype(BF16)
 
 
-def post_bwd(pos, tab, x, g, h, w1, w2, rs, n_exp, top_k):
-    n_tok, hid = x.shape
+def post_bwd(n_blocks, skip, pos, tab, x, g, h, w1, w2, rs, n_exp, top_k):
+    total, hid = x.shape[0] // BT, x.shape[1]
     rows = rs.shape[0]
-    n_blocks = n_tok // BT
     smem = pl.BlockSpec(memory_space=pltpu.SMEM)
-    blk = pl.BlockSpec((BT, hid), lambda i: (i, 0))
+    blk = pl.BlockSpec((BT, hid), lambda i: (skip + i, 0))
     whole = pl.BlockSpec((hid, hid), lambda i: (0, 0))
     return pl.pallas_call(
         functools.partial(post_bwd_kernel, n_blocks=n_blocks, top_k=top_k, n_exp=n_exp, rows=rows),
         grid=(n_blocks,),
-        in_specs=[*route_specs(top_k, n_blocks), smem, blk, blk, blk, whole, whole, pl.BlockSpec(memory_space=pl.ANY)],
-        out_specs=blk,
-        out_shape=jax.ShapeDtypeStruct((n_tok, hid), BF16),
+        in_specs=[*route_specs(top_k, n_blocks, 0, skip, total), smem, blk, blk, blk, whole, whole, pl.BlockSpec(memory_space=pl.ANY)],
+        out_specs=pl.BlockSpec((BT, hid), lambda i: (i, 0)),
+        out_shape=jax.ShapeDtypeStruct((n_blocks * BT, hid), BF16),
         scratch_shapes=[
             pltpu.VMEM((2 * rows + 8, hid // 2), F32),
             pltpu.VMEM((top_k, 2 * BT, hid // 2), F32),
@@ -638,23 +639,32 @@
         xs, dw_own = experts("own", xs, (near_sum,))
         xs, part = experts("far1", xs, (far_sum,))
         there.append(chip(part))
-        grad_x = post_bwd(pos2_b, tab_b, x_saved, grad_in, h_bwd, w1, w2, xs, n_exp, top_k)
-        x_fwd, grad_x = lax.optimization_barrier((x_fwd, grad_x))
-        dx_prev = lax.ppermute(grad_x[None], "pp", prev_perm)
-
-        parts = []
+
+        def chained(calls, perm, blocks_of, x_in):
+            pieces, skip = [], 0
+            for h, blocks in enumerate(blocks_of):
+                piece = calls(h, blocks, skip, x_in)
+                skip += blocks
+                x_in, piece = lax.optimization_barrier((x_in, piece))
+                pieces.append(lax.ppermute(piece, "pp", perm))
+            return pieces, x_in
+
+        def post_part(h, blocks, skip, x_in):
+            return post_bwd(blocks, skip, pos2_b, tab_b, x_saved, grad_in, h_bwd, w1, w2, x_in, n_exp, top_k)
+
+        dx_parts, xs = chained(post_part, prev_perm, POST_BLOCKS, xs)
+        x_fwd, xs = lax.optimization_barrier((x_fwd, xs))
+
         firsts = jnp.stack([first + i * half for first, ws in groups.values() for i in range(len(ws))])
         weights = [w for _, ws in groups.values() for w in ws]
-        skip = 0
-        for h, blocks in enumerate(FWD_BLOCKS):
-            y_half = fwd(blocks, skip, firsts, tab_f[h], pos2_f[h], gates_f, x_fwd, w1, w2, weights, rows_f[h], n_exp, top_k)
-            skip += blocks
-            if h + 1 < len(FWD_BLOCKS):
-                x_fwd, y_half = lax.optimization_barrier((x_fwd, y_half))
-            parts.append(lax.ppermute(y_half, "pp", next_perm))
+
+        def fwd_part(h, blocks, skip, x_in):
+            return fwd(blocks, skip, firsts, tab_f[h], pos2_f[h], gates_f, x_in, w1, w2, weights, rows_f[h], n_exp, top_k)
+
+        parts, _ = chained(fwd_part, next_perm, FWD_BLOCKS, x_fwd)
         y_next = jnp.concatenate(parts, axis=0)[None]
         dws = [jnp.concatenate([dw_own[i, at] + sums[i] for at, sums in zip(halves, there)], axis=0)[None] for i in range(3)]
-        dx_prev = jnp.where(me >= 0, dx_prev, jnp.zeros_like(dx_prev))
+        dx_prev = jnp.concatenate(dx_parts, axis=0)[None]
         return y_next, dx_prev, *dws
 
     in_specs = (tok_spec,) * 9 + (dense_spec, dense_spec, expert_spec, expert_spec, expert_spec)

time: 316 us -> 360 us (1.14)
  the two profiles are of different devices: /device:TPU:0 before, /device:TPU:4 now
where the time goes in v9:
time: 360 us; the launch traced here: 359 us
  Pallas kernels  181 us (50%)
  waiting for transfers between devices  135 us (38%)
  starting transfers between devices  22.9 us (6%)
  other arithmetic  14.8 us (4%)
    ppermute x4, waiting for transfers between devices, chip(): return lax.ppermute(a, 'ep', chip_perm)  93 us
    pallas_call x6, Pallas kernels, exp_bwd(): pl.pallas_call(functools.partial(exp_bwd_kernel, n_parts=len(weights), ha...  62.1 us
    pallas_call x2, Pallas kernels, fwd(): pl.pallas_call(functools.partial(fwd_kernel, n_blocks=n_blocks, top_k=top...  54.6 us
    ppermute x4, waiting for transfers between devices, chained(): pieces.append(lax.ppermute(piece, 'pp', perm))  42.5 us
    pallas_call x2, Pallas kernels, post_bwd(): pl.pallas_call(functools.partial(post_bwd_kernel, n_blocks=n_blocks, top_...  32.4 us
    pallas_call x1, Pallas kernels, pre_bwd(): pl.pallas_call(functools.partial(pre_bwd_kernel, n_blocks=n_blocks, top_k...  27.3 us
    ppermute x4, starting transfers between devices, chained(): pieces.append(lax.ppermute(piece, 'pp', perm))  13.6 us
  transfers between devices with their start and end apart: 15, of which 5 were waited for; matrix products, arithmetic and copies ran while one was open for 2% of the time, Pallas kernels for 51%

profile of v9, /device:TPU:4, one launch (start us, length us, event | category | flops | bytes accessed | tf_op | source)
XLA Modules:
  0.0 358.7 jit_solution(8219046860952357079)
XLA Ops:
  5.6 5.0 %rank.1 = (s32[8,128]{1,0:T(8,128)}, s32[128,128]{1,0:T(8,128)}, s32[128,128]{1,0:T(8,128)}, s32[2,8,128]{2,1,0:T(8,128)}, s32[80,128]{1,0:T(8,128)}, /*index=5*/s32[48,128]{1,0:T(8,128)}) custom-call(s32[4,4096]{1,0:T(4,128)} %bitcast.73, s32[4,4096]{1,0:T(4,128)} %bitcast.74, s32[4,4096]{1,0:T(4,128)} %bitcast.75, s32[4,4096]{1,0:T(4,128)} %bitcast.76), custom_call_target="tpu_custom_call" | custom-call | tf_op jit(solution)/shard_map/rank/pallas_call | solution.py:97
  10.6 29.6 %collective-permute-done.2.refs_18_.refs_0_ = bf16[4,3,256,256]{3,2,1,0:T(8,128)(2,1)} collective-permute-done((bf16[4,3,256,256]{3,2,1,0:T(8,128)(2,1)S(1)}, bf16[4,3,256,256]{3,2,1,0:T(8,128)(2,1)}, u32[]{:S(2)}, u32[]{:S(2)}) %collective-permute-start.2) | collective-permute-done | bytes 1572896 | tf_op jit(solution)/shard_map/ppermute | solution.py:593
  40.3 32.6 %collective-permute-done.3.refs_19_.refs_0_ = bf16[4,3,256,256]{3,2,1,0:T(8,128)(2,1)} collective-permute-done((bf16[4,3,256,256]{3,2,1,0:T(8,128)(2,1)S(1)}, bf16[4,3,256,256]{3,2,1,0:T(8,128)(2,1)}, u32[]{:S(2)}, u32[]{:S(2)}) %collective-permute-start.3) | collective-permute-done | bytes 1572896 | tf_op jit(solution)/shard_map/ppermute | solution.py:593
  72.8 27.3 %pre_bwd.1 = (bf16[4096,256]{1,0:T(8,128)(2,1)}, bf16[24576,256]{1,0:T(8,128)(2,1)}, bf16[24576,256]{1,0:T(8,128)(2,1)}) custom-call(s32[16384]{0:T(1024)} %bitcast.103, s32[16384]{0:T(1024)} %bitcast.104, s32[16384]{0:T(1024)} %bitcast.105, s32[16384]{0:T(1024)} %bitcast.106, s32[8,128]{1,0:T(8,128)} %get-tuple-element.38.refs_4_.tab_ref, ...), custom_call_target="tpu_custom_call" | custom-call | flops 30000001024 | bytes 30000000 | tf_op jit(solution)/shard_map/pre_bwd/pallas_call | solution.py:236
  101.4 5.2 %exp_bwd.6 = (bf16[24576,256]{1,0:T(8,128)(2,1)}, f32[3,4,256,256]{3,2,1,0:T(8,128)}) custom-call(s32[1]{0:T(128)} %bitcast.16.first_ref, s32[8,128]{1,0:T(8,128)} %get-tuple-element.38.refs_4_.tab_ref, bf16[24576,256]{1,0:T(8,128)(2,1)} %get-tuple-element.40.xs_hbm, bf16[24576,256]{1,0:T(8,128)(2,1)} %get-tuple-element.41.qs_hbm, ...), custom_call_target="tpu_custom_call", output_to_operand_aliasing={{0}: (2, {})} | custom-call | flops 8000000000 | bytes 20000000 | tf_op jit(solution)/shard_map/exp_bwd/pallas_call | solution.py:383
  106.6 2.8 collective-permute-start.8
  109.5 32.9 %fwd.2 = bf16[2560,256]{1,0:T(8,128)(2,1)} custom-call(s32[10240]{0:T(1024)} %bitcast.107, s32[10240]{0:T(1024)} %bitcast.108, s32[10240]{0:T(1024)} %bitcast.109, s32[10240]{0:T(1024)} %bitcast.110, s32[10240]{0:T(1024)} %bitcast.111, s32[10240]{0:T(1024)} %bitcast.112, s32[10240]{0:T(1024)} %bitcast.113, s32[10240]{0:T(1024)} %bitcast.114, ...), custom_call_target="tpu_custom_call" | custom-call | flops 80000000000 | bytes 30000000 | tf_op jit(solution)/shard_map/fwd/pallas_call | solution.py:556
  142.4 15.3 %exp_bwd.7 = (bf16[24576,256]{1,0:T(8,128)(2,1)}, f32[3,8,256,256]{3,2,1,0:T(8,128)}) custom-call(s32[1]{0:T(128)} %bitcast.12.first_ref, s32[8,128]{1,0:T(8,128)} %get-tuple-element.38.refs_4_.tab_ref, bf16[24576,256]{1,0:T(8,128)(2,1)} %get-tuple-element.42.xs_hbm, bf16[24576,256]{1,0:T(8,128)(2,1)} %get-tuple-element.41.qs_hbm, ...), custom_call_target="tpu_custom_call", output_to_operand_aliasing={{0}: (2, {})} | custom-call | flops 8000000000 | bytes 20000000 | tf_op jit(solution)/shard_map/exp_bwd/pallas_call | solution.py:383
  157.7 2.7 collective-permute-start.9
  160.5 7.8 %exp_bwd.8 = (bf16[24576,256]{1,0:T(8,128)(2,1)}, f32[3,4,256,256]{3,2,1,0:T(8,128)}) custom-call(s32[1]{0:T(128)} %bitcast.14.first_ref, s32[8,128]{1,0:T(8,128)} %get-tuple-element.38.refs_4_.tab_ref, bf16[24576,256]{1,0:T(8,128)(2,1)} %get-tuple-element.43.xs_hbm, bf16[24576,256]{1,0:T(8,128)(2,1)} %get-tuple-element.41.qs_hbm, ...), custom_call_target="tpu_custom_call", output_to_operand_aliasing={{0}: (2, {})} | custom-call | flops 8000000000 | bytes 20000000 | tf_op jit(solution)/shard_map/exp_bwd/pallas_call | solution.py:383
  168.3 8.2 %exp_bwd.9 = (bf16[24576,256]{1,0:T(8,128)(2,1)}, f32[3,4,256,256]{3,2,1,0:T(8,128)}) custom-call(s32[1]{0:T(128)} %bitcast.17.first_ref, s32[8,128]{1,0:T(8,128)} %get-tuple-element.38.refs_4_.tab_ref, bf16[24576,256]{1,0:T(8,128)(2,1)} %get-tuple-element.45.xs_hbm, bf16[24576,256]{1,0:T(8,128)(2,1)} %get-tuple-element.41.qs_hbm, ...), custom_call_target="tpu_custom_call", output_to_operand_aliasing={{0}: (2, {})} | custom-call | flops 8000000000 | bytes 20000000 | tf_op jit(solution)/shard_map/exp_bwd/pallas_call | solution.py:383
  176.5 21.6 %fwd.3 = bf16[1536,256]{1,0:T(8,128)(2,1)} custom-call(s32[6144]{0:T(1024)} %bitcast.118, s32[6144]{0:T(1024)} %bitcast.119, s32[6144]{0:T(1024)} %bitcast.120, s32[6144]{0:T(1024)} %bitcast.121, s32[6144]{0:T(1024)} %bitcast.122, s32[6144]{0:T(1024)} %bitcast.123, s32[6144]{0:T(1024)} %bitcast.124, s32[6144]{0:T(1024)} %bitcast.125, s32[8]{0:T(128)} %stack.41.refs_8_, ...), custom_call_target="tpu_custom_call" | custom-call | flops 80000000000 | bytes 30000000 | tf_op jit(solution)/shard_map/fwd/pallas_call | solution.py:556
  198.3 12.9 %collective-permute-start.6 = (bf16[2560,256]{1,0:T(8,128)(2,1)}, bf16[2560,256]{1,0:T(8,128)(2,1)}, u32[]{:S(2)}, u32[]{:S(2)}) collective-permute-start(bf16[2560,256]{1,0:T(8,128)(2,1)} %fwd.2), channel_id=1, source_target_pairs={{0,4},{4,8},{8,12},{12,0},{1,5},{5,9},{9,13},{13,1},{2,6},{6,10},{... | collective-permute-start | bytes 3932168 | tf_op jit(solution)/shard_map/ppermute | solution.py:649
  211.2 19.5 %exp_bwd.10 = (bf16[24576,256]{1,0:T(8,128)(2,1)}, f32[3,8,256,256]{3,2,1,0:T(8,128)}) custom-call(s32[1]{0:T(128)} %bitcast.10.first_ref, s32[8,128]{1,0:T(8,128)} %get-tuple-element.38.refs_4_.tab_ref, bf16[24576,256]{1,0:T(8,128)(2,1)} %get-tuple-element.46.xs_hbm, bf16[24576,256]{1,0:T(8,128)(2,1)} %get-tuple-element.41.qs_hbm, ...), custom_call_target="tpu_custom_call", output_to_operand_aliasing={{0}: (2, {})} | custom-call | flops 8000000000 | bytes 20000000 | tf_op jit(solution)/shard_map/exp_bwd/pallas_call | solution.py:383
  230.8 6.1 %exp_bwd.11 = (bf16[24576,256]{1,0:T(8,128)(2,1)}, f32[3,4,256,256]{3,2,1,0:T(8,128)}) custom-call(s32[1]{0:T(128)} %bitcast.15.first_ref, s32[8,128]{1,0:T(8,128)} %get-tuple-element.38.refs_4_.tab_ref, bf16[24576,256]{1,0:T(8,128)(2,1)} %get-tuple-element.48.xs_hbm, bf16[24576,256]{1,0:T(8,128)(2,1)} %get-tuple-element.41.qs_hbm, ...), custom_call_target="tpu_custom_call", output_to_operand_aliasing={{0}: (2, {})} | custom-call | flops 8000000000 | bytes 20000000 | tf_op jit(solution)/shard_map/exp_bwd/pallas_call | solution.py:383
  236.9 16.2 %post_bwd.2 = bf16[2048,256]{1,0:T(8,128)(2,1)} custom-call(s32[16384]{0:T(1024)} %bitcast.95, s32[16384]{0:T(1024)} %bitcast.96, s32[16384]{0:T(1024)} %bitcast.97, s32[16384]{0:T(1024)} %bitcast.98, s32[8,128]{1,0:T(8,128)} %get-tuple-element.38.refs_4_.tab_ref, bf16[4096,256]{1,0:T(8,128)(2,1)} %bitcast.80, bf16[4096,256]{1,0:T(8,128)(2,1)} %bitcast.83, ...), custom_call_target="tpu_custom_call" | custom-call | flops 30000001024 | bytes 30000000 | tf_op jit(solution)/shard_map/post_bwd/pallas_call | solution.py:452
  254.1 16.2 %post_bwd.3 = bf16[2048,256]{1,0:T(8,128)(2,1)} custom-call(s32[16384]{0:T(1024)} %bitcast.99, s32[16384]{0:T(1024)} %bitcast.100, s32[16384]{0:T(1024)} %bitcast.101, s32[16384]{0:T(1024)} %bitcast.102, s32[8,128]{1,0:T(8,128)} %get-tuple-element.38.refs_4_.tab_ref, bf16[4096,256]{1,0:T(8,128)(2,1)} %bitcast.81, bf16[4096,256]{1,0:T(8,128)(2,1)} %bitcast.84, ...), custom_call_target="tpu_custom_call" | custom-call | flops 30000001024 | bytes 30000000 | tf_op jit(solution)/shard_map/post_bwd/pallas_call | solution.py:452
  271.0 2.8 maximum_bitcast_fusion
  273.7 23.8 %collective-permute-done.12 = bf16[2048,256]{1,0:T(8,128)(2,1)S(1)} collective-permute-done((bf16[2048,256]{1,0:T(8,128)(2,1)}, bf16[2048,256]{1,0:T(8,128)(2,1)S(1)}, u32[]{:S(2)}, u32[]{:S(2)}) %collective-permute-start.12) | collective-permute-done | bytes 1048608 | tf_op jit(solution)/shard_map/ppermute | solution.py:649
  297.5 18.7 %collective-permute-done.11 = bf16[2048,256]{1,0:T(8,128)(2,1)S(1)} collective-permute-done((bf16[2048,256]{1,0:T(8,128)(2,1)}, bf16[2048,256]{1,0:T(8,128)(2,1)S(1)}, u32[]{:S(2)}, u32[]{:S(2)}) %collective-permute-start.11) | collective-permute-done | bytes 1048608 | tf_op jit(solution)/shard_map/ppermute | solution.py:649
  317.6 30.8 %collective-permute-done.14 = f32[3,4,256,256]{3,2,1,0:T(8,128)} collective-permute-done((f32[3,4,256,256]{3,2,1,0:T(8,128)}, f32[3,4,256,256]{3,2,1,0:T(8,128)}, u32[]{:S(2)}, u32[]{:S(2)}) %collective-permute-start.14) | collective-permute-done | bytes 3145760 | tf_op jit(solution)/shard_map/ppermute | solution.py:593
  348.4 5.7 %fusion.1 = (f32[4,256,256]{2,1,0:T(8,128)S(1)}, f32[4,256,256]{2,1,0:T(8,128)S(1)}, f32[4,256,256]{2,1,0:T(8,128)S(1)}, f32[4,256,256]{2,1,0:T(8,128)S(1)}, f32...) fusion(f32[3,4,256,256]{3,2,1,0:T(8,128)} %copy-done.2, f32[3,8,256,256]{3,2,1,0:T(8,128)} %get-tuple-element.56, ...), kind=kLoop, calls=%fused_computation.10 | loop fusion | flops 1572864 | bytes 18874368 | tf_op jit(solution)/shard_map/add | solution.py:666
  354.1 1.6 maximum_bitcast_fusion.4
  355.7 1.5 maximum_bitcast_fusion.3
  (42 shorter events, 10.9 us)
Async XLA Ops:
  0.6 1.5 copy-start.3
  0.6 1.8 copy-start.4
  2.8 97.3 %copy-start = (bf16[4,3,256,256]{3,2,1,0:T(8,128)(2,1)}, bf16[4,3,256,256]{3,2,1,0:T(8,128)(2,1)S(1)}, u32[]{:S(2)}) copy-start(bf16[4,3,256,256]{3,2,1,0:T(8,128)(2,1)S(1)} %pad_maximum_fusion.refs_14_.refs_0_) | copy-start | bytes 4718596
  2.9 37.4 %collective-permute-start.2 = (bf16[4,3,256,256]{3,2,1,0:T(8,128)(2,1)S(1)}, bf16[4,3,256,256]{3,2,1,0:T(8,128)(2,1)}, u32[]{:S(2)}, u32[]{:S(2)}) collective-permute-start(bf16[4,3,256,256]{3,2,1,0:T(8,128)(2,1)S(1)} %pad_maximum_fusion.refs_14_.refs_0_), channel_id=1, source_target_pairs={{0,2},{1,3},{2,0},{3,1},{4,6},{5,7},{6,4},{7,5},{8,10},{9,11},{10,... | collective-permute-start | bytes 4718600 | tf_op jit(solution)/shard_map/ppermute | solution.py:593
  4.6 95.6 %copy-start.1 = (bf16[4,3,256,256]{3,2,1,0:T(8,128)(2,1)}, bf16[4,3,256,256]{3,2,1,0:T(8,128)(2,1)S(1)}, u32[]{:S(2)}) copy-start(bf16[4,3,256,256]{3,2,1,0:T(8,128)(2,1)S(1)} %pad_maximum_fusion.1.refs_15_.refs_1_) | copy-start | bytes 4718596
  4.6 68.3 %collective-permute-start.3 = (bf16[4,3,256,256]{3,2,1,0:T(8,128)(2,1)S(1)}, bf16[4,3,256,256]{3,2,1,0:T(8,128)(2,1)}, u32[]{:S(2)}, u32[]{:S(2)}) collective-permute-start(bf16[4,3,256,256]{3,2,1,0:T(8,128)(2,1)S(1)} %pad_maximum_fusion.1.refs_15_.refs_1_), channel_id=1, source_target_pairs={{0,2},{1,3},{2,0},{3,1},{4,6},{5,7},{6,4},{7,5},{8,10},{9,11},{10,... | collective-permute-start | bytes 4718600 | tf_op jit(solution)/shard_map/ppermute | solution.py:593
  5.1 104.3 %collective-permute-start = (bf16[4,3,256,256]{3,2,1,0:T(8,128)(2,1)S(1)}, bf16[4,3,256,256]{3,2,1,0:T(8,128)(2,1)}, u32[]{:S(2)}, u32[]{:S(2)}) collective-permute-start(bf16[4,3,256,256]{3,2,1,0:T(8,128)(2,1)S(1)} %pad_maximum_fusion.refs_14_.refs_0_), channel_id=1, source_target_pairs={{0,1},{1,0},{2,3},{3,2},{4,5},{5,4},{6,7},{7,6},{8,9},{9,8},{10,11... | collective-permute-start | bytes 4718600 | tf_op jit(solution)/shard_map/ppermute | solution.py:590
  5.1 104.3 %collective-permute-start.1 = (bf16[4,3,256,256]{3,2,1,0:T(8,128)(2,1)S(1)}, bf16[4,3,256,256]{3,2,1,0:T(8,128)(2,1)}, u32[]{:S(2)}, u32[]{:S(2)}) collective-permute-start(bf16[4,3,256,256]{3,2,1,0:T(8,128)(2,1)S(1)} %pad_maximum_fusion.1.refs_15_.refs_1_), channel_id=1, source_target_pairs={{0,1},{1,0},{2,3},{3,2},{4,5},{5,4},{6,7},{7,6},{8,9},{9,8},{10,11... | collective-permute-start | bytes 4718600 | tf_op jit(solution)/shard_map/ppermute | solution.py:590
  40.3 61.2 %collective-permute-start.4 = (bf16[4,3,256,256]{3,2,1,0:T(8,128)(2,1)}, bf16[4,3,256,256]{3,2,1,0:T(8,128)(2,1)}, u32[]{:S(2)}, u32[]{:S(2)}) collective-permute-start(bf16[4,3,256,256]{3,2,1,0:T(8,128)(2,1)} %collective-permute-done.2.refs_18_.refs_0_), channel_id=1, source_target_pairs={{0,1},{1,0},{2,3},{3,2},{4,5},{5,4},{6,7},{7,6},{8,9},{9,8},{10,11... | collective-permute-start | bytes 4718600 | tf_op jit(solution)/shard_map/ppermute | solution.py:590
  72.8 36.6 %collective-permute-start.5 = (bf16[4,3,256,256]{3,2,1,0:T(8,128)(2,1)}, bf16[4,3,256,256]{3,2,1,0:T(8,128)(2,1)}, u32[]{:S(2)}, u32[]{:S(2)}) collective-permute-start(bf16[4,3,256,256]{3,2,1,0:T(8,128)(2,1)} %collective-permute-done.3.refs_19_.refs_0_), channel_id=1, source_target_pairs={{0,1},{1,0},{2,3},{3,2},{4,5},{5,4},{6,7},{7,6},{8,9},{9,8},{10,11... | collective-permute-start | bytes 4718600 | tf_op jit(solution)/shard_map/ppermute | solution.py:590
  72.8 28.0 %copy-start.5 = (s32[2,8,128]{2,1,0:T(8,128)S(1)}, s32[2,8,128]{2,1,0:T(8,128)}, u32[]{:S(2)}) copy-start(s32[2,8,128]{2,1,0:T(8,128)} %get-tuple-element.33) | copy-start | bytes 24580
  106.6 53.8 %collective-permute-start.8 = (f32[3,4,256,256]{3,2,1,0:T(8,128)}, f32[3,4,256,256]{3,2,1,0:T(8,128)}, u32[]{:S(2)}, u32[]{:S(2)}) collective-permute-start(f32[3,4,256,256]{3,2,1,0:T(8,128)} %get-tuple-element.44), channel_id=1, source_target_pairs={{0,1},{1,0},{2,3},{3,2},{4,5},{5,4},{6,7},{7,6},{8,9},{9,8},{10,11... | collective-permute-start | bytes 9437192 | tf_op jit(solution)/shard_map/ppermute | solution.py:590
  157.7 53.5 %collective-permute-start.9 = (f32[3,8,256,256]{3,2,1,0:T(8,128)}, f32[3,8,256,256]{3,2,1,0:T(8,128)}, u32[]{:S(2)}, u32[]{:S(2)}) collective-permute-start(f32[3,8,256,256]{3,2,1,0:T(8,128)} %get-tuple-element.47), channel_id=1, source_target_pairs={{0,1},{1,0},{2,3},{3,2},{4,5},{5,4},{6,7},{7,6},{8,9},{9,8},{10,11... | collective-permute-start | bytes 18874376 | tf_op jit(solution)/shard_map/ppermute | solution.py:590
  176.5 54.3 %collective-permute-start.10 = (f32[3,4,256,256]{3,2,1,0:T(8,128)}, f32[3,4,256,256]{3,2,1,0:T(8,128)}, u32[]{:S(2)}, u32[]{:S(2)}) collective-permute-start(f32[3,4,256,256]{3,2,1,0:T(8,128)} %get-tuple-element.49), channel_id=1, source_target_pairs={{0,1},{1,0},{2,3},{3,2},{4,5},{5,4},{6,7},{7,6},{8,9},{9,8},{10,11... | collective-permute-start | bytes 9437192 | tf_op jit(solution)/shard_map/ppermute | solution.py:590
  198.2 72.2 %collective-permute-start.7 = (bf16[1536,256]{1,0:T(8,128)(2,1)}, bf16[1536,256]{1,0:T(8,128)(2,1)S(1)}, u32[]{:S(2)}, u32[]{:S(2)}) collective-permute-start(bf16[1536,256]{1,0:T(8,128)(2,1)} %fwd.3), channel_id=1, source_target_pairs={{0,4},{4,8},{8,12},{12,0},{1,5},{5,9},{9,13},{13,1},{2,6},{6,10},{... | collective-permute-start | bytes 2359304 | tf_op jit(solution)/shard_map/ppermute | solution.py:649
  198.3 72.7 %collective-permute-start.6 = (bf16[2560,256]{1,0:T(8,128)(2,1)}, bf16[2560,256]{1,0:T(8,128)(2,1)}, u32[]{:S(2)}, u32[]{:S(2)}) collective-permute-start(bf16[2560,256]{1,0:T(8,128)(2,1)} %fwd.2), channel_id=1, source_target_pairs={{0,4},{4,8},{8,12},{12,0},{1,5},{5,9},{9,13},{13,1},{2,6},{6,10},{... | collective-permute-start | bytes 3932168 | tf_op jit(solution)/shard_map/ppermute | solution.py:649
  211.2 106.5 %collective-permute-start.13 = (f32[3,4,256,256]{3,2,1,0:T(8,128)}, f32[3,4,256,256]{3,2,1,0:T(8,128)S(1)}, u32[]{:S(2)}, u32[]{:S(2)}) collective-permute-start(f32[3,4,256,256]{3,2,1,0:T(8,128)} %get-tuple-element.57), channel_id=1, source_target_pairs={{0,2},{1,3},{2,0},{3,1},{4,6},{5,7},{6,4},{7,5},{8,10},{9,11},{10,... | collective-permute-start | bytes 9437192 | tf_op jit(solution)/shard_map/ppermute | solution.py:593
  253.0 95.4 %collective-permute-start.14 = (f32[3,4,256,256]{3,2,1,0:T(8,128)}, f32[3,4,256,256]{3,2,1,0:T(8,128)}, u32[]{:S(2)}, u32[]{:S(2)}) collective-permute-start(f32[3,4,256,256]{3,2,1,0:T(8,128)} %get-tuple-element.58), channel_id=1, source_target_pairs={{0,2},{1,3},{2,0},{3,1},{4,6},{5,7},{6,4},{7,5},{8,10},{9,11},{10,... | collective-permute-start | bytes 9437192 | tf_op jit(solution)/shard_map/ppermute | solution.py:593
  270.3 27.2 %collective-permute-start.12 = (bf16[2048,256]{1,0:T(8,128)(2,1)}, bf16[2048,256]{1,0:T(8,128)(2,1)S(1)}, u32[]{:S(2)}, u32[]{:S(2)}) collective-permute-start(bf16[2048,256]{1,0:T(8,128)(2,1)} %post_bwd.3), channel_id=1, source_target_pairs={{0,12},{4,0},{8,4},{12,8},{1,13},{5,1},{9,5},{13,9},{2,14},{6,2},{... | collective-permute-start | bytes 3145736 | tf_op jit(solution)/shard_map/ppermute | solution.py:649
  270.4 45.8 %collective-permute-start.11 = (bf16[2048,256]{1,0:T(8,128)(2,1)}, bf16[2048,256]{1,0:T(8,128)(2,1)S(1)}, u32[]{:S(2)}, u32[]{:S(2)}) collective-permute-start(bf16[2048,256]{1,0:T(8,128)(2,1)} %post_bwd.2), channel_id=1, source_target_pairs={{0,12},{4,0},{8,4},{12,8},{1,13},{5,1},{9,5},{13,9},{2,14},{6,2},{... | collective-permute-start | bytes 3145736 | tf_op jit(solution)/shard_map/ppermute | solution.py:649
  317.6 30.8 %copy-start.2 = (f32[3,4,256,256]{3,2,1,0:T(8,128)}, f32[3,4,256,256]{3,2,1,0:T(8,128)S(1)}, u32[]{:S(2)}) copy-start(f32[3,4,256,256]{3,2,1,0:T(8,128)S(1)} %collective-permute-done.13) | copy-start | bytes 9437188

commit v10 on v9

--- a/solution.py
+++ b/solution.py
@@ -13,8 +13,8 @@
 BT = 512
 DEPTH = 4
 QUEUE = 8
-FWD_BLOCKS = (5, 3)
-POST_BLOCKS = (4, 4)
+FWD_BLOCKS = (4, 4)
+POST_BLOCKS = (6, 2)
 F32 = jnp.float32
 BF16 = jnp.bfloat16
 VMEM_LIMIT = 60 * 1024 * 1024
@@ -76,36 +76,24 @@
     return jnp.concatenate([ref[r : r + 1, c * 128 : (c + 1) * 128] for r in range(ref.shape[0]) for c in range(first, last)], axis=0)
 
 
-def rank_kernel(n_exp, rows_b, rows_f, ids_b, slots_b, ids_f, slots_f, tab_b, pos4_b, pos2_b, tab_f, *pos2_f):
-    n = ids_b.shape[1] // 128
-    pos, tab_b[...] = rank_routes(chunks(ids_b, 0, n), chunks(slots_b, 0, n), n_exp, rows_b)
-    pos4_b[...] = (pos * 4.0).astype(jnp.int32)
-    pos2_b[...] = (pos * 2.0).astype(jnp.int32)
+def rank_kernel(n_exp, blocks_of, dumps, scales, ids, slots, tab, *tables):
     first = 0
-    for h, (blocks, dump) in enumerate(zip(FWD_BLOCKS, rows_f)):
+    for h, (blocks, dump) in enumerate(zip(blocks_of, dumps)):
         last = first + blocks * (BT // 128)
-        pos, tab_f[h] = rank_routes(chunks(ids_f, first, last), chunks(slots_f, first, last), n_exp, dump)
-        pos2_f[h][...] = (pos * 2.0).astype(jnp.int32)
+        pos, tab[h] = rank_routes(chunks(ids, first, last), chunks(slots, first, last), n_exp, dump)
+        for k, scale in enumerate(scales):
+            tables[h * len(scales) + k][...] = (pos * scale).astype(jnp.int32)
         first = last
 
 
-def route_ranks(ids_b, slots_b, ids_f, slots_f, n_exp, rows_b, rows_f):
-    def table(n_tok):
-        return jax.ShapeDtypeStruct((n_tok * ids_b.shape[1] // 128, 128), jnp.int32)
-
-    n_tok = ids_b.shape[0]
-    tab_b, pos4_b, pos2_b, tab_f, *pos2_f = pl.pallas_call(
-        functools.partial(rank_kernel, n_exp, rows_b, rows_f),
-        out_shape=(
-            jax.ShapeDtypeStruct((8, 128), jnp.int32),
-            table(n_tok),
-            table(n_tok),
-            jax.ShapeDtypeStruct((len(FWD_BLOCKS), 8, 128), jnp.int32),
-            *[table(blocks * BT) for blocks in FWD_BLOCKS],
-        ),
+def route_ranks(ids, slots, n_exp, blocks_of, dumps, scales):
+    tables = [jax.ShapeDtypeStruct((blocks * BT * ids.shape[1] // 128, 128), jnp.int32) for blocks in blocks_of for _ in scales]
+    tab, *pos = pl.pallas_call(
+        functools.partial(rank_kernel, n_exp, blocks_of, dumps, scales),
+        out_shape=(jax.ShapeDtypeStruct((len(blocks_of), 8, 128), jnp.int32), *tables),
         name="rank",
-    )(ids_b.T, slots_b.T, ids_f.T, slots_f.T)
-    return tab_b, pos4_b.reshape(-1), pos2_b.reshape(-1), tab_f, [p.reshape(-1) for p in pos2_f]
+    )(ids.T, slots.T)
+    return tab, [p.reshape(-1) for p in pos]
 
 
 def put_rows(ref, at, vals, pitch=2, off=0):
@@ -618,7 +606,9 @@
             "relay1": ((me ^ 3) * n_loc + half, relay[1:]),
         }
 
-        tab_b, pos4_b, pos2_b, tab_f, pos2_f = route_ranks(ids_bwd, slots_bwd, ids_fwd, slots_fwd, n_exp, rows, rows_f)
+        tab_b, (pos4_b, pos2_b) = route_ranks(ids_bwd, slots_bwd, n_exp, (ids_bwd.shape[0] // BT,), (rows,), (4.0, 2.0))
+        tab_b = tab_b[0]
+        tab_f, pos2_f = route_ranks(ids_fwd, slots_fwd, n_exp, FWD_BLOCKS, rows_f, (2.0,))
         gates_b = gates_bwd.T
         gates_f = gates_fwd.T
 
@@ -639,31 +629,31 @@
         xs, dw_own = experts("own", xs, (near_sum,))
         xs, part = experts("far1", xs, (far_sum,))
         there.append(chip(part))
-
-        def chained(calls, perm, blocks_of, x_in):
-            pieces, skip = [], 0
-            for h, blocks in enumerate(blocks_of):
-                piece = calls(h, blocks, skip, x_in)
-                skip += blocks
-                x_in, piece = lax.optimization_barrier((x_in, piece))
-                pieces.append(lax.ppermute(piece, "pp", perm))
-            return pieces, x_in
-
-        def post_part(h, blocks, skip, x_in):
-            return post_bwd(blocks, skip, pos2_b, tab_b, x_saved, grad_in, h_bwd, w1, w2, x_in, n_exp, top_k)
-
-        dx_parts, xs = chained(post_part, prev_perm, POST_BLOCKS, xs)
-        x_fwd, xs = lax.optimization_barrier((x_fwd, xs))
-
         firsts = jnp.stack([first + i * half for first, ws in groups.values() for i in range(len(ws))])
         weights = [w for _, ws in groups.values() for w in ws]
 
-        def fwd_part(h, blocks, skip, x_in):
+        def post_part(h, rs):
+            blocks, skip = POST_BLOCKS[h], sum(POST_BLOCKS[:h])
+            return post_bwd(blocks, skip, pos2_b, tab_b, x_saved, grad_in, h_bwd, w1, w2, rs, n_exp, top_k)
+
+        def fwd_part(h, x_in):
+            blocks, skip = FWD_BLOCKS[h], sum(FWD_BLOCKS[:h])
             return fwd(blocks, skip, firsts, tab_f[h], pos2_f[h], gates_f, x_in, w1, w2, weights, rows_f[h], n_exp, top_k)
 
-        parts, _ = chained(fwd_part, next_perm, FWD_BLOCKS, x_fwd)
+        def send(piece, perm):
+            return lax.ppermute(piece, "pp", perm)
+
+        dx_parts, parts = [], []
+        piece = post_part(0, xs)
+        x_fwd, piece = lax.optimization_barrier((x_fwd, piece))
+        dx_parts.append(send(piece, prev_perm))
+        for h in range(len(FWD_BLOCKS)):
+            piece = fwd_part(h, x_fwd)
+            x_fwd, xs, piece = lax.optimization_barrier((x_fwd, xs, piece))
+            parts.append(send(piece, next_perm))
+        dx_parts.append(send(post_part(1, xs), prev_perm))
         y_next = jnp.concatenate(parts, axis=0)[None]
-        dws = [jnp.concatenate([dw_own[i, at] + sums[i] for at, sums in zip(halves, there)], axis=0)[None] for i in range(3)]
+        dws = [(dw_own[i] + jnp.concatenate([sums[i] for sums in there], axis=0))[None] for i in range(3)]
         dx_prev = jnp.concatenate(dx_parts, axis=0)[None]
         return y_next, dx_prev, *dws
 

time: 360 us -> 332 us (0.922)
  the two profiles are of different devices: /device:TPU:4 before, /device:TPU:0 now
where the time goes in v10:
time: 332 us; the launch traced here: 330 us
  Pallas kernels  185 us (56%)
  waiting for transfers between devices  101 us (30%)
  starting transfers between devices  25.2 us (8%)
  local copies, waits for them, and re-layouts  10.8 us (3%)
  other arithmetic  7.6 us (2%)
    ppermute x4, waiting for transfers between devices, send(): return lax.ppermute(piece, 'pp', perm)  67.4 us
    pallas_call x6, Pallas kernels, exp_bwd(): pl.pallas_call(functools.partial(exp_bwd_kernel, n_parts=len(weights), ha...  61.7 us
    pallas_call x2, Pallas kernels, fwd(): pl.pallas_call(functools.partial(fwd_kernel, n_blocks=n_blocks, top_k=top...  56.5 us
    pallas_call x2, Pallas kernels, post_bwd(): pl.pallas_call(functools.partial(post_bwd_kernel, n_blocks=n_blocks, top_...  32.3 us
    ppermute x4, waiting for transfers between devices, chip(): return lax.ppermute(a, 'ep', chip_perm)  31.4 us
    pallas_call x1, Pallas kernels, pre_bwd(): pl.pallas_call(functools.partial(pre_bwd_kernel, n_blocks=n_blocks, top_k...  27.3 us
    ppermute x4, starting transfers between devices, chip(): return lax.ppermute(a, 'ep', chip_perm)  14.3 us
    pallas_call x2, Pallas kernels, route_ranks(): pl.pallas_call(functools.partial(rank_kernel, n_exp, blocks_of, dumps, sc...  6.85 us
  transfers between devices with their start and end apart: 15, of which 5 were waited for; matrix products, arithmetic and copies ran while one was open for 3% of the time, Pallas kernels for 56%

profile of v10, /device:TPU:0, one launch (start us, length us, event | category | flops | bytes accessed | tf_op | source)
XLA Modules:
  0.0 330.0 jit_solution(13943988735686153390)
XLA Ops:
  2.9 3.2 collective-permute-start
  6.9 3.2 rank.2
  10.1 31.3 %collective-permute-done.refs_0_.refs_18_ = bf16[4,3,256,256]{3,2,1,0:T(8,128)(2,1)} collective-permute-done((bf16[4,3,256,256]{3,2,1,0:T(8,128)(2,1)S(1)}, bf16[4,3,256,256]{3,2,1,0:T(8,128)(2,1)}, u32[]{:S(2)}, u32[]{:S(2)}) %collective-permute-start) | collective-permute-done | bytes 1572896 | tf_op jit(solution)/shard_map/ppermute | solution.py:581
  41.5 27.3 %pre_bwd.1 = (bf16[4096,256]{1,0:T(8,128)(2,1)}, bf16[24576,256]{1,0:T(8,128)(2,1)}, bf16[24576,256]{1,0:T(8,128)(2,1)}) custom-call(s32[16384]{0:T(1024)} %bitcast.97, s32[16384]{0:T(1024)} %bitcast.98, s32[16384]{0:T(1024)} %bitcast.99, s32[16384]{0:T(1024)} %bitcast.100, s32[8,128]{1,0:T(8,128)} %bitcast.62, bf16[4,4096]{1,0:T(4,128)(2,1)} %bitcast.101, ...), custom_call_target="tpu_custom_call" | custom-call | flops 30000001024 | bytes 30000000 | tf_op jit(solution)/shard_map/pre_bwd/pallas_call | solution.py:224
  68.8 6.4 %exp_bwd.6 = (bf16[24576,256]{1,0:T(8,128)(2,1)}, f32[3,4,256,256]{3,2,1,0:T(8,128)}) custom-call(s32[1]{0:T(128)} %bitcast.19.first_ref, s32[8,128]{1,0:T(8,128)} %bitcast.63, bf16[24576,256]{1,0:T(8,128)(2,1)} %get-tuple-element.37.xs_hbm, bf16[24576,256]{1,0:T(8,128)(2,1)} %get-tuple-element.38.qs_hbm, ...), custom_call_target="tpu_custom_call", output_to_operand_aliasing={{0}: (2, {})} | custom-call | flops 8000000000 | bytes 20000000 | tf_op jit(solution)/shard_map/exp_bwd/pallas_call | solution.py:371
  77.1 18.0 %exp_bwd.7 = (bf16[24576,256]{1,0:T(8,128)(2,1)}, f32[3,8,256,256]{3,2,1,0:T(8,128)}) custom-call(s32[1]{0:T(128)} %bitcast.18.first_ref, s32[8,128]{1,0:T(8,128)} %bitcast.64, bf16[24576,256]{1,0:T(8,128)(2,1)} %get-tuple-element.39.xs_hbm, bf16[24576,256]{1,0:T(8,128)(2,1)} %get-tuple-element.38.qs_hbm, ...), custom_call_target="tpu_custom_call", output_to_operand_aliasing={{0}: (2, {})} | custom-call | flops 8000000000 | bytes 20000000 | tf_op jit(solution)/shard_map/exp_bwd/pallas_call | solution.py:371
  95.7 10.1 %exp_bwd.8 = (bf16[24576,256]{1,0:T(8,128)(2,1)}, f32[3,4,256,256]{3,2,1,0:T(8,128)}) custom-call(s32[1]{0:T(128)} %bitcast.17.first_ref, s32[8,128]{1,0:T(8,128)} %bitcast.65, bf16[24576,256]{1,0:T(8,128)(2,1)} %get-tuple-element.40.xs_hbm, bf16[24576,256]{1,0:T(8,128)(2,1)} %get-tuple-element.38.qs_hbm, ...), custom_call_target="tpu_custom_call", output_to_operand_aliasing={{0}: (2, {})} | custom-call | flops 8000000000 | bytes 20000000 | tf_op jit(solution)/shard_map/exp_bwd/pallas_call | solution.py:371
  109.0 5.2 %exp_bwd.9 = (bf16[24576,256]{1,0:T(8,128)(2,1)}, f32[3,4,256,256]{3,2,1,0:T(8,128)}) custom-call(s32[1]{0:T(128)} %bitcast.16.first_ref, s32[8,128]{1,0:T(8,128)} %bitcast.66, bf16[24576,256]{1,0:T(8,128)(2,1)} %get-tuple-element.42.xs_hbm, bf16[24576,256]{1,0:T(8,128)(2,1)} %get-tuple-element.38.qs_hbm, ...), custom_call_target="tpu_custom_call", output_to_operand_aliasing={{0}: (2, {})} | custom-call | flops 8000000000 | bytes 20000000 | tf_op jit(solution)/shard_map/exp_bwd/pallas_call | solution.py:371
  114.1 2.8 collective-permute-start.8
  117.0 3.6 %rank.3 = (s32[2,8,128]{2,1,0:T(8,128)}, s32[64,128]{1,0:T(8,128)}, s32[64,128]{1,0:T(8,128)}) custom-call(s32[4,4096]{1,0:T(4,128)} %bitcast.60, s32[4,4096]{1,0:T(4,128)} %bitcast.61), custom_call_target="tpu_custom_call" | custom-call | tf_op jit(solution)/shard_map/rank/pallas_call | solution.py:91
  122.5 6.5 %collective-permute-start.13 = (f32[3,4,256,256]{3,2,1,0:T(8,128)}, f32[3,4,256,256]{3,2,1,0:T(8,128)}, u32[]{:S(2)}, u32[]{:S(2)}) collective-permute-start(f32[3,4,256,256]{3,2,1,0:T(8,128)} %get-tuple-element.59), channel_id=1, source_target_pairs={{0,2},{1,3},{2,0},{3,1},{4,6},{5,7},{6,4},{7,5},{8,10},{9,11},{10,... | collective-permute-start | bytes 9437192 | tf_op jit(solution)/shard_map/ppermute | solution.py:581
  129.0 13.8 %exp_bwd.10 = (bf16[24576,256]{1,0:T(8,128)(2,1)}, f32[3,8,256,256]{3,2,1,0:T(8,128)}) custom-call(s32[1]{0:T(128)} %bitcast.15.first_ref, s32[8,128]{1,0:T(8,128)} %bitcast.67, bf16[24576,256]{1,0:T(8,128)(2,1)} %get-tuple-element.43.xs_hbm, bf16[24576,256]{1,0:T(8,128)(2,1)} %get-tuple-element.38.qs_hbm, ...), custom_call_target="tpu_custom_call", output_to_operand_aliasing={{0}: (2, {})} | custom-call | flops 8000000000 | bytes 20000000 | tf_op jit(solution)/shard_map/exp_bwd/pallas_call | solution.py:371
  144.4 8.3 %exp_bwd.11 = (bf16[24576,256]{1,0:T(8,128)(2,1)}, f32[3,4,256,256]{3,2,1,0:T(8,128)}) custom-call(s32[1]{0:T(128)} %bitcast.14.first_ref, s32[8,128]{1,0:T(8,128)} %bitcast.68, bf16[24576,256]{1,0:T(8,128)(2,1)} %get-tuple-element.45.xs_hbm, bf16[24576,256]{1,0:T(8,128)(2,1)} %get-tuple-element.38.qs_hbm, ...), custom_call_target="tpu_custom_call", output_to_operand_aliasing={{0}: (2, {})} | custom-call | flops 8000000000 | bytes 20000000 | tf_op jit(solution)/shard_map/exp_bwd/pallas_call | solution.py:371
  152.7 4.5 %collective-permute-start.14 = (f32[3,4,256,256]{3,2,1,0:T(8,128)}, f32[3,4,256,256]{3,2,1,0:T(8,128)}, u32[]{:S(2)}, u32[]{:S(2)}) collective-permute-start(f32[3,4,256,256]{3,2,1,0:T(8,128)} %get-tuple-element.60), channel_id=1, source_target_pairs={{0,2},{1,3},{2,0},{3,1},{4,6},{5,7},{6,4},{7,5},{8,10},{9,11},{10,... | collective-permute-start | bytes 9437192 | tf_op jit(solution)/shard_map/ppermute | solution.py:581
  157.2 20.5 %post_bwd.2 = bf16[3072,256]{1,0:T(8,128)(2,1)} custom-call(s32[16384]{0:T(1024)} %bitcast.89, s32[16384]{0:T(1024)} %bitcast.90, s32[16384]{0:T(1024)} %bitcast.91, s32[16384]{0:T(1024)} %bitcast.92, s32[8,128]{1,0:T(8,128)} %bitcast.69, bf16[4096,256]{1,0:T(8,128)(2,1)} %bitcast.74, bf16[4096,256]{1,0:T(8,128)(2,1)} %bitcast.77, ...), custom_call_target="tpu_custom_call" | custom-call | flops 30000001024 | bytes 30000000 | tf_op jit(solution)/shard_map/post_bwd/pallas_call | solution.py:440
  177.7 28.6 %fwd.2 = bf16[2048,256]{1,0:T(8,128)(2,1)} custom-call(s32[8192]{0:T(1024)} %bitcast.112, s32[8192]{0:T(1024)} %bitcast.113, s32[8192]{0:T(1024)} %bitcast.114, s32[8192]{0:T(1024)} %bitcast.115, s32[8192]{0:T(1024)} %bitcast.116, s32[8192]{0:T(1024)} %bitcast.117, s32[8192]{0:T(1024)} %bitcast.118, s32[8192]{0:T(1024)} %bitcast.119, s32[8]{0:T(128)} %stack.49.refs_8_, ...), custom_call_target="tpu_custom_call" | custom-call | flops 80000000000 | bytes 30000000 | tf_op jit(solution)/shard_map/fwd/pallas_call | solution.py:544
  206.3 27.9 %fwd.3 = bf16[2048,256]{1,0:T(8,128)(2,1)} custom-call(s32[8192]{0:T(1024)} %bitcast.104, s32[8192]{0:T(1024)} %bitcast.105, s32[8192]{0:T(1024)} %bitcast.106, s32[8192]{0:T(1024)} %bitcast.107, s32[8192]{0:T(1024)} %bitcast.108, s32[8192]{0:T(1024)} %bitcast.109, s32[8192]{0:T(1024)} %bitcast.110, s32[8192]{0:T(1024)} %bitcast.111, s32[8]{0:T(128)} %stack.49.refs_8_, ...), custom_call_target="tpu_custom_call" | custom-call | flops 80000000000 | bytes 30000000 | tf_op jit(solution)/shard_map/fwd/pallas_call | solution.py:544
  236.3 11.9 %post_bwd.3 = bf16[1024,256]{1,0:T(8,128)(2,1)} custom-call(s32[16384]{0:T(1024)} %bitcast.93, s32[16384]{0:T(1024)} %bitcast.94, s32[16384]{0:T(1024)} %bitcast.95, s32[16384]{0:T(1024)} %bitcast.96, s32[8,128]{1,0:T(8,128)} %bitcast.70, bf16[4096,256]{1,0:T(8,128)(2,1)} %bitcast.75, bf16[4096,256]{1,0:T(8,128)(2,1)} %bitcast.78, ...), custom_call_target="tpu_custom_call" | custom-call | flops 30000001024 | bytes 30000000 | tf_op jit(solution)/shard_map/post_bwd/pallas_call | solution.py:440
  248.2 3.0 collective-permute-start.12
  253.2 41.0 %collective-permute-done.10 = bf16[2048,256]{1,0:T(8,128)(2,1)S(1)} collective-permute-done((bf16[2048,256]{1,0:T(8,128)(2,1)}, bf16[2048,256]{1,0:T(8,128)(2,1)S(1)}, u32[]{:S(2)}, u32[]{:S(2)}) %collective-permute-start.10) | collective-permute-done | bytes 1048608 | tf_op jit(solution)/shard_map/ppermute | solution.py:644
  294.2 22.6 %collective-permute-done.9 = bf16[2048,256]{1,0:T(8,128)(2,1)} collective-permute-done((bf16[2048,256]{1,0:T(8,128)(2,1)}, bf16[2048,256]{1,0:T(8,128)(2,1)}, u32[]{:S(2)}, u32[]{:S(2)}) %collective-permute-start.9) | collective-permute-done | bytes 1048608 | tf_op jit(solution)/shard_map/ppermute | solution.py:644
  316.8 2.8 maximum_bitcast_fusion
  319.6 3.8 %collective-permute-done.12 = bf16[1024,256]{1,0:T(8,128)(2,1)S(1)} collective-permute-done((bf16[1024,256]{1,0:T(8,128)(2,1)}, bf16[1024,256]{1,0:T(8,128)(2,1)S(1)}, u32[]{:S(2)}, u32[]{:S(2)}) %collective-permute-start.12) | collective-permute-done | bytes 524320 | tf_op jit(solution)/shard_map/ppermute | solution.py:644
  327.0 3.0 maximum_add_fusion.2
  (47 shorter events, 19.8 us)
Async XLA Ops:
  0.6 1.5 copy-start.4
  0.6 1.8 copy-start.3
  2.9 65.9 %copy-start = (bf16[4,3,256,256]{3,2,1,0:T(8,128)(2,1)}, bf16[4,3,256,256]{3,2,1,0:T(8,128)(2,1)S(1)}, u32[]{:S(2)}) copy-start(bf16[4,3,256,256]{3,2,1,0:T(8,128)(2,1)S(1)} %pad_maximum_fusion.refs_0_.refs_14_) | copy-start | bytes 4718596
  2.9 38.6 %collective-permute-start = (bf16[4,3,256,256]{3,2,1,0:T(8,128)(2,1)S(1)}, bf16[4,3,256,256]{3,2,1,0:T(8,128)(2,1)}, u32[]{:S(2)}, u32[]{:S(2)}) collective-permute-start(bf16[4,3,256,256]{3,2,1,0:T(8,128)(2,1)S(1)} %pad_maximum_fusion.refs_0_.refs_14_), channel_id=1, source_target_pairs={{0,2},{1,3},{2,0},{3,1},{4,6},{5,7},{6,4},{7,5},{8,10},{9,11},{10,... | collective-permute-start | bytes 4718600 | tf_op jit(solution)/shard_map/ppermute | solution.py:581
  6.1 71.0 %collective-permute-start.2 = (bf16[4,3,256,256]{3,2,1,0:T(8,128)(2,1)S(1)}, bf16[4,3,256,256]{3,2,1,0:T(8,128)(2,1)}, u32[]{:S(2)}, u32[]{:S(2)}) collective-permute-start(bf16[4,3,256,256]{3,2,1,0:T(8,128)(2,1)S(1)} %pad_maximum_fusion.refs_0_.refs_14_), channel_id=1, source_target_pairs={{0,1},{1,0},{2,3},{3,2},{4,5},{5,4},{6,7},{7,6},{8,9},{9,8},{10,11... | collective-permute-start | bytes 4718600 | tf_op jit(solution)/shard_map/ppermute | solution.py:578
  6.3 62.5 %copy-start.1 = (bf16[4,3,256,256]{3,2,1,0:T(8,128)(2,1)}, bf16[4,3,256,256]{3,2,1,0:T(8,128)(2,1)S(1)}, u32[]{:S(2)}) copy-start(bf16[4,3,256,256]{3,2,1,0:T(8,128)(2,1)S(1)} %pad_maximum_fusion.1.refs_1_.refs_15_) | copy-start | bytes 4718596
  6.3 70.8 %collective-permute-start.3 = (bf16[4,3,256,256]{3,2,1,0:T(8,128)(2,1)S(1)}, bf16[4,3,256,256]{3,2,1,0:T(8,128)(2,1)}, u32[]{:S(2)}, u32[]{:S(2)}) collective-permute-start(bf16[4,3,256,256]{3,2,1,0:T(8,128)(2,1)S(1)} %pad_maximum_fusion.1.refs_1_.refs_15_), channel_id=1, source_target_pairs={{0,1},{1,0},{2,3},{3,2},{4,5},{5,4},{6,7},{7,6},{8,9},{9,8},{10,11... | collective-permute-start | bytes 4718600 | tf_op jit(solution)/shard_map/ppermute | solution.py:578
  6.8 88.4 %collective-permute-start.5 = (bf16[4,3,256,256]{3,2,1,0:T(8,128)(2,1)S(1)}, bf16[4,3,256,256]{3,2,1,0:T(8,128)(2,1)}, u32[]{:S(2)}, u32[]{:S(2)}) collective-permute-start(bf16[4,3,256,256]{3,2,1,0:T(8,128)(2,1)S(1)} %pad_maximum_fusion.1.refs_1_.refs_15_), channel_id=1, source_target_pairs={{0,2},{1,3},{2,0},{3,1},{4,6},{5,7},{6,4},{7,5},{8,10},{9,11},{10,... | collective-permute-start | bytes 4718600 | tf_op jit(solution)/shard_map/ppermute | solution.py:581
  41.5 27.4 %collective-permute-start.1 = (bf16[4,3,256,256]{3,2,1,0:T(8,128)(2,1)}, bf16[4,3,256,256]{3,2,1,0:T(8,128)(2,1)}, u32[]{:S(2)}, u32[]{:S(2)}) collective-permute-start(bf16[4,3,256,256]{3,2,1,0:T(8,128)(2,1)} %collective-permute-done.refs_0_.refs_18_), channel_id=1, source_target_pairs={{0,1},{1,0},{2,3},{3,2},{4,5},{5,4},{6,7},{7,6},{8,9},{9,8},{10,11... | collective-permute-start | bytes 4718600 | tf_op jit(solution)/shard_map/ppermute | solution.py:578
  75.2 20.5 %collective-permute-start.4 = (f32[3,4,256,256]{3,2,1,0:T(8,128)}, f32[3,4,256,256]{3,2,1,0:T(8,128)}, u32[]{:S(2)}, u32[]{:S(2)}) collective-permute-start(f32[3,4,256,256]{3,2,1,0:T(8,128)} %get-tuple-element.41), channel_id=1, source_target_pairs={{0,1},{1,0},{2,3},{3,2},{4,5},{5,4},{6,7},{7,6},{8,9},{9,8},{10,11... | collective-permute-start | bytes 9437192 | tf_op jit(solution)/shard_map/ppermute | solution.py:578
  95.2 33.8 %collective-permute-start.7 = (f32[3,8,256,256]{3,2,1,0:T(8,128)}, f32[3,8,256,256]{3,2,1,0:T(8,128)}, u32[]{:S(2)}, u32[]{:S(2)}) collective-permute-start(f32[3,8,256,256]{3,2,1,0:T(8,128)} %get-tuple-element.44), channel_id=1, source_target_pairs={{0,1},{1,0},{2,3},{3,2},{4,5},{5,4},{6,7},{7,6},{8,9},{9,8},{10,11... | collective-permute-start | bytes 18874376 | tf_op jit(solution)/shard_map/ppermute | solution.py:578
  95.2 12.6 %collective-permute-start.6 = (bf16[4,3,256,256]{3,2,1,0:T(8,128)(2,1)}, bf16[4,3,256,256]{3,2,1,0:T(8,128)(2,1)S(1)}, u32[]{:S(2)}, u32[]{:S(2)}) collective-permute-start(bf16[4,3,256,256]{3,2,1,0:T(8,128)(2,1)} %collective-permute-done.5.refs_0_.refs_19_), channel_id=1, source_target_pairs={{0,1},{1,0},{2,3},{3,2},{4,5},{5,4},{6,7},{7,6},{8,9},{9,8},{10,11... | collective-permute-start | bytes 4718600 | tf_op jit(solution)/shard_map/ppermute | solution.py:578
  107.8 1.1 copy-start.5
  114.1 28.6 %collective-permute-start.8 = (f32[3,4,256,256]{3,2,1,0:T(8,128)}, f32[3,4,256,256]{3,2,1,0:T(8,128)S(1)}, u32[]{:S(2)}, u32[]{:S(2)}) collective-permute-start(f32[3,4,256,256]{3,2,1,0:T(8,128)} %get-tuple-element.46), channel_id=1, source_target_pairs={{0,1},{1,0},{2,3},{3,2},{4,5},{5,4},{6,7},{7,6},{8,9},{9,8},{10,11... | collective-permute-start | bytes 9437192 | tf_op jit(solution)/shard_map/ppermute | solution.py:578
  122.5 125.7 %collective-permute-start.13 = (f32[3,4,256,256]{3,2,1,0:T(8,128)}, f32[3,4,256,256]{3,2,1,0:T(8,128)}, u32[]{:S(2)}, u32[]{:S(2)}) collective-permute-start(f32[3,4,256,256]{3,2,1,0:T(8,128)} %get-tuple-element.59), channel_id=1, source_target_pairs={{0,2},{1,3},{2,0},{3,1},{4,6},{5,7},{6,4},{7,5},{8,10},{9,11},{10,... | collective-permute-start | bytes 9437192 | tf_op jit(solution)/shard_map/ppermute | solution.py:581
  142.8 1.6 copy-start.2
  152.7 172.2 %collective-permute-start.14 = (f32[3,4,256,256]{3,2,1,0:T(8,128)}, f32[3,4,256,256]{3,2,1,0:T(8,128)}, u32[]{:S(2)}, u32[]{:S(2)}) collective-permute-start(f32[3,4,256,256]{3,2,1,0:T(8,128)} %get-tuple-element.60), channel_id=1, source_target_pairs={{0,2},{1,3},{2,0},{3,1},{4,6},{5,7},{6,4},{7,5},{8,10},{9,11},{10,... | collective-permute-start | bytes 9437192 | tf_op jit(solution)/shard_map/ppermute | solution.py:581
  234.2 89.3 %collective-permute-start.11 = (bf16[3072,256]{1,0:T(8,128)(2,1)}, bf16[3072,256]{1,0:T(8,128)(2,1)S(1)}, u32[]{:S(2)}, u32[]{:S(2)}) collective-permute-start(bf16[3072,256]{1,0:T(8,128)(2,1)} %post_bwd.2), channel_id=1, source_target_pairs={{0,12},{4,0},{8,4},{12,8},{1,13},{5,1},{9,5},{13,9},{2,14},{6,2},{... | collective-permute-start | bytes 4718600 | tf_op jit(solution)/shard_map/ppermute | solution.py:644
  236.3 57.9 %collective-permute-start.10 = (bf16[2048,256]{1,0:T(8,128)(2,1)}, bf16[2048,256]{1,0:T(8,128)(2,1)S(1)}, u32[]{:S(2)}, u32[]{:S(2)}) collective-permute-start(bf16[2048,256]{1,0:T(8,128)(2,1)} %fwd.3), channel_id=1, source_target_pairs={{0,4},{4,8},{8,12},{12,0},{1,5},{5,9},{9,13},{13,1},{2,6},{6,10},{... | collective-permute-start | bytes 3145736 | tf_op jit(solution)/shard_map/ppermute | solution.py:644
  236.3 80.5 %collective-permute-start.9 = (bf16[2048,256]{1,0:T(8,128)(2,1)}, bf16[2048,256]{1,0:T(8,128)(2,1)}, u32[]{:S(2)}, u32[]{:S(2)}) collective-permute-start(bf16[2048,256]{1,0:T(8,128)(2,1)} %fwd.2), channel_id=1, source_target_pairs={{0,4},{4,8},{8,12},{12,0},{1,5},{5,9},{9,13},{13,1},{2,6},{6,10},{... | collective-permute-start | bytes 3145736 | tf_op jit(solution)/shard_map/ppermute | solution.py:644
  248.2 75.3 %collective-permute-start.12 = (bf16[1024,256]{1,0:T(8,128)(2,1)}, bf16[1024,256]{1,0:T(8,128)(2,1)S(1)}, u32[]{:S(2)}, u32[]{:S(2)}) collective-permute-start(bf16[1024,256]{1,0:T(8,128)(2,1)} %post_bwd.3), channel_id=1, source_target_pairs={{0,12},{4,0},{8,4},{12,8},{1,13},{5,1},{9,5},{13,9},{2,14},{6,2},{... | collective-permute-start | bytes 1572872 | tf_op jit(solution)/shard_map/ppermute | solution.py:644
  316.8 10.2 %slice-start = ((s8[6291456]{0:T(1024)(128)(4,1)}), s8[4194304]{0:T(1024)(128)(4,1)S(1)}, s32[]{:S(2)}) async-start(s8[6291456]{0:T(1024)(128)(4,1)} %bitcast.56), calls=%async_computation | async-start | bytes 8388608
  319.6 7.4 %slice-start.1 = ((s8[6291456]{0:T(1024)(128)(4,1)}), s8[2097152]{0:T(1024)(128)(4,1)S(1)}, s32[]{:S(2)}) async-start(s8[6291456]{0:T(1024)(128)(4,1)} %bitcast.56), calls=%async_computation.1 | async-start | bytes 4194304

commit v11 on v10

--- a/solution.py
+++ b/solution.py
@@ -13,8 +13,8 @@
 BT = 512
 DEPTH = 4
 QUEUE = 8
-FWD_BLOCKS = (4, 4)
-POST_BLOCKS = (6, 2)
+FWD_BLOCKS = (5, 3)
+POST_BLOCKS = (4, 4)
 F32 = jnp.float32
 BF16 = jnp.bfloat16
 VMEM_LIMIT = 60 * 1024 * 1024
@@ -629,29 +629,29 @@
         xs, dw_own = experts("own", xs, (near_sum,))
         xs, part = experts("far1", xs, (far_sum,))
         there.append(chip(part))
+
+        def chained(calls, perm, blocks_of, x_in):
+            pieces, skip = [], 0
+            for h, blocks in enumerate(blocks_of):
+                piece = calls(h, blocks, skip, x_in)
+                skip += blocks
+                x_in, piece = lax.optimization_barrier((x_in, piece))
+                pieces.append(lax.ppermute(piece, "pp", perm))
+            return pieces, x_in
+
+        def post_part(h, blocks, skip, x_in):
+            return post_bwd(blocks, skip, pos2_b, tab_b, x_saved, grad_in, h_bwd, w1, w2, x_in, n_exp, top_k)
+
+        dx_parts, xs = chained(post_part, prev_perm, POST_BLOCKS, xs)
+        x_fwd, xs = lax.optimization_barrier((x_fwd, xs))
+
         firsts = jnp.stack([first + i * half for first, ws in groups.values() for i in range(len(ws))])
         weights = [w for _, ws in groups.values() for w in ws]
 
-        def post_part(h, rs):
-            blocks, skip = POST_BLOCKS[h], sum(POST_BLOCKS[:h])
-            return post_bwd(blocks, skip, pos2_b, tab_b, x_saved, grad_in, h_bwd, w1, w2, rs, n_exp, top_k)
-
-        def fwd_part(h, x_in):
-            blocks, skip = FWD_BLOCKS[h], sum(FWD_BLOCKS[:h])
+        def fwd_part(h, blocks, skip, x_in):
             return fwd(blocks, skip, firsts, tab_f[h], pos2_f[h], gates_f, x_in, w1, w2, weights, rows_f[h], n_exp, top_k)
 
-        def send(piece, perm):
-            return lax.ppermute(piece, "pp", perm)
-
-        dx_parts, parts = [], []
-        piece = post_part(0, xs)
-        x_fwd, piece = lax.optimization_barrier((x_fwd, piece))
-        dx_parts.append(send(piece, prev_perm))
-        for h in range(len(FWD_BLOCKS)):
-            piece = fwd_part(h, x_fwd)
-            x_fwd, xs, piece = lax.optimization_barrier((x_fwd, xs, piece))
-            parts.append(send(piece, next_perm))
-        dx_parts.append(send(post_part(1, xs), prev_perm))
+        parts, _ = chained(fwd_part, next_perm, FWD_BLOCKS, x_fwd)
         y_next = jnp.concatenate(parts, axis=0)[None]
         dws = [(dw_own[i] + jnp.concatenate([sums[i] for sums in there], axis=0))[None] for i in range(3)]
         dx_prev = jnp.concatenate(dx_parts, axis=0)[None]

time: 332 us -> 359 us (1.081)
  the two profiles are of different devices: /device:TPU:0 before, /device:TPU:4 now
where the time goes in v11:
time: 359 us; the launch traced here: 357 us
  Pallas kernels  183 us (51%)
  waiting for transfers between devices  137 us (38%)
  starting transfers between devices  22.8 us (6%)
  other arithmetic  7.78 us (2%)
  local copies, waits for them, and re-layouts  6.24 us (2%)
    ppermute x4, waiting for transfers between devices, chip(): return lax.ppermute(a, 'ep', chip_perm)  103 us
    pallas_call x6, Pallas kernels, exp_bwd(): pl.pallas_call(functools.partial(exp_bwd_kernel, n_parts=len(weights), ha...  62 us
    pallas_call x2, Pallas kernels, fwd(): pl.pallas_call(functools.partial(fwd_kernel, n_blocks=n_blocks, top_k=top...  54.6 us
    ppermute x4, waiting for transfers between devices, chained(): pieces.append(lax.ppermute(piece, 'pp', perm))  33.5 us
    pallas_call x2, Pallas kernels, post_bwd(): pl.pallas_call(functools.partial(post_bwd_kernel, n_blocks=n_blocks, top_...  32.4 us
    pallas_call x1, Pallas kernels, pre_bwd(): pl.pallas_call(functools.partial(pre_bwd_kernel, n_blocks=n_blocks, top_k...  27.3 us
    ppermute x4, starting transfers between devices, chained(): pieces.append(lax.ppermute(piece, 'pp', perm))  13.6 us
  transfers between devices with their start and end apart: 15, of which 6 were waited for; matrix products, arithmetic and copies ran while one was open for 2% of the time, Pallas kernels for 51%

profile of v11, /device:TPU:4, one launch (start us, length us, event | category | flops | bytes accessed | tf_op | source)
XLA Modules:
  0.0 357.4 jit_solution(2199074622055421372)
XLA Ops:
  5.7 3.2 rank.3
  8.9 31.4 %collective-permute-done.2.refs_18_.refs_0_ = bf16[4,3,256,256]{3,2,1,0:T(8,128)(2,1)} collective-permute-done((bf16[4,3,256,256]{3,2,1,0:T(8,128)(2,1)S(1)}, bf16[4,3,256,256]{3,2,1,0:T(8,128)(2,1)}, u32[]{:S(2)}, u32[]{:S(2)}) %collective-permute-start.2) | collective-permute-done | bytes 1572896 | tf_op jit(solution)/shard_map/ppermute | solution.py:581
  40.3 32.6 %collective-permute-done.3.refs_19_.refs_0_ = bf16[4,3,256,256]{3,2,1,0:T(8,128)(2,1)} collective-permute-done((bf16[4,3,256,256]{3,2,1,0:T(8,128)(2,1)S(1)}, bf16[4,3,256,256]{3,2,1,0:T(8,128)(2,1)}, u32[]{:S(2)}, u32[]{:S(2)}) %collective-permute-start.3) | collective-permute-done | bytes 1572896 | tf_op jit(solution)/shard_map/ppermute | solution.py:581
  72.9 27.3 %pre_bwd.1 = (bf16[4096,256]{1,0:T(8,128)(2,1)}, bf16[24576,256]{1,0:T(8,128)(2,1)}, bf16[24576,256]{1,0:T(8,128)(2,1)}) custom-call(s32[16384]{0:T(1024)} %bitcast.97, s32[16384]{0:T(1024)} %bitcast.98, s32[16384]{0:T(1024)} %bitcast.99, s32[16384]{0:T(1024)} %bitcast.100, s32[8,128]{1,0:T(8,128)} %bitcast.62, bf16[4,4096]{1,0:T(4,128)(2,1)} %bitcast.109, ...), custom_call_target="tpu_custom_call" | custom-call | flops 30000001024 | bytes 30000000 | tf_op jit(solution)/shard_map/pre_bwd/pallas_call | solution.py:224
  100.2 3.4 rank.2
  105.5 5.2 %exp_bwd.6 = (bf16[24576,256]{1,0:T(8,128)(2,1)}, f32[3,4,256,256]{3,2,1,0:T(8,128)}) custom-call(s32[1]{0:T(128)} %bitcast.12.first_ref, s32[8,128]{1,0:T(8,128)} %bitcast.63, bf16[24576,256]{1,0:T(8,128)(2,1)} %get-tuple-element.40.xs_hbm, bf16[24576,256]{1,0:T(8,128)(2,1)} %get-tuple-element.41.qs_hbm, ...), custom_call_target="tpu_custom_call", output_to_operand_aliasing={{0}: (2, {})} | custom-call | flops 8000000000 | bytes 20000000 | tf_op jit(solution)/shard_map/exp_bwd/pallas_call | solution.py:371
  110.7 2.8 collective-permute-start.8
  113.5 32.9 %fwd.2 = bf16[2560,256]{1,0:T(8,128)(2,1)} custom-call(s32[10240]{0:T(1024)} %bitcast.101, s32[10240]{0:T(1024)} %bitcast.102, s32[10240]{0:T(1024)} %bitcast.103, s32[10240]{0:T(1024)} %bitcast.104, s32[10240]{0:T(1024)} %bitcast.105, s32[10240]{0:T(1024)} %bitcast.106, s32[10240]{0:T(1024)} %bitcast.107, s32[10240]{0:T(1024)} %bitcast.108, ...), custom_call_target="tpu_custom_call" | custom-call | flops 80000000000 | bytes 30000000 | tf_op jit(solution)/shard_map/fwd/pallas_call | solution.py:544
  146.5 15.3 %exp_bwd.7 = (bf16[24576,256]{1,0:T(8,128)(2,1)}, f32[3,8,256,256]{3,2,1,0:T(8,128)}) custom-call(s32[1]{0:T(128)} %bitcast.8.first_ref, s32[8,128]{1,0:T(8,128)} %bitcast.64, bf16[24576,256]{1,0:T(8,128)(2,1)} %get-tuple-element.42.xs_hbm, bf16[24576,256]{1,0:T(8,128)(2,1)} %get-tuple-element.41.qs_hbm, ...), custom_call_target="tpu_custom_call", output_to_operand_aliasing={{0}: (2, {})} | custom-call | flops 8000000000 | bytes 20000000 | tf_op jit(solution)/shard_map/exp_bwd/pallas_call | solution.py:371
  161.8 2.7 collective-permute-start.9
  164.5 7.8 %exp_bwd.8 = (bf16[24576,256]{1,0:T(8,128)(2,1)}, f32[3,4,256,256]{3,2,1,0:T(8,128)}) custom-call(s32[1]{0:T(128)} %bitcast.10.first_ref, s32[8,128]{1,0:T(8,128)} %bitcast.65, bf16[24576,256]{1,0:T(8,128)(2,1)} %get-tuple-element.43.xs_hbm, bf16[24576,256]{1,0:T(8,128)(2,1)} %get-tuple-element.41.qs_hbm, ...), custom_call_target="tpu_custom_call", output_to_operand_aliasing={{0}: (2, {})} | custom-call | flops 8000000000 | bytes 20000000 | tf_op jit(solution)/shard_map/exp_bwd/pallas_call | solution.py:371
  172.3 8.2 %exp_bwd.9 = (bf16[24576,256]{1,0:T(8,128)(2,1)}, f32[3,4,256,256]{3,2,1,0:T(8,128)}) custom-call(s32[1]{0:T(128)} %bitcast.13.first_ref, s32[8,128]{1,0:T(8,128)} %bitcast.66, bf16[24576,256]{1,0:T(8,128)(2,1)} %get-tuple-element.45.xs_hbm, bf16[24576,256]{1,0:T(8,128)(2,1)} %get-tuple-element.41.qs_hbm, ...), custom_call_target="tpu_custom_call", output_to_operand_aliasing={{0}: (2, {})} | custom-call | flops 8000000000 | bytes 20000000 | tf_op jit(solution)/shard_map/exp_bwd/pallas_call | solution.py:371
  180.6 21.6 %fwd.3 = bf16[1536,256]{1,0:T(8,128)(2,1)} custom-call(s32[6144]{0:T(1024)} %bitcast.112, s32[6144]{0:T(1024)} %bitcast.113, s32[6144]{0:T(1024)} %bitcast.114, s32[6144]{0:T(1024)} %bitcast.115, s32[6144]{0:T(1024)} %bitcast.116, s32[6144]{0:T(1024)} %bitcast.117, s32[6144]{0:T(1024)} %bitcast.118, s32[6144]{0:T(1024)} %bitcast.119, s32[8]{0:T(128)} %stack.41.refs_8_, ...), custom_call_target="tpu_custom_call" | custom-call | flops 80000000000 | bytes 30000000 | tf_op jit(solution)/shard_map/fwd/pallas_call | solution.py:544
  202.3 12.9 %collective-permute-start.6 = (bf16[2560,256]{1,0:T(8,128)(2,1)}, bf16[2560,256]{1,0:T(8,128)(2,1)}, u32[]{:S(2)}, u32[]{:S(2)}) collective-permute-start(bf16[2560,256]{1,0:T(8,128)(2,1)} %fwd.2), channel_id=1, source_target_pairs={{0,4},{4,8},{8,12},{12,0},{1,5},{5,9},{9,13},{13,1},{2,6},{6,10},{... | collective-permute-start | bytes 3932168 | tf_op jit(solution)/shard_map/ppermute | solution.py:639
  215.1 19.5 %exp_bwd.10 = (bf16[24576,256]{1,0:T(8,128)(2,1)}, f32[3,8,256,256]{3,2,1,0:T(8,128)}) custom-call(s32[1]{0:T(128)} %bitcast.6.first_ref, s32[8,128]{1,0:T(8,128)} %bitcast.67, bf16[24576,256]{1,0:T(8,128)(2,1)} %get-tuple-element.46.xs_hbm, bf16[24576,256]{1,0:T(8,128)(2,1)} %get-tuple-element.41.qs_hbm, ...), custom_call_target="tpu_custom_call", output_to_operand_aliasing={{0}: (2, {})} | custom-call | flops 8000000000 | bytes 20000000 | tf_op jit(solution)/shard_map/exp_bwd/pallas_call | solution.py:371
  234.7 6.1 %exp_bwd.11 = (bf16[24576,256]{1,0:T(8,128)(2,1)}, f32[3,4,256,256]{3,2,1,0:T(8,128)}) custom-call(s32[1]{0:T(128)} %bitcast.11.first_ref, s32[8,128]{1,0:T(8,128)} %bitcast.68, bf16[24576,256]{1,0:T(8,128)(2,1)} %get-tuple-element.48.xs_hbm, bf16[24576,256]{1,0:T(8,128)(2,1)} %get-tuple-element.41.qs_hbm, ...), custom_call_target="tpu_custom_call", output_to_operand_aliasing={{0}: (2, {})} | custom-call | flops 8000000000 | bytes 20000000 | tf_op jit(solution)/shard_map/exp_bwd/pallas_call | solution.py:371
  240.8 16.2 %post_bwd.2 = bf16[2048,256]{1,0:T(8,128)(2,1)} custom-call(s32[16384]{0:T(1024)} %bitcast.89, s32[16384]{0:T(1024)} %bitcast.90, s32[16384]{0:T(1024)} %bitcast.91, s32[16384]{0:T(1024)} %bitcast.92, s32[8,128]{1,0:T(8,128)} %bitcast.69, bf16[4096,256]{1,0:T(8,128)(2,1)} %bitcast.74, bf16[4096,256]{1,0:T(8,128)(2,1)} %bitcast.77, ...), custom_call_target="tpu_custom_call" | custom-call | flops 30000001024 | bytes 30000000 | tf_op jit(solution)/shard_map/post_bwd/pallas_call | solution.py:440
  258.0 16.2 %post_bwd.3 = bf16[2048,256]{1,0:T(8,128)(2,1)} custom-call(s32[16384]{0:T(1024)} %bitcast.93, s32[16384]{0:T(1024)} %bitcast.94, s32[16384]{0:T(1024)} %bitcast.95, s32[16384]{0:T(1024)} %bitcast.96, s32[8,128]{1,0:T(8,128)} %bitcast.70, bf16[4096,256]{1,0:T(8,128)(2,1)} %bitcast.75, bf16[4096,256]{1,0:T(8,128)(2,1)} %bitcast.78, ...), custom_call_target="tpu_custom_call" | custom-call | flops 30000001024 | bytes 30000000 | tf_op jit(solution)/shard_map/post_bwd/pallas_call | solution.py:440
  274.9 3.0 maximum_bitcast_fusion
  277.9 8.4 %collective-permute-done.13 = f32[3,4,256,256]{3,2,1,0:T(8,128)S(1)} collective-permute-done((f32[3,4,256,256]{3,2,1,0:T(8,128)}, f32[3,4,256,256]{3,2,1,0:T(8,128)S(1)}, u32[]{:S(2)}, u32[]{:S(2)}) %collective-permute-start.13) | collective-permute-done | bytes 3145760 | tf_op jit(solution)/shard_map/ppermute | solution.py:581
  286.5 14.8 %collective-permute-done.12 = bf16[2048,256]{1,0:T(8,128)(2,1)S(1)} collective-permute-done((bf16[2048,256]{1,0:T(8,128)(2,1)}, bf16[2048,256]{1,0:T(8,128)(2,1)S(1)}, u32[]{:S(2)}, u32[]{:S(2)}) %collective-permute-start.12) | collective-permute-done | bytes 1048608 | tf_op jit(solution)/shard_map/ppermute | solution.py:639
  301.4 18.7 %collective-permute-done.11 = bf16[2048,256]{1,0:T(8,128)(2,1)S(1)} collective-permute-done((bf16[2048,256]{1,0:T(8,128)(2,1)}, bf16[2048,256]{1,0:T(8,128)(2,1)S(1)}, u32[]{:S(2)}, u32[]{:S(2)}) %collective-permute-start.11) | collective-permute-done | bytes 1048608 | tf_op jit(solution)/shard_map/ppermute | solution.py:639
  321.5 30.8 %collective-permute-done.14 = f32[3,4,256,256]{3,2,1,0:T(8,128)} collective-permute-done((f32[3,4,256,256]{3,2,1,0:T(8,128)}, f32[3,4,256,256]{3,2,1,0:T(8,128)}, u32[]{:S(2)}, u32[]{:S(2)}) %collective-permute-start.14) | collective-permute-done | bytes 3145760 | tf_op jit(solution)/shard_map/ppermute | solution.py:581
  354.4 3.0 maximum_add_fusion.2
  (43 shorter events, 12.5 us)
Async XLA Ops:
  0.6 1.5 copy-start.2
  0.6 1.8 copy-start.3
  2.9 97.3 %copy-start = (bf16[4,3,256,256]{3,2,1,0:T(8,128)(2,1)}, bf16[4,3,256,256]{3,2,1,0:T(8,128)(2,1)S(1)}, u32[]{:S(2)}) copy-start(bf16[4,3,256,256]{3,2,1,0:T(8,128)(2,1)S(1)} %pad_maximum_fusion.refs_14_.refs_0_) | copy-start | bytes 4718596
  2.9 37.4 %collective-permute-start.2 = (bf16[4,3,256,256]{3,2,1,0:T(8,128)(2,1)S(1)}, bf16[4,3,256,256]{3,2,1,0:T(8,128)(2,1)}, u32[]{:S(2)}, u32[]{:S(2)}) collective-permute-start(bf16[4,3,256,256]{3,2,1,0:T(8,128)(2,1)S(1)} %pad_maximum_fusion.refs_14_.refs_0_), channel_id=1, source_target_pairs={{0,2},{1,3},{2,0},{3,1},{4,6},{5,7},{6,4},{7,5},{8,10},{9,11},{10,... | collective-permute-start | bytes 4718600 | tf_op jit(solution)/shard_map/ppermute | solution.py:581
  4.6 95.6 %copy-start.1 = (bf16[4,3,256,256]{3,2,1,0:T(8,128)(2,1)}, bf16[4,3,256,256]{3,2,1,0:T(8,128)(2,1)S(1)}, u32[]{:S(2)}) copy-start(bf16[4,3,256,256]{3,2,1,0:T(8,128)(2,1)S(1)} %pad_maximum_fusion.1.refs_15_.refs_1_) | copy-start | bytes 4718596
  4.6 68.3 %collective-permute-start.3 = (bf16[4,3,256,256]{3,2,1,0:T(8,128)(2,1)S(1)}, bf16[4,3,256,256]{3,2,1,0:T(8,128)(2,1)}, u32[]{:S(2)}, u32[]{:S(2)}) collective-permute-start(bf16[4,3,256,256]{3,2,1,0:T(8,128)(2,1)S(1)} %pad_maximum_fusion.1.refs_15_.refs_1_), channel_id=1, source_target_pairs={{0,2},{1,3},{2,0},{3,1},{4,6},{5,7},{6,4},{7,5},{8,10},{9,11},{10,... | collective-permute-start | bytes 4718600 | tf_op jit(solution)/shard_map/ppermute | solution.py:581
  5.2 108.3 %collective-permute-start = (bf16[4,3,256,256]{3,2,1,0:T(8,128)(2,1)S(1)}, bf16[4,3,256,256]{3,2,1,0:T(8,128)(2,1)}, u32[]{:S(2)}, u32[]{:S(2)}) collective-permute-start(bf16[4,3,256,256]{3,2,1,0:T(8,128)(2,1)S(1)} %pad_maximum_fusion.refs_14_.refs_0_), channel_id=1, source_target_pairs={{0,1},{1,0},{2,3},{3,2},{4,5},{5,4},{6,7},{7,6},{8,9},{9,8},{10,11... | collective-permute-start | bytes 4718600 | tf_op jit(solution)/shard_map/ppermute | solution.py:578
  5.2 108.3 %collective-permute-start.1 = (bf16[4,3,256,256]{3,2,1,0:T(8,128)(2,1)S(1)}, bf16[4,3,256,256]{3,2,1,0:T(8,128)(2,1)}, u32[]{:S(2)}, u32[]{:S(2)}) collective-permute-start(bf16[4,3,256,256]{3,2,1,0:T(8,128)(2,1)S(1)} %pad_maximum_fusion.1.refs_15_.refs_1_), channel_id=1, source_target_pairs={{0,1},{1,0},{2,3},{3,2},{4,5},{5,4},{6,7},{7,6},{8,9},{9,8},{10,11... | collective-permute-start | bytes 4718600 | tf_op jit(solution)/shard_map/ppermute | solution.py:578
  40.3 65.3 %collective-permute-start.4 = (bf16[4,3,256,256]{3,2,1,0:T(8,128)(2,1)}, bf16[4,3,256,256]{3,2,1,0:T(8,128)(2,1)}, u32[]{:S(2)}, u32[]{:S(2)}) collective-permute-start(bf16[4,3,256,256]{3,2,1,0:T(8,128)(2,1)} %collective-permute-done.2.refs_18_.refs_0_), channel_id=1, source_target_pairs={{0,1},{1,0},{2,3},{3,2},{4,5},{5,4},{6,7},{7,6},{8,9},{9,8},{10,11... | collective-permute-start | bytes 4718600 | tf_op jit(solution)/shard_map/ppermute | solution.py:578
  72.9 40.7 %collective-permute-start.5 = (bf16[4,3,256,256]{3,2,1,0:T(8,128)(2,1)}, bf16[4,3,256,256]{3,2,1,0:T(8,128)(2,1)}, u32[]{:S(2)}, u32[]{:S(2)}) collective-permute-start(bf16[4,3,256,256]{3,2,1,0:T(8,128)(2,1)} %collective-permute-done.3.refs_19_.refs_0_), channel_id=1, source_target_pairs={{0,1},{1,0},{2,3},{3,2},{4,5},{5,4},{6,7},{7,6},{8,9},{9,8},{10,11... | collective-permute-start | bytes 4718600 | tf_op jit(solution)/shard_map/ppermute | solution.py:578
  110.7 53.8 %collective-permute-start.8 = (f32[3,4,256,256]{3,2,1,0:T(8,128)}, f32[3,4,256,256]{3,2,1,0:T(8,128)}, u32[]{:S(2)}, u32[]{:S(2)}) collective-permute-start(f32[3,4,256,256]{3,2,1,0:T(8,128)} %get-tuple-element.44), channel_id=1, source_target_pairs={{0,1},{1,0},{2,3},{3,2},{4,5},{5,4},{6,7},{7,6},{8,9},{9,8},{10,11... | collective-permute-start | bytes 9437192 | tf_op jit(solution)/shard_map/ppermute | solution.py:578
  161.8 53.4 %collective-permute-start.9 = (f32[3,8,256,256]{3,2,1,0:T(8,128)}, f32[3,8,256,256]{3,2,1,0:T(8,128)}, u32[]{:S(2)}, u32[]{:S(2)}) collective-permute-start(f32[3,8,256,256]{3,2,1,0:T(8,128)} %get-tuple-element.47), channel_id=1, source_target_pairs={{0,1},{1,0},{2,3},{3,2},{4,5},{5,4},{6,7},{7,6},{8,9},{9,8},{10,11... | collective-permute-start | bytes 18874376 | tf_op jit(solution)/shard_map/ppermute | solution.py:578
  180.5 54.2 %collective-permute-start.10 = (f32[3,4,256,256]{3,2,1,0:T(8,128)}, f32[3,4,256,256]{3,2,1,0:T(8,128)}, u32[]{:S(2)}, u32[]{:S(2)}) collective-permute-start(f32[3,4,256,256]{3,2,1,0:T(8,128)} %get-tuple-element.49), channel_id=1, source_target_pairs={{0,1},{1,0},{2,3},{3,2},{4,5},{5,4},{6,7},{7,6},{8,9},{9,8},{10,11... | collective-permute-start | bytes 9437192 | tf_op jit(solution)/shard_map/ppermute | solution.py:578
  202.2 72.0 %collective-permute-start.7 = (bf16[1536,256]{1,0:T(8,128)(2,1)}, bf16[1536,256]{1,0:T(8,128)(2,1)}, u32[]{:S(2)}, u32[]{:S(2)}) collective-permute-start(bf16[1536,256]{1,0:T(8,128)(2,1)} %fwd.3), channel_id=1, source_target_pairs={{0,4},{4,8},{8,12},{12,0},{1,5},{5,9},{9,13},{13,1},{2,6},{6,10},{... | collective-permute-start | bytes 2359304 | tf_op jit(solution)/shard_map/ppermute | solution.py:639
  202.3 72.6 %collective-permute-start.6 = (bf16[2560,256]{1,0:T(8,128)(2,1)}, bf16[2560,256]{1,0:T(8,128)(2,1)}, u32[]{:S(2)}, u32[]{:S(2)}) collective-permute-start(bf16[2560,256]{1,0:T(8,128)(2,1)} %fwd.2), channel_id=1, source_target_pairs={{0,4},{4,8},{8,12},{12,0},{1,5},{5,9},{9,13},{13,1},{2,6},{6,10},{... | collective-permute-start | bytes 3932168 | tf_op jit(solution)/shard_map/ppermute | solution.py:639
  215.1 71.2 %collective-permute-start.13 = (f32[3,4,256,256]{3,2,1,0:T(8,128)}, f32[3,4,256,256]{3,2,1,0:T(8,128)S(1)}, u32[]{:S(2)}, u32[]{:S(2)}) collective-permute-start(f32[3,4,256,256]{3,2,1,0:T(8,128)} %get-tuple-element.57), channel_id=1, source_target_pairs={{0,2},{1,3},{2,0},{3,1},{4,6},{5,7},{6,4},{7,5},{8,10},{9,11},{10,... | collective-permute-start | bytes 9437192 | tf_op jit(solution)/shard_map/ppermute | solution.py:581
  256.9 95.4 %collective-permute-start.14 = (f32[3,4,256,256]{3,2,1,0:T(8,128)}, f32[3,4,256,256]{3,2,1,0:T(8,128)}, u32[]{:S(2)}, u32[]{:S(2)}) collective-permute-start(f32[3,4,256,256]{3,2,1,0:T(8,128)} %get-tuple-element.58), channel_id=1, source_target_pairs={{0,2},{1,3},{2,0},{3,1},{4,6},{5,7},{6,4},{7,5},{8,10},{9,11},{10,... | collective-permute-start | bytes 9437192 | tf_op jit(solution)/shard_map/ppermute | solution.py:581
  274.2 27.2 %collective-permute-start.12 = (bf16[2048,256]{1,0:T(8,128)(2,1)}, bf16[2048,256]{1,0:T(8,128)(2,1)S(1)}, u32[]{:S(2)}, u32[]{:S(2)}) collective-permute-start(bf16[2048,256]{1,0:T(8,128)(2,1)} %post_bwd.3), channel_id=1, source_target_pairs={{0,12},{4,0},{8,4},{12,8},{1,13},{5,1},{9,5},{13,9},{2,14},{6,2},{... | collective-permute-start | bytes 3145736 | tf_op jit(solution)/shard_map/ppermute | solution.py:639
  274.2 45.8 %collective-permute-start.11 = (bf16[2048,256]{1,0:T(8,128)(2,1)}, bf16[2048,256]{1,0:T(8,128)(2,1)S(1)}, u32[]{:S(2)}, u32[]{:S(2)}) collective-permute-start(bf16[2048,256]{1,0:T(8,128)(2,1)} %post_bwd.2), channel_id=1, source_target_pairs={{0,12},{4,0},{8,4},{12,8},{1,13},{5,1},{9,5},{13,9},{2,14},{6,2},{... | collective-permute-start | bytes 3145736 | tf_op jit(solution)/shard_map/ppermute | solution.py:639
  286.3 68.1 %slice-start = ((s8[6291456]{0:T(1024)(128)(4,1)}), s8[4194304]{0:T(1024)(128)(4,1)S(1)}, s32[]{:S(2)}) async-start(s8[6291456]{0:T(1024)(128)(4,1)} %bitcast.56), calls=%async_computation | async-start | bytes 8388608
  286.5 67.9 %slice-start.1 = ((s8[6291456]{0:T(1024)(128)(4,1)}), s8[2097152]{0:T(1024)(128)(4,1)S(1)}, s32[]{:S(2)}) async-start(s8[6291456]{0:T(1024)(128)(4,1)} %bitcast.56), calls=%async_computation.1 | async-start | bytes 4194304
